TPU v7x, 32 devices: a whole 2x2x4 slice. The times are simulated.
32 devices in a mesh: rep: 4 (over x, core), fsdp: 8 (over z, y).
Axes of the slice: x: 2, y: 2, z: 4, core: 2. Of those that a mesh axis runs over, the one named last changes fastest.
Arguments:
- tokens: bfloat16 [32768, 1024], P(('rep', 'fsdp')), may hold values from -6 to 6
- cotangent: bfloat16 [32768, 1024], P(('rep', 'fsdp')), may hold values from -6 to 6
- segment_ids: int32 [32, 1024], P(('rep', 'fsdp')), may hold values from 0 to 15, never falling along the last dimension, each value on 1 to 512 neighbouring positions
- attention_weight: float32 [4, 1024, 1024], P(None, 'fsdp'), may hold values from -0.375 to 0.375
- attention_momentum: float32 [4, 1024, 1024], P(None, 'fsdp'), may hold values from -0.1875 to 0.1875
- attention_first: float32 [4, 4, 1024, 1024], P('rep', None, 'fsdp'), may hold values from -112 to 112
- attention_second: float32 [4, 4, 1024, 1024], P('rep', None, 'fsdp'), may hold values from 54.8864 to 876.544
- expand_weight: float32 [1024, 4096], P('fsdp'), may hold values from -0.1875 to 0.1875
- expand_momentum: float32 [1024, 4096], P('fsdp'), may hold values from -0.1875 to 0.1875
- expand_first: float32 [4, 1024, 4096], P('rep', 'fsdp'), may hold values from -128 to 128
- expand_second: float32 [4, 1024, 4096], P('rep', 'fsdp'), may hold values from 85.1968 to 1368.064
- contract_weight: float32 [4096, 1024], P('fsdp'), may hold values from -0.09375 to 0.09375
- contract_momentum: float32 [4096, 1024], P('fsdp'), may hold values from -0.09375 to 0.09375
- contract_first: float32 [4, 4096, 1024], P('rep', 'fsdp'), may hold values from -256 to 256
- contract_second: float32 [4, 4096, 1024], P('rep', 'fsdp'), may hold values from 341.6064 to 5464.064
- vectors: float32 [12, 1024], P(None, 'fsdp'), may hold values from -0.6 to 1.4
- vectors_momentum: float32 [12, 1024], P(None, 'fsdp'), may hold values from -1.25 to 1.25
- vectors_first: float32 [4, 12, 1024], P('rep', None, 'fsdp'), may hold values from -448 to 448
- vectors_second: float32 [4, 12, 1024], P('rep', None, 'fsdp'), may hold values from 876.544 to 14008.32
Outputs:
- layer_output: bfloat16 [32768, 1024], P(('rep', 'fsdp'))
- input_grad: bfloat16 [32768, 1024], P(('rep', 'fsdp'))
- attention_first_new: float32 [4, 4, 1024, 1024], P('rep', None, 'fsdp')
- attention_second_new: float32 [4, 4, 1024, 1024], P('rep', None, 'fsdp')
- outer_attention: float32 [3, 4, 1024, 1024], P(None, None, 'fsdp')
- copy_attention: bfloat16 [4, 1024, 1024], P(None, 'fsdp')
- expand_first_new: float32 [4, 1024, 4096], P('rep', 'fsdp')
- expand_second_new: float32 [4, 1024, 4096], P('rep', 'fsdp')
- outer_expand: float32 [3, 1024, 4096], P(None, 'fsdp')
- copy_expand: bfloat16 [1024, 4096], P('fsdp')
- contract_first_new: float32 [4, 4096, 1024], P('rep', 'fsdp')
- contract_second_new: float32 [4, 4096, 1024], P('rep', 'fsdp')
- outer_contract: float32 [3, 4096, 1024], P(None, 'fsdp')
- copy_contract: bfloat16 [4096, 1024], P('fsdp')
- vectors_first_new: float32 [4, 12, 1024], P('rep', None, 'fsdp')
- vectors_second_new: float32 [4, 12, 1024], P('rep', None, 'fsdp')
- outer_vectors: float32 [3, 12, 1024], P(None, None, 'fsdp')
- copy_vectors: bfloat16 [12, 1024], P(None, 'fsdp')
Inputs may be any that keep to these rules, and one draw needn't show every extreme that they name: `segment_ids`: within a row the numbers never fall; a run of equal numbers is one document, and tokens attend only within their document.
All inputs are finite; a program needn't handle non-finite values.
Results may differ from a plain program's by a relative error of at most 0.012.
The roundings to bfloat16 on the way count: a program that leaves them out, or rounds other values in their place, can miss the bound.
Values may be sent and summed in bfloat16 or wider, within the bound.
A program may use at most 448 MiB of HBM per device.

v0:
```python
from functools import partial

import jax
import jax.numpy as jnp
from jax import lax
from jax.sharding import PartitionSpec as P

D = 1024
H = 16
HD = 64
FF = 4096
LEN = 1024
SEQ_DEV = 1
ADAM_STEP = 4
TOK_DEV = 1024


def norm_forward(values_in, gain_row, shift_row):
    center = values_in - jnp.mean(values_in, axis=-1, keepdims=True)
    inv_scale = lax.rsqrt(jnp.mean(center * center, axis=-1, keepdims=True) + 1e-05)
    normed = center * inv_scale
    return (normed * gain_row + shift_row, normed, inv_scale)


def norm_backward(grad_out, normed, inv_scale, gain_row):
    grad_gain = jnp.sum(grad_out * normed, axis=0)
    grad_shift = jnp.sum(grad_out, axis=0)
    scaled_grad = grad_out * gain_row
    grad_value = inv_scale * (
        scaled_grad
        - jnp.mean(scaled_grad, axis=-1, keepdims=True)
        - normed * jnp.mean(scaled_grad * normed, axis=-1, keepdims=True)
    )
    return (grad_value, grad_gain, grad_shift)


def product_over(left, right):
    return lax.dot_general(
        left, right, (((0,), (0,)), ((), ())), preferred_element_type=jnp.float32
    )


def product_back(left, right):
    return lax.dot_general(
        left, right, (((1,), (1,)), ((), ())), preferred_element_type=jnp.float32
    )


def block_scores(query_block, key_block, row_segments, all_segments):
    scores = jnp.einsum("qhd,khd->hqk", query_block, key_block, preferred_element_type=jnp.float32)
    same_doc = row_segments[:, None] == all_segments[None, :]
    return jnp.where(same_doc[None], scores, -1e30)


def inner_step(weight, gradient, first_moment, second_moment, learn_rate, weight_decay):
    first_new = 0.5 * first_moment + 0.5 * gradient
    second_new = 0.75 * second_moment + 0.25 * gradient * gradient
    update_dir = (
        first_new
        / (1.0 - 0.5**ADAM_STEP)
        / (jnp.sqrt(second_new / (1.0 - 0.75**ADAM_STEP)) + 1e-08)
    )
    return (weight - learn_rate * (update_dir + weight_decay * weight), first_new, second_new)


def per_device(
    tokens,
    cotangent,
    segment_ids,
    attention_weight,
    attention_momentum,
    attention_first,
    attention_second,
    expand_weight,
    expand_momentum,
    expand_first,
    expand_second,
    contract_weight,
    contract_momentum,
    contract_first,
    contract_second,
    vectors,
    vectors_momentum,
    vectors_first,
    vectors_second,
):
    attn_full, vector_full = (
        lax.all_gather(attention_weight.astype(jnp.bfloat16), "fsdp", axis=1, tiled=True),
        lax.all_gather(vectors.astype(jnp.bfloat16), "fsdp", axis=1, tiled=True),
    )
    vector_rows = vector_full.astype(jnp.float32)
    gain_one, gain_two, shift_one, shift_two = (
        vector_rows[0],
        vector_rows[1],
        vector_rows[2],
        vector_rows[3],
    )
    bias_query, bias_value, bias_mixed, bias_down = (
        vector_rows[4],
        vector_rows[5],
        vector_rows[6],
        vector_rows[7],
    )
    bias_up = vector_rows[8:].reshape(FF)
    projected = jnp.einsum("td,nde->nte", tokens, attn_full[:3], preferred_element_type=jnp.float32)
    query_all = ((projected[0] + bias_query) * 0.125).astype(jnp.bfloat16)
    key_all = projected[1].astype(jnp.bfloat16)
    value_all = (projected[2] + bias_value).astype(jnp.bfloat16)
    query_heads = query_all.reshape(SEQ_DEV, LEN, H, HD)
    key_heads = key_all.reshape(SEQ_DEV, LEN, H, HD)
    value_heads = value_all.reshape(SEQ_DEV, LEN, H, HD)
    block_rows = min(512, LEN)
    head_group = min(8, H)
    context_rows = []
    log_sums = []
    seq_index = 0
    for row_start in range(0, LEN, block_rows):
        block_pieces = []
        for head_start in range(0, H, head_group):
            head_part = slice(head_start, head_start + head_group)
            scores = block_scores(
                query_heads[seq_index, row_start : row_start + block_rows, head_part],
                key_heads[seq_index, :, head_part],
                segment_ids[seq_index, row_start : row_start + block_rows],
                segment_ids[seq_index],
            )
            row_max = jnp.max(scores, axis=-1, keepdims=True)
            exp_score = jnp.exp(scores - row_max)
            row_total = jnp.sum(exp_score, axis=-1, keepdims=True)
            probability = (exp_score / row_total).astype(jnp.bfloat16)
            block_pieces.append(
                jnp.einsum(
                    "hqk,khd->qhd",
                    probability,
                    value_heads[seq_index, :, head_part],
                    preferred_element_type=jnp.float32,
                )
            )
            log_sums.append(row_max + jnp.log(row_total))
        context_rows.append(jnp.concatenate(block_pieces, axis=1))
    mixed = jnp.concatenate(context_rows, axis=0).reshape(TOK_DEV, D).astype(jnp.bfloat16)
    attn_out = jnp.dot(mixed, attn_full[3], preferred_element_type=jnp.float32) + bias_mixed
    hidden, normed_one, scale_one = norm_forward(
        tokens.astype(jnp.float32) + attn_out, gain_one, shift_one
    )
    hidden_low = hidden.astype(jnp.bfloat16)
    ffn_expand, ffn_contract = (
        lax.all_gather(expand_weight.astype(jnp.bfloat16), "fsdp", axis=0, tiled=True),
        lax.all_gather(contract_weight.astype(jnp.bfloat16), "fsdp", axis=0, tiled=True),
    )
    pre_act = jnp.dot(hidden_low, ffn_expand, preferred_element_type=jnp.float32) + bias_up
    activated = jax.nn.gelu(pre_act, approximate=False).astype(jnp.bfloat16)
    branch = jnp.dot(activated, ffn_contract, preferred_element_type=jnp.float32) + bias_down
    layer_output, normed_two, scale_two = norm_forward(hidden + branch, gain_two, shift_two)
    grad_sum, grad_gain_two, grad_shift_two = norm_backward(
        cotangent.astype(jnp.float32), normed_two, scale_two, gain_two
    )
    grad_branch = grad_sum.astype(jnp.bfloat16)
    grad_act = product_back(grad_branch, ffn_contract)
    unused_value, gelu_pull = jax.vjp(partial(jax.nn.gelu, approximate=False), pre_act)
    grad_pre_low = gelu_pull(grad_act)[0].astype(jnp.bfloat16)
    grad_hidden = grad_sum + product_back(grad_pre_low, ffn_expand)
    contract_full = product_over(activated, grad_branch)
    expand_full = product_over(hidden_low, grad_pre_low)
    grad_expand, grad_contract = (
        lax.psum_scatter(expand_full, "fsdp", scatter_dimension=0, tiled=True),
        lax.psum_scatter(contract_full, "fsdp", scatter_dimension=0, tiled=True),
    )
    grad_resid, grad_gain_one, grad_shift_one = norm_backward(
        grad_hidden, normed_one, scale_one, gain_one
    )
    grad_attn_out = grad_resid.astype(jnp.bfloat16)
    grad_bias_mixed = jnp.sum(grad_attn_out.astype(jnp.float32), axis=0)
    grad_output_proj = product_over(mixed, grad_attn_out)
    grad_mixed = product_back(grad_attn_out, attn_full[3]).astype(jnp.bfloat16)
    grad_context = grad_mixed.reshape(SEQ_DEV, LEN, H, HD)
    query_grads = []
    lse_index = 0
    seq_index = 0
    key_totals = [
        jnp.zeros((LEN, head_group, HD), jnp.float32) for head_start in range(0, H, head_group)
    ]
    value_totals = [
        jnp.zeros((LEN, head_group, HD), jnp.float32) for head_start in range(0, H, head_group)
    ]
    for row_start in range(0, LEN, block_rows):
        block_pieces = []
        for group_index, head_start in enumerate(range(0, H, head_group)):
            head_part = slice(head_start, head_start + head_group)
            query_block = query_heads[seq_index, row_start : row_start + block_rows, head_part]
            key_block = key_heads[seq_index, :, head_part]
            value_block = value_heads[seq_index, :, head_part]
            ctx_grad = grad_context[seq_index, row_start : row_start + block_rows, head_part]
            scores = block_scores(
                query_block,
                key_block,
                segment_ids[seq_index, row_start : row_start + block_rows],
                segment_ids[seq_index],
            )
            probability = jnp.exp(scores - log_sums[lse_index])
            lse_index = lse_index + 1
            value_totals[group_index] = value_totals[group_index] + jnp.einsum(
                "hqk,qhd->khd",
                probability.astype(jnp.bfloat16),
                ctx_grad,
                preferred_element_type=jnp.float32,
            )
            prob_grad = jnp.einsum(
                "qhd,khd->hqk", ctx_grad, value_block, preferred_element_type=jnp.float32
            )
            row_dot = jnp.sum(probability * prob_grad, axis=-1, keepdims=True)
            score_grad = (probability * (prob_grad - row_dot)).astype(jnp.bfloat16)
            block_pieces.append(
                jnp.einsum(
                    "hqk,khd->qhd", score_grad, key_block, preferred_element_type=jnp.float32
                ).astype(jnp.bfloat16)
            )
            key_totals[group_index] = key_totals[group_index] + jnp.einsum(
                "hqk,qhd->khd", score_grad, query_block, preferred_element_type=jnp.float32
            )
        query_grads.append(jnp.concatenate(block_pieces, axis=1))
    key_grads = jnp.concatenate(
        [key_total.astype(jnp.bfloat16) for key_total in key_totals], axis=1
    )
    value_grads = jnp.concatenate(
        [value_total.astype(jnp.bfloat16) for value_total in value_totals], axis=1
    )
    grad_query = jnp.concatenate(query_grads, axis=0).reshape(TOK_DEV, D) * 0.125
    grad_keys = key_grads.reshape(TOK_DEV, D)
    grad_values = value_grads.reshape(TOK_DEV, D)
    stacked_grads = jnp.stack([grad_query, grad_keys, grad_values])
    grad_qkv = jnp.einsum("td,nte->nde", tokens, stacked_grads, preferred_element_type=jnp.float32)
    input_grad = (
        grad_resid
        + jnp.einsum(
            "nte,nde->td", stacked_grads, attn_full[:3], preferred_element_type=jnp.float32
        )
    ).astype(jnp.bfloat16)
    grad_attention_full = jnp.concatenate([grad_qkv, grad_output_proj[None]], axis=0)
    vector_head = jnp.stack(
        [
            grad_gain_one,
            grad_gain_two,
            grad_shift_one,
            grad_shift_two,
            jnp.sum(grad_query.astype(jnp.float32), axis=0),
            jnp.sum(grad_values.astype(jnp.float32), axis=0),
            grad_bias_mixed,
            jnp.sum(grad_branch.astype(jnp.float32), axis=0),
        ]
    )
    grad_bias_up = jnp.sum(grad_pre_low.astype(jnp.float32), axis=0).reshape(FF // D, D)
    grad_vectors_full = jnp.concatenate([vector_head, grad_bias_up], axis=0)
    grad_attention, grad_vectors = (
        lax.psum_scatter(grad_attention_full, "fsdp", scatter_dimension=1, tiled=True),
        lax.psum_scatter(grad_vectors_full, "fsdp", scatter_dimension=1, tiled=True),
    )
    attention_new = inner_step(
        attention_weight, grad_attention, attention_first[0], attention_second[0], 0.03, 0.1
    )
    expand_new = inner_step(
        expand_weight, grad_expand, expand_first[0], expand_second[0], 0.03, 0.1
    )
    contract_new = inner_step(
        contract_weight, grad_contract, contract_first[0], contract_second[0], 0.015, 0.1
    )
    vectors_new = inner_step(vectors, grad_vectors, vectors_first[0], vectors_second[0], 0.2, 0.0)
    summed = (
        lax.psum((attention_weight - attention_new[0]).astype(jnp.bfloat16), "rep").astype(
            jnp.float32
        ),
        lax.psum((expand_weight - expand_new[0]).astype(jnp.bfloat16), "rep").astype(jnp.float32),
        lax.psum((contract_weight - contract_new[0]).astype(jnp.bfloat16), "rep").astype(
            jnp.float32
        ),
        lax.psum((vectors - vectors_new[0]).astype(jnp.bfloat16), "rep").astype(jnp.float32),
    )
    groups_count = lax.axis_size("rep")
    results = []
    for weight_now, momentum_now, inner_new, diff_total in zip(
        (attention_weight, expand_weight, contract_weight, vectors),
        (attention_momentum, expand_momentum, contract_momentum, vectors_momentum),
        (attention_new, expand_new, contract_new, vectors_new),
        summed,
    ):
        mean_diff = diff_total / groups_count
        momentum_new = 0.5 * momentum_now + mean_diff
        outer_new = weight_now - 0.7 * (mean_diff + 0.5 * momentum_new)
        results.append(
            (
                inner_new[1][None],
                inner_new[2][None],
                jnp.stack([mean_diff, momentum_new, outer_new]),
                outer_new.astype(jnp.bfloat16),
            )
        )
    return (
        layer_output.astype(jnp.bfloat16),
        input_grad,
        results[0][0],
        results[0][1],
        results[0][2],
        results[0][3],
        results[1][0],
        results[1][1],
        results[1][2],
        results[1][3],
        results[2][0],
        results[2][1],
        results[2][2],
        results[2][3],
        results[3][0],
        results[3][1],
        results[3][2],
        results[3][3],
    )


def solution(mesh):
    placed = (
        P(("rep", "fsdp"), None),
        P(("rep", "fsdp"), None),
        P(("rep", "fsdp"), None),
        P(None, "fsdp", None),
        P(None, "fsdp", None),
        P("rep", None, "fsdp", None),
        P("rep", None, "fsdp", None),
        P("fsdp", None),
        P("fsdp", None),
        P("rep", "fsdp", None),
        P("rep", "fsdp", None),
        P("fsdp", None),
        P("fsdp", None),
        P("rep", "fsdp", None),
        P("rep", "fsdp", None),
        P(None, "fsdp"),
        P(None, "fsdp"),
        P("rep", None, "fsdp"),
        P("rep", None, "fsdp"),
    )
    return jax.shard_map(
        per_device,
        mesh=mesh,
        in_specs=placed,
        out_specs=(
            P(("rep", "fsdp"), None),
            P(("rep", "fsdp"), None),
            P("rep", None, "fsdp", None),
            P("rep", None, "fsdp", None),
            P(None, None, "fsdp", None),
            P(None, "fsdp", None),
            P("rep", "fsdp", None),
            P("rep", "fsdp", None),
            P(None, "fsdp", None),
            P("fsdp", None),
            P("rep", "fsdp", None),
            P("rep", "fsdp", None),
            P(None, "fsdp", None),
            P("fsdp", None),
            P("rep", None, "fsdp"),
            P("rep", None, "fsdp"),
            P(None, None, "fsdp"),
            P(None, "fsdp"),
        ),
        check_vma=False,
    )
```

profile of v0, /device:TPU:1, one launch (start us, length us, event | category | flops | bytes accessed | tf_op | source)
XLA Modules:
  0.0 1464.5 jit_solution(9158751748262666368)
XLA Ops:
  16.3 25.5 %all_gather.13 = bf16[12,1024]{1,0:T(8,128)(2,1)S(1)} all-gather(bf16[12,128]{1,0:T(8,128)(2,1)S(1)} %convert_element_type.221), channel_id=1, replica_groups=mesh['rep'=4,'fsdp'=8] {'fsdp'}, dimensions={1}, use_global_device_ids=true | all-gather | bytes 27648 | tf_op jit(solution)/shard_map/all_gather | solution.py:89
  50.5 86.8 %all-gather.4.cloned.1.call-done = bf16[4,1024,1024]{1,2,0:T(8,128)(2,1)} async-done(((bf16[4,128,1024]{1,2,0:T(8,128)(2,1)}), bf16[4,1024,1024]{1,2,0:T(8,128)(2,1)}) %all-gather.4.cloned.1.call-update) | async-done | bytes 8388624 | tf_op jit(solution)/shard_map/all_gather | solution.py:88
  175.6 13.4 fusion.6
  216.6 13.5 fusion.8
  262.8 48.0 %multiply_convert_fusion.4 = (bf16[1024,4096]{1,0:T(8,128)(2,1)}, f32[1024,4096]{1,0:T(8,128)}, f32[1024,4096]{1,0:T(8,128)}) fusion(f32[4096]{0:T(1024)S(1)} %bitcast.308, bf16[1024,4096]{1,0:T(8,128)(2,1)} %all-gather.6.cloned.1.call-done, bf16[1024,1024]{0,1:T(8,128)(2,1)S(1)} %fusion.134.clone.4), kind=kOutput, calls=%fused_computation.17 | convolution fusion | flops 8866758656 | bytes 52445184 | tf_op jit(solution)/shard_map/dot_general | solution.py:151
  310.7 77.4 %all-gather.8.cloned.1.call-done = bf16[4096,1024]{1,0:T(8,128)(2,1)} async-done(((bf16[512,1024]{1,0:T(8,128)(2,1)}), bf16[4096,1024]{1,0:T(8,128)(2,1)}) %all-gather.8.cloned.1.call-update) | async-done | bytes 8388624 | tf_op jit(solution)/shard_map/all_gather | solution.py:149
  388.2 14.9 %fusion.141 = (f32[1024]{0:T(1024)S(1)}, f32[1024,1024]{0,1:T(8,128)S(1)}) fusion(f32[1024]{0:T(1024)S(1)} %bitcast.316, bf16[1024,4096]{1,0:T(8,128)(2,1)} %get-tuple-element.65, bf16[4096,1024]{1,0:T(8,128)(2,1)} %all-gather.8.cloned.1.call-done, f32[1024]{0:T(1024)S(1)} %bitcast.304, f32[1024]{0:T(1024)S(1)} %bitcast.294, ...), kind=kOutput, calls=%fused_computation.264 | convolution fusion | flops 8597273600 | bytes 25190400 | tf_op jit(solution)/shard_map/dot_general | solution.py:153
  413.3 24.3 %convert_reduce_fusion = (f32[4096]{0:T(1024)}, bf16[1024,4096]{1,0:T(8,128)(2,1)}) fusion(f32[1024,4096]{1,0:T(8,128)} %get-tuple-element.66, f32[1024,4096]{1,0:T(8,128)} %get-tuple-element.120, f32[4096]{0:T(1024)S(1)} %bitcast.309, bf16[1024,1024]{0,1:T(8,128)(2,1)} %get-tuple-element.60, bf16[4096,1024]{1,0:T(8,128)(2,1)} %all-gather.8.cloned.1.call-done), kind=kOutput, calls=%fused_computation.3 | convolution fusion | flops 8661233664 | bytes 52461568 | tf_op jit(solution)/shard_map/dot_general | solution.py:44
  437.6 14.9 %fusion.131 = f32[1024,4096]{1,0:T(8,128)} fusion(bf16[1024,4096]{1,0:T(8,128)(2,1)} %get-tuple-element.58, f32[1024,1024]{0,1:T(8,128)S(1)} %copy-done.7, f32[1024]{0:T(1024)S(1)} %bitcast.305, f32[1024]{0:T(1024)S(1)} %bitcast.295, f32[1024]{0:T(1024)S(1)} %add_rsqrt_fusion.1, f32[1024]{0:T(1024)S(1)} %broadcast_multiply_fusion.5), kind=kOutput, calls=%fused_computation.258 | convolution fusion | flops 8595177472 | bytes 29376512 | tf_op jit(solution)/shard_map/dot_general | solution.py:38
  454.1 19.6 %multiply_reduce_fusion.4 = (f32[1024]{0:T(1024)}, f32[1024]{0:T(1024)S(1)}, f32[1024]{0:T(1024)S(1)}, f32[1024]{0:T(1024)}, f32[1024,1024]{0,1:T(8,128)S(1)}) fusion(f32[1024,1024]{0,1:T(8,128)} %copy-done.6, f32[1024]{0:T(1024)S(1)} %add_rsqrt_fusion.1, f32[1024]{0:T(1024)S(1)} %broadcast_multiply_fusion.5, f32[1024]{0:T(1024)S(1)} %bitcast.296, ...), kind=kOutput, calls=%fused_computation.96 | convolution fusion | flops 8608804864 | bytes 31506432 | tf_op jit(solution)/shard_map/dot_general | solution.py:44
  481.7 9.9 fusion.14
  491.6 9.9 fusion.16
  508.3 10.6 fusion.81
  524.7 9.4 fusion.95
  534.1 9.3 fusion.96
  543.5 21.2 %multiply_reduce_fusion.3 = (f32[8,512]{1,0:T(8,128)}, f32[8,512]{1,0:T(8,128)}, f32[8,512,1024]{2,1,0:T(8,128)}) fusion(f32[8,512,1024]{2,1,0:T(8,128)} %get-tuple-element.116, f32[8,512]{1,0:T(8,128)} %copy-done.50, pred[512,1024]{1,0:T(8,128)(4,1)S(1)} %copy-done.11, f32[8,512,1024]{2,1,0:T(8,128)} %fusion.96, f32[8,512]{1,0:T(8,128)} %copy-done.52, ...), kind=kOutput, calls=%fused_computation.14 | convolution fusion | flops 570417152 | bytes 69271552 | tf_op jit(solution)/shard_map/qhd,khd->hqk/dot_general | solution.py:208
  564.7 24.3 %multiply_reduce_fusion.1 = (f32[8,512]{1,0:T(8,128)S(1)}, f32[8,512]{1,0:T(8,128)S(1)}, f32[8,512,1024]{2,1,0:T(8,128)}) fusion(f32[8,512,1024]{2,1,0:T(8,128)} %get-tuple-element.113, f32[8,512]{1,0:T(8,128)} %copy-done.54, pred[512,1024]{1,0:T(8,128)(4,1)S(1)} %copy-done.13, f32[8,512,1024]{2,1,0:T(8,128)} %fusion.95, f32[8,512]{1,0:T(8,128)} %copy-done.56, ...), kind=kOutput, calls=%fused_computation.8 | convolution fusion | flops 570417152 | bytes 69271552 | tf_op jit(solution)/shard_map/qhd,khd->hqk/dot_general | solution.py:208
  589.1 52.9 %multiply_convert_fusion.1 = (bf16[8,512,1024]{2,1,0:T(8,128)(2,1)}, bf16[8,512,1024]{2,1,0:T(8,128)(2,1)S(1)}, bf16[8,512,1024]{2,1,0:T(8,128)(2,1)}, bf16[8,512,1024]{2,1,0:T(8,128)(2,1)}) fusion(f32[8,512,1024]{2,1,0:T(8,128)} %get-tuple-element.125, f32[8,512,1024]{2,1,0:T(8,128)} %get-tuple-element.113, f32[8,512]{1,0:T(8,128)S(1)} %get-tuple-element.44, ...), kind=kLoop, calls=%fused_computation.7 | loop fusion | flops 83886080 | bytes 168951808 | tf_op jit(solution)/shard_map/convert_element_type | solution.py:212
  708.6 14.9 %fusion.142 = f32[4096,1024]{1,0:T(8,128)} fusion(bf16[1024,4096]{1,0:T(8,128)(2,1)} %get-tuple-element.65, bf16[1024,1024]{0,1:T(8,128)(2,1)S(1)} %copy-done.45), kind=kOutput, calls=%fused_computation.265 | convolution fusion | flops 8589934592 | bytes 27262976 | tf_op jit(solution)/shard_map/dot_general | solution.py:38
  747.0 267.6 %reduce-scatter.5.cloned.1.call-done = f32[4,128,1024]{1,2,0:T(8,128)} async-done(((f32[4,1024,1024]{1,2,0:T(8,128)}), f32[4,128,1024]{1,2,0:T(8,128)}) %reduce-scatter.5.cloned.1.call-update) | async-done | bytes 2097168 | tf_op jit(solution)/shard_map/reduce_scatter | solution.py:255
  1020.7 276.8 %reduce-scatter.9.cloned.1.call-done = f32[512,1024]{1,0:T(8,128)} async-done(((f32[4096,1024]{1,0:T(8,128)}), f32[512,1024]{1,0:T(8,128)}) %reduce-scatter.9.cloned.1.call-update) | async-done | bytes 2097168 | tf_op jit(solution)/shard_map/reduce_scatter | solution.py:167
  1305.4 13.0 fusion.47
  1322.4 30.2 %reduce-scatter.11.cloned.1.call-done = f32[12,128]{1,0:T(8,128)} async-done(((f32[12,1024]{1,0:T(8,128)}), f32[12,128]{1,0:T(8,128)}) %reduce-scatter.11.cloned.1.call-update) | async-done | bytes 6160 | tf_op jit(solution)/shard_map/reduce_scatter | solution.py:256
  1369.8 56.1 %all-reduce.3.cloned.1.call-done = (bf16[4,128,1024]{1,2,0:T(8,128)(2,1)}, bf16[128,4096]{1,0:T(8,128)(2,1)}, bf16[512,1024]{1,0:T(8,128)(2,1)}) async-done(((bf16[4,128,1024]{1,2,0:T(8,128)(2,1)}, bf16[128,4096]{1,0:T(8,128)(2,1)}, bf16[512,1024]{1,0:T(8,128)(2,1)}), (bf16[4,128,1024]{1,2,0:T(8,128)(2,1)}, bf16[128,4096]{1,0:T(8,128)(2,1)}, bf16[512,1024]{1,0:T(8,128)(2,1)})) %all-reduce.3.cloned.1.call-update) | async-done | bytes 3145744 | tf_op jit(solution)/shard_map/psum | solution.py:269
  (337 shorter events, 304.0 us)
Async XLA Ops:
  7.2 130.1 %all-gather.4.cloned.1.call-start = ((), (), s32[]{:S(2)}) async-start(), calls=%async_computation.4 | async-start | bytes 9437184 | tf_op jit(solution)/shard_map/all_gather | solution.py:88
  10.5 32.0 %copy-start.84 = (s32[1,1024]{1,0:T(1,128)S(1)}, s32[1,1024]{1,0:T(1,128)}, u32[]{:S(2)}) copy-start(s32[1,1024]{1,0:T(1,128)} %param.21) | copy-start | bytes 12292
  10.5 252.3 %all-gather.6.cloned.1.call-start = ((), (), s32[]{:S(2)}) async-start(), calls=%async_computation.5 | async-start | bytes 9437184 | tf_op jit(solution)/shard_map/all_gather | solution.py:148
  13.3 374.9 %all-gather.8.cloned.1.call-start = ((), (), s32[]{:S(2)}) async-start(), calls=%async_computation.6 | async-start | bytes 9437184 | tf_op jit(solution)/shard_map/all_gather | solution.py:149
  13.3 29.9 %copy-start.36 = (bf16[1024,1024]{1,0:T(8,128)(2,1)S(1)}, bf16[1024,1024]{1,0:T(8,128)(2,1)}, u32[]{:S(2)}) copy-start(bf16[1024,1024]{1,0:T(8,128)(2,1)} %param.20) | copy-start | bytes 6291460
  16.2 722.7 %reduce-scatter.7.cloned.1.call-start = ((), (), s32[]{:S(2)}) async-start(), calls=%async_computation.8 | async-start | bytes 18874368 | tf_op jit(solution)/shard_map/reduce_scatter | solution.py:166
  45.8 91.6 %copy-start.37 = (bf16[1024,1024]{1,0:T(8,128)(2,1)S(1)}, bf16[1024,1024]{1,0:T(8,128)(2,1)}, u32[]{:S(2)}) copy-start(bf16[1024,1024]{1,0:T(8,128)(2,1)} %param.19) | copy-start | bytes 6291460
  50.5 157.1 %copy-start.10 = (pred[512,1024]{1,0:T(8,128)(4,1)}, pred[512,1024]{1,0:T(8,128)(4,1)S(1)}, u32[]{:S(2)}) copy-start(pred[512,1024]{1,0:T(8,128)(4,1)S(1)} %get-tuple-element.108) | copy-start | bytes 1572868
  50.5 195.6 %copy-start.12 = (pred[512,1024]{1,0:T(8,128)(4,1)}, pred[512,1024]{1,0:T(8,128)(4,1)S(1)}, u32[]{:S(2)}) copy-start(pred[512,1024]{1,0:T(8,128)(4,1)S(1)} %get-tuple-element.109) | copy-start | bytes 1572868
  151.6 65.0 %copy-start.4 = (bf16[1,1024,1024]{1,2,0:T(8,128)(2,1)}, bf16[1,1024,1024]{1,2,0:T(8,128)(2,1)S(1)}, u32[]{:S(2)}) copy-start(bf16[1,1024,1024]{1,2,0:T(8,128)(2,1)S(1)} %slice.220) | copy-start | bytes 6291460
  157.1 59.5 %copy-start.16 = (bf16[1,1024,16,64]{1,3,2,0:T(8,128)(2,1)}, bf16[1,1024,16,64]{1,3,2,0:T(8,128)(2,1)S(1)}, u32[]{:S(2)}) copy-start(bf16[1,1024,16,64]{1,3,2,0:T(8,128)(2,1)S(1)} %multiply_convert_fusion.5) | copy-start | bytes 6291460
  165.5 80.6 %copy-start.58 = (f32[8,512]{1,0:T(8,128)}, f32[8,512]{1,0:T(8,128)S(1)}, u32[]{:S(2)}) copy-start(f32[8,512]{1,0:T(8,128)S(1)} %get-tuple-element.112) | copy-start | bytes 49156
  173.9 33.7 %copy-start.60 = (f32[8,512]{1,0:T(8,128)}, f32[8,512]{1,0:T(8,128)S(1)}, u32[]{:S(2)}) copy-start(f32[8,512]{1,0:T(8,128)S(1)} %get-tuple-element.115) | copy-start | bytes 49156
  262.8 125.4 %copy-start.94 = (f32[1,1024]{1,0:T(1,128)S(1)}, f32[1,1024]{1,0:T(1,128)}, u32[]{:S(2)}) copy-start(f32[1,1024]{1,0:T(1,128)} %get-tuple-element.99) | copy-start | bytes 12292
  452.7 561.9 %reduce-scatter.5.cloned.1.call-start = ((), (), s32[]{:S(2)}) async-start(), calls=%async_computation.7 | async-start | bytes 18874368 | tf_op jit(solution)/shard_map/reduce_scatter | solution.py:255
  473.8 34.5 %copy-start.50 = (f32[8,512]{1,0:T(8,128)}, f32[8,512]{1,0:T(8,128)S(1)}, u32[]{:S(2)}) copy-start(f32[8,512]{1,0:T(8,128)S(1)} %log_add_fusion.3) | copy-start | bytes 49156
  707.0 590.5 %reduce-scatter.9.cloned.1.call-start = ((), (), s32[]{:S(2)}) async-start(), calls=%async_computation.9 | async-start | bytes 18874368 | tf_op jit(solution)/shard_map/reduce_scatter | solution.py:167
  723.5 629.2 %reduce-scatter.11.cloned.1.call-start = ((), (), s32[]{:S(2)}) async-start(), calls=%async_computation.10 | async-start | bytes 73728 | tf_op jit(solution)/shard_map/reduce_scatter | solution.py:256
  738.6 276.0 %copy-start.15 = (f32[4,128,1024]{1,2,0:T(8,128)S(1)}, f32[4,128,1024]{1,2,0:T(8,128)}, u32[]{:S(2)}) copy-start(f32[4,128,1024]{1,2,0:T(8,128)} %copy-done.14) | copy-start | bytes 6291460
  738.6 687.3 %all-reduce.3.cloned.1.call-start = ((), (), s32[]{:S(2)}) async-start(), calls=%async_computation.11 | async-start | bytes 6291456 | tf_op jit(solution)/shard_map/psum | solution.py:269
  1318.4 34.2 %copy-start.67 = (f32[12,128]{1,0:T(8,128)S(1)}, f32[12,128]{1,0:T(8,128)}, u32[]{:S(2)}) copy-start(f32[12,128]{1,0:T(8,128)} %param.34) | copy-start | bytes 18436
  1318.4 34.2 %copy-start.90 = (f32[1,12,128]{2,0,1:T(1,128)S(1)}, f32[1,12,128]{2,0,1:T(1,128)}, u32[]{:S(2)}) copy-start(f32[1,12,128]{2,0,1:T(1,128)} %param.36) | copy-start | bytes 18436
  1318.4 34.2 %copy-start.91 = (f32[1,12,128]{2,0,1:T(1,128)S(1)}, f32[1,12,128]{2,0,1:T(1,128)}, u32[]{:S(2)}) copy-start(f32[1,12,128]{2,0,1:T(1,128)} %param.37) | copy-start | bytes 18436
  1318.4 44.4 %copy-start.89 = (f32[12,128]{1,0:T(8,128)S(1)}, f32[12,128]{1,0:T(8,128)}, u32[]{:S(2)}) copy-start(f32[12,128]{1,0:T(8,128)} %param.35) | copy-start | bytes 18436
  (92 other events, 929.9 us)
Sparse Core Ops, SparseCore 0:
  10.6 126.6 all-gather.3
  140.0 122.6 all-gather.5
  265.5 122.6 all-gather.7
  452.7 278.8 reduce-scatter.6
  735.2 279.3 reduce-scatter.4
  1018.2 279.2 reduce-scatter.8
  1300.7 51.9 reduce-scatter.10
  1356.3 69.5 all-reduce.2
where the time goes:
time: 1480 us; the launch traced here: 1460 us
  waiting for transfers between devices  796 us (54%)
  matrix products  386 us (26%)
  other arithmetic  150 us (10%)
  local copies, waits for them, and re-layouts  82 us (6%)
  blocking collectives  33.7 us (2%)
  between operations  16 us (1%)
    reduce_scatter x1, waiting for transfers between devices, per_device(): lax.psum_scatter(contract_full, 'fsdp', scatter_dimension=0, tiled=True)  277 us
    reduce_scatter x1, waiting for transfers between devices, per_device(): lax.psum_scatter(grad_attention_full, 'fsdp', scatter_dimension=1, tiled=...  268 us
    all_gather x1, waiting for transfers between devices, per_device(): lax.all_gather(attention_weight.astype(jnp.bfloat16), 'fsdp', axis=1, til...  86.8 us
    all_gather x1, waiting for transfers between devices, per_device(): lax.all_gather(contract_weight.astype(jnp.bfloat16), 'fsdp', axis=0, tile...  77.4 us
    dot_general x4, matrix products, per_device(): jnp.einsum('qhd,khd->hqk', ctx_grad, value_block, preferred_element_type=...  64.3 us
    unnamed x230, local copies, waits for them, and re-layouts  62 us
    psum x1, waiting for transfers between devices, per_device(): lax.psum((attention_weight - attention_new[0]).astype(jnp.bfloat16), 'rep')  56.1 us
    convert_element_type x1, other arithmetic, per_device(): score_grad = (probability * (prob_grad - row_dot)).astype(jnp.bfloat16)  52.9 us
  transfers between devices with their start and end apart: 8, of which 7 were waited for; matrix products, arithmetic and copies ran while one was open for 34% of the time, Pallas kernels for 0%

commit v1 on v0

--- a/solution.py
+++ b/solution.py
@@ -3,6 +3,8 @@
 import jax
 import jax.numpy as jnp
 from jax import lax
+from jax.experimental import pallas as pl
+from jax.experimental.pallas import tpu as pltpu
 from jax.sharding import PartitionSpec as P
 
 D = 1024
@@ -316,6 +318,927 @@
     )
 
 
+NEG=-1e30
+QB=256
+def attn_windows(seg_row):
+    length = seg_row.shape[0]
+    nb = length // QB
+    firsts = seg_row[::QB]
+    lasts = seg_row[QB-1::QB]
+    begin = jnp.sum((seg_row[None, :] < firsts[:, None]).astype(jnp.int32), axis=1)
+    end = jnp.sum((seg_row[None, :] <= lasts[:, None]).astype(jnp.int32), axis=1)
+    start = begin // 128
+    count = (end - start * 128 + QB - 1) // QB
+    start = jnp.minimum(start, (length - count * QB) // 128)
+    return start.astype(jnp.int32), count.astype(jnp.int32)
+def lane_half(shape, h):
+    lane = lax.broadcasted_iota(jnp.int32, shape, len(shape)-1)
+    return (lane < 64) if h == 0 else (lane >= 64)
+def dot(a, b, ca, cb):
+    return lax.dot_general(a, b, (((ca,), (cb,)), ((), ())), preferred_element_type=jnp.float32)
+def fold(value, join):
+    part = value.shape[0] // 8
+    parts = [value[i * part:(i + 1) * part] for i in range(8)]
+    while len(parts) > 1:
+        parts = [join(a, b) for a, b in zip(parts[::2], parts[1::2])]
+    return parts[0]
+def fwd_kernel(start_ref, count_ref, qkv_ref, segr_ref, segc_ref, o_ref, lse_ref, vt_ref):
+    length = qkv_ref.shape[0]
+    vt_ref[...] = qkv_ref[:, 256:384].T
+    nb = length // QB
+    for i in range(nb):
+        rows = slice(i*QB, (i+1)*QB)
+        for nn in range(1, nb+1):
+            @pl.when(count_ref[i] == nn)
+            def _():
+                nk = nn*QB
+                lo = pl.multiple_of(start_ref[i]*128, 128)
+                kw = qkv_ref[pl.ds(lo, nk), 128:256]
+                qb = qkv_ref[rows, 0:128]
+                same = segc_ref[pl.ds(lo, nk), :] == segr_ref[:, rows]
+                outs = []
+                for h in range(2):
+                    qh = jnp.where(lane_half(qb.shape, h), qb, jnp.zeros_like(qb))
+                    st = jnp.where(same, dot(kw, qh, 1, 1), NEG)
+                    m = jnp.max(fold(st, jnp.maximum), axis=0, keepdims=True)
+                    p = jnp.exp(st - m)
+                    l = jnp.sum(fold(p, jnp.add), axis=0, keepdims=True)
+                    weighted = dot(vt_ref[h*64:(h+1)*64, pl.ds(lo, nk)], p.astype(jnp.bfloat16), 1, 0)
+                    outs.append(weighted * (1.0 / l))
+                    lse_ref[0, h:h+1, rows] = m + jnp.log(l)
+                o_ref[rows, :] = jnp.concatenate(outs, axis=0).T.astype(jnp.bfloat16)
+def bwd_kernel(start_ref, count_ref, qkv_ref, do_ref, lse_ref, segr_ref, segc_ref, d_ref, sums_ref, dk_acc, dv_acc, kt_ref):
+    length = qkv_ref.shape[0]
+    kt_ref[...] = qkv_ref[:, 128:256].T
+    nb = length // QB
+    dk_acc[...] = jnp.zeros_like(dk_acc)
+    dv_acc[...] = jnp.zeros_like(dv_acc)
+    for i in range(nb):
+        rows = slice(i*QB, (i+1)*QB)
+        for nn in range(1, nb+1):
+            @pl.when(count_ref[i] == nn)
+            def _():
+                nk = nn*QB
+                lo = pl.multiple_of(start_ref[i]*128, 128)
+                win = pl.ds(lo, nk)
+                kw = qkv_ref[win, 128:256]
+                vw = qkv_ref[win, 256:384]
+                qb = qkv_ref[rows, 0:128]
+                db = do_ref[rows, :]
+                same = segc_ref[win, :] == segr_ref[:, rows]
+                dqs = []; dks = 0.0; dvs = 0.0
+                for h in range(2):
+                    hm = lane_half(qb.shape, h)
+                    qh = jnp.where(hm, qb, jnp.zeros_like(qb))
+                    dh = jnp.where(hm, db, jnp.zeros_like(db))
+                    st = jnp.where(same, dot(kw, qh, 1, 1), NEG)
+                    p = jnp.exp(st - lse_ref[0, h:h+1, rows])
+                    dpt = dot(vw, dh, 1, 1)
+                    rd = jnp.sum(fold(p * dpt, jnp.add), axis=0, keepdims=True)
+                    ds = (p * (dpt - rd)).astype(jnp.bfloat16)
+                    dvs = dvs + dot(p.astype(jnp.bfloat16), dh, 1, 0)
+                    dks = dks + dot(ds, qh, 1, 0)
+                    dqs.append(dot(kt_ref[h*64:(h+1)*64, win], ds, 1, 0))
+                d_ref[rows, 0:128] = jnp.concatenate(dqs, axis=0).T.astype(jnp.bfloat16) * 0.125
+                dk_acc[win, :] += dks
+                dv_acc[win, :] += dvs
+    d_ref[:, 128:256] = dk_acc[...].astype(jnp.bfloat16)
+    d_ref[:, 256:384] = dv_acc[...].astype(jnp.bfloat16)
+    sums_ref[0] = jnp.sum(d_ref[...].astype(jnp.float32), axis=0, keepdims=True)
+def attn_fwd(qkv, seg):
+    T, width = qkv.shape
+    start, count = attn_windows(seg[0])
+    segc = seg.reshape(T, 1)
+    heads = width // 384
+    return pl.pallas_call(
+        fwd_kernel,
+        out_shape=(jax.ShapeDtypeStruct((T, width // 3), jnp.bfloat16), jax.ShapeDtypeStruct((heads, 2, T), jnp.float32)),
+        grid_spec=pltpu.PrefetchScalarGridSpec(
+            num_scalar_prefetch=2, grid=(heads,),
+            in_specs=[
+                pl.BlockSpec((T, 384), lambda h, *_: (0, h)),
+                pl.BlockSpec((1, T), lambda h, *_: (0, 0)),
+                pl.BlockSpec((T, 1), lambda h, *_: (0, 0)),
+            ],
+            out_specs=(pl.BlockSpec((T, 128), lambda h, *_: (0, h)), pl.BlockSpec((1, 2, T), lambda h, *_: (h, 0, 0))),
+            scratch_shapes=[pltpu.VMEM((128, T), jnp.bfloat16)],
+        ),
+        cost_estimate=cost(20 * T * T * width, 3 * T * width, T * T * width // 128),
+        name="attn_fwd",
+    )(start, count, qkv, seg, segc)
+
+
+def attn_bwd(qkv, do, lse, seg, part):
+    T, width = qkv.shape
+    start, count = attn_windows(seg[0])
+    segc = seg.reshape(T, 1)
+    heads = width // 768
+    first = part * heads
+    return pl.pallas_call(
+        bwd_kernel,
+        out_shape=(jax.ShapeDtypeStruct((T, width // 2), jnp.bfloat16), jax.ShapeDtypeStruct((heads, 1, 384), jnp.float32)),
+        grid_spec=pltpu.PrefetchScalarGridSpec(
+            num_scalar_prefetch=2, grid=(heads,),
+            in_specs=[
+                pl.BlockSpec((T, 384), lambda h, *_: (0, first + h)),
+                pl.BlockSpec((T, 128), lambda h, *_: (0, first + h)),
+                pl.BlockSpec((1, 2, T), lambda h, *_: (first + h, 0, 0)),
+                pl.BlockSpec((1, T), lambda h, *_: (0, 0)),
+                pl.BlockSpec((T, 1), lambda h, *_: (0, 0)),
+            ],
+            out_specs=(pl.BlockSpec((T, 384), lambda h, *_: (0, h)), pl.BlockSpec((1, 1, 384), lambda h, *_: (h, 0, 0))),
+            scratch_shapes=[pltpu.VMEM((T, 128), jnp.float32)] * 2 + [pltpu.VMEM((128, T), jnp.bfloat16)],
+        ),
+        cost_estimate=cost(20 * T * T * width, 6 * T * width, T * T * width // 64),
+        name="attn_bwd",
+    )(start, count, qkv, do, lse, seg, segc)
+
+
+MESH_ID = pl.DeviceIdType.MESH
+
+
+def bits_of():
+    rep = lax.axis_index("rep")
+    fsdp = lax.axis_index("fsdp")
+    return dict(
+        rep=rep, fsdp=fsdp, x=rep // 2, c=rep % 2, z1=fsdp // 4, z0=(fsdp // 2) % 2, y=fsdp % 2
+    )
+
+
+def partner_of(at, which):
+    rep, fsdp = at["rep"], at["fsdp"]
+    if which == "c":
+        rep = rep + 1 - 2 * at["c"]
+    elif which == "x":
+        rep = rep + 2 - 4 * at["x"]
+    elif which == "y":
+        fsdp = fsdp + 1 - 2 * at["y"]
+    elif which == "z0":
+        fsdp = fsdp + 2 - 4 * at["z0"]
+    elif which == "z1":
+        fsdp = fsdp + 4 - 8 * at["z1"]
+    else:
+        rep = rep + 1 - 2 * at["c"]
+        fsdp = fsdp + 4 - 8 * at["z1"]
+    return (rep, fsdp)
+
+
+REL = [(a, b, d) for d in (0, 1) for b in (0, 1) for a in (0, 1)]
+
+
+def gather_kernel(
+    qkv_in, wo_in, we_in, wc_in, vec_in, tok_in, seg_in,
+    qkv_out, wo_out, we_out, wc_out, vec_out, tok_out, seg_out,
+    tok_buf, seg_buf, send_sem, recv_sem, local_sem,
+):
+    at = bits_of()
+    other = {k: partner_of(at, k) for k in ("c", "x", "y", "z0", "z1", "swap")}
+    barrier = pltpu.get_barrier_semaphore()
+    for k in ("c", "x", "y", "z0", "z1"):
+        pl.semaphore_signal(barrier, inc=1, device_id=other[k], device_id_type=MESH_ID)
+    moves = at["c"] != at["z1"]
+
+    @pl.when(moves)
+    def _():
+        pl.semaphore_signal(barrier, inc=1, device_id=other["swap"], device_id_type=MESH_ID)
+        pl.semaphore_wait(barrier, 6)
+
+    @pl.when(jnp.logical_not(moves))
+    def _():
+        pl.semaphore_wait(barrier, 5)
+
+    def flip(bit, rel):
+        return bit + rel - 2 * bit * rel
+
+    def shard(rel):
+        return 4 * flip(at["z1"], rel[1]) + 2 * flip(at["z0"], rel[0]) + flip(at["y"], rel[2])
+
+    counter = [0]
+    started = []
+
+    def send(src, dst, which):
+        k = counter[0]
+        counter[0] += 1
+        copy = pltpu.make_async_remote_copy(
+            src_ref=src, dst_ref=dst, send_sem=send_sem.at[k], recv_sem=recv_sem.at[k],
+            device_id=other[which], device_id_type=MESH_ID,
+        )
+        copy.start()
+        started.append(copy)
+        return copy
+
+    class Piece:
+        def __init__(self, own, slot, split_x):
+            self.own, self.slot, self.split_x = own, slot, split_x
+            self.part = (2 * at["x"] + at["c"]) if split_x else at["c"]
+            self.part_x = (2 * (1 - at["x"]) + at["c"]) if split_x else None
+            self.copies = {}
+
+        def first(self):
+            zero = (0, 0, 0)
+            for which in ("z1", "z0", "y"):
+                self.copies[which, zero] = send(
+                    self.own(self.part), self.slot(shard(zero), self.part), which
+                )
+            self.copies["c", zero] = send(self.own(None), self.slot(shard(zero), None), "c")
+
+        def onward(self, rel):
+            here = self.slot(shard(rel), self.part)
+            if rel == (0, 1, 0):
+                self.copies["z0", rel] = send(here, here, "z0")
+            if rel[2] == 0:
+                self.copies["y", rel] = send(here, here, "y")
+            if self.split_x:
+                self.copies["x", rel] = send(here, here, "x")
+            self.copies["c", rel] = send(here, here, "c")
+
+        def arrive(self, which, came):
+            self.copies[which, came].wait_recv()
+            step = {"z0": (1, 0, 0), "z1": (0, 1, 0), "y": (0, 0, 1)}[which]
+            self.onward(tuple(p + q for p, q in zip(came, step)))
+
+        def near(self):
+            self.arrive("z1", (0, 0, 0))
+            self.arrive("z0", (0, 0, 0))
+
+        def rest(self):
+            self.arrive("y", (0, 0, 0))
+            self.arrive("z0", (0, 1, 0))
+            self.arrive("y", (0, 1, 0))
+            self.arrive("y", (1, 0, 0))
+            self.arrive("y", (1, 1, 0))
+
+        def last(self):
+            if self.split_x:
+                for rel in REL[1:]:
+                    self.copies["x", rel].wait_recv()
+                    there = self.slot(shard(rel), self.part_x)
+                    self.copies["cx", rel] = send(there, there, "c")
+
+        def finish(self):
+            for (which, rel), copy in self.copies.items():
+                if which in ("c", "cx"):
+                    copy.wait_recv()
+
+    def rows(ref, count):
+        full = ref.shape[-2] // 8
+        def slot(f, part):
+            if part is None:
+                at_row, n = f * full, full
+            else:
+                at_row, n = f * full + part * (full // count), full // count
+            at_row = pl.multiple_of(at_row, 8)
+            return ref.at[pl.ds(at_row, n), :]
+        return slot
+
+    def own_rows(ref, count):
+        full = ref.shape[-2]
+        def own(part):
+            if part is None:
+                return ref
+            row = pl.multiple_of(part * (full // count), 8)
+            n = full // count
+            return ref.at[pl.ds(row, n), :]
+        return own
+
+    qkv, wo, we, wc = pieces = [
+        Piece(own_rows(qkv_in, 4), rows(qkv_out, 4), True),
+        Piece(own_rows(wo_in, 4), rows(wo_out, 4), True),
+        Piece(own_rows(we_in, 2), rows(we_out, 2), False),
+        Piece(own_rows(wc_in, 4), rows(wc_out, 4), True),
+    ]
+    zero = (0, 0, 0)
+    vec_copies = [
+        send(vec_in, vec_out.at[shard(zero)], which) for which in ("c", "z1", "z0", "y")
+    ]
+    pieces[0].first()
+    tok_k, seg_k = counter[0], counter[0] + 1
+    counter[0] += 2
+
+    def swap_copy(src, dst, k):
+        return pltpu.make_async_remote_copy(
+            src_ref=src, dst_ref=dst, send_sem=send_sem.at[k], recv_sem=recv_sem.at[k],
+            device_id=other["swap"], device_id_type=MESH_ID,
+        )
+
+    @pl.when(moves)
+    def _():
+        swap_copy(tok_in, tok_out, tok_k).start()
+        swap_copy(seg_in, seg_out, seg_k).start()
+
+    @pl.when(jnp.logical_not(moves))
+    def _():
+        one = pltpu.make_async_copy(tok_in, tok_buf, local_sem.at[0])
+        two = pltpu.make_async_copy(seg_in, seg_buf, local_sem.at[1])
+        one.start()
+        two.start()
+        one.wait()
+        two.wait()
+        three = pltpu.make_async_copy(tok_buf, tok_out, local_sem.at[0])
+        four = pltpu.make_async_copy(seg_buf, seg_out, local_sem.at[1])
+        three.start()
+        four.start()
+        three.wait()
+        four.wait()
+
+    wo.first()
+    qkv.near()
+    we.first()
+    vec_copies[1].wait_recv()
+    here = vec_out.at[shard((0, 1, 0))]
+    vec_far = send(here, here, "z0")
+    vec_more = [send(here, here, "y")]
+    vec_copies[2].wait_recv()
+    here = vec_out.at[shard((1, 0, 0))]
+    vec_more.append(send(here, here, "y"))
+    qkv.rest()
+    wo.near()
+    wo.rest()
+    vec_far.wait_recv()
+    here = vec_out.at[shard((1, 1, 0))]
+    vec_more.append(send(here, here, "y"))
+    we.near()
+    wc.first()
+    qkv.last()
+    we.rest()
+    wo.last()
+    wc.near()
+    wc.rest()
+    wc.last()
+    for piece in pieces:
+        piece.finish()
+    for copy in [vec_copies[0], vec_copies[3]] + vec_more:
+        copy.wait_recv()
+    for copy in started:
+        copy.wait_send()
+
+    @pl.when(moves)
+    def _():
+        swap_copy(tok_in, tok_out, tok_k).wait()
+        swap_copy(seg_in, seg_out, seg_k).wait()
+
+
+GATHER_COPIES = 29 * 3 + 15 + 8 + 2
+
+
+def gather_all(qkv, wo, we, wc, vec, tok, seg):
+    bf = jnp.bfloat16
+    shape = jax.ShapeDtypeStruct
+    whole = pl.BlockSpec(memory_space=pl.ANY)
+    return pl.pallas_call(
+        gather_kernel,
+        out_shape=(
+            shape((8 * qkv.shape[0], qkv.shape[1]), bf),
+            shape((8 * wo.shape[0], wo.shape[1]), bf),
+            shape((8 * we.shape[0], we.shape[1]), bf),
+            shape((8 * wc.shape[0], wc.shape[1]), bf),
+            shape((8,) + vec.shape, bf),
+            shape(tok.shape, bf),
+            shape(seg.shape, seg.dtype),
+        ),
+        in_specs=[whole] * 7,
+        out_specs=(whole,) * 7,
+        scratch_shapes=[
+            pltpu.VMEM(tok.shape, bf),
+            pltpu.VMEM(seg.shape, seg.dtype),
+            pltpu.SemaphoreType.DMA((GATHER_COPIES,)),
+            pltpu.SemaphoreType.DMA((GATHER_COPIES,)),
+            pltpu.SemaphoreType.DMA((2,)),
+        ],
+        compiler_params=pltpu.CompilerParams(collective_id=0, has_side_effects=True),
+        name="gather_weights",
+    )(qkv, wo, we, wc, vec, tok, seg)
+
+
+SHRINK = 1000
+BF, F32 = jnp.bfloat16, jnp.float32
+SHAPE = jax.ShapeDtypeStruct
+
+
+def full_spec(shape):
+    return pl.BlockSpec(shape, lambda *_: (0,) * len(shape), pipeline_mode=pl.Buffered(1))
+
+
+def cost(flops, moved, exps=0):
+    return pl.CostEstimate(flops=int(flops) // SHRINK, bytes_accessed=int(moved) // SHRINK, transcendentals=int(exps) // SHRINK)
+
+
+def qkv_kernel(x_ref, w_ref, bias_ref, scale_ref, o_ref):
+    for i in range(4):
+        rows = slice(i * 256, (i + 1) * 256)
+        z = dot(x_ref[rows, :], w_ref[...], 1, 0)
+        o_ref[rows, :] = ((z + bias_ref[...]) * scale_ref[...]).astype(BF)
+
+
+def qkv_call(x, w, bias, scale):
+    tokens, width = x.shape[0], w.shape[1]
+    tile = 768
+    return pl.pallas_call(
+        qkv_kernel,
+        out_shape=SHAPE((tokens, width), BF),
+        grid=(width // tile,),
+        in_specs=[
+            full_spec(x.shape),
+            pl.BlockSpec((x.shape[1], tile), lambda j: (0, j)),
+            pl.BlockSpec((1, tile), lambda j: (0, j)),
+            pl.BlockSpec((1, tile), lambda j: (0, j)),
+        ],
+        out_specs=pl.BlockSpec((tokens, tile), lambda j: (0, j)),
+        cost_estimate=cost(2 * tokens * D * width, 2 * (tokens * D + D * width + tokens * width)),
+        name="qkv",
+    )(x, w, bias, scale)
+
+
+def mean_row(value):
+    return jnp.mean(value, axis=-1, keepdims=True)
+
+
+def mix_kernel(c_ref, w_ref, x_ref, rows_ref, n_ref, q_ref, low_ref):
+    value = x_ref[...].astype(F32) + dot(c_ref[...], w_ref[...], 1, 0) + rows_ref[6:7, :]
+    center = value - mean_row(value)
+    inv = lax.rsqrt(mean_row(center * center) + 1e-05)
+    normed = center * inv
+    n_ref[...] = normed
+    q_ref[...] = inv
+    low_ref[...] = (normed * rows_ref[0:1, :] + rows_ref[2:3, :]).astype(BF)
+
+
+def mix_call(mixed, w_out, tok, rows):
+    t = tok.shape[0]
+    tile = pl.BlockSpec((256, D), lambda i: (i, 0))
+    return pl.pallas_call(
+        mix_kernel,
+        out_shape=(SHAPE((t, D), F32), SHAPE((t, 1), F32), SHAPE((t, D), BF)),
+        grid=(t // 256,),
+        in_specs=[tile, full_spec((D, D)), tile, full_spec(rows.shape)],
+        out_specs=(tile, pl.BlockSpec((256, 1), lambda i: (i, 0)), tile),
+        cost_estimate=cost(2 * t * D * D, 12 * t * D + 2 * D * D),
+        name="mix_norm",
+    )(mixed, w_out, tok, rows)
+
+
+def up_kernel(h_ref, w_ref, bias_ref, g_ref, s_ref):
+    for i in range(8):
+        rows = slice(i * 128, (i + 1) * 128)
+        z = dot(h_ref[rows, :], w_ref[...], 1, 0) + bias_ref[...]
+        phi, bell = erf_parts(z)
+        g_ref[rows, :] = (z * phi).astype(BF)
+        s_ref[rows, :] = (phi + z * bell * 0.3989422804014327).astype(BF)
+
+
+def up_call(low, w_in, bias):
+    t = low.shape[0]
+    tile = 512
+    out = pl.BlockSpec((t, tile), lambda j: (0, j))
+    return pl.pallas_call(
+        up_kernel,
+        out_shape=(SHAPE((t, FF), BF), SHAPE((t, FF), BF)),
+        grid=(FF // tile,),
+        in_specs=[
+            full_spec(low.shape),
+            pl.BlockSpec((D, tile), lambda j: (0, j)),
+            pl.BlockSpec((1, tile), lambda j: (0, j)),
+        ],
+        out_specs=(out, out),
+        cost_estimate=cost(2 * t * D * FF, 2 * (t * D + D * FF + 2 * t * FF), 2 * t * FF),
+        name="up_gelu",
+    )(low, w_in, bias)
+
+
+def row_sum(value):
+    return jnp.sum(value, axis=0, keepdims=True)
+
+
+def norm_back(grad, normed, inv, gain):
+    scaled = grad * gain
+    return inv * (scaled - mean_row(scaled) - normed * mean_row(scaled * normed))
+
+
+def down_kernel(g_ref, w_ref, n_ref, cot_ref, rows_ref, out_ref, dr_ref, dm_ref, sums_ref):
+    hidden = n_ref[...] * rows_ref[0:1, :] + rows_ref[2:3, :]
+    value = hidden + dot(g_ref[...], w_ref[...], 1, 0) + rows_ref[7:8, :]
+    center = value - mean_row(value)
+    inv = lax.rsqrt(mean_row(center * center) + 1e-05)
+    normed = center * inv
+    gain = rows_ref[1:2, :]
+    out_ref[...] = (normed * gain + rows_ref[3:4, :]).astype(BF)
+    grad = cot_ref[...].astype(F32)
+    back = norm_back(grad, normed, inv, gain)
+    low = back.astype(BF)
+    dr_ref[...] = back
+    dm_ref[...] = low
+
+    @pl.when(pl.program_id(0) == 0)
+    def _():
+        sums_ref[...] = jnp.zeros_like(sums_ref)
+
+    sums_ref[0:1, :] += row_sum(grad * normed)
+    sums_ref[1:2, :] += row_sum(grad)
+    sums_ref[2:3, :] += row_sum(low.astype(F32))
+
+
+def down_call(act, w_down, normed, cot, rows):
+    t = act.shape[0]
+    tile = pl.BlockSpec((256, D), lambda i: (i, 0))
+    return pl.pallas_call(
+        down_kernel,
+        out_shape=(SHAPE((t, D), BF), SHAPE((t, D), F32), SHAPE((t, D), BF), SHAPE((8, D), F32)),
+        grid=(t // 256,),
+        in_specs=[
+            pl.BlockSpec((256, FF), lambda i: (i, 0)), full_spec((FF, D)), tile, tile,
+            full_spec(rows.shape),
+        ],
+        out_specs=(tile, tile, tile, pl.BlockSpec((8, D), lambda i: (0, 0))),
+        cost_estimate=cost(2 * t * D * FF, 2 * (t * FF + D * FF) + 14 * t * D),
+        name="down_norm",
+    )(act, w_down, normed, cot, rows)
+
+
+def slope_kernel(dm_ref, w_ref, s_ref, o_ref, sums_ref):
+    total = 0.0
+    for i in range(4):
+        rows = slice(i * 256, (i + 1) * 256)
+        z = (dot(dm_ref[rows, :], w_ref[...], 1, 1) * s_ref[rows, :].astype(F32)).astype(BF)
+        o_ref[rows, :] = z
+        total = total + row_sum(z.astype(F32))
+    sums_ref[...] = total
+
+
+def slope_call(dm, w_down, slope):
+    t = dm.shape[0]
+    tile = 512
+    wide = pl.BlockSpec((t, tile), lambda j: (0, j))
+    return pl.pallas_call(
+        slope_kernel,
+        out_shape=(SHAPE((t, FF), BF), SHAPE((1, FF), F32)),
+        grid=(FF // tile,),
+        in_specs=[full_spec(dm.shape), pl.BlockSpec((tile, D), lambda j: (j, 0)), wide],
+        out_specs=(wide, pl.BlockSpec((1, tile), lambda j: (0, j))),
+        cost_estimate=cost(2 * t * D * FF, 2 * (t * D + D * FF + 2 * t * FF)),
+        name="down_back",
+    )(dm, w_down, slope)
+
+
+def hidden_kernel(dz_ref, w_ref, dr_ref, n_ref, q_ref, wo_ref, rows_ref, r_ref, a_ref, c_ref, sums_ref):
+    grad = dr_ref[...] + dot(dz_ref[...], w_ref[...], 1, 1)
+    normed = n_ref[...]
+    back = norm_back(grad, normed, q_ref[...], rows_ref[0:1, :])
+    low = back.astype(BF)
+    r_ref[...] = back
+    a_ref[...] = low
+    c_ref[...] = dot(low, wo_ref[...], 1, 1).astype(BF)
+
+    @pl.when(pl.program_id(0) == 0)
+    def _():
+        sums_ref[...] = jnp.zeros_like(sums_ref)
+
+    sums_ref[0:1, :] += row_sum(grad * normed)
+    sums_ref[1:2, :] += row_sum(grad)
+    sums_ref[2:3, :] += row_sum(low.astype(F32))
+
+
+def hidden_call(dz, w_in, dr, normed, inv, w_out, rows):
+    t = dz.shape[0]
+    tile = pl.BlockSpec((256, D), lambda i: (i, 0))
+    return pl.pallas_call(
+        hidden_kernel,
+        out_shape=(SHAPE((t, D), F32), SHAPE((t, D), BF), SHAPE((t, D), BF), SHAPE((8, D), F32)),
+        grid=(t // 256,),
+        in_specs=[
+            pl.BlockSpec((256, FF), lambda i: (i, 0)), full_spec((D, FF)), tile, tile,
+            pl.BlockSpec((256, 1), lambda i: (i, 0)), full_spec((D, D)), full_spec(rows.shape),
+        ],
+        out_specs=(tile, tile, tile, pl.BlockSpec((8, D), lambda i: (0, 0))),
+        cost_estimate=cost(2 * t * D * (FF + D), 2 * (t * FF + D * FF) + 16 * t * D),
+        name="up_back_norm",
+    )(dz, w_in, dr, normed, inv, w_out, rows)
+
+
+def input_kernel(a_ref, b_ref, w_ref, r_ref, o_ref):
+    half = a_ref.shape[1]
+    value = dot(a_ref[...], w_ref[:, :half], 1, 1) + dot(b_ref[...], w_ref[:, half:], 1, 1)
+    o_ref[...] = (r_ref[...] + value).astype(BF)
+
+
+def input_call(part_a, part_b, w_qkv, resid):
+    t, width = part_a.shape
+    tile = pl.BlockSpec((256, D), lambda i: (i, 0))
+    wide = pl.BlockSpec((256, width), lambda i: (i, 0))
+    return pl.pallas_call(
+        input_kernel,
+        out_shape=SHAPE((t, D), BF),
+        grid=(t // 256,),
+        in_specs=[wide, wide, full_spec(w_qkv.shape), tile],
+        out_specs=tile,
+        cost_estimate=cost(4 * t * D * width, 4 * (t * width + D * width) + 6 * t * D),
+        name="input_back",
+    )(part_a, part_b, w_qkv, resid)
+
+
+def weight_kernel(half_ref, left_ref, right_ref, *refs):
+    o_ref, turned = refs[-2], refs[-1]
+
+    @pl.when(pl.program_id(1) == 0)
+    def _():
+        turned[...] = left_ref[...].T
+
+    value = dot(turned[...], right_ref[...], 1, 0)
+    if len(refs) == 3:
+        value = value + refs[0][...].astype(F32)
+    o_ref[...] = value.astype(BF)
+
+
+def weight_call(left, right, half, came=None):
+    t, rows = left.shape
+    width = right.shape[1]
+    bm = 512
+    bn = 1024 if width == 1024 else 512
+    steps = rows // 2 // bm
+    specs = [
+        pl.BlockSpec((t, bm), lambda i, j, h: (0, h[0] * steps + i)),
+        pl.BlockSpec((t, bn), lambda i, j, h: (0, j)),
+    ]
+    values = [left, right]
+    out = pl.BlockSpec((bm, bn), lambda i, j, h: (i, j))
+    if came is not None:
+        specs.append(out)
+        values.append(came)
+    return pl.pallas_call(
+        weight_kernel,
+        out_shape=SHAPE((rows // 2, width), BF),
+        grid_spec=pltpu.PrefetchScalarGridSpec(
+            num_scalar_prefetch=1, grid=(steps, width // bn), in_specs=specs, out_specs=out,
+            scratch_shapes=[pltpu.VMEM((bm, t), BF)],
+        ),
+        cost_estimate=cost(t * rows * width, t * rows + 2 * t * width + 2 * rows * width),
+        name="weight_grad",
+    )(half.reshape(1), *values)
+
+
+def inner_kernel(rate, decay, w_ref, g_ref, m_ref, v_ref, m_out, v_out, d_out):
+    weight = w_ref[...]
+    new, m_out[...], v_out[...] = inner_step(
+        weight, g_ref[...].astype(F32), m_ref[...], v_ref[...], rate, decay
+    )
+    d_out[...] = (weight - new).astype(BF)
+
+
+def inner_call(weight, grad, first, second, rate, decay):
+    rows, width = weight.shape
+    block = 32 * 4096 // width
+    tile = pl.BlockSpec((block, width), lambda i: (i, 0))
+    like = SHAPE((rows, width), F32)
+    return pl.pallas_call(
+        partial(inner_kernel, rate, decay),
+        out_shape=(like, like, SHAPE((rows, width), BF)),
+        grid=(rows // block,),
+        in_specs=[tile] * 4,
+        out_specs=(tile,) * 3,
+        cost_estimate=cost(20 * rows * width, 24 * rows * width),
+        name="inner_step",
+    )(weight, grad, first, second)
+
+
+def outer_kernel(core_ref, w_ref, u_ref, own_ref, came_ref, o_ref, c_ref):
+    mine = (core_ref[0] == pl.program_id(0)).astype(F32)
+    total = own_ref[...].astype(F32) * mine + came_ref[...].astype(F32) * (1.0 - mine)
+    mean = total * 0.25
+    weight = w_ref[...]
+    momentum = 0.5 * u_ref[...] + mean
+    new = weight - 0.7 * (mean + 0.5 * momentum)
+    o_ref[0] = mean
+    o_ref[1] = momentum
+    o_ref[2] = new
+    c_ref[...] = new.astype(BF)
+
+
+def outer_call(weight, momentum, own, came, core):
+    rows, width = weight.shape
+    block = 32 * 4096 // width
+    steps = rows // 2 // block
+    tile = pl.BlockSpec((block, width), lambda h, i, c: (h * steps + i, 0))
+    part = pl.BlockSpec((block, width), lambda h, i, c: (i, 0))
+    return pl.pallas_call(
+        outer_kernel,
+        out_shape=(SHAPE((3, rows, width), F32), SHAPE((rows, width), BF)),
+        grid_spec=pltpu.PrefetchScalarGridSpec(
+            num_scalar_prefetch=1, grid=(2, steps), in_specs=[tile, tile, part, part],
+            out_specs=(pl.BlockSpec((3, block, width), lambda h, i, c: (0, h * steps + i, 0)), tile),
+        ),
+        cost_estimate=cost(10 * rows * width, 26 * rows * width),
+        name="outer_step",
+    )(core.reshape(1), weight, momentum, own, came)
+
+
+def erf_parts(value):
+    size = jnp.abs(value) * 0.7071067811865476
+    share = 1.0 / (1.0 + 0.5 * size)
+    inner = 0.17087277
+    for coefficient in (
+        -0.82215223, 1.48851587, -1.13520398, 0.27886807, -0.18628806, 0.09678418, 0.37409196, 1.00002368
+    ):
+        inner = coefficient + share * inner
+    square = size * size
+    half = 0.5 * share * jnp.exp(share * inner - 1.26551223 - square)
+    return jnp.where(value >= 0, 1.0 - half, half), jnp.exp(-square)
+
+
+def xor_pairs(bits):
+    place = {"y": 0, "z0": 1, "z1": 2, "c": 3, "x": 4}
+    flip = sum(1 << place[bit] for bit in bits)
+    pairs = []
+    for device in range(32):
+        if bits == ("c", "z1") and ((device >> 3) & 1) == ((device >> 2) & 1):
+            continue
+        pairs.append((device, device ^ flip))
+    return pairs
+
+
+def exchange(value, *bits):
+    return lax.ppermute(value, ("rep", "fsdp"), xor_pairs(bits))
+
+
+def swap(at, value):
+    return jnp.where(at["c"] != at["z1"], exchange(value, "c", "z1"), value)
+
+
+def add_low(left, right):
+    return (left.astype(jnp.float32) + right.astype(jnp.float32)).astype(jnp.bfloat16)
+
+
+def pick(value, index, axis):
+    return lax.dynamic_index_in_dim(value, index, axis, keepdims=False)
+
+
+def stage(at, total, which):
+    axis = 1 if which == "y" and total.ndim == 4 else 0
+    came = exchange(pick(total, 1 - at[which], axis), which)
+    return add_low(pick(total, at[which], axis), came)
+
+
+def slabs(total):
+    return total.reshape(2, 2, -1, total.shape[-1])
+
+
+def after(value, *earlier):
+    return lax.optimization_barrier((value,) + earlier)[0]
+
+
+def rep_total(at, diff):
+    halves = diff.reshape(2, diff.shape[0] // 2, diff.shape[1])
+    came = exchange(pick(halves, 1 - at["c"], 0), "c")
+    total = add_low(pick(halves, at["c"], 0), came)
+    total = add_low(total, exchange(total, "x"))
+    return total, exchange(total, "c")
+
+
+def weave(value):
+    rows = value.shape[1]
+    return jnp.transpose(value.reshape(3, rows, D // 128, 128), (1, 2, 0, 3)).reshape(rows, 3 * D)
+
+
+def unweave(value):
+    rows = value.shape[0]
+    return jnp.transpose(value.reshape(rows, D // 128, 3, 128), (2, 0, 1, 3)).reshape(3, rows, D)
+
+
+def per_device_fast(
+    tokens,
+    cotangent,
+    segment_ids,
+    attention_weight,
+    attention_momentum,
+    attention_first,
+    attention_second,
+    expand_weight,
+    expand_momentum,
+    expand_first,
+    expand_second,
+    contract_weight,
+    contract_momentum,
+    contract_first,
+    contract_second,
+    vectors,
+    vectors_momentum,
+    vectors_first,
+    vectors_second,
+):
+    bf, f32 = jnp.bfloat16, jnp.float32
+    at = bits_of()
+    core = at["c"].astype(jnp.int32)
+    attn_low = attention_weight.astype(bf)
+    w_qkv, w_out, w_in, w_down, vector_full, tok, seg = gather_all(
+        weave(attn_low[:3]), attn_low[3], expand_weight.astype(bf), contract_weight.astype(bf),
+        vectors.astype(bf), tokens, segment_ids,
+    )
+    cot = swap(at, after(cotangent, w_qkv))
+    rows = jnp.swapaxes(vector_full, 0, 1).reshape(-1, D).astype(f32)
+    bias_up = rows[8:].reshape(1, FF)
+    bias_qkv = weave(jnp.stack([rows[4], jnp.zeros_like(rows[4]), rows[5]])[:, None])
+    scale_qkv = weave(jnp.stack([jnp.full((1, D), 0.125, f32)] + [jnp.ones((1, D), f32)] * 2))
+    qkv = qkv_call(tok, w_qkv, bias_qkv, scale_qkv)
+    mixed, log_sum = attn_fwd(qkv, seg)
+    normed, inv, hidden_low = mix_call(mixed, w_out, tok, rows)
+    activated, slope = up_call(hidden_low, w_in, bias_up)
+    layer_output, grad_sum, grad_branch, sums_two = down_call(activated, w_down, normed, cot, rows)
+    down_send = weight_call(activated, grad_branch, 1 - core)
+    grad_pre, sums_up = slope_call(after(grad_branch, down_send), w_down, slope)
+    down_came = exchange(down_send, "c")
+    up_send = weight_call(hidden_low, grad_pre, 1 - core)
+    down_total = weight_call(activated, after(grad_branch, up_send), core, down_came)
+    up_came = exchange(up_send, "c")
+    up_total = weight_call(hidden_low, after(grad_pre, down_total), core, up_came)
+    grad_resid, grad_attn, grad_mixed, sums_one = hidden_call(
+        after(grad_pre, up_total), w_in, grad_sum, normed, inv, w_out, rows
+    )
+    down_one = stage(at, slabs(down_total), "y")
+    up_one = stage(at, slabs(up_total), "z0")
+    proj_send = weight_call(mixed, grad_attn, 1 - core)
+    proj_came = exchange(proj_send, "c")
+    grad_a, sums_a = attn_bwd(qkv, after(grad_mixed, proj_send), log_sum, seg, 0)
+    qkv_send_a = weight_call(tok, grad_a, 1 - core)
+    down_one, up_one, qkv_send_a = lax.optimization_barrier((down_one, up_one, qkv_send_a))
+    came_a = exchange(qkv_send_a, "c")
+    down_two = stage(at, down_one, "z0")
+    up_two = stage(at, up_one, "y")
+    proj_total = weight_call(mixed, after(grad_attn, qkv_send_a, down_one, up_one), core, proj_came)
+    total_a = weight_call(tok, after(grad_a, proj_total), core, came_a)
+    proj_one = stage(at, slabs(proj_total), "y")
+    a_one = stage(at, slabs(total_a), "z0")
+    grad_b, sums_b = attn_bwd(qkv, after(grad_mixed, total_a), log_sum, seg, 1)
+    qkv_send_b = weight_call(tok, grad_b, 1 - core)
+    down_two, up_two, proj_one, a_one, qkv_send_b = lax.optimization_barrier(
+        (down_two, up_two, proj_one, a_one, qkv_send_b)
+    )
+    came_b = exchange(qkv_send_b, "c")
+    grad_contract = swap(at, down_two)
+    grad_expand = swap(at, up_two)
+    proj_two = stage(at, proj_one, "z0")
+    a_two = stage(at, a_one, "y")
+    input_grad = input_call(after(grad_a, down_two, qkv_send_b), grad_b, w_qkv, grad_resid)
+    total_b = weight_call(tok, after(grad_b, input_grad), core, came_b)
+    b_one = stage(at, slabs(total_b), "y")
+    b_two = stage(at, b_one, "z0")
+    sums_qkv = jnp.concatenate([sums_a, sums_b], axis=0).reshape(D // 128, 3, 128)
+    vector_grad = jnp.concatenate(
+        [
+            sums_one[0:1],
+            sums_two[0:1],
+            sums_one[1:2],
+            sums_two[1:2],
+            sums_qkv[:, 0].reshape(1, D),
+            sums_qkv[:, 2].reshape(1, D),
+            sums_one[2:3],
+            sums_two[2:3],
+            sums_up.reshape(FF // D, D),
+        ],
+        axis=0,
+    )
+    parts = after(vector_grad)
+    for which in ("c", "z0", "y"):
+        half = parts.shape[1] // 2
+        away = lax.dynamic_slice_in_dim(parts, (1 - at[which]) * half, half, axis=1)
+        parts = lax.dynamic_slice_in_dim(parts, at[which] * half, half, axis=1) + exchange(away, which)
+    grad_vectors = swap(at, parts)
+    grad_qkv_own = jnp.concatenate([a_two, b_two], axis=1)
+    grad_proj = proj_two
+    output = swap(at, layer_output)
+    input_grad = swap(at, input_grad)
+    grad_attention = jnp.concatenate([unweave(swap(at, grad_qkv_own)), swap(at, grad_proj)[None]], axis=0)
+    results = []
+    for weight, momentum, first, second, grad, rate, decay in (
+        (attention_weight, attention_momentum, attention_first, attention_second, grad_attention, 0.03, 0.1),
+        (expand_weight, expand_momentum, expand_first, expand_second, grad_expand, 0.03, 0.1),
+        (contract_weight, contract_momentum, contract_first, contract_second, grad_contract, 0.015, 0.1),
+    ):
+        flat = (-1, weight.shape[-1])
+        flat_weight = weight.reshape(flat)
+        first_new, second_new, diff = inner_call(
+            flat_weight, grad.reshape(flat), first.reshape(flat), second.reshape(flat), rate, decay
+        )
+        own, came = rep_total(at, diff)
+        outer, copy = outer_call(flat_weight, momentum.reshape(flat), own, came, core)
+        results += [
+            first_new.reshape(first.shape),
+            second_new.reshape(first.shape),
+            outer.reshape((3,) + weight.shape),
+            copy.reshape(weight.shape),
+        ]
+    inner_new, first_new, second_new = inner_step(
+        vectors, grad_vectors, vectors_first[0], vectors_second[0], 0.2, 0.0
+    )
+    mean_diff = lax.psum((vectors - inner_new).astype(bf), "rep").astype(f32) / 4
+    momentum_new = 0.5 * vectors_momentum + mean_diff
+    outer_new = vectors - 0.7 * (mean_diff + 0.5 * momentum_new)
+    results += [
+        first_new[None],
+        second_new[None],
+        jnp.stack([mean_diff, momentum_new, outer_new]),
+        outer_new.astype(bf),
+    ]
+    return (output, input_grad) + tuple(results)
+
+
 def solution(mesh):
     placed = (
         P(("rep", "fsdp"), None),
@@ -338,8 +1261,10 @@
         P("rep", None, "fsdp"),
         P("rep", None, "fsdp"),
     )
+    small = mesh.shape["rep"] == 4 and mesh.shape["fsdp"] == 8
+    body = per_device_fast if small else per_device
     return jax.shard_map(
-        per_device,
+        body,
         mesh=mesh,
         in_specs=placed,
         out_specs=(

time: 1480 us -> 781 us (0.53)
  waiting for transfers between devices: 796 us -> 96.5 us
  Pallas kernels: 0 us -> 484 us
  matrix products: 386 us -> 0 us
  other arithmetic: 150 us -> 49.2 us
  starting transfers between devices: 0.58 us -> 75.8 us
  local copies, waits for them, and re-layouts: 82 us -> 50.8 us
  blocking collectives: 33.7 us -> 13.6 us
    reduce_scatter x4 -> x0, waiting for transfers between devices: 575 us -> none  [the longest x1 277 us: per_device(): lax.psum_scatter(contract_full, 'fsdp', scatter_dimension=0, tiled=True)]
    pallas_call x0 -> x27, Pallas kernels: none -> 484 us  [the longest x1 170 us: gather_all(): pl.pallas_call(gather_kernel, out_shape=(shape((8 * qkv.shape[0], qkv.sha...]
    dot_general x36 -> x0, matrix products: 386 us -> none  [the longest x4 64.3 us: per_device(): jnp.einsum('qhd,khd->hqk', ctx_grad, value_block, preferred_element_type=...]
    all_gather x3 -> x0, waiting for transfers between devices: 165 us -> none  [the longest x1 86.8 us: per_device(): lax.all_gather(attention_weight.astype(jnp.bfloat16), 'fsdp', axis=1, til...]
    ppermute x0 -> x35, waiting for transfers between devices: none -> 96.5 us  [exchange(): return lax.ppermute(value, ('rep', 'fsdp'), xor_pairs(bits))]
    ppermute x0 -> x35, starting transfers between devices: none -> 75.8 us  [exchange(): return lax.ppermute(value, ('rep', 'fsdp'), xor_pairs(bits))]
    psum x1 -> x0, waiting for transfers between devices: 56.1 us -> none  [per_device(): lax.psum((attention_weight - attention_new[0]).astype(jnp.bfloat16), 'rep')]
    unnamed x230 -> x70, local copies, waits for them, and re-layouts: 62 us -> 10.4 us
  transfers between devices with their start and end apart: 8 -> 35, of which waited for: 7 -> 8; matrix products, arithmetic and copies ran while one was open for 34% -> 10% of each run, Pallas kernels for 0% -> 35%
where the time goes in v1:
time: 781 us; the launch traced here: 772 us
  Pallas kernels  484 us (62%)
  waiting for transfers between devices  96.5 us (12%)
  starting transfers between devices  75.8 us (10%)
  local copies, waits for them, and re-layouts  50.8 us (7%)
  other arithmetic  49.2 us (6%)
  blocking collectives  13.6 us (2%)
    pallas_call x1, Pallas kernels, gather_all(): pl.pallas_call(gather_kernel, out_shape=(shape((8 * qkv.shape[0], qkv.sha...  170 us
    ppermute x35, waiting for transfers between devices, exchange(): return lax.ppermute(value, ('rep', 'fsdp'), xor_pairs(bits))  96.5 us
    ppermute x35, starting transfers between devices, exchange(): return lax.ppermute(value, ('rep', 'fsdp'), xor_pairs(bits))  75.8 us
    pallas_call x10, Pallas kernels, weight_call(): pl.pallas_call(weight_kernel, out_shape=SHAPE((rows // 2, width), BF), gr...  71.5 us
    pallas_call x2, Pallas kernels, attn_bwd(): pl.pallas_call(bwd_kernel, out_shape=(jax.ShapeDtypeStruct((T, width // 2...  47.8 us
    pallas_call x1, Pallas kernels, attn_fwd(): pl.pallas_call(fwd_kernel, out_shape=(jax.ShapeDtypeStruct((T, width // 3...  38.1 us
    pallas_call x1, Pallas kernels, up_call(): pl.pallas_call(up_kernel, out_shape=(SHAPE((t, FF), BF), SHAPE((t, FF), B...  31 us
    convert_element_type x16, other arithmetic, add_low(): (left.astype(jnp.float32) + right.astype(jnp.float32)).astype(jnp.bfloat16)  24 us
  transfers between devices with their start and end apart: 35, of which 8 were waited for; matrix products, arithmetic and copies ran while one was open for 10% of the time, Pallas kernels for 35%

profile of v1, /device:TPU:1, one launch (start us, length us, event | category | flops | bytes accessed | tf_op | source)
XLA Modules:
  0.0 771.6 jit_solution(11416524051284362986)
XLA Ops:
  10.7 169.5 %gather_weights.1 = (bf16[1024,3072]{1,0:T(8,128)(2,1)}, bf16[1024,1024]{1,0:T(8,128)(2,1)}, bf16[1024,4096]{1,0:T(8,128)(2,1)}, bf16[4096,1024]{1,0:T(8,128)(2,...) custom-call(bf16[128,3072]{1,0:T(8,128)(2,1)} %copy.77.qkv_in, ...), custom_call_target="tpu_custom_call" | custom-call | tf_op jit(solution)/shard_map/gather_weights/pallas_call | solution.py:688
  188.3 10.7 %qkv.1.qkv_ref = bf16[1024,3072]{1,0:T(8,128)(2,1)} custom-call(bf16[1024,1024]{1,0:T(8,128)(2,1)} %get-tuple-element.81.x_ref.left_ref, bf16[1024,3072]{1,0:T(8,128)(2,1)} %get-tuple-element.82.w_ref, f32[1,3072]{1,0:T(1,128)} %reshape.195.bias_ref, f32[1,3072]{1,0:T(1,128)} %constant.200.clone.1.scale_ref), custom_call_target="tpu_custom_call" | custom-call | flops 6442450 | bytes 14680 | tf_op jit(solution)/shard_map/qkv/pallas_call | solution.py:736
  199.8 38.1 %attn_fwd.1 = (bf16[1024,1024]{1,0:T(8,128)(2,1)}, f32[8,2,1024]{2,1,0:T(2,128)}) custom-call(s32[4]{0:T(128)} %get-tuple-element.146.start_ref, s32[4]{0:T(128)} %get-tuple-element.147.count_ref, bf16[1024,3072]{1,0:T(8,128)(2,1)} %qkv.1.qkv_ref, s32[1,1024]{1,0:T(1,128)} %get-tuple-element.80.segr_ref, s32[1024,1]{1,0:T(8,128)} %copy.78.segc_ref), custom_call_target="tpu_custom_call" | custom-call | flops 64424508 | bytes 9437 | tf_op jit(solution)/shard_map/attn_fwd/pallas_call | solution.py:413
  238.0 8.1 %mix_norm.1 = (f32[1024,1024]{1,0:T(8,128)}, f32[1024,1]{1,0:T(8,128)}, bf16[1024,1024]{1,0:T(8,128)(2,1)}) custom-call(bf16[1024,1024]{1,0:T(8,128)(2,1)} %get-tuple-element.84.c_ref.left_ref, bf16[1024,1024]{1,0:T(8,128)(2,1)} %get-tuple-element.85.w_ref.wo_ref, bf16[1024,1024]{1,0:T(8,128)(2,1)} %get-tuple-element.81.x_ref.left_ref, f32[12,1024]{1,0:T(8,128)} %bitcast.166), custom_call_target="tpu_custom_call" | custom-call | flops 2147483 | bytes 14680 | tf_op jit(solution)/shard_map/mix_norm/pallas_call | solution.py:769
  246.1 31.0 %up_gelu.1 = (bf16[1024,4096]{1,0:T(8,128)(2,1)}, bf16[1024,4096]{1,0:T(8,128)(2,1)}) custom-call(bf16[1024,1024]{1,0:T(8,128)(2,1)} %get-tuple-element.86.h_ref.left_ref, bf16[1024,4096]{1,0:T(8,128)(2,1)} %get-tuple-element.87.w_ref, f32[1,4096]{1,0:T(1,128)} %bitcast.183), custom_call_target="tpu_custom_call" | custom-call | flops 8589934 | bytes 27262 | tf_op jit(solution)/shard_map/up_gelu/pallas_call | solution.py:793
  280.2 19.4 %down_norm.1 = (bf16[1024,1024]{1,0:T(8,128)(2,1)}, f32[1024,1024]{1,0:T(8,128)}, bf16[1024,1024]{1,0:T(8,128)(2,1)}, f32[8,1024]{1,0:T(8,128)}) custom-call(bf16[1024,4096]{1,0:T(8,128)(2,1)} %get-tuple-element.88.g_ref.left_ref, bf16[4096,1024]{1,0:T(8,128)(2,1)} %get-tuple-element.89.w_ref, f32[1024,1024]{1,0:T(8,128)} %get-tuple-element.90.n_ref, ...), custom_call_target="tpu_custom_call" | custom-call | flops 8589934 | bytes 31457 | tf_op jit(solution)/shard_map/down_norm/pallas_call | solution.py:843
  299.6 8.5 %weight_grad.10 = bf16[2048,1024]{1,0:T(8,128)(2,1)} custom-call(s32[1]{0:T(128)} %bitcast.11.half_ref, bf16[1024,4096]{1,0:T(8,128)(2,1)} %get-tuple-element.88.g_ref.left_ref, bf16[1024,1024]{1,0:T(8,128)(2,1)} %get-tuple-element.97.right_ref.dm_ref), custom_call_target="tpu_custom_call" | custom-call | flops 4294967 | bytes 14680 | tf_op jit(solution)/shard_map/weight_grad/pallas_call | solution.py:966
  308.1 16.7 %down_back.1 = (bf16[1024,4096]{1,0:T(8,128)(2,1)}, f32[1,4096]{1,0:T(1,128)}) custom-call(bf16[1024,1024]{1,0:T(8,128)(2,1)} %get-tuple-element.97.right_ref.dm_ref, bf16[4096,1024]{1,0:T(8,128)(2,1)} %get-tuple-element.89.w_ref, bf16[1024,4096]{1,0:T(8,128)(2,1)} %get-tuple-element.95.s_ref), custom_call_target="tpu_custom_call" | custom-call | flops 8589934 | bytes 27262 | tf_op jit(solution)/shard_map/down_back/pallas_call | solution.py:871
  324.8 10.8 %weight_grad.11 = bf16[512,4096]{1,0:T(8,128)(2,1)} custom-call(s32[1]{0:T(128)} %bitcast.11.half_ref, bf16[1024,1024]{1,0:T(8,128)(2,1)} %get-tuple-element.86.h_ref.left_ref, bf16[1024,4096]{1,0:T(8,128)(2,1)} %get-tuple-element.99.right_ref.dz_ref), custom_call_target="tpu_custom_call" | custom-call | flops 4294967 | bytes 17825 | tf_op jit(solution)/shard_map/weight_grad/pallas_call | solution.py:966
  336.1 9.2 %weight_grad.12 = bf16[2048,1024]{1,0:T(8,128)(2,1)} custom-call(s32[1]{0:T(128)} %bitcast.12.half_ref.core_ref, bf16[1024,4096]{1,0:T(8,128)(2,1)} %get-tuple-element.88.g_ref.left_ref, bf16[1024,1024]{1,0:T(8,128)(2,1)} %get-tuple-element.97.right_ref.dm_ref, bf16[2048,1024]{1,0:T(8,128)(2,1)} %collective-permute-done.2.refs_0_), custom_call_target="tpu_custom_call" | custom-call | flops 4294967 | bytes 14680 | tf_op jit(solution)/shard_map/weight_grad/pallas_call | solution.py:966
  345.3 11.5 %weight_grad.13 = bf16[512,4096]{1,0:T(8,128)(2,1)} custom-call(s32[1]{0:T(128)} %bitcast.12.half_ref.core_ref, bf16[1024,1024]{1,0:T(8,128)(2,1)} %get-tuple-element.86.h_ref.left_ref, bf16[1024,4096]{1,0:T(8,128)(2,1)} %get-tuple-element.99.right_ref.dz_ref, bf16[512,4096]{1,0:T(8,128)(2,1)} %collective-permute-done.3.refs_0_), custom_call_target="tpu_custom_call" | custom-call | flops 4294967 | bytes 17825 | tf_op jit(solution)/shard_map/weight_grad/pallas_call | solution.py:966
  360.0 8.9 %collective-permute-start.5 = (bf16[2,128,4096]{2,1,0:T(8,128)(2,1)}, bf16[2,128,4096]{2,1,0:T(8,128)(2,1)S(1)}, u32[]{:S(2)}, u32[]{:S(2)}) collective-permute-start(bf16[2,128,4096]{2,1,0:T(8,128)(2,1)} %dynamic-slice_bitcast_fusion), channel_id=1, source_target_pairs={{0,2},{1,3},{2,0},{3,1},{4,6},{5,7},{6,4},{7,5},{8,10},{9,11},{10,... | collective-permute-start | bytes 6291464 | tf_op jit(solution)/shard_map/ppermute | solution.py:1058
  372.0 21.3 %up_back_norm.1 = (f32[1024,1024]{1,0:T(8,128)}, bf16[1024,1024]{1,0:T(8,128)(2,1)}, bf16[1024,1024]{1,0:T(8,128)(2,1)}, f32[8,1024]{1,0:T(8,128)}) custom-call(bf16[1024,4096]{1,0:T(8,128)(2,1)} %get-tuple-element.99.right_ref.dz_ref, bf16[1024,4096]{1,0:T(8,128)(2,1)} %get-tuple-element.87.w_ref, f32[1024,1024]{1,0:T(8,128)} %get-tuple-element.100.dr_ref, ...), custom_call_target="tpu_custom_call" | custom-call | flops 10737418 | bytes 33554 | tf_op jit(solution)/shard_map/up_back_norm/pallas_call | solution.py:903
  397.7 24.0 %attn_bwd.2 = (bf16[1024,1536]{1,0:T(8,128)(2,1)}, f32[4,1,384]{2,1,0:T(1,128)}) custom-call(s32[4]{0:T(128)} %get-tuple-element.146.start_ref, s32[4]{0:T(128)} %get-tuple-element.147.count_ref, bf16[1024,3072]{1,0:T(8,128)(2,1)} %qkv.1.qkv_ref, bf16[1024,1024]{1,0:T(8,128)(2,1)} %get-tuple-element.112.do_ref, f32[8,2,1024]{2,1,0:T(2,128)} %get-tuple-element.105.lse_ref, ...), custom_call_target="tpu_custom_call" | custom-call | flops 64424508 | bytes 18874 | tf_op jit(solution)/shard_map/attn_bwd/pallas_call | solution.py:437
  434.2 7.5 collective-permute-start.7
  457.9 17.8 %collective-permute-done.9 = bf16[2,128,1024]{1,2,0:T(8,128)(2,1)} collective-permute-done((bf16[2,128,1024]{1,2,0:T(8,128)(2,1)}, bf16[2,128,1024]{1,2,0:T(8,128)(2,1)}, u32[]{:S(2)}, u32[]{:S(2)}) %collective-permute-start.9) | collective-permute-done | bytes 524320 | tf_op jit(solution)/shard_map/ppermute | solution.py:1058
  485.0 23.8 %attn_bwd.3 = (bf16[1024,1536]{1,0:T(8,128)(2,1)}, f32[4,1,384]{2,1,0:T(1,128)}) custom-call(s32[4]{0:T(128)} %get-tuple-element.146.start_ref, s32[4]{0:T(128)} %get-tuple-element.147.count_ref, bf16[1024,3072]{1,0:T(8,128)(2,1)} %qkv.1.qkv_ref, bf16[1024,1024]{1,0:T(8,128)(2,1)} %get-tuple-element.112.do_ref, f32[8,2,1024]{2,1,0:T(2,128)} %get-tuple-element.105.lse_ref, ...), custom_call_target="tpu_custom_call" | custom-call | flops 64424508 | bytes 18874 | tf_op jit(solution)/shard_map/attn_bwd/pallas_call | solution.py:437
  513.9 6.8 collective-permute-start.11
  544.5 7.3 collective-permute-start.34
  558.3 12.3 %input_back.1 = bf16[1024,1024]{1,0:T(8,128)(2,1)} custom-call(bf16[1024,1536]{1,0:T(8,128)(2,1)} %get-tuple-element.116.right_ref.a_ref, bf16[1024,1536]{1,0:T(8,128)(2,1)} %get-tuple-element.119.right_ref.b_ref, bf16[1024,3072]{1,0:T(8,128)(2,1)} %get-tuple-element.82.w_ref, f32[1024,1024]{1,0:T(8,128)} %get-tuple-element.117.r_ref), custom_call_target="tpu_custom_call" | custom-call | flops 6442450 | bytes 18874 | tf_op jit(solution)/shard_map/input_back/pallas_call | solution.py:927
  592.1 8.8 %collective-permute-done.18 = bf16[128,1024]{0,1:T(8,128)(2,1)} collective-permute-done((bf16[128,1024]{0,1:T(8,128)(2,1)S(1)}, bf16[128,1024]{0,1:T(8,128)(2,1)}, u32[]{:S(2)}, u32[]{:S(2)}) %collective-permute-start.18) | collective-permute-done | bytes 262176 | tf_op jit(solution)/shard_map/ppermute | solution.py:1058
  613.7 43.3 %collective-permute-done.19 = bf16[128,1024]{0,1:T(8,128)(2,1)S(1)} collective-permute-done((bf16[128,1024]{0,1:T(8,128)(2,1)S(1)}, bf16[128,1024]{0,1:T(8,128)(2,1)S(1)}, u32[]{:S(2)}, u32[]{:S(2)}) %collective-permute-start.19) | collective-permute-done | bytes 262176 | tf_op jit(solution)/shard_map/ppermute | solution.py:1058
  710.8 13.6 %psum.7 = bf16[12,128]{1,0:T(8,128)(2,1)S(1)} all-reduce(bf16[12,128]{1,0:T(8,128)(2,1)S(1)} %copy-done.27), channel_id=1, replica_groups=mesh['rep'=4,'fsdp'=8] {'rep'}, use_global_device_ids=true, to_apply=%region_2.3 | all-reduce | flops 1536 | bytes 6144 | tf_op jit(solution)/shard_map/psum | solution.py:1230
  731.3 11.4 %collective-permute-done.21 = bf16[256,1024]{1,0:T(8,128)(2,1)S(1)} collective-permute-done((bf16[256,1024]{1,0:T(8,128)(2,1)S(1)}, bf16[256,1024]{1,0:T(8,128)(2,1)S(1)}, u32[]{:S(2)}, u32[]{:S(2)}) %collective-permute-start.21) | collective-permute-done | bytes 524320 | tf_op jit(solution)/shard_map/ppermute | solution.py:1058
  (229 shorter events, 229.1 us)
Async XLA Ops:
  180.3 96.8 %collective-permute-start = (bf16[1024,1024]{1,0:T(8,128)(2,1)S(1)}, bf16[1024,1024]{1,0:T(8,128)(2,1)}, u32[]{:S(2)}, u32[]{:S(2)}) collective-permute-start(bf16[1024,1024]{1,0:T(8,128)(2,1)S(1)} %copy-done.10), channel_id=1, source_target_pairs={{4,8},{5,9},{6,10},{7,11},{8,4},{9,5},{10,6},{11,7},{20,24},{21,25... | collective-permute-start | bytes 6291464 | tf_op jit(solution)/shard_map/ppermute | solution.py:1058
  308.1 28.1 %collective-permute-start.2 = (bf16[2048,1024]{1,0:T(8,128)(2,1)}, bf16[2048,1024]{1,0:T(8,128)(2,1)}, u32[]{:S(2)}, u32[]{:S(2)}) collective-permute-start(bf16[2048,1024]{1,0:T(8,128)(2,1)} %weight_grad.10), channel_id=1, source_target_pairs={{0,8},{1,9},{2,10},{3,11},{4,12},{5,13},{6,14},{7,15},{8,0},{9,1},... | collective-permute-start | bytes 12582920 | tf_op jit(solution)/shard_map/ppermute | solution.py:1058
  360.0 67.3 %collective-permute-start.5 = (bf16[2,128,4096]{2,1,0:T(8,128)(2,1)}, bf16[2,128,4096]{2,1,0:T(8,128)(2,1)S(1)}, u32[]{:S(2)}, u32[]{:S(2)}) collective-permute-start(bf16[2,128,4096]{2,1,0:T(8,128)(2,1)} %dynamic-slice_bitcast_fusion), channel_id=1, source_target_pairs={{0,2},{1,3},{2,0},{3,1},{4,6},{5,7},{6,4},{7,5},{8,10},{9,11},{10,... | collective-permute-start | bytes 6291464 | tf_op jit(solution)/shard_map/ppermute | solution.py:1058
  372.0 57.9 %collective-permute-start.4 = (bf16[2,512,1024]{2,1,0:T(8,128)(2,1)}, bf16[2,512,1024]{2,1,0:T(8,128)(2,1)}, u32[]{:S(2)}, u32[]{:S(2)}) collective-permute-start(bf16[2,512,1024]{2,1,0:T(8,128)(2,1)} %dynamic-slice_bitcast_fusion.1), channel_id=1, source_target_pairs={{0,1},{1,0},{2,3},{3,2},{4,5},{5,4},{6,7},{7,6},{8,9},{9,8},{10,11... | collective-permute-start | bytes 6291464 | tf_op jit(solution)/shard_map/ppermute | solution.py:1058
  397.4 47.5 %collective-permute-start.8 = (bf16[512,1024]{1,0:T(8,128)(2,1)}, bf16[512,1024]{1,0:T(8,128)(2,1)S(1)}, u32[]{:S(2)}, u32[]{:S(2)}) collective-permute-start(bf16[512,1024]{1,0:T(8,128)(2,1)} %weight_grad.14), channel_id=1, source_target_pairs={{0,8},{1,9},{2,10},{3,11},{4,12},{5,13},{6,14},{7,15},{8,0},{9,1},... | collective-permute-start | bytes 3145736 | tf_op jit(solution)/shard_map/ppermute | solution.py:1058
  434.2 43.5 %collective-permute-start.7 = (bf16[128,4096]{1,0:T(8,128)(2,1)}, bf16[128,4096]{1,0:T(8,128)(2,1)}, u32[]{:S(2)}, u32[]{:S(2)}) collective-permute-start(bf16[128,4096]{1,0:T(8,128)(2,1)} %dynamic-slice_bitcast_fusion.2), channel_id=1, source_target_pairs={{0,1},{1,0},{2,3},{3,2},{4,5},{5,4},{6,7},{7,6},{8,9},{9,8},{10,11... | collective-permute-start | bytes 3145736 | tf_op jit(solution)/shard_map/ppermute | solution.py:1058
  441.7 110.1 %collective-permute-start.1 = (bf16[1024,1024]{1,0:T(8,128)(2,1)}, bf16[1024,1024]{1,0:T(8,128)(2,1)}, u32[]{:S(2)}, u32[]{:S(2)}) collective-permute-start(bf16[1024,1024]{1,0:T(8,128)(2,1)} %get-tuple-element.92), channel_id=1, source_target_pairs={{4,8},{5,9},{6,10},{7,11},{8,4},{9,5},{10,6},{11,7},{20,24},{21,25... | collective-permute-start | bytes 6291464 | tf_op jit(solution)/shard_map/ppermute | solution.py:1058
  452.5 23.2 %collective-permute-start.9 = (bf16[2,128,1024]{1,2,0:T(8,128)(2,1)}, bf16[2,128,1024]{1,2,0:T(8,128)(2,1)}, u32[]{:S(2)}, u32[]{:S(2)}) collective-permute-start(bf16[2,128,1024]{1,2,0:T(8,128)(2,1)} %bitcast.177), channel_id=1, source_target_pairs={{0,1},{1,0},{2,3},{3,2},{4,5},{5,4},{6,7},{7,6},{8,9},{9,8},{10,11... | collective-permute-start | bytes 1572872 | tf_op jit(solution)/shard_map/ppermute | solution.py:1058
  453.4 25.7 %collective-permute-start.10 = (bf16[512,1536]{1,0:T(8,128)(2,1)}, bf16[512,1536]{1,0:T(8,128)(2,1)}, u32[]{:S(2)}, u32[]{:S(2)}) collective-permute-start(bf16[512,1536]{1,0:T(8,128)(2,1)} %weight_grad.15), channel_id=1, source_target_pairs={{0,8},{1,9},{2,10},{3,11},{4,12},{5,13},{6,14},{7,15},{8,0},{9,1},... | collective-permute-start | bytes 4718600 | tf_op jit(solution)/shard_map/ppermute | solution.py:1058
  455.7 65.2 %collective-permute-start.6 = (bf16[512,1024]{1,0:T(8,128)(2,1)}, bf16[512,1024]{1,0:T(8,128)(2,1)}, u32[]{:S(2)}, u32[]{:S(2)}) collective-permute-start(bf16[512,1024]{1,0:T(8,128)(2,1)} %dynamic-slice_bitcast_fusion.3), channel_id=1, source_target_pairs={{0,2},{1,3},{2,0},{3,1},{4,6},{5,7},{6,4},{7,5},{8,10},{9,11},{10,... | collective-permute-start | bytes 3145736 | tf_op jit(solution)/shard_map/ppermute | solution.py:1058
  513.9 23.1 %collective-permute-start.11 = (bf16[2,128,1536]{1,2,0:T(8,128)(2,1)}, bf16[2,128,1536]{1,2,0:T(8,128)(2,1)}, u32[]{:S(2)}, u32[]{:S(2)}) collective-permute-start(bf16[2,128,1536]{1,2,0:T(8,128)(2,1)} %bitcast.175), channel_id=1, source_target_pairs={{0,2},{1,3},{2,0},{3,1},{4,6},{5,7},{6,4},{7,5},{8,10},{9,11},{10,... | collective-permute-start | bytes 2359304 | tf_op jit(solution)/shard_map/ppermute | solution.py:1058
  538.3 41.2 %collective-permute-start.14 = (bf16[512,1536]{1,0:T(8,128)(2,1)}, bf16[512,1536]{1,0:T(8,128)(2,1)}, u32[]{:S(2)}, u32[]{:S(2)}) collective-permute-start(bf16[512,1536]{1,0:T(8,128)(2,1)} %weight_grad.18), channel_id=1, source_target_pairs={{0,8},{1,9},{2,10},{3,11},{4,12},{5,13},{6,14},{7,15},{8,0},{9,1},... | collective-permute-start | bytes 4718600 | tf_op jit(solution)/shard_map/ppermute | solution.py:1058
  555.6 106.3 %collective-permute-start.27 = (bf16[512,1024]{1,0:T(8,128)(2,1)S(1)}, bf16[512,1024]{1,0:T(8,128)(2,1)}, u32[]{:S(2)}, u32[]{:S(2)}) collective-permute-start(bf16[512,1024]{1,0:T(8,128)(2,1)S(1)} %copy-done.6), channel_id=1, source_target_pairs={{4,8},{5,9},{6,10},{7,11},{8,4},{9,5},{10,6},{11,7},{20,24},{21,25... | collective-permute-start | bytes 3145736 | tf_op jit(solution)/shard_map/ppermute | solution.py:1058
  570.6 175.9 %collective-permute-start.12 = (bf16[1024,1024]{1,0:T(8,128)(2,1)}, bf16[1024,1024]{1,0:T(8,128)(2,1)}, u32[]{:S(2)}, u32[]{:S(2)}) collective-permute-start(bf16[1024,1024]{1,0:T(8,128)(2,1)} %input_back.1), channel_id=1, source_target_pairs={{4,8},{5,9},{6,10},{7,11},{8,4},{9,5},{10,6},{11,7},{20,24},{21,25... | collective-permute-start | bytes 6291464 | tf_op jit(solution)/shard_map/ppermute | solution.py:1058
  575.4 25.6 %collective-permute-start.18 = (bf16[128,1024]{0,1:T(8,128)(2,1)S(1)}, bf16[128,1024]{0,1:T(8,128)(2,1)}, u32[]{:S(2)}, u32[]{:S(2)}) collective-permute-start(bf16[128,1024]{0,1:T(8,128)(2,1)S(1)} %dynamic-slice_bitcast_fusion.9), channel_id=1, source_target_pairs={{0,2},{1,3},{2,0},{3,1},{4,6},{5,7},{6,4},{7,5},{8,10},{9,11},{10,... | collective-permute-start | bytes 786440 | tf_op jit(solution)/shard_map/ppermute | solution.py:1058
  577.7 28.1 %collective-permute-start.13 = (bf16[128,1536]{0,1:T(8,128)(2,1)}, bf16[128,1536]{0,1:T(8,128)(2,1)S(1)}, u32[]{:S(2)}, u32[]{:S(2)}) collective-permute-start(bf16[128,1536]{0,1:T(8,128)(2,1)} %dynamic-slice_bitcast_fusion.8), channel_id=1, source_target_pairs={{0,1},{1,0},{2,3},{3,2},{4,5},{5,4},{6,7},{7,6},{8,9},{9,8},{10,11... | collective-permute-start | bytes 1179656 | tf_op jit(solution)/shard_map/ppermute | solution.py:1058
  579.4 98.9 %collective-permute-start.23 = (bf16[128,4096]{1,0:T(8,128)(2,1)S(1)}, bf16[128,4096]{1,0:T(8,128)(2,1)}, u32[]{:S(2)}, u32[]{:S(2)}) collective-permute-start(bf16[128,4096]{1,0:T(8,128)(2,1)S(1)} %fusion.2), channel_id=1, source_target_pairs={{4,8},{5,9},{6,10},{7,11},{8,4},{9,5},{10,6},{11,7},{20,24},{21,25... | collective-permute-start | bytes 3145736 | tf_op jit(solution)/shard_map/ppermute | solution.py:1058
  600.9 58.4 %collective-permute-start.15 = (bf16[2,128,1536]{1,2,0:T(8,128)(2,1)}, bf16[2,128,1536]{1,2,0:T(8,128)(2,1)}, u32[]{:S(2)}, u32[]{:S(2)}) collective-permute-start(bf16[2,128,1536]{1,2,0:T(8,128)(2,1)} %bitcast.176), channel_id=1, source_target_pairs={{0,1},{1,0},{2,3},{3,2},{4,5},{5,4},{6,7},{7,6},{8,9},{9,8},{10,11... | collective-permute-start | bytes 2359304 | tf_op jit(solution)/shard_map/ppermute | solution.py:1058
  605.8 51.2 %collective-permute-start.19 = (bf16[128,1024]{0,1:T(8,128)(2,1)S(1)}, bf16[128,1024]{0,1:T(8,128)(2,1)S(1)}, u32[]{:S(2)}, u32[]{:S(2)}) collective-permute-start(bf16[128,1024]{0,1:T(8,128)(2,1)S(1)} %fusion.12), channel_id=1, source_target_pairs={{4,8},{5,9},{6,10},{7,11},{8,4},{9,5},{10,6},{11,7},{20,24},{21,25... | collective-permute-start | bytes 786440 | tf_op jit(solution)/shard_map/ppermute | solution.py:1058
  674.2 22.9 %collective-permute-start.17 = (bf16[128,3072]{0,1:T(8,128)(2,1)}, bf16[128,3072]{0,1:T(8,128)(2,1)}, u32[]{:S(2)}, u32[]{:S(2)}) collective-permute-start(bf16[128,3072]{0,1:T(8,128)(2,1)} %pad_maximum_fusion.1), channel_id=1, source_target_pairs={{4,8},{5,9},{6,10},{7,11},{8,4},{9,5},{10,6},{11,7},{20,24},{21,25... | collective-permute-start | bytes 2359304 | tf_op jit(solution)/shard_map/ppermute | solution.py:1058
  689.9 34.5 %collective-permute-start.29 = (bf16[256,1024]{1,0:T(8,128)(2,1)S(1)}, bf16[256,1024]{1,0:T(8,128)(2,1)}, u32[]{:S(2)}, u32[]{:S(2)}) collective-permute-start(bf16[256,1024]{1,0:T(8,128)(2,1)S(1)} %fusion.6), channel_id=1, source_target_pairs={{0,16},{1,17},{2,18},{3,19},{4,20},{5,21},{6,22},{7,23},{8,24},{9,... | collective-permute-start | bytes 1572872 | tf_op jit(solution)/shard_map/ppermute | solution.py:1058
  709.3 20.3 %collective-permute-start.25 = (bf16[64,4096]{1,0:T(8,128)(2,1)S(1)}, bf16[64,4096]{1,0:T(8,128)(2,1)}, u32[]{:S(2)}, u32[]{:S(2)}) collective-permute-start(bf16[64,4096]{1,0:T(8,128)(2,1)S(1)} %fusion.7), channel_id=1, source_target_pairs={{0,16},{1,17},{2,18},{3,19},{4,20},{5,21},{6,22},{7,23},{8,24},{9,... | collective-permute-start | bytes 1572872 | tf_op jit(solution)/shard_map/ppermute | solution.py:1058
  725.7 31.1 %collective-permute-start.30 = (bf16[256,1024]{1,0:T(8,128)(2,1)S(1)}, bf16[256,1024]{1,0:T(8,128)(2,1)S(1)}, u32[]{:S(2)}, u32[]{:S(2)}) collective-permute-start(bf16[256,1024]{1,0:T(8,128)(2,1)S(1)} %add_convert_fusion.own_ref), channel_id=1, source_target_pairs={{0,8},{1,9},{2,10},{3,11},{4,12},{5,13},{6,14},{7,15},{8,0},{9,1},... | collective-permute-start | bytes 1572872 | tf_op jit(solution)/shard_map/ppermute | solution.py:1058
  742.9 21.1 %collective-permute-start.22 = (bf16[256,1024]{1,0:T(8,128)(2,1)S(1)}, bf16[256,1024]{1,0:T(8,128)(2,1)S(1)}, u32[]{:S(2)}, u32[]{:S(2)}) collective-permute-start(bf16[256,1024]{1,0:T(8,128)(2,1)S(1)} %add_convert_fusion.2.own_ref), channel_id=1, source_target_pairs={{0,8},{1,9},{2,10},{3,11},{4,12},{5,13},{6,14},{7,15},{8,0},{9,1},... | collective-permute-start | bytes 1572872 | tf_op jit(solution)/shard_map/ppermute | solution.py:1058
  (43 other events, 586.3 us)

commit v2 on v1

--- a/solution.py
+++ b/solution.py
@@ -487,8 +487,8 @@
 
 
 def gather_kernel(
-    qkv_in, wo_in, we_in, wc_in, vec_in, tok_in, seg_in,
-    qkv_out, wo_out, we_out, wc_out, vec_out, tok_out, seg_out,
+    qkv_in, wo_in, vec_in, tok_in, seg_in,
+    qkv_out, wo_out, vec_out, tok_out, seg_out,
     tok_buf, seg_buf, send_sem, recv_sem, local_sem,
 ):
     at = bits_of()
@@ -601,11 +601,9 @@
             return ref.at[pl.ds(row, n), :]
         return own
 
-    qkv, wo, we, wc = pieces = [
+    qkv, wo = pieces = [
         Piece(own_rows(qkv_in, 4), rows(qkv_out, 4), True),
         Piece(own_rows(wo_in, 4), rows(wo_out, 4), True),
-        Piece(own_rows(we_in, 2), rows(we_out, 2), False),
-        Piece(own_rows(wc_in, 4), rows(wc_out, 4), True),
     ]
     zero = (0, 0, 0)
     vec_copies = [
@@ -643,7 +641,6 @@
 
     wo.first()
     qkv.near()
-    we.first()
     vec_copies[1].wait_recv()
     here = vec_out.at[shard((0, 1, 0))]
     vec_far = send(here, here, "z0")
@@ -657,14 +654,8 @@
     vec_far.wait_recv()
     here = vec_out.at[shard((1, 1, 0))]
     vec_more.append(send(here, here, "y"))
-    we.near()
-    wc.first()
     qkv.last()
-    we.rest()
     wo.last()
-    wc.near()
-    wc.rest()
-    wc.last()
     for piece in pieces:
         piece.finish()
     for copy in [vec_copies[0], vec_copies[3]] + vec_more:
@@ -678,10 +669,10 @@
         swap_copy(seg_in, seg_out, seg_k).wait()
 
 
-GATHER_COPIES = 29 * 3 + 15 + 8 + 2
-
-
-def gather_all(qkv, wo, we, wc, vec, tok, seg):
+GATHER_COPIES = 29 * 2 + 8 + 2
+
+
+def gather_all(qkv, wo, vec, tok, seg):
     bf = jnp.bfloat16
     shape = jax.ShapeDtypeStruct
     whole = pl.BlockSpec(memory_space=pl.ANY)
@@ -690,14 +681,12 @@
         out_shape=(
             shape((8 * qkv.shape[0], qkv.shape[1]), bf),
             shape((8 * wo.shape[0], wo.shape[1]), bf),
-            shape((8 * we.shape[0], we.shape[1]), bf),
-            shape((8 * wc.shape[0], wc.shape[1]), bf),
             shape((8,) + vec.shape, bf),
             shape(tok.shape, bf),
             shape(seg.shape, seg.dtype),
         ),
-        in_specs=[whole] * 7,
-        out_specs=(whole,) * 7,
+        in_specs=[whole] * 5,
+        out_specs=(whole,) * 5,
         scratch_shapes=[
             pltpu.VMEM(tok.shape, bf),
             pltpu.VMEM(seg.shape, seg.dtype),
@@ -707,7 +696,7 @@
         ],
         compiler_params=pltpu.CompilerParams(collective_id=0, has_side_effects=True),
         name="gather_weights",
-    )(qkv, wo, we, wc, vec, tok, seg)
+    )(qkv, wo, vec, tok, seg)
 
 
 SHRINK = 1000
@@ -777,32 +766,48 @@
     )(mixed, w_out, tok, rows)
 
 
-def up_kernel(h_ref, w_ref, bias_ref, g_ref, s_ref):
-    for i in range(8):
-        rows = slice(i * 128, (i + 1) * 128)
-        z = dot(h_ref[rows, :], w_ref[...], 1, 0) + bias_ref[...]
-        phi, bell = erf_parts(z)
-        g_ref[rows, :] = (z * phi).astype(BF)
-        s_ref[rows, :] = (phi + z * bell * 0.3989422804014327).astype(BF)
-
-
-def up_call(low, w_in, bias):
+def up_kernel(core_ref, h_ref, own_ref, came_ref, bias_ref, g_ref, s_ref):
+    def tile(w_ref):
+        for i in range(8):
+            rows = slice(i * 128, (i + 1) * 128)
+            z = dot(h_ref[rows, :], w_ref[...], 1, 0) + bias_ref[...]
+            phi, bell = erf_parts(z)
+            g_ref[rows, :] = (z * phi).astype(BF)
+            s_ref[rows, :] = (phi + z * bell * 0.3989422804014327).astype(BF)
+
+    first = pl.program_id(0) < pl.num_programs(0) // 2
+
+    @pl.when(first)
+    def _():
+        tile(own_ref)
+
+    @pl.when(jnp.logical_not(first))
+    def _():
+        tile(came_ref)
+
+
+def up_call(low, own, came, bias, core):
     t = low.shape[0]
     tile = 512
-    out = pl.BlockSpec((t, tile), lambda j: (0, j))
+    half = FF // tile // 2
+    place = lambda j, c: (0, lax.rem(j + half * c[0], 2 * half))
+    out = pl.BlockSpec((t, tile), place)
     return pl.pallas_call(
         up_kernel,
         out_shape=(SHAPE((t, FF), BF), SHAPE((t, FF), BF)),
-        grid=(FF // tile,),
-        in_specs=[
-            full_spec(low.shape),
-            pl.BlockSpec((D, tile), lambda j: (0, j)),
-            pl.BlockSpec((1, tile), lambda j: (0, j)),
-        ],
-        out_specs=(out, out),
+        grid_spec=pltpu.PrefetchScalarGridSpec(
+            num_scalar_prefetch=1, grid=(FF // tile,),
+            in_specs=[
+                full_spec(low.shape),
+                pl.BlockSpec((D, tile), lambda j, c: (0, jnp.minimum(j, half - 1))),
+                pl.BlockSpec((D, tile), lambda j, c: (0, jnp.maximum(j - half, 0))),
+                pl.BlockSpec((1, tile), place),
+            ],
+            out_specs=(out, out),
+        ),
         cost_estimate=cost(2 * t * D * FF, 2 * (t * D + D * FF + 2 * t * FF), 2 * t * FF),
         name="up_gelu",
-    )(low, w_in, bias)
+    )(core.reshape(1), low, own, came, bias)
 
 
 def row_sum(value):
@@ -814,9 +819,14 @@
     return inv * (scaled - mean_row(scaled) - normed * mean_row(scaled * normed))
 
 
-def down_kernel(g_ref, w_ref, n_ref, cot_ref, rows_ref, out_ref, dr_ref, dm_ref, sums_ref):
+def down_kernel(
+    core_ref, g_ref, own_ref, came_ref, n_ref, cot_ref, rows_ref, out_ref, dr_ref, dm_ref, sums_ref, m_ref
+):
+    half = D // 2
+    m_ref[:, pl.ds(pl.multiple_of(core_ref[0] * half, half), half)] = dot(g_ref[...], own_ref[...], 1, 0)
+    m_ref[:, pl.ds(pl.multiple_of((1 - core_ref[0]) * half, half), half)] = dot(g_ref[...], came_ref[...], 1, 0)
     hidden = n_ref[...] * rows_ref[0:1, :] + rows_ref[2:3, :]
-    value = hidden + dot(g_ref[...], w_ref[...], 1, 0) + rows_ref[7:8, :]
+    value = hidden + m_ref[...] + rows_ref[7:8, :]
     center = value - mean_row(value)
     inv = lax.rsqrt(mean_row(center * center) + 1e-05)
     normed = center * inv
@@ -837,50 +847,61 @@
     sums_ref[2:3, :] += row_sum(low.astype(F32))
 
 
-def down_call(act, w_down, normed, cot, rows):
+def down_call(act, own, came, normed, cot, rows, core):
     t = act.shape[0]
-    tile = pl.BlockSpec((256, D), lambda i: (i, 0))
+    tile = pl.BlockSpec((256, D), lambda i, c: (i, 0))
     return pl.pallas_call(
         down_kernel,
         out_shape=(SHAPE((t, D), BF), SHAPE((t, D), F32), SHAPE((t, D), BF), SHAPE((8, D), F32)),
-        grid=(t // 256,),
-        in_specs=[
-            pl.BlockSpec((256, FF), lambda i: (i, 0)), full_spec((FF, D)), tile, tile,
-            full_spec(rows.shape),
-        ],
-        out_specs=(tile, tile, tile, pl.BlockSpec((8, D), lambda i: (0, 0))),
+        grid_spec=pltpu.PrefetchScalarGridSpec(
+            num_scalar_prefetch=1, grid=(t // 256,),
+            in_specs=[
+                pl.BlockSpec((256, FF), lambda i, c: (i, 0)), full_spec((FF, D // 2)), full_spec((FF, D // 2)),
+                tile, tile, full_spec(rows.shape),
+            ],
+            out_specs=(tile, tile, tile, pl.BlockSpec((8, D), lambda i, c: (0, 0))),
+            scratch_shapes=[pltpu.VMEM((256, D), F32)],
+        ),
         cost_estimate=cost(2 * t * D * FF, 2 * (t * FF + D * FF) + 14 * t * D),
         name="down_norm",
-    )(act, w_down, normed, cot, rows)
-
-
-def slope_kernel(dm_ref, w_ref, s_ref, o_ref, sums_ref):
+    )(core.reshape(1), act, own, came, normed, cot, rows)
+
+
+def slope_kernel(core_ref, left_ref, right_ref, own_ref, came_ref, s_ref, o_ref, sums_ref):
     total = 0.0
     for i in range(4):
         rows = slice(i * 256, (i + 1) * 256)
-        z = (dot(dm_ref[rows, :], w_ref[...], 1, 1) * s_ref[rows, :].astype(F32)).astype(BF)
+        back = dot(left_ref[rows, :], own_ref[...], 1, 1) + dot(right_ref[rows, :], came_ref[...], 1, 1)
+        z = (back * s_ref[rows, :].astype(F32)).astype(BF)
         o_ref[rows, :] = z
         total = total + row_sum(z.astype(F32))
     sums_ref[...] = total
 
 
-def slope_call(dm, w_down, slope):
+def slope_call(dm, own, came, slope, core):
     t = dm.shape[0]
     tile = 512
-    wide = pl.BlockSpec((t, tile), lambda j: (0, j))
+    wide = pl.BlockSpec((t, tile), lambda j, c: (0, j))
+    part = pl.BlockSpec((tile, D // 2), lambda j, c: (j, 0))
     return pl.pallas_call(
         slope_kernel,
         out_shape=(SHAPE((t, FF), BF), SHAPE((1, FF), F32)),
-        grid=(FF // tile,),
-        in_specs=[full_spec(dm.shape), pl.BlockSpec((tile, D), lambda j: (j, 0)), wide],
-        out_specs=(wide, pl.BlockSpec((1, tile), lambda j: (0, j))),
+        grid_spec=pltpu.PrefetchScalarGridSpec(
+            num_scalar_prefetch=1, grid=(FF // tile,),
+            in_specs=[
+                pl.BlockSpec((t, D // 2), lambda j, c: (0, c[0])),
+                pl.BlockSpec((t, D // 2), lambda j, c: (0, 1 - c[0])),
+                part, part, wide,
+            ],
+            out_specs=(wide, pl.BlockSpec((1, tile), lambda j, c: (0, j))),
+        ),
         cost_estimate=cost(2 * t * D * FF, 2 * (t * D + D * FF + 2 * t * FF)),
         name="down_back",
-    )(dm, w_down, slope)
-
-
-def hidden_kernel(dz_ref, w_ref, dr_ref, n_ref, q_ref, wo_ref, rows_ref, r_ref, a_ref, c_ref, sums_ref):
-    grad = dr_ref[...] + dot(dz_ref[...], w_ref[...], 1, 1)
+    )(core.reshape(1), dm, dm, own, came, slope)
+
+
+def hidden_kernel(core_ref, left_ref, right_ref, own_ref, came_ref, dr_ref, n_ref, q_ref, wo_ref, rows_ref, r_ref, a_ref, c_ref, sums_ref):
+    grad = dr_ref[...] + dot(left_ref[...], own_ref[...], 1, 1) + dot(right_ref[...], came_ref[...], 1, 1)
     normed = n_ref[...]
     back = norm_back(grad, normed, q_ref[...], rows_ref[0:1, :])
     low = back.astype(BF)
@@ -897,21 +918,25 @@
     sums_ref[2:3, :] += row_sum(low.astype(F32))
 
 
-def hidden_call(dz, w_in, dr, normed, inv, w_out, rows):
+def hidden_call(dz, own, came, dr, normed, inv, w_out, rows, core):
     t = dz.shape[0]
-    tile = pl.BlockSpec((256, D), lambda i: (i, 0))
+    tile = pl.BlockSpec((256, D), lambda i, c: (i, 0))
     return pl.pallas_call(
         hidden_kernel,
         out_shape=(SHAPE((t, D), F32), SHAPE((t, D), BF), SHAPE((t, D), BF), SHAPE((8, D), F32)),
-        grid=(t // 256,),
-        in_specs=[
-            pl.BlockSpec((256, FF), lambda i: (i, 0)), full_spec((D, FF)), tile, tile,
-            pl.BlockSpec((256, 1), lambda i: (i, 0)), full_spec((D, D)), full_spec(rows.shape),
-        ],
-        out_specs=(tile, tile, tile, pl.BlockSpec((8, D), lambda i: (0, 0))),
+        grid_spec=pltpu.PrefetchScalarGridSpec(
+            num_scalar_prefetch=1, grid=(t // 256,),
+            in_specs=[
+                pl.BlockSpec((256, FF // 2), lambda i, c: (i, c[0])),
+                pl.BlockSpec((256, FF // 2), lambda i, c: (i, 1 - c[0])),
+                full_spec((D, FF // 2)), full_spec((D, FF // 2)), tile, tile,
+                pl.BlockSpec((256, 1), lambda i, c: (i, 0)), full_spec((D, D)), full_spec(rows.shape),
+            ],
+            out_specs=(tile, tile, tile, pl.BlockSpec((8, D), lambda i, c: (0, 0))),
+        ),
         cost_estimate=cost(2 * t * D * (FF + D), 2 * (t * FF + D * FF) + 16 * t * D),
         name="up_back_norm",
-    )(dz, w_in, dr, normed, inv, w_out, rows)
+    )(core.reshape(1), dz, dz, own, came, dr, normed, inv, w_out, rows)
 
 
 def input_kernel(a_ref, b_ref, w_ref, r_ref, o_ref):
@@ -1070,10 +1095,17 @@
     return lax.dynamic_index_in_dim(value, index, axis, keepdims=False)
 
 
-def stage(at, total, which):
-    axis = 1 if which == "y" and total.ndim == 4 else 0
-    came = exchange(pick(total, 1 - at[which], axis), which)
-    return add_low(pick(total, at[which], axis), came)
+def half_axis(total, which):
+    return 1 if which == "y" and total.ndim == 4 else 0
+
+
+def halve(at, total, which):
+    away = pick(total, 1 - at[which], half_axis(total, which))
+    return away, exchange(away, which)
+
+
+def join(at, total, came, which, *gates):
+    return add_low(pick(total, at[which], half_axis(total, which)), after(came, *gates))
 
 
 def slabs(total):
@@ -1082,14 +1114,6 @@
 
 def after(value, *earlier):
     return lax.optimization_barrier((value,) + earlier)[0]
-
-
-def rep_total(at, diff):
-    halves = diff.reshape(2, diff.shape[0] // 2, diff.shape[1])
-    came = exchange(pick(halves, 1 - at["c"], 0), "c")
-    total = add_low(pick(halves, at["c"], 0), came)
-    total = add_low(total, exchange(total, "x"))
-    return total, exchange(total, "c")
 
 
 def weave(value):
@@ -1126,59 +1150,77 @@
     bf, f32 = jnp.bfloat16, jnp.float32
     at = bits_of()
     core = at["c"].astype(jnp.int32)
+    def swapped(value, came):
+        return jnp.where(at["c"] != at["z1"], came, value)
+
+    def cross(value):
+        return exchange(value, "c", "z1")
+
+    def half_of(weight):
+        part = weight.shape[1] // 2
+        return lax.dynamic_slice_in_dim(weight, core * part, part, axis=1).astype(bf)
+
+    in_own = lax.all_gather(half_of(expand_weight), "fsdp", axis=0, tiled=True)
+    down_own = lax.all_gather(half_of(contract_weight), "fsdp", axis=0, tiled=True)
     attn_low = attention_weight.astype(bf)
-    w_qkv, w_out, w_in, w_down, vector_full, tok, seg = gather_all(
-        weave(attn_low[:3]), attn_low[3], expand_weight.astype(bf), contract_weight.astype(bf),
-        vectors.astype(bf), tokens, segment_ids,
-    )
-    cot = swap(at, after(cotangent, w_qkv))
+    w_qkv, w_out, vector_full, tok, seg = gather_all(
+        weave(attn_low[:3]), attn_low[3], vectors.astype(bf), tokens, segment_ids,
+    )
+    cot_came = cross(after(cotangent, w_qkv))
     rows = jnp.swapaxes(vector_full, 0, 1).reshape(-1, D).astype(f32)
     bias_up = rows[8:].reshape(1, FF)
     bias_qkv = weave(jnp.stack([rows[4], jnp.zeros_like(rows[4]), rows[5]])[:, None])
     scale_qkv = weave(jnp.stack([jnp.full((1, D), 0.125, f32)] + [jnp.ones((1, D), f32)] * 2))
     qkv = qkv_call(tok, w_qkv, bias_qkv, scale_qkv)
     mixed, log_sum = attn_fwd(qkv, seg)
+    in_other = exchange(after(in_own, mixed), "c")
     normed, inv, hidden_low = mix_call(mixed, w_out, tok, rows)
-    activated, slope = up_call(hidden_low, w_in, bias_up)
-    layer_output, grad_sum, grad_branch, sums_two = down_call(activated, w_down, normed, cot, rows)
+    down_other = exchange(after(down_own, hidden_low), "c")
+    activated, slope = up_call(hidden_low, in_own, in_other, bias_up, core)
+    cot = swapped(cotangent, after(cot_came, activated))
+    layer_output, grad_sum, grad_branch, sums_two = down_call(
+        activated, down_own, down_other, normed, cot, rows, core
+    )
+    output_came = cross(layer_output)
     down_send = weight_call(activated, grad_branch, 1 - core)
-    grad_pre, sums_up = slope_call(after(grad_branch, down_send), w_down, slope)
+    grad_pre, sums_up = slope_call(after(grad_branch, down_send), down_own, down_other, slope, core)
     down_came = exchange(down_send, "c")
     up_send = weight_call(hidden_low, grad_pre, 1 - core)
-    down_total = weight_call(activated, after(grad_branch, up_send), core, down_came)
+    down_total = slabs(weight_call(activated, after(grad_branch, up_send), core, down_came))
     up_came = exchange(up_send, "c")
-    up_total = weight_call(hidden_low, after(grad_pre, down_total), core, up_came)
+    away_d, came_d = halve(at, down_total, "y")
+    up_total = slabs(weight_call(hidden_low, after(grad_pre, away_d), core, up_came))
+    away_u, came_u = halve(at, up_total, "z0")
     grad_resid, grad_attn, grad_mixed, sums_one = hidden_call(
-        after(grad_pre, up_total), w_in, grad_sum, normed, inv, w_out, rows
-    )
-    down_one = stage(at, slabs(down_total), "y")
-    up_one = stage(at, slabs(up_total), "z0")
+        after(grad_pre, away_u), in_own, in_other, grad_sum, normed, inv, w_out, rows, core
+    )
     proj_send = weight_call(mixed, grad_attn, 1 - core)
     proj_came = exchange(proj_send, "c")
-    grad_a, sums_a = attn_bwd(qkv, after(grad_mixed, proj_send), log_sum, seg, 0)
-    qkv_send_a = weight_call(tok, grad_a, 1 - core)
-    down_one, up_one, qkv_send_a = lax.optimization_barrier((down_one, up_one, qkv_send_a))
-    came_a = exchange(qkv_send_a, "c")
-    down_two = stage(at, down_one, "z0")
-    up_two = stage(at, up_one, "y")
-    proj_total = weight_call(mixed, after(grad_attn, qkv_send_a, down_one, up_one), core, proj_came)
-    total_a = weight_call(tok, after(grad_a, proj_total), core, came_a)
-    proj_one = stage(at, slabs(proj_total), "y")
-    a_one = stage(at, slabs(total_a), "z0")
-    grad_b, sums_b = attn_bwd(qkv, after(grad_mixed, total_a), log_sum, seg, 1)
-    qkv_send_b = weight_call(tok, grad_b, 1 - core)
-    down_two, up_two, proj_one, a_one, qkv_send_b = lax.optimization_barrier(
-        (down_two, up_two, proj_one, a_one, qkv_send_b)
-    )
-    came_b = exchange(qkv_send_b, "c")
-    grad_contract = swap(at, down_two)
-    grad_expand = swap(at, up_two)
-    proj_two = stage(at, proj_one, "z0")
-    a_two = stage(at, a_one, "y")
-    input_grad = input_call(after(grad_a, down_two, qkv_send_b), grad_b, w_qkv, grad_resid)
-    total_b = weight_call(tok, after(grad_b, input_grad), core, came_b)
-    b_one = stage(at, slabs(total_b), "y")
-    b_two = stage(at, b_one, "z0")
+    output = swapped(layer_output, after(output_came, proj_send))
+    grad_a, sums_a = attn_bwd(qkv, after(grad_mixed, proj_send, output), log_sum, seg, 0)
+    send_a = weight_call(tok, grad_a, 1 - core)
+    came_a = exchange(send_a, "c")
+    down_one = join(at, down_total, came_d, "y", send_a)
+    away_d, came_d = halve(at, down_one, "z0")
+    up_one = join(at, up_total, came_u, "z0", away_d)
+    away_u, came_u = halve(at, up_one, "y")
+    proj_total = slabs(weight_call(mixed, after(grad_attn, away_u), core, proj_came))
+    away_p, came_p = halve(at, proj_total, "y")
+    total_a = slabs(weight_call(tok, after(grad_a, away_p), core, came_a))
+    away_a, came_one = halve(at, total_a, "z0")
+    grad_b, sums_b = attn_bwd(qkv, after(grad_mixed, away_a), log_sum, seg, 1)
+    send_b = weight_call(tok, grad_b, 1 - core)
+    came_b = exchange(send_b, "c")
+    down_two = join(at, down_one, came_d, "z0", send_b)
+    cross_d = cross(down_two)
+    up_two = join(at, up_one, came_u, "y", down_two)
+    cross_u = cross(up_two)
+    proj_one = join(at, proj_total, came_p, "y", up_two)
+    away_p, came_p = halve(at, proj_one, "z0")
+    a_one = join(at, total_a, came_one, "z0", away_p)
+    away_a, came_a = halve(at, a_one, "y")
+    total_b = slabs(weight_call(tok, after(grad_b, away_a), core, came_b))
+    away_b, came_b = halve(at, total_b, "y")
     sums_qkv = jnp.concatenate([sums_a, sums_b], axis=0).reshape(D // 128, 3, 128)
     vector_grad = jnp.concatenate(
         [
@@ -1194,42 +1236,104 @@
         ],
         axis=0,
     )
-    parts = after(vector_grad)
-    for which in ("c", "z0", "y"):
+
+    def vector_send(parts, which):
         half = parts.shape[1] // 2
         away = lax.dynamic_slice_in_dim(parts, (1 - at[which]) * half, half, axis=1)
-        parts = lax.dynamic_slice_in_dim(parts, at[which] * half, half, axis=1) + exchange(away, which)
-    grad_vectors = swap(at, parts)
-    grad_qkv_own = jnp.concatenate([a_two, b_two], axis=1)
-    grad_proj = proj_two
-    output = swap(at, layer_output)
-    input_grad = swap(at, input_grad)
-    grad_attention = jnp.concatenate([unweave(swap(at, grad_qkv_own)), swap(at, grad_proj)[None]], axis=0)
+        return exchange(away, which)
+
+    def vector_join(parts, came, which, *gates):
+        half = parts.shape[1] // 2
+        return lax.dynamic_slice_in_dim(parts, at[which] * half, half, axis=1) + after(came, *gates)
+
+    vec_came = vector_send(vector_grad, "c")
+    input_grad = input_call(after(grad_a, away_b), grad_b, w_qkv, grad_resid)
+    vec_one = vector_join(vector_grad, vec_came, "c", input_grad)
+    vec_came = vector_send(vec_one, "z0")
+    proj_two = join(at, proj_one, came_p, "z0", input_grad)
+    a_two = join(at, a_one, came_a, "y", input_grad)
+    cross_pa = cross(jnp.concatenate([proj_two, a_two], axis=1))
+    b_one = join(at, total_b, came_b, "y", proj_two, a_two)
+    away_b, came_b = halve(at, b_one, "z0")
+
+    def inner(weight, grad, first, second, rate, decay):
+        flat = (-1, weight.shape[-1])
+        return inner_call(
+            weight.reshape(flat), grad.reshape(flat), first.reshape(flat), second.reshape(flat), rate, decay
+        )
+
+    def rep_send(diff):
+        halves = diff.reshape(2, diff.shape[0] // 2, diff.shape[1])
+        away = pick(halves, 1 - at["c"], 0)
+        return away, exchange(away, "c")
+
+    def rep_join(diff, came, *gates):
+        halves = diff.reshape(2, diff.shape[0] // 2, diff.shape[1])
+        return add_low(pick(halves, at["c"], 0), after(came, *gates))
+
+    vec_two = vector_join(vec_one, vec_came, "z0", away_b)
+    vec_came = vector_send(vec_two, "y")
+    grad_contract = swapped(down_two, after(cross_d, away_b))
+    contract_new = inner(contract_weight, grad_contract, contract_first, contract_second, 0.015, 0.1)
+    sent_c, came_c = rep_send(contract_new[2])
+    b_two = join(at, b_one, came_b, "z0", sent_c)
+    cross_b = cross(b_two)
+    input_came = cross(after(input_grad, b_two))
+    grad_expand = swapped(up_two, after(cross_u, b_two))
+    expand_new = inner(expand_weight, grad_expand, expand_first, expand_second, 0.03, 0.1)
+    sent_e, came_e = rep_send(expand_new[2])
+    half_c = rep_join(contract_new[2], came_c, sent_e)
+    rest_c = exchange(half_c, "x")
+    vec_three = vector_join(vec_two, vec_came, "y", half_c)
+    vec_cross = cross(vec_three)
+    half_e = rep_join(expand_new[2], came_e, half_c)
+    rest_e = exchange(half_e, "x")
+    pa = swapped(jnp.concatenate([proj_two, a_two], axis=1), after(cross_pa, half_e))
+    b_own = swapped(b_two, after(cross_b, half_e))
+    grad_qkv = jnp.concatenate([pa[:, D:], b_own], axis=1)
+    grad_attention = jnp.concatenate([unweave(grad_qkv), pa[None, :, :D]], axis=0)
+    attention_new = inner(attention_weight, grad_attention, attention_first, attention_second, 0.03, 0.1)
+    sent_a, came_a = rep_send(attention_new[2])
+    grad_vectors = swapped(vec_three, after(vec_cross, sent_a))
+    inner_new, first_new, second_new = inner_step(
+        vectors, grad_vectors, vectors_first[0], vectors_second[0], 0.2, 0.0
+    )
+    vec_diff = (vectors - inner_new).astype(bf)
+    vec_near = exchange(vec_diff, "c")
+    full_c = add_low(half_c, after(rest_c, sent_a))
+    back_c = exchange(full_c, "c")
+    half_a = rep_join(attention_new[2], came_a, full_c)
+    rest_a = exchange(half_a, "x")
+    full_e = add_low(half_e, after(rest_e, half_a))
+    back_e = exchange(full_e, "c")
+    vec_half = add_low(vec_diff, after(vec_near, full_e))
+    vec_far = exchange(vec_half, "x")
+
+    def outer(weight, momentum, own, came):
+        flat = (-1, weight.shape[-1])
+        return outer_call(weight.reshape(flat), momentum.reshape(flat), own, came, core)
+
+    outer_c = outer(contract_weight, contract_momentum, after(full_c, vec_half), back_c)
+    full_a = add_low(half_a, after(rest_a, outer_c[1]))
+    back_a = exchange(full_a, "c")
+    outer_e = outer(expand_weight, expand_momentum, after(full_e, full_a), back_e)
+    mean_diff = add_low(vec_half, after(vec_far, outer_e[1])).astype(f32) / 4
+    momentum_new = 0.5 * vectors_momentum + mean_diff
+    outer_new = vectors - 0.7 * (mean_diff + 0.5 * momentum_new)
+    outer_a = outer(attention_weight, attention_momentum, after(full_a, outer_e[1]), back_a)
+    input_grad = swapped(input_grad, after(input_came, outer_e[1]))
     results = []
-    for weight, momentum, first, second, grad, rate, decay in (
-        (attention_weight, attention_momentum, attention_first, attention_second, grad_attention, 0.03, 0.1),
-        (expand_weight, expand_momentum, expand_first, expand_second, grad_expand, 0.03, 0.1),
-        (contract_weight, contract_momentum, contract_first, contract_second, grad_contract, 0.015, 0.1),
+    for weight, first, new, (total, copy) in (
+        (attention_weight, attention_first, attention_new, outer_a),
+        (expand_weight, expand_first, expand_new, outer_e),
+        (contract_weight, contract_first, contract_new, outer_c),
     ):
-        flat = (-1, weight.shape[-1])
-        flat_weight = weight.reshape(flat)
-        first_new, second_new, diff = inner_call(
-            flat_weight, grad.reshape(flat), first.reshape(flat), second.reshape(flat), rate, decay
-        )
-        own, came = rep_total(at, diff)
-        outer, copy = outer_call(flat_weight, momentum.reshape(flat), own, came, core)
         results += [
-            first_new.reshape(first.shape),
-            second_new.reshape(first.shape),
-            outer.reshape((3,) + weight.shape),
+            new[0].reshape(first.shape),
+            new[1].reshape(first.shape),
+            total.reshape((3,) + weight.shape),
             copy.reshape(weight.shape),
         ]
-    inner_new, first_new, second_new = inner_step(
-        vectors, grad_vectors, vectors_first[0], vectors_second[0], 0.2, 0.0
-    )
-    mean_diff = lax.psum((vectors - inner_new).astype(bf), "rep").astype(f32) / 4
-    momentum_new = 0.5 * vectors_momentum + mean_diff
-    outer_new = vectors - 0.7 * (mean_diff + 0.5 * momentum_new)
     results += [
         first_new[None],
         second_new[None],

time: 781 us -> 687 us (0.88)
  waiting for transfers between devices: 96.5 us -> 63.2 us
  starting transfers between devices: 75.8 us -> 46.1 us
  Pallas kernels: 484 us -> 457 us
  blocking collectives: 13.6 us -> 0 us
  between operations: 1.86 us -> 15.3 us
    pallas_call x1, Pallas kernels: 170 us -> 125 us  [gather_all(): pl.pallas_call(gather_kernel, out_shape=(shape((8 * qkv.shape[0], qkv.sha...]
    ppermute x35 -> x39, waiting for transfers between devices: 96.5 us -> 63.1 us  [exchange(): return lax.ppermute(value, ('rep', 'fsdp'), xor_pairs(bits))]
    ppermute x35 -> x39, starting transfers between devices: 75.8 us -> 46 us  [exchange(): return lax.ppermute(value, ('rep', 'fsdp'), xor_pairs(bits))]
    psum x1 -> x0, blocking collectives: 13.6 us -> none  [per_device_fast(): lax.psum((vectors - inner_new).astype(bf), 'rep').astype(f32) / 4]
    pallas_call x2, Pallas kernels: 47.8 us -> 56.6 us  [attn_bwd(): pl.pallas_call(bwd_kernel, out_shape=(jax.ShapeDtypeStruct((T, width // 2...]
    convert_element_type x16 -> x17, other arithmetic: 24 us -> 22.1 us  [add_low(): (left.astype(jnp.float32) + right.astype(jnp.float32)).astype(jnp.bfloat16)]
  transfers between devices with their start and end apart: 35 -> 41, of which waited for: 8 -> 7; matrix products, arithmetic and copies ran while one was open for 10% -> 13% of each run, Pallas kernels for 35% -> 62%
where the time goes in v2:
time: 687 us; the launch traced here: 679 us
  Pallas kernels  457 us (67%)
  waiting for transfers between devices  63.2 us (9%)
  local copies, waits for them, and re-layouts  52.7 us (8%)
  starting transfers between devices  46.1 us (7%)
  other arithmetic  45.1 us (7%)
  between operations  15.3 us (2%)
    pallas_call x1, Pallas kernels, gather_all(): pl.pallas_call(gather_kernel, out_shape=(shape((8 * qkv.shape[0], qkv.sha...  125 us
    pallas_call x10, Pallas kernels, weight_call(): pl.pallas_call(weight_kernel, out_shape=SHAPE((rows // 2, width), BF), gr...  71.8 us
    ppermute x39, waiting for transfers between devices, exchange(): return lax.ppermute(value, ('rep', 'fsdp'), xor_pairs(bits))  63.1 us
    pallas_call x2, Pallas kernels, attn_bwd(): pl.pallas_call(bwd_kernel, out_shape=(jax.ShapeDtypeStruct((T, width // 2...  56.6 us
    ppermute x39, starting transfers between devices, exchange(): return lax.ppermute(value, ('rep', 'fsdp'), xor_pairs(bits))  46 us
    pallas_call x1, Pallas kernels, attn_fwd(): pl.pallas_call(fwd_kernel, out_shape=(jax.ShapeDtypeStruct((T, width // 3...  44.8 us
    pallas_call x1, Pallas kernels, up_call(): pl.pallas_call(up_kernel, out_shape=(SHAPE((t, FF), BF), SHAPE((t, FF), B...  31.8 us
    convert_element_type x17, other arithmetic, add_low(): (left.astype(jnp.float32) + right.astype(jnp.float32)).astype(jnp.bfloat16)  22.1 us
  transfers between devices with their start and end apart: 41, of which 7 were waited for; matrix products, arithmetic and copies ran while one was open for 13% of the time, Pallas kernels for 62%

profile of v2, /device:TPU:1, one launch (start us, length us, event | category | flops | bytes accessed | tf_op | source)
XLA Modules:
  0.0 678.8 jit_solution(3745015403615346813)
XLA Ops:
  15.2 125.5 %gather_weights.1 = (bf16[1024,3072]{1,0:T(8,128)(2,1)}, bf16[1024,1024]{1,0:T(8,128)(2,1)}, bf16[8,12,128]{2,1,0:T(8,128)(2,1)}, bf16[1024,1024]{1,0:T(8,128)(2,1)}, s32[1,1024]{1,0:T(1,128)}) custom-call(bf16[128,3072]{1,0:T(8,128)(2,1)} %copy.80.qkv_in, bf16[128,1024]{1,0:T(8,128)(2,1)} %slice_bitcast_fusion.1.wo_in, ...), custom_call_target="tpu_custom_call" | custom-call | tf_op jit(solution)/shard_map/gather_weights/pallas_call | solution.py:679
  145.4 10.8 %qkv.1.qkv_ref = bf16[1024,3072]{1,0:T(8,128)(2,1)} custom-call(bf16[1024,1024]{1,0:T(8,128)(2,1)} %get-tuple-element.106.x_ref.left_ref, bf16[1024,3072]{1,0:T(8,128)(2,1)} %get-tuple-element.107.w_ref, f32[1,3072]{1,0:T(1,128)} %reshape.204.bias_ref, f32[1,3072]{1,0:T(1,128)} %constant.202.clone.1.scale_ref), custom_call_target="tpu_custom_call" | custom-call | flops 6442450 | bytes 14680 | tf_op jit(solution)/shard_map/qkv/pallas_call | solution.py:725
  157.0 44.8 %attn_fwd.1 = (bf16[1024,1024]{1,0:T(8,128)(2,1)}, f32[8,2,1024]{2,1,0:T(2,128)}) custom-call(s32[4]{0:T(128)} %get-tuple-element.196.start_ref, s32[4]{0:T(128)} %get-tuple-element.197.count_ref, bf16[1024,3072]{1,0:T(8,128)(2,1)} %qkv.1.qkv_ref, s32[1,1024]{1,0:T(1,128)} %get-tuple-element.105.segr_ref, s32[1024,1]{1,0:T(8,128)} %copy.81.segc_ref), custom_call_target="tpu_custom_call" | custom-call | flops 64424508 | bytes 9437 | tf_op jit(solution)/shard_map/attn_fwd/pallas_call | solution.py:413
  205.1 8.2 %mix_norm.1 = (f32[1024,1024]{1,0:T(8,128)}, f32[1024,1]{1,0:T(8,128)}, bf16[1024,1024]{1,0:T(8,128)(2,1)}) custom-call(bf16[1024,1024]{1,0:T(8,128)(2,1)} %get-tuple-element.109.c_ref.left_ref, bf16[1024,1024]{1,0:T(8,128)(2,1)} %get-tuple-element.110.w_ref.wo_ref, bf16[1024,1024]{1,0:T(8,128)(2,1)} %get-tuple-element.106.x_ref.left_ref, f32[12,1024]{1,0:T(8,128)} %bitcast.166), custom_call_target="tpu_custom_call" | custom-call | flops 2147483 | bytes 14680 | tf_op jit(solution)/shard_map/mix_norm/pallas_call | solution.py:758
  217.2 31.8 %up_gelu.1 = (bf16[1024,4096]{1,0:T(8,128)(2,1)}, bf16[1024,4096]{1,0:T(8,128)(2,1)}) custom-call(s32[1]{0:T(128)} %bitcast.core_ref.half_ref, bf16[1024,1024]{1,0:T(8,128)(2,1)} %get-tuple-element.111.h_ref.left_ref, bf16[1024,2048]{1,0:T(8,128)(2,1)} %all-gather.3.cloned.1.call-done.own_ref, bf16[1024,2048]{1,0:T(8,128)(2,1)} %collective-permute-done.came_ref, ...), custom_call_target="tpu_custom_call" | custom-call | flops 8589934 | bytes 27262 | tf_op jit(solution)/shard_map/up_gelu/pallas_call | solution.py:795
  249.0 15.2 %collective-permute-done.2 = bf16[1024,1024]{1,0:T(8,128)(2,1)} collective-permute-done((bf16[1024,1024]{1,0:T(8,128)(2,1)S(1)}, bf16[1024,1024]{1,0:T(8,128)(2,1)}, u32[]{:S(2)}, u32[]{:S(2)}) %collective-permute-start.2) | collective-permute-done | bytes 2097184 | tf_op jit(solution)/shard_map/ppermute | solution.py:1083
  267.3 19.9 %down_norm.1 = (bf16[1024,1024]{1,0:T(8,128)(2,1)}, f32[1024,1024]{1,0:T(8,128)}, bf16[1024,1024]{1,0:T(8,128)(2,1)}, f32[8,1024]{1,0:T(8,128)}) custom-call(s32[1]{0:T(128)} %bitcast.core_ref.half_ref, bf16[1024,4096]{1,0:T(8,128)(2,1)} %get-tuple-element.113.g_ref.left_ref, bf16[4096,512]{1,0:T(8,128)(2,1)} %all-gather.5.cloned.1.call-done.own_ref, ...), custom_call_target="tpu_custom_call" | custom-call | flops 8589934 | bytes 31457 | tf_op jit(solution)/shard_map/down_norm/pallas_call | solution.py:853
  287.2 8.5 %weight_grad.10 = bf16[2048,1024]{1,0:T(8,128)(2,1)} custom-call(s32[1]{0:T(128)} %bitcast.12.half_ref, bf16[1024,4096]{1,0:T(8,128)(2,1)} %get-tuple-element.113.g_ref.left_ref, bf16[1024,1024]{1,0:T(8,128)(2,1)} %get-tuple-element.123.right_ref.left_ref), custom_call_target="tpu_custom_call" | custom-call | flops 4294967 | bytes 14680 | tf_op jit(solution)/shard_map/weight_grad/pallas_call | solution.py:991
  295.7 16.3 %down_back.1 = (bf16[1024,4096]{1,0:T(8,128)(2,1)}, f32[1,4096]{1,0:T(1,128)}) custom-call(s32[1]{0:T(128)} %bitcast.core_ref.half_ref, bf16[1024,1024]{1,0:T(8,128)(2,1)} %get-tuple-element.123.right_ref.left_ref, bf16[1024,1024]{1,0:T(8,128)(2,1)} %get-tuple-element.123.right_ref.left_ref, bf16[4096,512]{1,0:T(8,128)(2,1)} %all-gather.5.cloned.1.call-done.own_ref, ...), custom_call_target="tpu_custom_call" | custom-call | flops 8589934 | bytes 27262 | tf_op jit(solution)/shard_map/down_back/pallas_call | solution.py:886
  312.0 11.1 %weight_grad.11 = bf16[512,4096]{1,0:T(8,128)(2,1)} custom-call(s32[1]{0:T(128)} %bitcast.12.half_ref, bf16[1024,1024]{1,0:T(8,128)(2,1)} %get-tuple-element.111.h_ref.left_ref, bf16[1024,4096]{1,0:T(8,128)(2,1)} %get-tuple-element.125.right_ref.left_ref), custom_call_target="tpu_custom_call" | custom-call | flops 4294967 | bytes 17825 | tf_op jit(solution)/shard_map/weight_grad/pallas_call | solution.py:991
  325.6 9.3 %weight_grad.12 = bf16[2048,1024]{1,0:T(8,128)(2,1)} custom-call(s32[1]{0:T(128)} %bitcast.core_ref.half_ref, bf16[1024,4096]{1,0:T(8,128)(2,1)} %get-tuple-element.113.g_ref.left_ref, bf16[1024,1024]{1,0:T(8,128)(2,1)} %get-tuple-element.123.right_ref.left_ref, bf16[2048,1024]{1,0:T(8,128)(2,1)} %collective-permute-done.4.refs_0_), custom_call_target="tpu_custom_call" | custom-call | flops 4294967 | bytes 14680 | tf_op jit(solution)/shard_map/weight_grad/pallas_call | solution.py:991
  338.7 11.6 %weight_grad.13 = bf16[512,4096]{1,0:T(8,128)(2,1)} custom-call(s32[1]{0:T(128)} %bitcast.core_ref.half_ref, bf16[1024,1024]{1,0:T(8,128)(2,1)} %get-tuple-element.111.h_ref.left_ref, bf16[1024,4096]{1,0:T(8,128)(2,1)} %get-tuple-element.125.right_ref.left_ref, bf16[512,4096]{1,0:T(8,128)(2,1)} %collective-permute-done.5.refs_0_), custom_call_target="tpu_custom_call" | custom-call | flops 4294967 | bytes 17825 | tf_op jit(solution)/shard_map/weight_grad/pallas_call | solution.py:991
  356.7 21.2 %up_back_norm.1 = (f32[1024,1024]{1,0:T(8,128)}, bf16[1024,1024]{1,0:T(8,128)(2,1)}, bf16[1024,1024]{1,0:T(8,128)(2,1)}, f32[8,1024]{1,0:T(8,128)}) custom-call(s32[1]{0:T(128)} %bitcast.core_ref.half_ref, bf16[1024,4096]{1,0:T(8,128)(2,1)} %get-tuple-element.125.right_ref.left_ref, bf16[1024,4096]{1,0:T(8,128)(2,1)} %get-tuple-element.125.right_ref.left_ref, ...), custom_call_target="tpu_custom_call" | custom-call | flops 10737418 | bytes 33554 | tf_op jit(solution)/shard_map/up_back_norm/pallas_call | solution.py:924
  385.2 28.4 %attn_bwd.2 = (bf16[1024,1536]{1,0:T(8,128)(2,1)}, f32[4,1,384]{2,1,0:T(1,128)}) custom-call(s32[4]{0:T(128)} %get-tuple-element.196.start_ref, s32[4]{0:T(128)} %get-tuple-element.197.count_ref, bf16[1024,3072]{1,0:T(8,128)(2,1)} %qkv.1.qkv_ref, bf16[1024,1024]{1,0:T(8,128)(2,1)} %get-tuple-element.138.do_ref, f32[8,2,1024]{2,1,0:T(2,128)} %get-tuple-element.132.lse_ref, ...), custom_call_target="tpu_custom_call" | custom-call | flops 64424508 | bytes 18874 | tf_op jit(solution)/shard_map/attn_bwd/pallas_call | solution.py:437
  450.9 28.2 %attn_bwd.3 = (bf16[1024,1536]{1,0:T(8,128)(2,1)}, f32[4,1,384]{2,1,0:T(1,128)}) custom-call(s32[4]{0:T(128)} %get-tuple-element.196.start_ref, s32[4]{0:T(128)} %get-tuple-element.197.count_ref, bf16[1024,3072]{1,0:T(8,128)(2,1)} %qkv.1.qkv_ref, bf16[1024,1024]{1,0:T(8,128)(2,1)} %get-tuple-element.138.do_ref, f32[8,2,1024]{2,1,0:T(2,128)} %get-tuple-element.132.lse_ref, ...), custom_call_target="tpu_custom_call" | custom-call | flops 64424508 | bytes 18874 | tf_op jit(solution)/shard_map/attn_bwd/pallas_call | solution.py:437
  518.4 12.3 %input_back.1 = bf16[1024,1024]{1,0:T(8,128)(2,1)} custom-call(bf16[1024,1536]{1,0:T(8,128)(2,1)} %get-tuple-element.145.right_ref.a_ref, bf16[1024,1536]{1,0:T(8,128)(2,1)} %get-tuple-element.144.right_ref.b_ref, bf16[1024,3072]{1,0:T(8,128)(2,1)} %get-tuple-element.107.w_ref, f32[1024,1024]{1,0:T(8,128)} %get-tuple-element.146.r_ref), custom_call_target="tpu_custom_call" | custom-call | flops 6442450 | bytes 18874 | tf_op jit(solution)/shard_map/input_back/pallas_call | solution.py:952
  541.7 6.6 collective-permute-done.15
  561.3 12.3 %collective-permute-done.18 = bf16[128,1536]{0,1:T(8,128)(2,1)} collective-permute-done((bf16[128,1536]{0,1:T(8,128)(2,1)}, bf16[128,1536]{0,1:T(8,128)(2,1)}, u32[]{:S(2)}, u32[]{:S(2)}) %collective-permute-start.18) | collective-permute-done | bytes 393248 | tf_op jit(solution)/shard_map/ppermute | solution.py:1083
  592.8 6.7 collective-permute-done.26
  619.1 10.9 %collective-permute-done.24 = bf16[64,4096]{1,0:T(8,128)(2,1)S(1)} collective-permute-done((bf16[64,4096]{1,0:T(8,128)(2,1)S(1)}, bf16[64,4096]{1,0:T(8,128)(2,1)S(1)}, u32[]{:S(2)}, u32[]{:S(2)}) %collective-permute-start.24) | collective-permute-done | bytes 524320 | tf_op jit(solution)/shard_map/ppermute | solution.py:1083
  634.6 6.4 outer_step.3
  642.7 6.4 outer_step.4
  650.3 11.0 %collective-permute-done.20 = bf16[1024,1024]{1,0:T(8,128)(2,1)} collective-permute-done((bf16[1024,1024]{1,0:T(8,128)(2,1)S(1)}, bf16[1024,1024]{1,0:T(8,128)(2,1)}, u32[]{:S(2)}, u32[]{:S(2)}) %collective-permute-start.20) | collective-permute-done | bytes 2097184 | tf_op jit(solution)/shard_map/ppermute | solution.py:1083
  665.2 6.3 outer_step.5
  (248 shorter events, 194.1 us)
Async XLA Ops:
  7.2 194.6 %all-gather.3.cloned.1.call-start = ((), (), s32[]{:S(2)}) async-start(), calls=%async_computation | async-start | bytes 4718592 | tf_op jit(solution)/shard_map/all_gather | solution.py:1163
  9.5 203.8 %all-gather.5.cloned.1.call-start = ((), (), s32[]{:S(2)}) async-start(), calls=%async_computation.1 | async-start | bytes 4718592 | tf_op jit(solution)/shard_map/all_gather | solution.py:1164
  213.3 54.0 %collective-permute-start.1 = (bf16[4096,512]{1,0:T(8,128)(2,1)}, bf16[4096,512]{1,0:T(8,128)(2,1)}, u32[]{:S(2)}, u32[]{:S(2)}) collective-permute-start(bf16[4096,512]{1,0:T(8,128)(2,1)} %all-gather.5.cloned.1.call-done.own_ref), channel_id=1, source_target_pairs={{0,8},{1,9},{2,10},{3,11},{4,12},{5,13},{6,14},{7,15},{8,0},{9,1},... | collective-permute-start | bytes 12582920 | tf_op jit(solution)/shard_map/ppermute | solution.py:1083
  213.3 50.8 %collective-permute-start.2 = (bf16[1024,1024]{1,0:T(8,128)(2,1)S(1)}, bf16[1024,1024]{1,0:T(8,128)(2,1)}, u32[]{:S(2)}, u32[]{:S(2)}) collective-permute-start(bf16[1024,1024]{1,0:T(8,128)(2,1)S(1)} %copy-done.10), channel_id=1, source_target_pairs={{4,8},{5,9},{6,10},{7,11},{8,4},{9,5},{10,6},{11,7},{20,24},{21,25... | collective-permute-start | bytes 6291464 | tf_op jit(solution)/shard_map/ppermute | solution.py:1083
  295.7 29.9 %collective-permute-start.4 = (bf16[2048,1024]{1,0:T(8,128)(2,1)}, bf16[2048,1024]{1,0:T(8,128)(2,1)}, u32[]{:S(2)}, u32[]{:S(2)}) collective-permute-start(bf16[2048,1024]{1,0:T(8,128)(2,1)} %weight_grad.10), channel_id=1, source_target_pairs={{0,8},{1,9},{2,10},{3,11},{4,12},{5,13},{6,14},{7,15},{8,0},{9,1},... | collective-permute-start | bytes 12582920 | tf_op jit(solution)/shard_map/ppermute | solution.py:1083
  323.6 58.5 %collective-permute-start.3 = (bf16[1024,1024]{1,0:T(8,128)(2,1)S(1)}, bf16[1024,1024]{1,0:T(8,128)(2,1)}, u32[]{:S(2)}, u32[]{:S(2)}) collective-permute-start(bf16[1024,1024]{1,0:T(8,128)(2,1)S(1)} %copy-done.11), channel_id=1, source_target_pairs={{4,8},{5,9},{6,10},{7,11},{8,4},{9,5},{10,6},{11,7},{20,24},{21,25... | collective-permute-start | bytes 6291464 | tf_op jit(solution)/shard_map/ppermute | solution.py:1083
  337.9 82.6 %collective-permute-start.7 = (bf16[2,512,1024]{2,1,0:T(8,128)(2,1)}, bf16[2,512,1024]{2,1,0:T(8,128)(2,1)}, u32[]{:S(2)}, u32[]{:S(2)}) collective-permute-start(bf16[2,512,1024]{2,1,0:T(8,128)(2,1)} %dynamic-slice_bitcast_fusion.1), channel_id=1, source_target_pairs={{0,1},{1,0},{2,3},{3,2},{4,5},{5,4},{6,7},{7,6},{8,9},{9,8},{10,11... | collective-permute-start | bytes 6291464 | tf_op jit(solution)/shard_map/ppermute | solution.py:1083
  353.4 72.1 %collective-permute-start.6 = (bf16[2,128,4096]{2,1,0:T(8,128)(2,1)}, bf16[2,128,4096]{2,1,0:T(8,128)(2,1)}, u32[]{:S(2)}, u32[]{:S(2)}) collective-permute-start(bf16[2,128,4096]{2,1,0:T(8,128)(2,1)} %dynamic-slice_bitcast_fusion), channel_id=1, source_target_pairs={{0,2},{1,3},{2,0},{3,1},{4,6},{5,7},{6,4},{7,5},{8,10},{9,11},{10,... | collective-permute-start | bytes 6291464 | tf_op jit(solution)/shard_map/ppermute | solution.py:1083
  382.1 50.2 %collective-permute-start.8 = (bf16[512,1024]{1,0:T(8,128)(2,1)}, bf16[512,1024]{1,0:T(8,128)(2,1)S(1)}, u32[]{:S(2)}, u32[]{:S(2)}) collective-permute-start(bf16[512,1024]{1,0:T(8,128)(2,1)} %weight_grad.14), channel_id=1, source_target_pairs={{0,8},{1,9},{2,10},{3,11},{4,12},{5,13},{6,14},{7,15},{8,0},{9,1},... | collective-permute-start | bytes 3145736 | tf_op jit(solution)/shard_map/ppermute | solution.py:1083
  424.9 66.1 %collective-permute-start.13 = (bf16[512,1024]{1,0:T(8,128)(2,1)}, bf16[512,1024]{1,0:T(8,128)(2,1)}, u32[]{:S(2)}, u32[]{:S(2)}) collective-permute-start(bf16[512,1024]{1,0:T(8,128)(2,1)} %dynamic-slice_bitcast_fusion.3), channel_id=1, source_target_pairs={{0,2},{1,3},{2,0},{3,1},{4,6},{5,7},{6,4},{7,5},{8,10},{9,11},{10,... | collective-permute-start | bytes 3145736 | tf_op jit(solution)/shard_map/ppermute | solution.py:1083
  430.2 62.7 %collective-permute-start.12 = (bf16[128,4096]{1,0:T(8,128)(2,1)}, bf16[128,4096]{1,0:T(8,128)(2,1)}, u32[]{:S(2)}, u32[]{:S(2)}) collective-permute-start(bf16[128,4096]{1,0:T(8,128)(2,1)} %dynamic-slice_bitcast_fusion.2), channel_id=1, source_target_pairs={{0,1},{1,0},{2,3},{3,2},{4,5},{5,4},{6,7},{7,6},{8,9},{9,8},{10,11... | collective-permute-start | bytes 3145736 | tf_op jit(solution)/shard_map/ppermute | solution.py:1083
  440.0 54.5 %collective-permute-start.11 = (bf16[2,128,1024]{1,2,0:T(8,128)(2,1)}, bf16[2,128,1024]{1,2,0:T(8,128)(2,1)}, u32[]{:S(2)}, u32[]{:S(2)}) collective-permute-start(bf16[2,128,1024]{1,2,0:T(8,128)(2,1)} %bitcast.177), channel_id=1, source_target_pairs={{0,1},{1,0},{2,3},{3,2},{4,5},{5,4},{6,7},{7,6},{8,9},{9,8},{10,11... | collective-permute-start | bytes 1572872 | tf_op jit(solution)/shard_map/ppermute | solution.py:1083
  450.5 46.0 %collective-permute-start.10 = (bf16[2,128,1536]{1,2,0:T(8,128)(2,1)}, bf16[2,128,1536]{1,2,0:T(8,128)(2,1)}, u32[]{:S(2)}, u32[]{:S(2)}) collective-permute-start(bf16[2,128,1536]{1,2,0:T(8,128)(2,1)} %bitcast.175), channel_id=1, source_target_pairs={{0,2},{1,3},{2,0},{3,1},{4,6},{5,7},{6,4},{7,5},{8,10},{9,11},{10,... | collective-permute-start | bytes 2359304 | tf_op jit(solution)/shard_map/ppermute | solution.py:1083
  480.5 50.2 %collective-permute-start.30 = (f32[12,512]{1,0:T(8,128)}, f32[12,512]{1,0:T(8,128)}, u32[]{:S(2)}, u32[]{:S(2)}) collective-permute-start(f32[12,512]{1,0:T(8,128)} %constant_dynamic-slice_fusion.3), channel_id=1, source_target_pairs={{0,8},{1,9},{2,10},{3,11},{4,12},{5,13},{6,14},{7,15},{8,0},{9,1},... | collective-permute-start | bytes 73736 | tf_op jit(solution)/shard_map/ppermute | solution.py:1083
  498.7 33.4 %collective-permute-start.17 = (bf16[128,1536]{0,1:T(8,128)(2,1)}, bf16[128,1536]{0,1:T(8,128)(2,1)S(1)}, u32[]{:S(2)}, u32[]{:S(2)}) collective-permute-start(bf16[128,1536]{0,1:T(8,128)(2,1)} %dynamic-slice_bitcast_fusion.8), channel_id=1, source_target_pairs={{0,1},{1,0},{2,3},{3,2},{4,5},{5,4},{6,7},{7,6},{8,9},{9,8},{10,11... | collective-permute-start | bytes 1179656 | tf_op jit(solution)/shard_map/ppermute | solution.py:1083
  499.3 34.2 %collective-permute-start.16 = (bf16[128,1024]{0,1:T(8,128)(2,1)S(1)}, bf16[128,1024]{0,1:T(8,128)(2,1)}, u32[]{:S(2)}, u32[]{:S(2)}) collective-permute-start(bf16[128,1024]{0,1:T(8,128)(2,1)S(1)} %dynamic-slice_bitcast_fusion.9), channel_id=1, source_target_pairs={{0,2},{1,3},{2,0},{3,1},{4,6},{5,7},{6,4},{7,5},{8,10},{9,11},{10,... | collective-permute-start | bytes 786440 | tf_op jit(solution)/shard_map/ppermute | solution.py:1083
  500.3 51.5 %collective-permute-start.19 = (bf16[512,1024]{1,0:T(8,128)(2,1)S(1)}, bf16[512,1024]{1,0:T(8,128)(2,1)}, u32[]{:S(2)}, u32[]{:S(2)}) collective-permute-start(bf16[512,1024]{1,0:T(8,128)(2,1)S(1)} %fusion.2), channel_id=1, source_target_pairs={{4,8},{5,9},{6,10},{7,11},{8,4},{9,5},{10,6},{11,7},{20,24},{21,25... | collective-permute-start | bytes 3145736 | tf_op jit(solution)/shard_map/ppermute | solution.py:1083
  505.2 70.3 %collective-permute-start.21 = (bf16[128,4096]{1,0:T(8,128)(2,1)S(1)}, bf16[128,4096]{1,0:T(8,128)(2,1)}, u32[]{:S(2)}, u32[]{:S(2)}) collective-permute-start(bf16[128,4096]{1,0:T(8,128)(2,1)S(1)} %fusion.3), channel_id=1, source_target_pairs={{4,8},{5,9},{6,10},{7,11},{8,4},{9,5},{10,6},{11,7},{20,24},{21,25... | collective-permute-start | bytes 3145736 | tf_op jit(solution)/shard_map/ppermute | solution.py:1083
  532.1 28.0 %collective-permute-start.31 = (f32[12,256]{1,0:T(8,128)}, f32[12,256]{1,0:T(8,128)}, u32[]{:S(2)}, u32[]{:S(2)}) collective-permute-start(f32[12,256]{1,0:T(8,128)} %constant_dynamic-slice_fusion.2), channel_id=1, source_target_pairs={{0,2},{1,3},{2,0},{3,1},{4,6},{5,7},{6,4},{7,5},{8,10},{9,11},{10,... | collective-permute-start | bytes 36872 | tf_op jit(solution)/shard_map/ppermute | solution.py:1083
  537.9 53.6 %collective-permute-start.25 = (bf16[128,2560]{0,1:T(8,128)(2,1)}, bf16[128,2560]{0,1:T(8,128)(2,1)}, u32[]{:S(2)}, u32[]{:S(2)}) collective-permute-start(bf16[128,2560]{0,1:T(8,128)(2,1)} %pad_maximum_fusion.2), channel_id=1, source_target_pairs={{4,8},{5,9},{6,10},{7,11},{8,4},{9,5},{10,6},{11,7},{20,24},{21,25... | collective-permute-start | bytes 1966088 | tf_op jit(solution)/shard_map/ppermute | solution.py:1083
  551.2 22.4 %collective-permute-start.18 = (bf16[128,1536]{0,1:T(8,128)(2,1)}, bf16[128,1536]{0,1:T(8,128)(2,1)}, u32[]{:S(2)}, u32[]{:S(2)}) collective-permute-start(bf16[128,1536]{0,1:T(8,128)(2,1)} %dynamic-slice_bitcast_fusion.7), channel_id=1, source_target_pairs={{0,2},{1,3},{2,0},{3,1},{4,6},{5,7},{6,4},{7,5},{8,10},{9,11},{10,... | collective-permute-start | bytes 1179656 | tf_op jit(solution)/shard_map/ppermute | solution.py:1083
  561.3 26.6 %collective-permute-start.23 = (bf16[256,1024]{1,0:T(8,128)(2,1)S(1)}, bf16[256,1024]{1,0:T(8,128)(2,1)}, u32[]{:S(2)}, u32[]{:S(2)}) collective-permute-start(bf16[256,1024]{1,0:T(8,128)(2,1)S(1)} %dynamic-slice_bitcast_fusion.6), channel_id=1, source_target_pairs={{0,8},{1,9},{2,10},{3,11},{4,12},{5,13},{6,14},{7,15},{8,0},{9,1},... | collective-permute-start | bytes 1572872 | tf_op jit(solution)/shard_map/ppermute | solution.py:1083
  589.1 28.3 %collective-permute-start.28 = (bf16[256,1024]{1,0:T(8,128)(2,1)S(1)}, bf16[256,1024]{1,0:T(8,128)(2,1)}, u32[]{:S(2)}, u32[]{:S(2)}) collective-permute-start(bf16[256,1024]{1,0:T(8,128)(2,1)S(1)} %fusion.7), channel_id=1, source_target_pairs={{0,16},{1,17},{2,18},{3,19},{4,20},{5,21},{6,22},{7,23},{8,24},{9,... | collective-permute-start | bytes 1572872 | tf_op jit(solution)/shard_map/ppermute | solution.py:1083
  610.5 50.8 %collective-permute-start.20 = (bf16[1024,1024]{1,0:T(8,128)(2,1)S(1)}, bf16[1024,1024]{1,0:T(8,128)(2,1)}, u32[]{:S(2)}, u32[]{:S(2)}) collective-permute-start(bf16[1024,1024]{1,0:T(8,128)(2,1)S(1)} %copy-done.2), channel_id=1, source_target_pairs={{4,8},{5,9},{6,10},{7,11},{8,4},{9,5},{10,6},{11,7},{20,24},{21,25... | collective-permute-start | bytes 6291464 | tf_op jit(solution)/shard_map/ppermute | solution.py:1083
  (50 other events, 474.3 us)
Sparse Core Ops, SparseCore 0:
  10.7 119.0 all-gather.2
  132.5 72.2 all-gather.4

commit v3 on v2

--- a/solution.py
+++ b/solution.py
@@ -766,7 +766,10 @@
     )(mixed, w_out, tok, rows)
 
 
-def up_kernel(core_ref, h_ref, own_ref, came_ref, bias_ref, g_ref, s_ref):
+def up_kernel(place_ref, h_ref, *refs):
+    parts, (bias_ref, g_ref, s_ref) = refs[:4], refs[4:]
+    each = pl.num_programs(0) // 4
+
     def tile(w_ref):
         for i in range(8):
             rows = slice(i * 128, (i + 1) * 128)
@@ -775,39 +778,31 @@
             g_ref[rows, :] = (z * phi).astype(BF)
             s_ref[rows, :] = (phi + z * bell * 0.3989422804014327).astype(BF)
 
-    first = pl.program_id(0) < pl.num_programs(0) // 2
-
-    @pl.when(first)
-    def _():
-        tile(own_ref)
-
-    @pl.when(jnp.logical_not(first))
-    def _():
-        tile(came_ref)
-
-
-def up_call(low, own, came, bias, core):
+    for k in range(4):
+        pl.when(pl.program_id(0) // each == k)(partial(tile, parts[k]))
+
+
+def up_call(low, parts, place, bias):
     t = low.shape[0]
     tile = 512
-    half = FF // tile // 2
-    place = lambda j, c: (0, lax.rem(j + half * c[0], 2 * half))
-    out = pl.BlockSpec((t, tile), place)
+    each = FF // tile // 4
+    where = lambda j, p: (0, p[j // each] * each + lax.rem(j, each))
+    out = pl.BlockSpec((t, tile), where)
+
+    def part(k):
+        return pl.BlockSpec((D, tile), lambda j, p: (0, jnp.clip(j - k * each, 0, each - 1)))
+
     return pl.pallas_call(
         up_kernel,
         out_shape=(SHAPE((t, FF), BF), SHAPE((t, FF), BF)),
         grid_spec=pltpu.PrefetchScalarGridSpec(
             num_scalar_prefetch=1, grid=(FF // tile,),
-            in_specs=[
-                full_spec(low.shape),
-                pl.BlockSpec((D, tile), lambda j, c: (0, jnp.minimum(j, half - 1))),
-                pl.BlockSpec((D, tile), lambda j, c: (0, jnp.maximum(j - half, 0))),
-                pl.BlockSpec((1, tile), place),
-            ],
+            in_specs=[full_spec(low.shape)] + [part(k) for k in range(4)] + [pl.BlockSpec((1, tile), where)],
             out_specs=(out, out),
         ),
         cost_estimate=cost(2 * t * D * FF, 2 * (t * D + D * FF + 2 * t * FF), 2 * t * FF),
         name="up_gelu",
-    )(core.reshape(1), low, own, came, bias)
+    )(place, low, *parts, bias)
 
 
 def row_sum(value):
@@ -900,8 +895,12 @@
     )(core.reshape(1), dm, dm, own, came, slope)
 
 
-def hidden_kernel(core_ref, left_ref, right_ref, own_ref, came_ref, dr_ref, n_ref, q_ref, wo_ref, rows_ref, r_ref, a_ref, c_ref, sums_ref):
-    grad = dr_ref[...] + dot(left_ref[...], own_ref[...], 1, 1) + dot(right_ref[...], came_ref[...], 1, 1)
+def hidden_kernel(place_ref, *refs):
+    grads, parts = refs[:4], refs[4:8]
+    dr_ref, n_ref, q_ref, wo_ref, rows_ref, r_ref, a_ref, c_ref, sums_ref = refs[8:]
+    grad = dr_ref[...]
+    for grad_ref, w_ref in zip(grads, parts):
+        grad = grad + dot(grad_ref[...], w_ref[...], 1, 1)
     normed = n_ref[...]
     back = norm_back(grad, normed, q_ref[...], rows_ref[0:1, :])
     low = back.astype(BF)
@@ -918,25 +917,27 @@
     sums_ref[2:3, :] += row_sum(low.astype(F32))
 
 
-def hidden_call(dz, own, came, dr, normed, inv, w_out, rows, core):
+def hidden_call(dz, parts, place, dr, normed, inv, w_out, rows):
     t = dz.shape[0]
-    tile = pl.BlockSpec((256, D), lambda i, c: (i, 0))
+    tile = pl.BlockSpec((256, D), lambda i, p: (i, 0))
+
+    def quarter(k):
+        return pl.BlockSpec((256, FF // 4), lambda i, p: (i, p[k]))
+
     return pl.pallas_call(
         hidden_kernel,
         out_shape=(SHAPE((t, D), F32), SHAPE((t, D), BF), SHAPE((t, D), BF), SHAPE((8, D), F32)),
         grid_spec=pltpu.PrefetchScalarGridSpec(
             num_scalar_prefetch=1, grid=(t // 256,),
-            in_specs=[
-                pl.BlockSpec((256, FF // 2), lambda i, c: (i, c[0])),
-                pl.BlockSpec((256, FF // 2), lambda i, c: (i, 1 - c[0])),
-                full_spec((D, FF // 2)), full_spec((D, FF // 2)), tile, tile,
-                pl.BlockSpec((256, 1), lambda i, c: (i, 0)), full_spec((D, D)), full_spec(rows.shape),
+            in_specs=[quarter(k) for k in range(4)] + [full_spec((D, FF // 4))] * 4 + [
+                tile, tile,
+                pl.BlockSpec((256, 1), lambda i, p: (i, 0)), full_spec((D, D)), full_spec(rows.shape),
             ],
-            out_specs=(tile, tile, tile, pl.BlockSpec((8, D), lambda i, c: (0, 0))),
+            out_specs=(tile, tile, tile, pl.BlockSpec((8, D), lambda i, p: (0, 0))),
         ),
         cost_estimate=cost(2 * t * D * (FF + D), 2 * (t * FF + D * FF) + 16 * t * D),
         name="up_back_norm",
-    )(core.reshape(1), dz, dz, own, came, dr, normed, inv, w_out, rows)
+    )(place, *([dz] * 4), *parts, dr, normed, inv, w_out, rows)
 
 
 def input_kernel(a_ref, b_ref, w_ref, r_ref, o_ref):
@@ -1156,12 +1157,12 @@
     def cross(value):
         return exchange(value, "c", "z1")
 
-    def half_of(weight):
-        part = weight.shape[1] // 2
-        return lax.dynamic_slice_in_dim(weight, core * part, part, axis=1).astype(bf)
-
-    in_own = lax.all_gather(half_of(expand_weight), "fsdp", axis=0, tiled=True)
-    down_own = lax.all_gather(half_of(contract_weight), "fsdp", axis=0, tiled=True)
+    quarter = 2 * core + at["x"].astype(jnp.int32)
+    place = jnp.stack([quarter, 2 * (1 - core) + quarter - 2 * core, quarter + 1 - 2 * at["x"], 3 - quarter])
+    part = expand_weight.shape[1] // 4
+    in_own = lax.all_gather(
+        lax.dynamic_slice_in_dim(expand_weight, quarter * part, part, axis=1).astype(bf), "fsdp", axis=0, tiled=True
+    )
     attn_low = attention_weight.astype(bf)
     w_qkv, w_out, vector_full, tok, seg = gather_all(
         weave(attn_low[:3]), attn_low[3], vectors.astype(bf), tokens, segment_ids,
@@ -1171,13 +1172,19 @@
     bias_up = rows[8:].reshape(1, FF)
     bias_qkv = weave(jnp.stack([rows[4], jnp.zeros_like(rows[4]), rows[5]])[:, None])
     scale_qkv = weave(jnp.stack([jnp.full((1, D), 0.125, f32)] + [jnp.ones((1, D), f32)] * 2))
+    part = contract_weight.shape[1] // 2
+    down_half = lax.dynamic_slice_in_dim(contract_weight, core * part, part, axis=1).astype(bf)
+    down_own = lax.all_gather(after(down_half, w_qkv), "fsdp", axis=0, tiled=True)
+    in_near = after(in_own, w_qkv)
+    in_far = exchange(in_near, "x")
+    in_side = exchange(in_near, "c")
     qkv = qkv_call(tok, w_qkv, bias_qkv, scale_qkv)
     mixed, log_sum = attn_fwd(qkv, seg)
-    in_other = exchange(after(in_own, mixed), "c")
+    in_parts = [in_own, after(in_side, mixed), in_far, exchange(after(in_far, mixed), "c")]
     normed, inv, hidden_low = mix_call(mixed, w_out, tok, rows)
-    down_other = exchange(after(down_own, hidden_low), "c")
-    activated, slope = up_call(hidden_low, in_own, in_other, bias_up, core)
-    cot = swapped(cotangent, after(cot_came, activated))
+    cot = swapped(cotangent, after(cot_came, hidden_low))
+    activated, slope = up_call(after(hidden_low, cot), in_parts, place, bias_up)
+    down_other = exchange(after(down_own, activated), "c")
     layer_output, grad_sum, grad_branch, sums_two = down_call(
         activated, down_own, down_other, normed, cot, rows, core
     )
@@ -1192,7 +1199,7 @@
     up_total = slabs(weight_call(hidden_low, after(grad_pre, away_d), core, up_came))
     away_u, came_u = halve(at, up_total, "z0")
     grad_resid, grad_attn, grad_mixed, sums_one = hidden_call(
-        after(grad_pre, away_u), in_own, in_other, grad_sum, normed, inv, w_out, rows, core
+        after(grad_pre, away_u), in_parts, place, grad_sum, normed, inv, w_out, rows
     )
     proj_send = weight_call(mixed, grad_attn, 1 - core)
     proj_came = exchange(proj_send, "c")
@@ -1250,12 +1257,6 @@
     input_grad = input_call(after(grad_a, away_b), grad_b, w_qkv, grad_resid)
     vec_one = vector_join(vector_grad, vec_came, "c", input_grad)
     vec_came = vector_send(vec_one, "z0")
-    proj_two = join(at, proj_one, came_p, "z0", input_grad)
-    a_two = join(at, a_one, came_a, "y", input_grad)
-    cross_pa = cross(jnp.concatenate([proj_two, a_two], axis=1))
-    b_one = join(at, total_b, came_b, "y", proj_two, a_two)
-    away_b, came_b = halve(at, b_one, "z0")
-
     def inner(weight, grad, first, second, rate, decay):
         flat = (-1, weight.shape[-1])
         return inner_call(
@@ -1271,57 +1272,61 @@
         halves = diff.reshape(2, diff.shape[0] // 2, diff.shape[1])
         return add_low(pick(halves, at["c"], 0), after(came, *gates))
 
+    def outer(weight, momentum, own, came):
+        flat = (-1, weight.shape[-1])
+        return outer_call(weight.reshape(flat), momentum.reshape(flat), own, came, core)
+
+    proj_two = join(at, proj_one, came_p, "z0", input_grad)
+    a_two = join(at, a_one, came_a, "y", input_grad)
+    cross_pa = cross(jnp.concatenate([proj_two, a_two], axis=1))
+    grad_contract = swapped(down_two, after(cross_d, proj_two, a_two))
+    contract_new = inner(contract_weight, grad_contract, contract_first, contract_second, 0.015, 0.1)
+    sent_c, came_c = rep_send(contract_new[2])
+    b_one = join(at, total_b, came_b, "y", sent_c)
+    away_b, came_b = halve(at, b_one, "z0")
     vec_two = vector_join(vec_one, vec_came, "z0", away_b)
     vec_came = vector_send(vec_two, "y")
-    grad_contract = swapped(down_two, after(cross_d, away_b))
-    contract_new = inner(contract_weight, grad_contract, contract_first, contract_second, 0.015, 0.1)
-    sent_c, came_c = rep_send(contract_new[2])
-    b_two = join(at, b_one, came_b, "z0", sent_c)
-    cross_b = cross(b_two)
-    input_came = cross(after(input_grad, b_two))
-    grad_expand = swapped(up_two, after(cross_u, b_two))
+    grad_expand = swapped(up_two, after(cross_u, away_b))
     expand_new = inner(expand_weight, grad_expand, expand_first, expand_second, 0.03, 0.1)
     sent_e, came_e = rep_send(expand_new[2])
     half_c = rep_join(contract_new[2], came_c, sent_e)
     rest_c = exchange(half_c, "x")
-    vec_three = vector_join(vec_two, vec_came, "y", half_c)
+    b_two = join(at, b_one, came_b, "z0", half_c)
+    cross_b = cross(b_two)
+    half_e = rep_join(expand_new[2], came_e, b_two)
+    rest_e = exchange(half_e, "x")
+    vec_three = vector_join(vec_two, vec_came, "y", half_e)
     vec_cross = cross(vec_three)
-    half_e = rep_join(expand_new[2], came_e, half_c)
-    rest_e = exchange(half_e, "x")
-    pa = swapped(jnp.concatenate([proj_two, a_two], axis=1), after(cross_pa, half_e))
-    b_own = swapped(b_two, after(cross_b, half_e))
+    full_c = add_low(half_c, after(rest_c, half_e))
+    back_c = exchange(full_c, "c")
+    pa = swapped(jnp.concatenate([proj_two, a_two], axis=1), after(cross_pa, full_c))
+    outer_c = outer(contract_weight, contract_momentum, full_c, after(back_c, pa))
+    grad_vectors = swapped(vec_three, after(vec_cross, outer_c[1]))
+    inner_new, first_new, second_new = inner_step(
+        vectors, grad_vectors, vectors_first[0], vectors_second[0], 0.2, 0.0
+    )
+    vec_diff = (vectors - inner_new).astype(bf)
+    vec_near = exchange(vec_diff, "c")
+    input_came = cross(after(input_grad, b_two, vec_diff))
+    b_own = swapped(b_two, after(cross_b, vec_diff))
     grad_qkv = jnp.concatenate([pa[:, D:], b_own], axis=1)
     grad_attention = jnp.concatenate([unweave(grad_qkv), pa[None, :, :D]], axis=0)
     attention_new = inner(attention_weight, grad_attention, attention_first, attention_second, 0.03, 0.1)
     sent_a, came_a = rep_send(attention_new[2])
-    grad_vectors = swapped(vec_three, after(vec_cross, sent_a))
-    inner_new, first_new, second_new = inner_step(
-        vectors, grad_vectors, vectors_first[0], vectors_second[0], 0.2, 0.0
-    )
-    vec_diff = (vectors - inner_new).astype(bf)
-    vec_near = exchange(vec_diff, "c")
-    full_c = add_low(half_c, after(rest_c, sent_a))
-    back_c = exchange(full_c, "c")
-    half_a = rep_join(attention_new[2], came_a, full_c)
+    vec_half = add_low(vec_diff, after(vec_near, sent_a))
+    vec_far = exchange(vec_half, "x")
+    full_e = add_low(half_e, after(rest_e, sent_a))
+    back_e = exchange(full_e, "c")
+    half_a = rep_join(attention_new[2], came_a, full_e)
     rest_a = exchange(half_a, "x")
-    full_e = add_low(half_e, after(rest_e, half_a))
-    back_e = exchange(full_e, "c")
-    vec_half = add_low(vec_diff, after(vec_near, full_e))
-    vec_far = exchange(vec_half, "x")
-
-    def outer(weight, momentum, own, came):
-        flat = (-1, weight.shape[-1])
-        return outer_call(weight.reshape(flat), momentum.reshape(flat), own, came, core)
-
-    outer_c = outer(contract_weight, contract_momentum, after(full_c, vec_half), back_c)
-    full_a = add_low(half_a, after(rest_a, outer_c[1]))
+    outer_e = outer(expand_weight, expand_momentum, full_e, after(back_e, half_a))
+    full_a = add_low(half_a, after(rest_a, outer_e[1]))
     back_a = exchange(full_a, "c")
-    outer_e = outer(expand_weight, expand_momentum, after(full_e, full_a), back_e)
-    mean_diff = add_low(vec_half, after(vec_far, outer_e[1])).astype(f32) / 4
+    mean_diff = add_low(vec_half, after(vec_far, full_a)).astype(f32) / 4
     momentum_new = 0.5 * vectors_momentum + mean_diff
     outer_new = vectors - 0.7 * (mean_diff + 0.5 * momentum_new)
-    outer_a = outer(attention_weight, attention_momentum, after(full_a, outer_e[1]), back_a)
-    input_grad = swapped(input_grad, after(input_came, outer_e[1]))
+    input_grad = swapped(input_grad, after(input_came, full_a))
+    outer_a = outer(attention_weight, attention_momentum, full_a, back_a)
     results = []
     for weight, first, new, (total, copy) in (
         (attention_weight, attention_first, attention_new, outer_a),

time: 687 us -> 675 us (0.983)
  Pallas kernels: 457 us -> 441 us
    pallas_call x1, Pallas kernels: 125 us -> 101 us  [gather_all(): pl.pallas_call(gather_kernel, out_shape=(shape((8 * qkv.shape[0], qkv.sha...]
    ppermute x39 -> x41, starting transfers between devices: 46 us -> 51.2 us  [exchange(): return lax.ppermute(value, ('rep', 'fsdp'), xor_pairs(bits))]
    ppermute x39 -> x41, waiting for transfers between devices: 63.1 us -> 63.4 us  [exchange(): return lax.ppermute(value, ('rep', 'fsdp'), xor_pairs(bits))]
  transfers between devices with their start and end apart: 41 -> 43, of which waited for: 7 -> 8; matrix products, arithmetic and copies ran while one was open for 13% -> 13% of each run, Pallas kernels for 62% -> 62%
where the time goes in v3:
time: 675 us; the launch traced here: 668 us
  Pallas kernels  441 us (65%)
  waiting for transfers between devices  63.5 us (9%)
  local copies, waits for them, and re-layouts  53.2 us (8%)
  starting transfers between devices  51.3 us (8%)
  other arithmetic  44.2 us (7%)
  between operations  15.2 us (2%)
    pallas_call x1, Pallas kernels, gather_all(): pl.pallas_call(gather_kernel, out_shape=(shape((8 * qkv.shape[0], qkv.sha...  101 us
    pallas_call x10, Pallas kernels, weight_call(): pl.pallas_call(weight_kernel, out_shape=SHAPE((rows // 2, width), BF), gr...  71.8 us
    ppermute x41, waiting for transfers between devices, exchange(): return lax.ppermute(value, ('rep', 'fsdp'), xor_pairs(bits))  63.4 us
    pallas_call x2, Pallas kernels, attn_bwd(): pl.pallas_call(bwd_kernel, out_shape=(jax.ShapeDtypeStruct((T, width // 2...  59.6 us
    ppermute x41, starting transfers between devices, exchange(): return lax.ppermute(value, ('rep', 'fsdp'), xor_pairs(bits))  51.2 us
    pallas_call x1, Pallas kernels, attn_fwd(): pl.pallas_call(fwd_kernel, out_shape=(jax.ShapeDtypeStruct((T, width // 3...  46.9 us
    pallas_call x1, Pallas kernels, up_call(): pl.pallas_call(up_kernel, out_shape=(SHAPE((t, FF), BF), SHAPE((t, FF), B...  34.2 us
    pallas_call x1, Pallas kernels, hidden_call(): pl.pallas_call(hidden_kernel, out_shape=(SHAPE((t, D), F32), SHAPE((t, D)...  22.1 us
  transfers between devices with their start and end apart: 43, of which 8 were waited for; matrix products, arithmetic and copies ran while one was open for 13% of the time, Pallas kernels for 62%

profile of v3, /device:TPU:1, one launch (start us, length us, event | category | flops | bytes accessed | tf_op | source)
XLA Modules:
  0.0 668.3 jit_solution(10256250428887071734)
XLA Ops:
  14.2 101.5 %gather_weights.1 = (bf16[1024,3072]{1,0:T(8,128)(2,1)}, bf16[1024,1024]{1,0:T(8,128)(2,1)}, bf16[8,12,128]{2,1,0:T(8,128)(2,1)}, bf16[1024,1024]{1,0:T(8,128)(2,1)}, s32[1,1024]{1,0:T(1,128)}) custom-call(bf16[128,3072]{1,0:T(8,128)(2,1)} %copy.80.qkv_in, bf16[128,1024]{1,0:T(8,128)(2,1)} %slice_bitcast_fusion.1.wo_in, ...), custom_call_target="tpu_custom_call" | custom-call | tf_op jit(solution)/shard_map/gather_weights/pallas_call | solution.py:679
  125.5 10.7 %qkv.1.qkv_ref = bf16[1024,3072]{1,0:T(8,128)(2,1)} custom-call(bf16[1024,1024]{1,0:T(8,128)(2,1)} %get-tuple-element.109.x_ref.left_ref, bf16[1024,3072]{1,0:T(8,128)(2,1)} %get-tuple-element.110.w_ref, f32[1,3072]{1,0:T(1,128)} %reshape.202.bias_ref, f32[1,3072]{1,0:T(1,128)} %constant.209.clone.1.scale_ref), custom_call_target="tpu_custom_call" | custom-call | flops 6442450 | bytes 14680 | tf_op jit(solution)/shard_map/qkv/pallas_call | solution.py:725
  137.1 46.9 %attn_fwd.1 = (bf16[1024,1024]{1,0:T(8,128)(2,1)}, f32[8,2,1024]{2,1,0:T(2,128)}) custom-call(s32[4]{0:T(128)} %get-tuple-element.202.start_ref, s32[4]{0:T(128)} %get-tuple-element.203.count_ref, bf16[1024,3072]{1,0:T(8,128)(2,1)} %qkv.1.qkv_ref, s32[1,1024]{1,0:T(1,128)} %get-tuple-element.108.segr_ref, s32[1024,1]{1,0:T(8,128)} %copy.81.segc_ref), custom_call_target="tpu_custom_call" | custom-call | flops 64424508 | bytes 9437 | tf_op jit(solution)/shard_map/attn_fwd/pallas_call | solution.py:413
  185.9 8.1 %mix_norm.1 = (f32[1024,1024]{1,0:T(8,128)}, f32[1024,1]{1,0:T(8,128)}, bf16[1024,1024]{1,0:T(8,128)(2,1)}) custom-call(bf16[1024,1024]{1,0:T(8,128)(2,1)} %get-tuple-element.112.c_ref.left_ref, bf16[1024,1024]{1,0:T(8,128)(2,1)} %get-tuple-element.113.w_ref.refs_11_, bf16[1024,1024]{1,0:T(8,128)(2,1)} %get-tuple-element.109.x_ref.left_ref, f32[12,1024]{1,0:T(8,128)} %bitcast.170), custom_call_target="tpu_custom_call" | custom-call | flops 2147483 | bytes 14680 | tf_op jit(solution)/shard_map/mix_norm/pallas_call | solution.py:758
  194.6 25.2 %collective-permute-done = bf16[1024,1024]{1,0:T(8,128)(2,1)} collective-permute-done((bf16[1024,1024]{1,0:T(8,128)(2,1)}, bf16[1024,1024]{1,0:T(8,128)(2,1)}, u32[]{:S(2)}, u32[]{:S(2)}) %collective-permute-start) | collective-permute-done | bytes 2097184 | tf_op jit(solution)/shard_map/ppermute | solution.py:1084
  222.9 34.2 %up_gelu.1 = (bf16[1024,4096]{1,0:T(8,128)(2,1)}, bf16[1024,4096]{1,0:T(8,128)(2,1)}) custom-call(s32[4]{0:T(128)} %pad_add_fusion.place_ref, bf16[1024,1024]{1,0:T(8,128)(2,1)} %get-tuple-element.117.h_ref.left_ref, bf16[1024,1024]{1,0:T(8,128)(2,1)} %all-gather.3.cloned.1.call-done.refs_0_.refs_4_, ...), custom_call_target="tpu_custom_call" | custom-call | flops 8589934 | bytes 27262 | tf_op jit(solution)/shard_map/up_gelu/pallas_call | solution.py:795
  257.2 7.5 %collective-permute-done.4.came_ref = bf16[4096,512]{1,0:T(8,128)(2,1)} collective-permute-done((bf16[4096,512]{1,0:T(8,128)(2,1)}, bf16[4096,512]{1,0:T(8,128)(2,1)}, u32[]{:S(2)}, u32[]{:S(2)}) %collective-permute-start.4) | collective-permute-done | bytes 4194336 | tf_op jit(solution)/shard_map/ppermute | solution.py:1084
  264.7 19.9 %down_norm.1 = (bf16[1024,1024]{1,0:T(8,128)(2,1)}, f32[1024,1024]{1,0:T(8,128)}, bf16[1024,1024]{1,0:T(8,128)(2,1)}, f32[8,1024]{1,0:T(8,128)}) custom-call(s32[1]{0:T(128)} %bitcast.core_ref.half_ref, bf16[1024,4096]{1,0:T(8,128)(2,1)} %get-tuple-element.121.g_ref.left_ref, bf16[4096,512]{1,0:T(8,128)(2,1)} %all-gather.5.cloned.1.call-done.own_ref, ...), custom_call_target="tpu_custom_call" | custom-call | flops 8589934 | bytes 31457 | tf_op jit(solution)/shard_map/down_norm/pallas_call | solution.py:848
  284.6 8.5 %weight_grad.10 = bf16[2048,1024]{1,0:T(8,128)(2,1)} custom-call(s32[1]{0:T(128)} %bitcast.16.half_ref, bf16[1024,4096]{1,0:T(8,128)(2,1)} %get-tuple-element.121.g_ref.left_ref, bf16[1024,1024]{1,0:T(8,128)(2,1)} %get-tuple-element.130.right_ref.left_ref), custom_call_target="tpu_custom_call" | custom-call | flops 4294967 | bytes 14680 | tf_op jit(solution)/shard_map/weight_grad/pallas_call | solution.py:992
  293.2 16.3 %down_back.1 = (bf16[1024,4096]{1,0:T(8,128)(2,1)}, f32[1,4096]{1,0:T(1,128)}) custom-call(s32[1]{0:T(128)} %bitcast.core_ref.half_ref, bf16[1024,1024]{1,0:T(8,128)(2,1)} %get-tuple-element.130.right_ref.left_ref, bf16[1024,1024]{1,0:T(8,128)(2,1)} %get-tuple-element.130.right_ref.left_ref, bf16[4096,512]{1,0:T(8,128)(2,1)} %all-gather.5.cloned.1.call-done.own_ref, ...), custom_call_target="tpu_custom_call" | custom-call | flops 8589934 | bytes 27262 | tf_op jit(solution)/shard_map/down_back/pallas_call | solution.py:881
  309.5 11.0 %weight_grad.11 = bf16[512,4096]{1,0:T(8,128)(2,1)} custom-call(s32[1]{0:T(128)} %bitcast.16.half_ref, bf16[1024,1024]{1,0:T(8,128)(2,1)} %get-tuple-element.117.h_ref.left_ref, bf16[1024,4096]{1,0:T(8,128)(2,1)} %get-tuple-element.132.right_ref.refs_0_.refs_1_.refs_2_.refs_3_), custom_call_target="tpu_custom_call" | custom-call | flops 4294967 | bytes 17825 | tf_op jit(solution)/shard_map/weight_grad/pallas_call | solution.py:992
  322.9 9.3 %weight_grad.12 = bf16[2048,1024]{1,0:T(8,128)(2,1)} custom-call(s32[1]{0:T(128)} %bitcast.core_ref.half_ref, bf16[1024,4096]{1,0:T(8,128)(2,1)} %get-tuple-element.121.g_ref.left_ref, bf16[1024,1024]{1,0:T(8,128)(2,1)} %get-tuple-element.130.right_ref.left_ref, bf16[2048,1024]{1,0:T(8,128)(2,1)} %collective-permute-done.6.refs_0_), custom_call_target="tpu_custom_call" | custom-call | flops 4294967 | bytes 14680 | tf_op jit(solution)/shard_map/weight_grad/pallas_call | solution.py:992
  336.5 11.6 %weight_grad.13 = bf16[512,4096]{1,0:T(8,128)(2,1)} custom-call(s32[1]{0:T(128)} %bitcast.core_ref.half_ref, bf16[1024,1024]{1,0:T(8,128)(2,1)} %get-tuple-element.117.h_ref.left_ref, bf16[1024,4096]{1,0:T(8,128)(2,1)} %get-tuple-element.132.right_ref.refs_0_.refs_1_.refs_2_.refs_3_, bf16[512,4096]{1,0:T(8,128)(2,1)} %collective-permute-done.7.refs_0_), custom_call_target="tpu_custom_call" | custom-call | flops 4294967 | bytes 17825 | tf_op jit(solution)/shard_map/weight_grad/pallas_call | solution.py:992
  352.4 22.1 %up_back_norm.1 = (f32[1024,1024]{1,0:T(8,128)}, bf16[1024,1024]{1,0:T(8,128)(2,1)}, bf16[1024,1024]{1,0:T(8,128)(2,1)}, f32[8,1024]{1,0:T(8,128)}) custom-call(s32[4]{0:T(128)} %pad_add_fusion.place_ref, bf16[1024,4096]{1,0:T(8,128)(2,1)} %get-tuple-element.132.right_ref.refs_0_.refs_1_.refs_2_.refs_3_, ...), custom_call_target="tpu_custom_call" | custom-call | flops 10737418 | bytes 33554 | tf_op jit(solution)/shard_map/up_back_norm/pallas_call | solution.py:927
  381.8 29.8 %attn_bwd.2 = (bf16[1024,1536]{1,0:T(8,128)(2,1)}, f32[4,1,384]{2,1,0:T(1,128)}) custom-call(s32[4]{0:T(128)} %get-tuple-element.202.start_ref, s32[4]{0:T(128)} %get-tuple-element.203.count_ref, bf16[1024,3072]{1,0:T(8,128)(2,1)} %qkv.1.qkv_ref, bf16[1024,1024]{1,0:T(8,128)(2,1)} %get-tuple-element.145.do_ref, f32[8,2,1024]{2,1,0:T(2,128)} %get-tuple-element.139.lse_ref, ...), custom_call_target="tpu_custom_call" | custom-call | flops 64424508 | bytes 18874 | tf_op jit(solution)/shard_map/attn_bwd/pallas_call | solution.py:437
  454.4 29.8 %attn_bwd.3 = (bf16[1024,1536]{1,0:T(8,128)(2,1)}, f32[4,1,384]{2,1,0:T(1,128)}) custom-call(s32[4]{0:T(128)} %get-tuple-element.202.start_ref, s32[4]{0:T(128)} %get-tuple-element.203.count_ref, bf16[1024,3072]{1,0:T(8,128)(2,1)} %qkv.1.qkv_ref, bf16[1024,1024]{1,0:T(8,128)(2,1)} %get-tuple-element.145.do_ref, f32[8,2,1024]{2,1,0:T(2,128)} %get-tuple-element.139.lse_ref, ...), custom_call_target="tpu_custom_call" | custom-call | flops 64424508 | bytes 18874 | tf_op jit(solution)/shard_map/attn_bwd/pallas_call | solution.py:437
  516.0 12.3 %input_back.1 = bf16[1024,1024]{1,0:T(8,128)(2,1)} custom-call(bf16[1024,1536]{1,0:T(8,128)(2,1)} %get-tuple-element.152.right_ref.a_ref, bf16[1024,1536]{1,0:T(8,128)(2,1)} %get-tuple-element.151.right_ref.b_ref, bf16[1024,3072]{1,0:T(8,128)(2,1)} %get-tuple-element.110.w_ref, f32[1024,1024]{1,0:T(8,128)} %get-tuple-element.153.r_ref), custom_call_target="tpu_custom_call" | custom-call | flops 6442450 | bytes 18874 | tf_op jit(solution)/shard_map/input_back/pallas_call | solution.py:953
  549.2 6.1 inner_step.3
  561.6 6.1 inner_step.4
  590.7 6.3 outer_step.3
  599.7 6.2 inner_step.5
  616.3 6.4 outer_step.4
  633.7 6.3 outer_step.5
  640.0 18.1 %collective-permute-done.32 = bf16[1024,1024]{1,0:T(8,128)(2,1)} collective-permute-done((bf16[1024,1024]{1,0:T(8,128)(2,1)S(1)}, bf16[1024,1024]{1,0:T(8,128)(2,1)}, u32[]{:S(2)}, u32[]{:S(2)}) %collective-permute-start.32) | collective-permute-done | bytes 2097184 | tf_op jit(solution)/shard_map/ppermute | solution.py:1084
  (255 shorter events, 192.9 us)
Async XLA Ops:
  7.2 110.6 %all-gather.3.cloned.1.call-start = ((), (), s32[]{:S(2)}) async-start(), calls=%async_computation | async-start | bytes 2359296 | tf_op jit(solution)/shard_map/all_gather | solution.py:1163
  9.1 248.1 %all-gather.5.cloned.1.call-start = ((), (), s32[]{:S(2)}) async-start(), calls=%async_computation.1 | async-start | bytes 4718592 | tf_op jit(solution)/shard_map/all_gather | solution.py:1177
  117.8 66.2 %collective-permute-start.2 = (bf16[1024,1024]{1,0:T(8,128)(2,1)}, bf16[1024,1024]{1,0:T(8,128)(2,1)}, u32[]{:S(2)}, u32[]{:S(2)}) collective-permute-start(bf16[1024,1024]{1,0:T(8,128)(2,1)} %all-gather.3.cloned.1.call-done.refs_0_.refs_4_), channel_id=1, source_target_pairs={{0,16},{1,17},{2,18},{3,19},{4,20},{5,21},{6,22},{7,23},{8,24},{9,... | collective-permute-start | bytes 6291464 | tf_op jit(solution)/shard_map/ppermute | solution.py:1084
  118.1 101.6 %collective-permute-start = (bf16[1024,1024]{1,0:T(8,128)(2,1)}, bf16[1024,1024]{1,0:T(8,128)(2,1)}, u32[]{:S(2)}, u32[]{:S(2)}) collective-permute-start(bf16[1024,1024]{1,0:T(8,128)(2,1)} %param.20), channel_id=1, source_target_pairs={{4,8},{5,9},{6,10},{7,11},{8,4},{9,5},{10,6},{11,7},{20,24},{21,25... | collective-permute-start | bytes 6291464 | tf_op jit(solution)/shard_map/ppermute | solution.py:1084
  184.0 38.9 %collective-permute-start.1 = (bf16[1024,1024]{1,0:T(8,128)(2,1)S(1)}, bf16[1024,1024]{1,0:T(8,128)(2,1)}, u32[]{:S(2)}, u32[]{:S(2)}) collective-permute-start(bf16[1024,1024]{1,0:T(8,128)(2,1)S(1)} %copy-done.4), channel_id=1, source_target_pairs={{0,8},{1,9},{2,10},{3,11},{4,12},{5,13},{6,14},{7,15},{8,0},{9,1},... | collective-permute-start | bytes 6291464 | tf_op jit(solution)/shard_map/ppermute | solution.py:1084
  184.0 38.8 %collective-permute-start.3 = (bf16[1024,1024]{1,0:T(8,128)(2,1)}, bf16[1024,1024]{1,0:T(8,128)(2,1)}, u32[]{:S(2)}, u32[]{:S(2)}) collective-permute-start(bf16[1024,1024]{1,0:T(8,128)(2,1)} %collective-permute-done.2.refs_2_.refs_6_), channel_id=1, source_target_pairs={{0,8},{1,9},{2,10},{3,11},{4,12},{5,13},{6,14},{7,15},{8,0},{9,1},... | collective-permute-start | bytes 6291464 | tf_op jit(solution)/shard_map/ppermute | solution.py:1084
  293.1 29.8 %collective-permute-start.6 = (bf16[2048,1024]{1,0:T(8,128)(2,1)}, bf16[2048,1024]{1,0:T(8,128)(2,1)}, u32[]{:S(2)}, u32[]{:S(2)}) collective-permute-start(bf16[2048,1024]{1,0:T(8,128)(2,1)} %weight_grad.10), channel_id=1, source_target_pairs={{0,8},{1,9},{2,10},{3,11},{4,12},{5,13},{6,14},{7,15},{8,0},{9,1},... | collective-permute-start | bytes 12582920 | tf_op jit(solution)/shard_map/ppermute | solution.py:1084
  320.9 57.8 %collective-permute-start.5 = (bf16[1024,1024]{1,0:T(8,128)(2,1)S(1)}, bf16[1024,1024]{1,0:T(8,128)(2,1)}, u32[]{:S(2)}, u32[]{:S(2)}) collective-permute-start(bf16[1024,1024]{1,0:T(8,128)(2,1)S(1)} %copy-done.8), channel_id=1, source_target_pairs={{4,8},{5,9},{6,10},{7,11},{8,4},{9,5},{10,6},{11,7},{20,24},{21,25... | collective-permute-start | bytes 6291464 | tf_op jit(solution)/shard_map/ppermute | solution.py:1084
  335.2 81.9 %collective-permute-start.9 = (bf16[2,512,1024]{2,1,0:T(8,128)(2,1)}, bf16[2,512,1024]{2,1,0:T(8,128)(2,1)}, u32[]{:S(2)}, u32[]{:S(2)}) collective-permute-start(bf16[2,512,1024]{2,1,0:T(8,128)(2,1)} %dynamic-slice_bitcast_fusion.1), channel_id=1, source_target_pairs={{0,1},{1,0},{2,3},{3,2},{4,5},{5,4},{6,7},{7,6},{8,9},{9,8},{10,11... | collective-permute-start | bytes 6291464 | tf_op jit(solution)/shard_map/ppermute | solution.py:1084
  351.2 70.4 %collective-permute-start.8 = (bf16[2,128,4096]{2,1,0:T(8,128)(2,1)}, bf16[2,128,4096]{2,1,0:T(8,128)(2,1)}, u32[]{:S(2)}, u32[]{:S(2)}) collective-permute-start(bf16[2,128,4096]{2,1,0:T(8,128)(2,1)} %dynamic-slice_bitcast_fusion), channel_id=1, source_target_pairs={{0,2},{1,3},{2,0},{3,1},{4,6},{5,7},{6,4},{7,5},{8,10},{9,11},{10,... | collective-permute-start | bytes 6291464 | tf_op jit(solution)/shard_map/ppermute | solution.py:1084
  378.6 52.5 %collective-permute-start.10 = (bf16[512,1024]{1,0:T(8,128)(2,1)}, bf16[512,1024]{1,0:T(8,128)(2,1)S(1)}, u32[]{:S(2)}, u32[]{:S(2)}) collective-permute-start(bf16[512,1024]{1,0:T(8,128)(2,1)} %weight_grad.14), channel_id=1, source_target_pairs={{0,8},{1,9},{2,10},{3,11},{4,12},{5,13},{6,14},{7,15},{8,0},{9,1},... | collective-permute-start | bytes 3145736 | tf_op jit(solution)/shard_map/ppermute | solution.py:1084
  421.6 68.4 %collective-permute-start.15 = (bf16[512,1024]{1,0:T(8,128)(2,1)}, bf16[512,1024]{1,0:T(8,128)(2,1)}, u32[]{:S(2)}, u32[]{:S(2)}) collective-permute-start(bf16[512,1024]{1,0:T(8,128)(2,1)} %dynamic-slice_bitcast_fusion.3), channel_id=1, source_target_pairs={{0,2},{1,3},{2,0},{3,1},{4,6},{5,7},{6,4},{7,5},{8,10},{9,11},{10,... | collective-permute-start | bytes 3145736 | tf_op jit(solution)/shard_map/ppermute | solution.py:1084
  426.3 65.4 %collective-permute-start.14 = (bf16[128,4096]{1,0:T(8,128)(2,1)}, bf16[128,4096]{1,0:T(8,128)(2,1)}, u32[]{:S(2)}, u32[]{:S(2)}) collective-permute-start(bf16[128,4096]{1,0:T(8,128)(2,1)} %dynamic-slice_bitcast_fusion.2), channel_id=1, source_target_pairs={{0,1},{1,0},{2,3},{3,2},{4,5},{5,4},{6,7},{7,6},{8,9},{9,8},{10,11... | collective-permute-start | bytes 3145736 | tf_op jit(solution)/shard_map/ppermute | solution.py:1084
  438.9 54.5 %collective-permute-start.13 = (bf16[2,128,1024]{1,2,0:T(8,128)(2,1)}, bf16[2,128,1024]{1,2,0:T(8,128)(2,1)}, u32[]{:S(2)}, u32[]{:S(2)}) collective-permute-start(bf16[2,128,1024]{1,2,0:T(8,128)(2,1)} %bitcast.181), channel_id=1, source_target_pairs={{0,1},{1,0},{2,3},{3,2},{4,5},{5,4},{6,7},{7,6},{8,9},{9,8},{10,11... | collective-permute-start | bytes 1572872 | tf_op jit(solution)/shard_map/ppermute | solution.py:1084
  450.8 44.6 %collective-permute-start.12 = (bf16[2,128,1536]{1,2,0:T(8,128)(2,1)}, bf16[2,128,1536]{1,2,0:T(8,128)(2,1)}, u32[]{:S(2)}, u32[]{:S(2)}) collective-permute-start(bf16[2,128,1536]{1,2,0:T(8,128)(2,1)} %bitcast.180), channel_id=1, source_target_pairs={{0,2},{1,3},{2,0},{3,1},{4,6},{5,7},{6,4},{7,5},{8,10},{9,11},{10,... | collective-permute-start | bytes 2359304 | tf_op jit(solution)/shard_map/ppermute | solution.py:1084
  498.4 29.9 %collective-permute-start.20 = (bf16[128,1536]{0,1:T(8,128)(2,1)}, bf16[128,1536]{0,1:T(8,128)(2,1)S(1)}, u32[]{:S(2)}, u32[]{:S(2)}) collective-permute-start(bf16[128,1536]{0,1:T(8,128)(2,1)} %dynamic-slice_bitcast_fusion.8), channel_id=1, source_target_pairs={{0,1},{1,0},{2,3},{3,2},{4,5},{5,4},{6,7},{7,6},{8,9},{9,8},{10,11... | collective-permute-start | bytes 1179656 | tf_op jit(solution)/shard_map/ppermute | solution.py:1084
  499.6 39.4 %collective-permute-start.24 = (f32[12,512]{1,0:T(8,128)S(1)}, f32[12,512]{1,0:T(8,128)S(1)}, u32[]{:S(2)}, u32[]{:S(2)}) collective-permute-start(f32[12,512]{1,0:T(8,128)S(1)} %constant_dynamic-slice_fusion.3), channel_id=1, source_target_pairs={{0,8},{1,9},{2,10},{3,11},{4,12},{5,13},{6,14},{7,15},{8,0},{9,1},... | collective-permute-start | bytes 73736 | tf_op jit(solution)/shard_map/ppermute | solution.py:1084
  500.2 30.8 %collective-permute-start.19 = (bf16[128,1024]{0,1:T(8,128)(2,1)}, bf16[128,1024]{0,1:T(8,128)(2,1)}, u32[]{:S(2)}, u32[]{:S(2)}) collective-permute-start(bf16[128,1024]{0,1:T(8,128)(2,1)} %dynamic-slice_bitcast_fusion.9), channel_id=1, source_target_pairs={{0,2},{1,3},{2,0},{3,1},{4,6},{5,7},{6,4},{7,5},{8,10},{9,11},{10,... | collective-permute-start | bytes 786440 | tf_op jit(solution)/shard_map/ppermute | solution.py:1084
  500.2 46.7 %collective-permute-start.18 = (bf16[512,1024]{1,0:T(8,128)(2,1)S(1)}, bf16[512,1024]{1,0:T(8,128)(2,1)}, u32[]{:S(2)}, u32[]{:S(2)}) collective-permute-start(bf16[512,1024]{1,0:T(8,128)(2,1)S(1)} %fusion.2), channel_id=1, source_target_pairs={{4,8},{5,9},{6,10},{7,11},{8,4},{9,5},{10,6},{11,7},{20,24},{21,25... | collective-permute-start | bytes 3145736 | tf_op jit(solution)/shard_map/ppermute | solution.py:1084
  503.7 55.5 %collective-permute-start.23 = (bf16[128,4096]{1,0:T(8,128)(2,1)S(1)}, bf16[128,4096]{1,0:T(8,128)(2,1)}, u32[]{:S(2)}, u32[]{:S(2)}) collective-permute-start(bf16[128,4096]{1,0:T(8,128)(2,1)S(1)} %fusion.3), channel_id=1, source_target_pairs={{4,8},{5,9},{6,10},{7,11},{8,4},{9,5},{10,6},{11,7},{20,24},{21,25... | collective-permute-start | bytes 3145736 | tf_op jit(solution)/shard_map/ppermute | solution.py:1084
  528.4 28.7 %collective-permute-start.17 = (bf16[2,128,1536]{1,2,0:T(8,128)(2,1)}, bf16[2,128,1536]{1,2,0:T(8,128)(2,1)}, u32[]{:S(2)}, u32[]{:S(2)}) collective-permute-start(bf16[2,128,1536]{1,2,0:T(8,128)(2,1)} %bitcast.179), channel_id=1, source_target_pairs={{0,1},{1,0},{2,3},{3,2},{4,5},{5,4},{6,7},{7,6},{8,9},{9,8},{10,11... | collective-permute-start | bytes 2359304 | tf_op jit(solution)/shard_map/ppermute | solution.py:1084
  532.9 55.5 %collective-permute-start.31 = (bf16[128,2560]{0,1:T(8,128)(2,1)}, bf16[128,2560]{0,1:T(8,128)(2,1)}, u32[]{:S(2)}, u32[]{:S(2)}) collective-permute-start(bf16[128,2560]{0,1:T(8,128)(2,1)} %pad_maximum_fusion.2), channel_id=1, source_target_pairs={{4,8},{5,9},{6,10},{7,11},{8,4},{9,5},{10,6},{11,7},{20,24},{21,25... | collective-permute-start | bytes 1966088 | tf_op jit(solution)/shard_map/ppermute | solution.py:1084
  539.0 29.9 %collective-permute-start.25 = (f32[12,256]{1,0:T(8,128)S(1)}, f32[12,256]{1,0:T(8,128)S(1)}, u32[]{:S(2)}, u32[]{:S(2)}) collective-permute-start(f32[12,256]{1,0:T(8,128)S(1)} %constant_dynamic-slice_fusion.2), channel_id=1, source_target_pairs={{0,2},{1,3},{2,0},{3,1},{4,6},{5,7},{6,4},{7,5},{8,10},{9,11},{10,... | collective-permute-start | bytes 36872 | tf_op jit(solution)/shard_map/ppermute | solution.py:1084
  607.2 51.0 %collective-permute-start.32 = (bf16[1024,1024]{1,0:T(8,128)(2,1)S(1)}, bf16[1024,1024]{1,0:T(8,128)(2,1)}, u32[]{:S(2)}, u32[]{:S(2)}) collective-permute-start(bf16[1024,1024]{1,0:T(8,128)(2,1)S(1)} %copy-done.1), channel_id=1, source_target_pairs={{4,8},{5,9},{6,10},{7,11},{8,4},{9,5},{10,6},{11,7},{20,24},{21,25... | collective-permute-start | bytes 6291464 | tf_op jit(solution)/shard_map/ppermute | solution.py:1084
  (53 other events, 458.5 us)
Sparse Core Ops, SparseCore 0:
  10.7 75.5 all-gather.2
  117.9 99.7 all-gather.4

commit v4 on v3

--- a/solution.py
+++ b/solution.py
@@ -479,7 +479,7 @@
         fsdp = fsdp + 4 - 8 * at["z1"]
     else:
         rep = rep + 1 - 2 * at["c"]
-        fsdp = fsdp + 4 - 8 * at["z1"]
+        fsdp = fsdp + 2 - 4 * at["z0"]
     return (rep, fsdp)
 
 
@@ -496,7 +496,7 @@
     barrier = pltpu.get_barrier_semaphore()
     for k in ("c", "x", "y", "z0", "z1"):
         pl.semaphore_signal(barrier, inc=1, device_id=other[k], device_id_type=MESH_ID)
-    moves = at["c"] != at["z1"]
+    moves = at["c"] != at["z0"]
 
     @pl.when(moves)
     def _():
@@ -961,12 +961,14 @@
     )(part_a, part_b, w_qkv, resid)
 
 
-def weight_kernel(half_ref, left_ref, right_ref, *refs):
+def weight_kernel(half_ref, first_ref, second_ref, right_ref, *refs):
     o_ref, turned = refs[-2], refs[-1]
 
     @pl.when(pl.program_id(1) == 0)
     def _():
-        turned[...] = left_ref[...].T
+        part = first_ref.shape[1]
+        turned[:part, :] = first_ref[...].T
+        turned[part:, :] = second_ref[...].T
 
     value = dot(turned[...], right_ref[...], 1, 0)
     if len(refs) == 3:
@@ -980,11 +982,19 @@
     bm = 512
     bn = 1024 if width == 1024 else 512
     steps = rows // 2 // bm
+    if steps == 1:
+        first = lambda i, j, h: (0, h[0])
+        second = lambda i, j, h: (0, 2 + h[0])
+    else:
+        block = lambda i, h: lax.div(i, steps // 2) * steps + h[0] * (steps // 2) + lax.rem(i, steps // 2)
+        first = lambda i, j, h: (0, 2 * block(i, h))
+        second = lambda i, j, h: (0, 2 * block(i, h) + 1)
     specs = [
-        pl.BlockSpec((t, bm), lambda i, j, h: (0, h[0] * steps + i)),
+        pl.BlockSpec((t, bm // 2), first),
+        pl.BlockSpec((t, bm // 2), second),
         pl.BlockSpec((t, bn), lambda i, j, h: (0, j)),
     ]
-    values = [left, right]
+    values = [left, left, right]
     out = pl.BlockSpec((bm, bn), lambda i, j, h: (i, j))
     if came is not None:
         specs.append(out)
@@ -1074,7 +1084,7 @@
     flip = sum(1 << place[bit] for bit in bits)
     pairs = []
     for device in range(32):
-        if bits == ("c", "z1") and ((device >> 3) & 1) == ((device >> 2) & 1):
+        if bits == ("c", "z0") and ((device >> 3) & 1) == ((device >> 1) & 1):
             continue
         pairs.append((device, device ^ flip))
     return pairs
@@ -1082,10 +1092,6 @@
 
 def exchange(value, *bits):
     return lax.ppermute(value, ("rep", "fsdp"), xor_pairs(bits))
-
-
-def swap(at, value):
-    return jnp.where(at["c"] != at["z1"], exchange(value, "c", "z1"), value)
 
 
 def add_low(left, right):
@@ -1152,10 +1158,10 @@
     at = bits_of()
     core = at["c"].astype(jnp.int32)
     def swapped(value, came):
-        return jnp.where(at["c"] != at["z1"], came, value)
+        return jnp.where(at["c"] != at["z0"], came, value)
 
     def cross(value):
-        return exchange(value, "c", "z1")
+        return exchange(value, "c", "z0")
 
     quarter = 2 * core + at["x"].astype(jnp.int32)
     place = jnp.stack([quarter, 2 * (1 - core) + quarter - 2 * core, quarter + 1 - 2 * at["x"], 3 - quarter])
@@ -1197,7 +1203,7 @@
     up_came = exchange(up_send, "c")
     away_d, came_d = halve(at, down_total, "y")
     up_total = slabs(weight_call(hidden_low, after(grad_pre, away_d), core, up_came))
-    away_u, came_u = halve(at, up_total, "z0")
+    away_u, came_u = halve(at, up_total, "z1")
     grad_resid, grad_attn, grad_mixed, sums_one = hidden_call(
         after(grad_pre, away_u), in_parts, place, grad_sum, normed, inv, w_out, rows
     )
@@ -1208,24 +1214,24 @@
     send_a = weight_call(tok, grad_a, 1 - core)
     came_a = exchange(send_a, "c")
     down_one = join(at, down_total, came_d, "y", send_a)
-    away_d, came_d = halve(at, down_one, "z0")
-    up_one = join(at, up_total, came_u, "z0", away_d)
-    away_u, came_u = halve(at, up_one, "y")
-    proj_total = slabs(weight_call(mixed, after(grad_attn, away_u), core, proj_came))
+    away_d, came_d = halve(at, down_one, "z1")
+    proj_total = slabs(weight_call(mixed, after(grad_attn, away_d), core, proj_came))
     away_p, came_p = halve(at, proj_total, "y")
     total_a = slabs(weight_call(tok, after(grad_a, away_p), core, came_a))
-    away_a, came_one = halve(at, total_a, "z0")
-    grad_b, sums_b = attn_bwd(qkv, after(grad_mixed, away_a), log_sum, seg, 1)
+    away_a, came_one = halve(at, total_a, "y")
+    up_one = join(at, up_total, came_u, "z1", away_a)
+    away_u, came_u = halve(at, up_one, "y")
+    grad_b, sums_b = attn_bwd(qkv, after(grad_mixed, away_u), log_sum, seg, 1)
     send_b = weight_call(tok, grad_b, 1 - core)
     came_b = exchange(send_b, "c")
-    down_two = join(at, down_one, came_d, "z0", send_b)
+    down_two = join(at, down_one, came_d, "z1", send_b)
     cross_d = cross(down_two)
     up_two = join(at, up_one, came_u, "y", down_two)
     cross_u = cross(up_two)
     proj_one = join(at, proj_total, came_p, "y", up_two)
-    away_p, came_p = halve(at, proj_one, "z0")
-    a_one = join(at, total_a, came_one, "z0", away_p)
-    away_a, came_a = halve(at, a_one, "y")
+    away_p, came_p = halve(at, proj_one, "z1")
+    a_one = join(at, total_a, came_one, "y", away_p)
+    away_a, came_a = halve(at, a_one, "z1")
     total_b = slabs(weight_call(tok, after(grad_b, away_a), core, came_b))
     away_b, came_b = halve(at, total_b, "y")
     sums_qkv = jnp.concatenate([sums_a, sums_b], axis=0).reshape(D // 128, 3, 128)
@@ -1253,10 +1259,10 @@
         half = parts.shape[1] // 2
         return lax.dynamic_slice_in_dim(parts, at[which] * half, half, axis=1) + after(came, *gates)
 
-    vec_came = vector_send(vector_grad, "c")
+    vec_came = vector_send(vector_grad, "z1")
     input_grad = input_call(after(grad_a, away_b), grad_b, w_qkv, grad_resid)
-    vec_one = vector_join(vector_grad, vec_came, "c", input_grad)
-    vec_came = vector_send(vec_one, "z0")
+    vec_one = vector_join(vector_grad, vec_came, "z1", input_grad)
+    vec_came = vector_send(vec_one, "c")
     def inner(weight, grad, first, second, rate, decay):
         flat = (-1, weight.shape[-1])
         return inner_call(
@@ -1276,22 +1282,22 @@
         flat = (-1, weight.shape[-1])
         return outer_call(weight.reshape(flat), momentum.reshape(flat), own, came, core)
 
-    proj_two = join(at, proj_one, came_p, "z0", input_grad)
-    a_two = join(at, a_one, came_a, "y", input_grad)
+    proj_two = join(at, proj_one, came_p, "z1", input_grad)
+    a_two = join(at, a_one, came_a, "z1", input_grad)
     cross_pa = cross(jnp.concatenate([proj_two, a_two], axis=1))
     grad_contract = swapped(down_two, after(cross_d, proj_two, a_two))
     contract_new = inner(contract_weight, grad_contract, contract_first, contract_second, 0.015, 0.1)
     sent_c, came_c = rep_send(contract_new[2])
     b_one = join(at, total_b, came_b, "y", sent_c)
-    away_b, came_b = halve(at, b_one, "z0")
-    vec_two = vector_join(vec_one, vec_came, "z0", away_b)
+    away_b, came_b = halve(at, b_one, "z1")
+    vec_two = vector_join(vec_one, vec_came, "c", away_b)
     vec_came = vector_send(vec_two, "y")
     grad_expand = swapped(up_two, after(cross_u, away_b))
     expand_new = inner(expand_weight, grad_expand, expand_first, expand_second, 0.03, 0.1)
     sent_e, came_e = rep_send(expand_new[2])
     half_c = rep_join(contract_new[2], came_c, sent_e)
     rest_c = exchange(half_c, "x")
-    b_two = join(at, b_one, came_b, "z0", half_c)
+    b_two = join(at, b_one, came_b, "z1", half_c)
     cross_b = cross(b_two)
     half_e = rep_join(expand_new[2], came_e, b_two)
     rest_e = exchange(half_e, "x")

time: 675 us -> 644 us (0.954)
  waiting for transfers between devices: 63.5 us -> 51.3 us
  starting transfers between devices: 51.3 us -> 40.3 us
  Pallas kernels: 441 us -> 431 us
    ppermute x41, waiting for transfers between devices: 63.4 us -> 51.2 us  [exchange(): return lax.ppermute(value, ('rep', 'fsdp'), xor_pairs(bits))]
    ppermute x41, starting transfers between devices: 51.2 us -> 40.3 us  [exchange(): return lax.ppermute(value, ('rep', 'fsdp'), xor_pairs(bits))]
    pallas_call x1, Pallas kernels: 101 us -> 91.8 us  [gather_all(): pl.pallas_call(gather_kernel, out_shape=(shape((8 * qkv.shape[0], qkv.sha...]
  transfers between devices with their start and end apart: 43 -> 43, of which waited for: 8 -> 9; matrix products, arithmetic and copies ran while one was open for 13% -> 14% of each run, Pallas kernels for 62% -> 63%
where the time goes in v4:
time: 644 us; the launch traced here: 636 us
  Pallas kernels  431 us (67%)
  local copies, waits for them, and re-layouts  53.3 us (8%)
  waiting for transfers between devices  51.3 us (8%)
  other arithmetic  44.7 us (7%)
  starting transfers between devices  40.3 us (6%)
  between operations  15.2 us (2%)
    pallas_call x1, Pallas kernels, gather_all(): pl.pallas_call(gather_kernel, out_shape=(shape((8 * qkv.shape[0], qkv.sha...  91.8 us
    pallas_call x10, Pallas kernels, weight_call(): pl.pallas_call(weight_kernel, out_shape=SHAPE((rows // 2, width), BF), gr...  71.9 us
    pallas_call x2, Pallas kernels, attn_bwd(): pl.pallas_call(bwd_kernel, out_shape=(jax.ShapeDtypeStruct((T, width // 2...  59.6 us
    ppermute x41, waiting for transfers between devices, exchange(): return lax.ppermute(value, ('rep', 'fsdp'), xor_pairs(bits))  51.2 us
    pallas_call x1, Pallas kernels, attn_fwd(): pl.pallas_call(fwd_kernel, out_shape=(jax.ShapeDtypeStruct((T, width // 3...  46.9 us
    ppermute x41, starting transfers between devices, exchange(): return lax.ppermute(value, ('rep', 'fsdp'), xor_pairs(bits))  40.3 us
    pallas_call x1, Pallas kernels, up_call(): pl.pallas_call(up_kernel, out_shape=(SHAPE((t, FF), BF), SHAPE((t, FF), B...  34.2 us
    pallas_call x1, Pallas kernels, hidden_call(): pl.pallas_call(hidden_kernel, out_shape=(SHAPE((t, D), F32), SHAPE((t, D)...  22.1 us
  transfers between devices with their start and end apart: 43, of which 9 were waited for; matrix products, arithmetic and copies ran while one was open for 14% of the time, Pallas kernels for 63%

profile of v4, /device:TPU:1, one launch (start us, length us, event | category | flops | bytes accessed | tf_op | source)
XLA Modules:
  0.0 636.2 jit_solution(7329450946131844808)
XLA Ops:
  14.2 91.8 %gather_weights.1 = (bf16[1024,3072]{1,0:T(8,128)(2,1)}, bf16[1024,1024]{1,0:T(8,128)(2,1)}, bf16[8,12,128]{2,1,0:T(8,128)(2,1)}, bf16[1024,1024]{1,0:T(8,128)(2,1)}, s32[1,1024]{1,0:T(1,128)}) custom-call(bf16[128,3072]{1,0:T(8,128)(2,1)} %copy.81.qkv_in, bf16[128,1024]{1,0:T(8,128)(2,1)} %slice_bitcast_fusion.1.wo_in, ...), custom_call_target="tpu_custom_call" | custom-call | tf_op jit(solution)/shard_map/gather_weights/pallas_call | solution.py:679
  115.7 10.8 %qkv.1.qkv_ref = bf16[1024,3072]{1,0:T(8,128)(2,1)} custom-call(bf16[1024,1024]{1,0:T(8,128)(2,1)} %get-tuple-element.109.x_ref.first_ref.second_ref, bf16[1024,3072]{1,0:T(8,128)(2,1)} %get-tuple-element.110.w_ref, f32[1,3072]{1,0:T(1,128)} %reshape.202.bias_ref, f32[1,3072]{1,0:T(1,128)} %constant.207.clone.1.scale_ref), custom_call_target="tpu_custom_call" | custom-call | flops 6442450 | bytes 14680 | tf_op jit(solution)/shard_map/qkv/pallas_call | solution.py:725
  127.3 46.9 %attn_fwd.1 = (bf16[1024,1024]{1,0:T(8,128)(2,1)}, f32[8,2,1024]{2,1,0:T(2,128)}) custom-call(s32[4]{0:T(128)} %get-tuple-element.202.start_ref, s32[4]{0:T(128)} %get-tuple-element.203.count_ref, bf16[1024,3072]{1,0:T(8,128)(2,1)} %qkv.1.qkv_ref, s32[1,1024]{1,0:T(1,128)} %get-tuple-element.108.segr_ref, s32[1024,1]{1,0:T(8,128)} %copy.82.segc_ref), custom_call_target="tpu_custom_call" | custom-call | flops 64424508 | bytes 9437 | tf_op jit(solution)/shard_map/attn_fwd/pallas_call | solution.py:413
  176.0 8.1 %mix_norm.1 = (f32[1024,1024]{1,0:T(8,128)}, f32[1024,1]{1,0:T(8,128)}, bf16[1024,1024]{1,0:T(8,128)(2,1)}) custom-call(bf16[1024,1024]{1,0:T(8,128)(2,1)} %get-tuple-element.112.c_ref.first_ref.second_ref, bf16[1024,1024]{1,0:T(8,128)(2,1)} %get-tuple-element.113.w_ref.refs_11_, bf16[1024,1024]{1,0:T(8,128)(2,1)} %get-tuple-element.109.x_ref.first_ref.second_ref, ...), custom_call_target="tpu_custom_call" | custom-call | flops 2147483 | bytes 14680 | tf_op jit(solution)/shard_map/mix_norm/pallas_call | solution.py:758
  187.9 34.2 %up_gelu.1 = (bf16[1024,4096]{1,0:T(8,128)(2,1)}, bf16[1024,4096]{1,0:T(8,128)(2,1)}) custom-call(s32[4]{0:T(128)} %pad_add_fusion.place_ref, bf16[1024,1024]{1,0:T(8,128)(2,1)} %get-tuple-element.117.h_ref.first_ref.second_ref, bf16[1024,1024]{1,0:T(8,128)(2,1)} %all-gather.3.cloned.1.call-done.refs_0_.refs_4_, ...), custom_call_target="tpu_custom_call" | custom-call | flops 8589934 | bytes 27262 | tf_op jit(solution)/shard_map/up_gelu/pallas_call | solution.py:795
  222.3 7.4 %collective-permute-done.4.came_ref = bf16[4096,512]{1,0:T(8,128)(2,1)} collective-permute-done((bf16[4096,512]{1,0:T(8,128)(2,1)}, bf16[4096,512]{1,0:T(8,128)(2,1)}, u32[]{:S(2)}, u32[]{:S(2)}) %collective-permute-start.4) | collective-permute-done | bytes 4194336 | tf_op jit(solution)/shard_map/ppermute | solution.py:1094
  229.7 19.9 %down_norm.1 = (bf16[1024,1024]{1,0:T(8,128)(2,1)}, f32[1024,1024]{1,0:T(8,128)}, bf16[1024,1024]{1,0:T(8,128)(2,1)}, f32[8,1024]{1,0:T(8,128)}) custom-call(s32[1]{0:T(128)} %bitcast.core_ref.half_ref, bf16[1024,4096]{1,0:T(8,128)(2,1)} %get-tuple-element.121.g_ref.first_ref.second_ref, bf16[4096,512]{1,0:T(8,128)(2,1)} %all-gather.5.cloned.1.call-done.own_ref, ...), custom_call_target="tpu_custom_call" | custom-call | flops 8589934 | bytes 31457 | tf_op jit(solution)/shard_map/down_norm/pallas_call | solution.py:848
  249.6 8.5 %weight_grad.10 = bf16[2048,1024]{1,0:T(8,128)(2,1)} custom-call(s32[1]{0:T(128)} %bitcast.16.half_ref, bf16[1024,4096]{1,0:T(8,128)(2,1)} %get-tuple-element.121.g_ref.first_ref.second_ref, bf16[1024,4096]{1,0:T(8,128)(2,1)} %get-tuple-element.121.g_ref.first_ref.second_ref, bf16[1024,1024]{1,0:T(8,128)(2,1)} %get-tuple-element.130.right_ref.left_ref), custom_call_target="tpu_custom_call" | custom-call | flops 4294967 | bytes 14680 | tf_op jit(solution)/shard_map/weight_grad/pallas_call | solution.py:1002
  258.2 16.3 %down_back.1 = (bf16[1024,4096]{1,0:T(8,128)(2,1)}, f32[1,4096]{1,0:T(1,128)}) custom-call(s32[1]{0:T(128)} %bitcast.core_ref.half_ref, bf16[1024,1024]{1,0:T(8,128)(2,1)} %get-tuple-element.130.right_ref.left_ref, bf16[1024,1024]{1,0:T(8,128)(2,1)} %get-tuple-element.130.right_ref.left_ref, bf16[4096,512]{1,0:T(8,128)(2,1)} %all-gather.5.cloned.1.call-done.own_ref, ...), custom_call_target="tpu_custom_call" | custom-call | flops 8589934 | bytes 27262 | tf_op jit(solution)/shard_map/down_back/pallas_call | solution.py:881
  274.5 11.0 %weight_grad.11 = bf16[512,4096]{1,0:T(8,128)(2,1)} custom-call(s32[1]{0:T(128)} %bitcast.16.half_ref, bf16[1024,1024]{1,0:T(8,128)(2,1)} %get-tuple-element.117.h_ref.first_ref.second_ref, bf16[1024,1024]{1,0:T(8,128)(2,1)} %get-tuple-element.117.h_ref.first_ref.second_ref, bf16[1024,4096]{1,0:T(8,128)(2,1)} %get-tuple-element.132.right_ref.refs_0_.refs_1_.refs_2_.refs_3_), custom_call_target="tpu_custom_call" | custom-call | flops 4294967 | bytes 17825 | tf_op jit(solution)/shard_map/weight_grad/pallas_call | solution.py:1002
  287.8 9.5 %weight_grad.12 = bf16[2048,1024]{1,0:T(8,128)(2,1)} custom-call(s32[1]{0:T(128)} %bitcast.core_ref.half_ref, bf16[1024,4096]{1,0:T(8,128)(2,1)} %get-tuple-element.121.g_ref.first_ref.second_ref, bf16[1024,4096]{1,0:T(8,128)(2,1)} %get-tuple-element.121.g_ref.first_ref.second_ref, bf16[1024,1024]{1,0:T(8,128)(2,1)} %get-tuple-element.130.right_ref.left_ref, ...), custom_call_target="tpu_custom_call" | custom-call | flops 4294967 | bytes 14680 | tf_op jit(solution)/shard_map/weight_grad/pallas_call | solution.py:1002
  303.0 11.6 %weight_grad.13 = bf16[512,4096]{1,0:T(8,128)(2,1)} custom-call(s32[1]{0:T(128)} %bitcast.core_ref.half_ref, bf16[1024,1024]{1,0:T(8,128)(2,1)} %get-tuple-element.117.h_ref.first_ref.second_ref, bf16[1024,1024]{1,0:T(8,128)(2,1)} %get-tuple-element.117.h_ref.first_ref.second_ref, ...), custom_call_target="tpu_custom_call" | custom-call | flops 4294967 | bytes 17825 | tf_op jit(solution)/shard_map/weight_grad/pallas_call | solution.py:1002
  319.0 22.1 %up_back_norm.1 = (f32[1024,1024]{1,0:T(8,128)}, bf16[1024,1024]{1,0:T(8,128)(2,1)}, bf16[1024,1024]{1,0:T(8,128)(2,1)}, f32[8,1024]{1,0:T(8,128)}) custom-call(s32[4]{0:T(128)} %pad_add_fusion.place_ref, bf16[1024,4096]{1,0:T(8,128)(2,1)} %get-tuple-element.132.right_ref.refs_0_.refs_1_.refs_2_.refs_3_, ...), custom_call_target="tpu_custom_call" | custom-call | flops 10737418 | bytes 33554 | tf_op jit(solution)/shard_map/up_back_norm/pallas_call | solution.py:927
  348.4 29.8 %attn_bwd.2 = (bf16[1024,1536]{1,0:T(8,128)(2,1)}, f32[4,1,384]{2,1,0:T(1,128)}) custom-call(s32[4]{0:T(128)} %get-tuple-element.202.start_ref, s32[4]{0:T(128)} %get-tuple-element.203.count_ref, bf16[1024,3072]{1,0:T(8,128)(2,1)} %qkv.1.qkv_ref, bf16[1024,1024]{1,0:T(8,128)(2,1)} %get-tuple-element.145.do_ref, f32[8,2,1024]{2,1,0:T(2,128)} %get-tuple-element.139.lse_ref, ...), custom_call_target="tpu_custom_call" | custom-call | flops 64424508 | bytes 18874 | tf_op jit(solution)/shard_map/attn_bwd/pallas_call | solution.py:437
  407.1 26.5 %collective-permute-done.8 = bf16[2,128,4096]{2,1,0:T(8,128)(2,1)} collective-permute-done((bf16[2,128,4096]{2,1,0:T(8,128)(2,1)}, bf16[2,128,4096]{2,1,0:T(8,128)(2,1)}, u32[]{:S(2)}, u32[]{:S(2)}) %collective-permute-start.8) | collective-permute-done | bytes 2097184 | tf_op jit(solution)/shard_map/ppermute | solution.py:1094
  447.3 29.8 %attn_bwd.3 = (bf16[1024,1536]{1,0:T(8,128)(2,1)}, f32[4,1,384]{2,1,0:T(1,128)}) custom-call(s32[4]{0:T(128)} %get-tuple-element.202.start_ref, s32[4]{0:T(128)} %get-tuple-element.203.count_ref, bf16[1024,3072]{1,0:T(8,128)(2,1)} %qkv.1.qkv_ref, bf16[1024,1024]{1,0:T(8,128)(2,1)} %get-tuple-element.145.do_ref, f32[8,2,1024]{2,1,0:T(2,128)} %get-tuple-element.139.lse_ref, ...), custom_call_target="tpu_custom_call" | custom-call | flops 64424508 | bytes 18874 | tf_op jit(solution)/shard_map/attn_bwd/pallas_call | solution.py:437
  513.0 12.3 %input_back.1 = bf16[1024,1024]{1,0:T(8,128)(2,1)} custom-call(bf16[1024,1536]{1,0:T(8,128)(2,1)} %get-tuple-element.152.right_ref.a_ref, bf16[1024,1536]{1,0:T(8,128)(2,1)} %get-tuple-element.151.right_ref.b_ref, bf16[1024,3072]{1,0:T(8,128)(2,1)} %get-tuple-element.110.w_ref, f32[1024,1024]{1,0:T(8,128)} %get-tuple-element.153.r_ref), custom_call_target="tpu_custom_call" | custom-call | flops 6442450 | bytes 18874 | tf_op jit(solution)/shard_map/input_back/pallas_call | solution.py:953
  537.8 6.1 inner_step.3
  551.4 6.1 inner_step.4
  561.2 7.1 %collective-permute-done.21 = bf16[128,1536]{0,1:T(8,128)(2,1)} collective-permute-done((bf16[128,1536]{0,1:T(8,128)(2,1)}, bf16[128,1536]{0,1:T(8,128)(2,1)}, u32[]{:S(2)}, u32[]{:S(2)}) %collective-permute-start.21) | collective-permute-done | bytes 393248 | tf_op jit(solution)/shard_map/ppermute | solution.py:1094
  579.0 6.3 outer_step.3
  588.0 6.2 inner_step.5
  601.6 6.4 outer_step.4
  619.7 6.3 outer_step.5
  (253 shorter events, 180.1 us)
Async XLA Ops:
  7.2 101.0 %all-gather.3.cloned.1.call-start = ((), (), s32[]{:S(2)}) async-start(), calls=%async_computation | async-start | bytes 2359296 | tf_op jit(solution)/shard_map/all_gather | solution.py:1169
  9.1 213.1 %all-gather.5.cloned.1.call-start = ((), (), s32[]{:S(2)}) async-start(), calls=%async_computation.1 | async-start | bytes 4718592 | tf_op jit(solution)/shard_map/all_gather | solution.py:1183
  108.2 66.0 %collective-permute-start.2 = (bf16[1024,1024]{1,0:T(8,128)(2,1)}, bf16[1024,1024]{1,0:T(8,128)(2,1)}, u32[]{:S(2)}, u32[]{:S(2)}) collective-permute-start(bf16[1024,1024]{1,0:T(8,128)(2,1)} %all-gather.3.cloned.1.call-done.refs_0_.refs_4_), channel_id=1, source_target_pairs={{0,16},{1,17},{2,18},{3,19},{4,20},{5,21},{6,22},{7,23},{8,24},{9,... | collective-permute-start | bytes 6291464 | tf_op jit(solution)/shard_map/ppermute | solution.py:1094
  108.5 76.3 %collective-permute-start = (bf16[1024,1024]{1,0:T(8,128)(2,1)}, bf16[1024,1024]{1,0:T(8,128)(2,1)}, u32[]{:S(2)}, u32[]{:S(2)}) collective-permute-start(bf16[1024,1024]{1,0:T(8,128)(2,1)} %param.20), channel_id=1, source_target_pairs={{2,8},{3,9},{6,12},{7,13},{8,2},{9,3},{12,6},{13,7},{18,24},{19,25... | collective-permute-start | bytes 6291464 | tf_op jit(solution)/shard_map/ppermute | solution.py:1094
  258.1 29.7 %collective-permute-start.6 = (bf16[2048,1024]{1,0:T(8,128)(2,1)}, bf16[2048,1024]{1,0:T(8,128)(2,1)}, u32[]{:S(2)}, u32[]{:S(2)}) collective-permute-start(bf16[2048,1024]{1,0:T(8,128)(2,1)} %weight_grad.10), channel_id=1, source_target_pairs={{0,8},{1,9},{2,10},{3,11},{4,12},{5,13},{6,14},{7,15},{8,0},{9,1},... | collective-permute-start | bytes 12582920 | tf_op jit(solution)/shard_map/ppermute | solution.py:1094
  285.9 59.4 %collective-permute-start.5 = (bf16[1024,1024]{1,0:T(8,128)(2,1)S(1)}, bf16[1024,1024]{1,0:T(8,128)(2,1)}, u32[]{:S(2)}, u32[]{:S(2)}) collective-permute-start(bf16[1024,1024]{1,0:T(8,128)(2,1)S(1)} %copy-done.7), channel_id=1, source_target_pairs={{2,8},{3,9},{6,12},{7,13},{8,2},{9,3},{12,6},{13,7},{18,24},{19,25... | collective-permute-start | bytes 6291464 | tf_op jit(solution)/shard_map/ppermute | solution.py:1094
  300.4 83.9 %collective-permute-start.9 = (bf16[2,512,1024]{2,1,0:T(8,128)(2,1)}, bf16[2,512,1024]{2,1,0:T(8,128)(2,1)}, u32[]{:S(2)}, u32[]{:S(2)}) collective-permute-start(bf16[2,512,1024]{2,1,0:T(8,128)(2,1)} %dynamic-slice_bitcast_fusion.1), channel_id=1, source_target_pairs={{0,1},{1,0},{2,3},{3,2},{4,5},{5,4},{6,7},{7,6},{8,9},{9,8},{10,11... | collective-permute-start | bytes 6291464 | tf_op jit(solution)/shard_map/ppermute | solution.py:1094
  317.7 115.9 %collective-permute-start.8 = (bf16[2,128,4096]{2,1,0:T(8,128)(2,1)}, bf16[2,128,4096]{2,1,0:T(8,128)(2,1)}, u32[]{:S(2)}, u32[]{:S(2)}) collective-permute-start(bf16[2,128,4096]{2,1,0:T(8,128)(2,1)} %dynamic-slice_bitcast_fusion), channel_id=1, source_target_pairs={{0,4},{1,5},{2,6},{3,7},{4,0},{5,1},{6,2},{7,3},{8,12},{9,13},{10,... | collective-permute-start | bytes 6291464 | tf_op jit(solution)/shard_map/ppermute | solution.py:1094
  388.5 94.2 %collective-permute-start.15 = (bf16[512,1024]{1,0:T(8,128)(2,1)}, bf16[512,1024]{1,0:T(8,128)(2,1)}, u32[]{:S(2)}, u32[]{:S(2)}) collective-permute-start(bf16[512,1024]{1,0:T(8,128)(2,1)} %dynamic-slice_bitcast_fusion.3), channel_id=1, source_target_pairs={{0,4},{1,5},{2,6},{3,7},{4,0},{5,1},{6,2},{7,3},{8,12},{9,13},{10,... | collective-permute-start | bytes 3145736 | tf_op jit(solution)/shard_map/ppermute | solution.py:1094
  438.9 45.6 %collective-permute-start.14 = (bf16[128,4096]{1,0:T(8,128)(2,1)}, bf16[128,4096]{1,0:T(8,128)(2,1)}, u32[]{:S(2)}, u32[]{:S(2)}) collective-permute-start(bf16[128,4096]{1,0:T(8,128)(2,1)} %dynamic-slice_bitcast_fusion.2), channel_id=1, source_target_pairs={{0,1},{1,0},{2,3},{3,2},{4,5},{5,4},{6,7},{7,6},{8,9},{9,8},{10,11... | collective-permute-start | bytes 3145736 | tf_op jit(solution)/shard_map/ppermute | solution.py:1094
  443.7 42.5 %collective-permute-start.13 = (bf16[2,128,1024]{1,2,0:T(8,128)(2,1)}, bf16[2,128,1024]{1,2,0:T(8,128)(2,1)}, u32[]{:S(2)}, u32[]{:S(2)}) collective-permute-start(bf16[2,128,1024]{1,2,0:T(8,128)(2,1)} %bitcast.181), channel_id=1, source_target_pairs={{0,1},{1,0},{2,3},{3,2},{4,5},{5,4},{6,7},{7,6},{8,9},{9,8},{10,11... | collective-permute-start | bytes 1572872 | tf_op jit(solution)/shard_map/ppermute | solution.py:1094
  445.1 46.7 %collective-permute-start.12 = (bf16[2,128,1536]{1,2,0:T(8,128)(2,1)}, bf16[2,128,1536]{1,2,0:T(8,128)(2,1)}, u32[]{:S(2)}, u32[]{:S(2)}) collective-permute-start(bf16[2,128,1536]{1,2,0:T(8,128)(2,1)} %bitcast.179), channel_id=1, source_target_pairs={{0,1},{1,0},{2,3},{3,2},{4,5},{5,4},{6,7},{7,6},{8,9},{9,8},{10,11... | collective-permute-start | bytes 2359304 | tf_op jit(solution)/shard_map/ppermute | solution.py:1094
  482.7 18.9 %collective-permute-start.16 = (bf16[512,1536]{1,0:T(8,128)(2,1)}, bf16[512,1536]{1,0:T(8,128)(2,1)}, u32[]{:S(2)}, u32[]{:S(2)}) collective-permute-start(bf16[512,1536]{1,0:T(8,128)(2,1)} %weight_grad.18), channel_id=1, source_target_pairs={{0,8},{1,9},{2,10},{3,11},{4,12},{5,13},{6,14},{7,15},{8,0},{9,1},... | collective-permute-start | bytes 4718600 | tf_op jit(solution)/shard_map/ppermute | solution.py:1094
  494.9 30.4 %collective-permute-start.20 = (bf16[128,1536]{0,1:T(8,128)(2,1)}, bf16[128,1536]{0,1:T(8,128)(2,1)S(1)}, u32[]{:S(2)}, u32[]{:S(2)}) collective-permute-start(bf16[128,1536]{0,1:T(8,128)(2,1)} %dynamic-slice_bitcast_fusion.8), channel_id=1, source_target_pairs={{0,4},{1,5},{2,6},{3,7},{4,0},{5,1},{6,2},{7,3},{8,12},{9,13},{10,... | collective-permute-start | bytes 1179656 | tf_op jit(solution)/shard_map/ppermute | solution.py:1094
  495.0 40.3 %collective-permute-start.24 = (f32[12,512]{1,0:T(8,128)S(1)}, f32[12,512]{1,0:T(8,128)S(1)}, u32[]{:S(2)}, u32[]{:S(2)}) collective-permute-start(f32[12,512]{1,0:T(8,128)S(1)} %constant_dynamic-slice_fusion.3), channel_id=1, source_target_pairs={{0,4},{1,5},{2,6},{3,7},{4,0},{5,1},{6,2},{7,3},{8,12},{9,13},{10,... | collective-permute-start | bytes 73736 | tf_op jit(solution)/shard_map/ppermute | solution.py:1094
  497.4 29.7 %collective-permute-start.19 = (bf16[128,1024]{0,1:T(8,128)(2,1)}, bf16[128,1024]{0,1:T(8,128)(2,1)}, u32[]{:S(2)}, u32[]{:S(2)}) collective-permute-start(bf16[128,1024]{0,1:T(8,128)(2,1)} %dynamic-slice_bitcast_fusion.9), channel_id=1, source_target_pairs={{0,4},{1,5},{2,6},{3,7},{4,0},{5,1},{6,2},{7,3},{8,12},{9,13},{10,... | collective-permute-start | bytes 786440 | tf_op jit(solution)/shard_map/ppermute | solution.py:1094
  497.5 37.9 %collective-permute-start.18 = (bf16[512,1024]{1,0:T(8,128)(2,1)S(1)}, bf16[512,1024]{1,0:T(8,128)(2,1)}, u32[]{:S(2)}, u32[]{:S(2)}) collective-permute-start(bf16[512,1024]{1,0:T(8,128)(2,1)S(1)} %fusion.2), channel_id=1, source_target_pairs={{2,8},{3,9},{6,12},{7,13},{8,2},{9,3},{12,6},{13,7},{18,24},{19,25... | collective-permute-start | bytes 3145736 | tf_op jit(solution)/shard_map/ppermute | solution.py:1094
  501.6 47.4 %collective-permute-start.23 = (bf16[128,4096]{1,0:T(8,128)(2,1)S(1)}, bf16[128,4096]{1,0:T(8,128)(2,1)}, u32[]{:S(2)}, u32[]{:S(2)}) collective-permute-start(bf16[128,4096]{1,0:T(8,128)(2,1)S(1)} %fusion.3), channel_id=1, source_target_pairs={{2,8},{3,9},{6,12},{7,13},{8,2},{9,3},{12,6},{13,7},{18,24},{19,25... | collective-permute-start | bytes 3145736 | tf_op jit(solution)/shard_map/ppermute | solution.py:1094
  525.3 20.4 %collective-permute-start.17 = (bf16[2,128,1536]{1,2,0:T(8,128)(2,1)}, bf16[2,128,1536]{1,2,0:T(8,128)(2,1)}, u32[]{:S(2)}, u32[]{:S(2)}) collective-permute-start(bf16[2,128,1536]{1,2,0:T(8,128)(2,1)} %bitcast.180), channel_id=1, source_target_pairs={{0,1},{1,0},{2,3},{3,2},{4,5},{5,4},{6,7},{7,6},{8,9},{9,8},{10,11... | collective-permute-start | bytes 2359304 | tf_op jit(solution)/shard_map/ppermute | solution.py:1094
  529.1 47.2 %collective-permute-start.31 = (bf16[128,2560]{0,1:T(8,128)(2,1)}, bf16[128,2560]{0,1:T(8,128)(2,1)}, u32[]{:S(2)}, u32[]{:S(2)}) collective-permute-start(bf16[128,2560]{0,1:T(8,128)(2,1)} %pad_maximum_fusion.2), channel_id=1, source_target_pairs={{2,8},{3,9},{6,12},{7,13},{8,2},{9,3},{12,6},{13,7},{18,24},{19,25... | collective-permute-start | bytes 1966088 | tf_op jit(solution)/shard_map/ppermute | solution.py:1094
  535.4 23.4 %collective-permute-start.25 = (f32[12,256]{1,0:T(8,128)S(1)}, f32[12,256]{1,0:T(8,128)S(1)}, u32[]{:S(2)}, u32[]{:S(2)}) collective-permute-start(f32[12,256]{1,0:T(8,128)S(1)} %constant_dynamic-slice_fusion.2), channel_id=1, source_target_pairs={{0,8},{1,9},{2,10},{3,11},{4,12},{5,13},{6,14},{7,15},{8,0},{9,1},... | collective-permute-start | bytes 36872 | tf_op jit(solution)/shard_map/ppermute | solution.py:1094
  547.8 20.5 %collective-permute-start.21 = (bf16[128,1536]{0,1:T(8,128)(2,1)}, bf16[128,1536]{0,1:T(8,128)(2,1)}, u32[]{:S(2)}, u32[]{:S(2)}) collective-permute-start(bf16[128,1536]{0,1:T(8,128)(2,1)} %dynamic-slice_bitcast_fusion.7), channel_id=1, source_target_pairs={{0,4},{1,5},{2,6},{3,7},{4,0},{5,1},{6,2},{7,3},{8,12},{9,13},{10,... | collective-permute-start | bytes 1179656 | tf_op jit(solution)/shard_map/ppermute | solution.py:1094
  571.5 23.9 %collective-permute-start.35 = (bf16[64,4096]{1,0:T(8,128)(2,1)S(1)}, bf16[64,4096]{1,0:T(8,128)(2,1)}, u32[]{:S(2)}, u32[]{:S(2)}) collective-permute-start(bf16[64,4096]{1,0:T(8,128)(2,1)S(1)} %fusion.7), channel_id=1, source_target_pairs={{0,16},{1,17},{2,18},{3,19},{4,20},{5,21},{6,22},{7,23},{8,24},{9,... | collective-permute-start | bytes 1572872 | tf_op jit(solution)/shard_map/ppermute | solution.py:1094
  595.5 30.6 %collective-permute-start.32 = (bf16[1024,1024]{1,0:T(8,128)(2,1)S(1)}, bf16[1024,1024]{1,0:T(8,128)(2,1)}, u32[]{:S(2)}, u32[]{:S(2)}) collective-permute-start(bf16[1024,1024]{1,0:T(8,128)(2,1)S(1)} %copy-done), channel_id=1, source_target_pairs={{2,8},{3,9},{6,12},{7,13},{8,2},{9,3},{12,6},{13,7},{18,24},{19,25... | collective-permute-start | bytes 6291464 | tf_op jit(solution)/shard_map/ppermute | solution.py:1094
  (52 other events, 421.7 us)
Sparse Core Ops, SparseCore 0:
  10.7 63.0 all-gather.2
  108.3 78.5 all-gather.4

commit v5 on v4

--- a/solution.py
+++ b/solution.py
@@ -1203,7 +1203,7 @@
     up_came = exchange(up_send, "c")
     away_d, came_d = halve(at, down_total, "y")
     up_total = slabs(weight_call(hidden_low, after(grad_pre, away_d), core, up_came))
-    away_u, came_u = halve(at, up_total, "z1")
+    away_u, came_u = halve(at, up_total, "y")
     grad_resid, grad_attn, grad_mixed, sums_one = hidden_call(
         after(grad_pre, away_u), in_parts, place, grad_sum, normed, inv, w_out, rows
     )
@@ -1219,14 +1219,14 @@
     away_p, came_p = halve(at, proj_total, "y")
     total_a = slabs(weight_call(tok, after(grad_a, away_p), core, came_a))
     away_a, came_one = halve(at, total_a, "y")
-    up_one = join(at, up_total, came_u, "z1", away_a)
-    away_u, came_u = halve(at, up_one, "y")
+    up_one = join(at, up_total, came_u, "y", away_a)
+    away_u, came_u = halve(at, up_one, "z1")
     grad_b, sums_b = attn_bwd(qkv, after(grad_mixed, away_u), log_sum, seg, 1)
     send_b = weight_call(tok, grad_b, 1 - core)
     came_b = exchange(send_b, "c")
     down_two = join(at, down_one, came_d, "z1", send_b)
     cross_d = cross(down_two)
-    up_two = join(at, up_one, came_u, "y", down_two)
+    up_two = join(at, up_one, came_u, "z1", down_two)
     cross_u = cross(up_two)
     proj_one = join(at, proj_total, came_p, "y", up_two)
     away_p, came_p = halve(at, proj_one, "z1")
@@ -1260,9 +1260,7 @@
         return lax.dynamic_slice_in_dim(parts, at[which] * half, half, axis=1) + after(came, *gates)
 
     vec_came = vector_send(vector_grad, "z1")
-    input_grad = input_call(after(grad_a, away_b), grad_b, w_qkv, grad_resid)
-    vec_one = vector_join(vector_grad, vec_came, "z1", input_grad)
-    vec_came = vector_send(vec_one, "c")
+
     def inner(weight, grad, first, second, rate, decay):
         flat = (-1, weight.shape[-1])
         return inner_call(
@@ -1282,31 +1280,35 @@
         flat = (-1, weight.shape[-1])
         return outer_call(weight.reshape(flat), momentum.reshape(flat), own, came, core)
 
+    grad_contract = swapped(down_two, after(cross_d, away_b))
+    contract_new = inner(contract_weight, grad_contract, contract_first, contract_second, 0.015, 0.1)
+    sent_c, came_c = rep_send(contract_new[2])
+    vec_one = vector_join(vector_grad, vec_came, "z1", sent_c)
+    vec_came = vector_send(vec_one, "c")
+    grad_expand = swapped(up_two, after(cross_u, sent_c))
+    expand_new = inner(expand_weight, grad_expand, expand_first, expand_second, 0.03, 0.1)
+    sent_e, came_e = rep_send(expand_new[2])
+    b_one = join(at, total_b, came_b, "y", sent_e)
+    away_b, came_b = halve(at, b_one, "z1")
+    half_c = rep_join(contract_new[2], came_c, away_b)
+    rest_c = exchange(half_c, "x")
+    half_e = rep_join(expand_new[2], came_e, half_c)
+    rest_e = exchange(half_e, "x")
+    vec_two = vector_join(vec_one, vec_came, "c", half_e)
+    vec_came = vector_send(vec_two, "y")
+    input_grad = input_call(after(grad_a, away_b, half_e), grad_b, w_qkv, grad_resid)
     proj_two = join(at, proj_one, came_p, "z1", input_grad)
     a_two = join(at, a_one, came_a, "z1", input_grad)
     cross_pa = cross(jnp.concatenate([proj_two, a_two], axis=1))
-    grad_contract = swapped(down_two, after(cross_d, proj_two, a_two))
-    contract_new = inner(contract_weight, grad_contract, contract_first, contract_second, 0.015, 0.1)
-    sent_c, came_c = rep_send(contract_new[2])
-    b_one = join(at, total_b, came_b, "y", sent_c)
-    away_b, came_b = halve(at, b_one, "z1")
-    vec_two = vector_join(vec_one, vec_came, "c", away_b)
-    vec_came = vector_send(vec_two, "y")
-    grad_expand = swapped(up_two, after(cross_u, away_b))
-    expand_new = inner(expand_weight, grad_expand, expand_first, expand_second, 0.03, 0.1)
-    sent_e, came_e = rep_send(expand_new[2])
-    half_c = rep_join(contract_new[2], came_c, sent_e)
-    rest_c = exchange(half_c, "x")
-    b_two = join(at, b_one, came_b, "z1", half_c)
+    vec_three = vector_join(vec_two, vec_came, "y", proj_two, a_two)
+    vec_cross = cross(vec_three)
+    full_c = add_low(half_c, after(rest_c, vec_three))
+    back_c = exchange(full_c, "c")
+    b_two = join(at, b_one, came_b, "z1", full_c)
     cross_b = cross(b_two)
-    half_e = rep_join(expand_new[2], came_e, b_two)
-    rest_e = exchange(half_e, "x")
-    vec_three = vector_join(vec_two, vec_came, "y", half_e)
-    vec_cross = cross(vec_three)
-    full_c = add_low(half_c, after(rest_c, half_e))
-    back_c = exchange(full_c, "c")
-    pa = swapped(jnp.concatenate([proj_two, a_two], axis=1), after(cross_pa, full_c))
-    outer_c = outer(contract_weight, contract_momentum, full_c, after(back_c, pa))
+    full_e = add_low(half_e, after(rest_e, b_two))
+    back_e = exchange(full_e, "c")
+    outer_c = outer(contract_weight, contract_momentum, full_c, after(back_c, full_e))
     grad_vectors = swapped(vec_three, after(vec_cross, outer_c[1]))
     inner_new, first_new, second_new = inner_step(
         vectors, grad_vectors, vectors_first[0], vectors_second[0], 0.2, 0.0
@@ -1314,16 +1316,15 @@
     vec_diff = (vectors - inner_new).astype(bf)
     vec_near = exchange(vec_diff, "c")
     input_came = cross(after(input_grad, b_two, vec_diff))
-    b_own = swapped(b_two, after(cross_b, vec_diff))
+    pa = swapped(jnp.concatenate([proj_two, a_two], axis=1), after(cross_pa, outer_c[1]))
+    b_own = swapped(b_two, after(cross_b, vec_diff, pa))
     grad_qkv = jnp.concatenate([pa[:, D:], b_own], axis=1)
     grad_attention = jnp.concatenate([unweave(grad_qkv), pa[None, :, :D]], axis=0)
     attention_new = inner(attention_weight, grad_attention, attention_first, attention_second, 0.03, 0.1)
     sent_a, came_a = rep_send(attention_new[2])
     vec_half = add_low(vec_diff, after(vec_near, sent_a))
     vec_far = exchange(vec_half, "x")
-    full_e = add_low(half_e, after(rest_e, sent_a))
-    back_e = exchange(full_e, "c")
-    half_a = rep_join(attention_new[2], came_a, full_e)
+    half_a = rep_join(attention_new[2], came_a, vec_half)
     rest_a = exchange(half_a, "x")
     outer_e = outer(expand_weight, expand_momentum, full_e, after(back_e, half_a))
     full_a = add_low(half_a, after(rest_a, outer_e[1]))

time: 644 us -> 636 us (0.988)
  starting transfers between devices: 40.3 us -> 65 us
  Pallas kernels: 431 us -> 411 us
  waiting for transfers between devices: 51.3 us -> 39.6 us
    ppermute x41, starting transfers between devices: 40.3 us -> 64.9 us  [exchange(): return lax.ppermute(value, ('rep', 'fsdp'), xor_pairs(bits))]
    ppermute x41, waiting for transfers between devices: 51.2 us -> 39.5 us  [exchange(): return lax.ppermute(value, ('rep', 'fsdp'), xor_pairs(bits))]
    pallas_call x2, Pallas kernels: 59.6 us -> 48.1 us  [attn_bwd(): pl.pallas_call(bwd_kernel, out_shape=(jax.ShapeDtypeStruct((T, width // 2...]
    pallas_call x1, Pallas kernels: 46.9 us -> 37.9 us  [attn_fwd(): pl.pallas_call(fwd_kernel, out_shape=(jax.ShapeDtypeStruct((T, width // 3...]
  transfers between devices with their start and end apart: 43 -> 43, of which waited for: 9 -> 7; matrix products, arithmetic and copies ran while one was open for 14% -> 14% of each run, Pallas kernels for 63% -> 61%
where the time goes in v5:
time: 636 us; the launch traced here: 628 us
  Pallas kernels  411 us (65%)
  starting transfers between devices  65 us (10%)
  local copies, waits for them, and re-layouts  51.6 us (8%)
  other arithmetic  45.8 us (7%)
  waiting for transfers between devices  39.6 us (6%)
  between operations  15.1 us (2%)
    pallas_call x1, Pallas kernels, gather_all(): pl.pallas_call(gather_kernel, out_shape=(shape((8 * qkv.shape[0], qkv.sha...  91.8 us
    pallas_call x10, Pallas kernels, weight_call(): pl.pallas_call(weight_kernel, out_shape=SHAPE((rows // 2, width), BF), gr...  71.8 us
    ppermute x41, starting transfers between devices, exchange(): return lax.ppermute(value, ('rep', 'fsdp'), xor_pairs(bits))  64.9 us
    pallas_call x2, Pallas kernels, attn_bwd(): pl.pallas_call(bwd_kernel, out_shape=(jax.ShapeDtypeStruct((T, width // 2...  48.1 us
    ppermute x41, waiting for transfers between devices, exchange(): return lax.ppermute(value, ('rep', 'fsdp'), xor_pairs(bits))  39.5 us
    pallas_call x1, Pallas kernels, attn_fwd(): pl.pallas_call(fwd_kernel, out_shape=(jax.ShapeDtypeStruct((T, width // 3...  37.9 us
    pallas_call x1, Pallas kernels, up_call(): pl.pallas_call(up_kernel, out_shape=(SHAPE((t, FF), BF), SHAPE((t, FF), B...  34.3 us
    pallas_call x1, Pallas kernels, hidden_call(): pl.pallas_call(hidden_kernel, out_shape=(SHAPE((t, D), F32), SHAPE((t, D)...  22.1 us
  transfers between devices with their start and end apart: 43, of which 7 were waited for; matrix products, arithmetic and copies ran while one was open for 14% of the time, Pallas kernels for 61%

profile of v5, /device:TPU:1, one launch (start us, length us, event | category | flops | bytes accessed | tf_op | source)
XLA Modules:
  0.0 628.0 jit_solution(5220520300931195653)
XLA Ops:
  14.2 91.8 %gather_weights.1 = (bf16[1024,3072]{1,0:T(8,128)(2,1)}, bf16[1024,1024]{1,0:T(8,128)(2,1)}, bf16[8,12,128]{2,1,0:T(8,128)(2,1)}, bf16[1024,1024]{1,0:T(8,128)(2,1)}, s32[1,1024]{1,0:T(1,128)}) custom-call(bf16[128,3072]{1,0:T(8,128)(2,1)} %copy.83.qkv_in, bf16[128,1024]{1,0:T(8,128)(2,1)} %slice_bitcast_fusion.1.wo_in, ...), custom_call_target="tpu_custom_call" | custom-call | tf_op jit(solution)/shard_map/gather_weights/pallas_call | solution.py:679
  115.7 10.8 %qkv.1.qkv_ref = bf16[1024,3072]{1,0:T(8,128)(2,1)} custom-call(bf16[1024,1024]{1,0:T(8,128)(2,1)} %get-tuple-element.109.x_ref.first_ref.second_ref, bf16[1024,3072]{1,0:T(8,128)(2,1)} %get-tuple-element.110.w_ref, f32[1,3072]{1,0:T(1,128)} %reshape.202.bias_ref, f32[1,3072]{1,0:T(1,128)} %constant.207.clone.1.scale_ref), custom_call_target="tpu_custom_call" | custom-call | flops 6442450 | bytes 14680 | tf_op jit(solution)/shard_map/qkv/pallas_call | solution.py:725
  127.3 37.9 %attn_fwd.1 = (bf16[1024,1024]{1,0:T(8,128)(2,1)}, f32[8,2,1024]{2,1,0:T(2,128)}) custom-call(s32[4]{0:T(128)} %get-tuple-element.202.start_ref, s32[4]{0:T(128)} %get-tuple-element.203.count_ref, bf16[1024,3072]{1,0:T(8,128)(2,1)} %qkv.1.qkv_ref, s32[1,1024]{1,0:T(1,128)} %get-tuple-element.108.segr_ref, s32[1024,1]{1,0:T(8,128)} %copy.84.segc_ref), custom_call_target="tpu_custom_call" | custom-call | flops 64424508 | bytes 9437 | tf_op jit(solution)/shard_map/attn_fwd/pallas_call | solution.py:413
  165.2 8.9 %collective-permute-start.1 = (bf16[1024,1024]{1,0:T(8,128)(2,1)S(1)}, bf16[1024,1024]{1,0:T(8,128)(2,1)}, u32[]{:S(2)}, u32[]{:S(2)}) collective-permute-start(bf16[1024,1024]{1,0:T(8,128)(2,1)S(1)} %copy-done.3), channel_id=1, source_target_pairs={{0,8},{1,9},{2,10},{3,11},{4,12},{5,13},{6,14},{7,15},{8,0},{9,1},... | collective-permute-start | bytes 6291464 | tf_op jit(solution)/shard_map/ppermute | solution.py:1094
  175.5 8.1 %mix_norm.1 = (f32[1024,1024]{1,0:T(8,128)}, f32[1024,1]{1,0:T(8,128)}, bf16[1024,1024]{1,0:T(8,128)(2,1)}) custom-call(bf16[1024,1024]{1,0:T(8,128)(2,1)} %get-tuple-element.112.c_ref.first_ref.second_ref, bf16[1024,1024]{1,0:T(8,128)(2,1)} %get-tuple-element.113.w_ref.refs_11_, bf16[1024,1024]{1,0:T(8,128)(2,1)} %get-tuple-element.109.x_ref.first_ref.second_ref, ...), custom_call_target="tpu_custom_call" | custom-call | flops 2147483 | bytes 14680 | tf_op jit(solution)/shard_map/mix_norm/pallas_call | solution.py:758
  187.4 34.3 %up_gelu.1 = (bf16[1024,4096]{1,0:T(8,128)(2,1)}, bf16[1024,4096]{1,0:T(8,128)(2,1)}) custom-call(s32[4]{0:T(128)} %pad_add_fusion.place_ref, bf16[1024,1024]{1,0:T(8,128)(2,1)} %get-tuple-element.117.h_ref.first_ref.second_ref, bf16[1024,1024]{1,0:T(8,128)(2,1)} %all-gather.3.cloned.1.call-done.refs_0_.refs_4_, ...), custom_call_target="tpu_custom_call" | custom-call | flops 8589934 | bytes 27262 | tf_op jit(solution)/shard_map/up_gelu/pallas_call | solution.py:795
  222.2 7.1 %collective-permute-done.4.came_ref = bf16[4096,512]{1,0:T(8,128)(2,1)} collective-permute-done((bf16[4096,512]{1,0:T(8,128)(2,1)}, bf16[4096,512]{1,0:T(8,128)(2,1)}, u32[]{:S(2)}, u32[]{:S(2)}) %collective-permute-start.4) | collective-permute-done | bytes 4194336 | tf_op jit(solution)/shard_map/ppermute | solution.py:1094
  229.4 19.9 %down_norm.1 = (bf16[1024,1024]{1,0:T(8,128)(2,1)}, f32[1024,1024]{1,0:T(8,128)}, bf16[1024,1024]{1,0:T(8,128)(2,1)}, f32[8,1024]{1,0:T(8,128)}) custom-call(s32[1]{0:T(128)} %bitcast.core_ref.half_ref, bf16[1024,4096]{1,0:T(8,128)(2,1)} %get-tuple-element.121.g_ref.first_ref.second_ref, bf16[4096,512]{1,0:T(8,128)(2,1)} %all-gather.5.cloned.1.call-done.own_ref, ...), custom_call_target="tpu_custom_call" | custom-call | flops 8589934 | bytes 31457 | tf_op jit(solution)/shard_map/down_norm/pallas_call | solution.py:848
  249.3 8.5 %weight_grad.10 = bf16[2048,1024]{1,0:T(8,128)(2,1)} custom-call(s32[1]{0:T(128)} %bitcast.16.half_ref, bf16[1024,4096]{1,0:T(8,128)(2,1)} %get-tuple-element.121.g_ref.first_ref.second_ref, bf16[1024,4096]{1,0:T(8,128)(2,1)} %get-tuple-element.121.g_ref.first_ref.second_ref, bf16[1024,1024]{1,0:T(8,128)(2,1)} %get-tuple-element.130.right_ref.left_ref), custom_call_target="tpu_custom_call" | custom-call | flops 4294967 | bytes 14680 | tf_op jit(solution)/shard_map/weight_grad/pallas_call | solution.py:1002
  258.1 16.3 %down_back.1 = (bf16[1024,4096]{1,0:T(8,128)(2,1)}, f32[1,4096]{1,0:T(1,128)}) custom-call(s32[1]{0:T(128)} %bitcast.core_ref.half_ref, bf16[1024,1024]{1,0:T(8,128)(2,1)} %get-tuple-element.130.right_ref.left_ref, bf16[1024,1024]{1,0:T(8,128)(2,1)} %get-tuple-element.130.right_ref.left_ref, bf16[4096,512]{1,0:T(8,128)(2,1)} %all-gather.5.cloned.1.call-done.own_ref, ...), custom_call_target="tpu_custom_call" | custom-call | flops 8589934 | bytes 27262 | tf_op jit(solution)/shard_map/down_back/pallas_call | solution.py:881
  274.4 10.9 %weight_grad.11 = bf16[512,4096]{1,0:T(8,128)(2,1)} custom-call(s32[1]{0:T(128)} %bitcast.16.half_ref, bf16[1024,1024]{1,0:T(8,128)(2,1)} %get-tuple-element.117.h_ref.first_ref.second_ref, bf16[1024,1024]{1,0:T(8,128)(2,1)} %get-tuple-element.117.h_ref.first_ref.second_ref, bf16[1024,4096]{1,0:T(8,128)(2,1)} %get-tuple-element.132.right_ref.refs_0_.refs_1_.refs_2_.refs_3_), custom_call_target="tpu_custom_call" | custom-call | flops 4294967 | bytes 17825 | tf_op jit(solution)/shard_map/weight_grad/pallas_call | solution.py:1002
  287.8 9.5 %weight_grad.12 = bf16[2048,1024]{1,0:T(8,128)(2,1)} custom-call(s32[1]{0:T(128)} %bitcast.core_ref.half_ref, bf16[1024,4096]{1,0:T(8,128)(2,1)} %get-tuple-element.121.g_ref.first_ref.second_ref, bf16[1024,4096]{1,0:T(8,128)(2,1)} %get-tuple-element.121.g_ref.first_ref.second_ref, bf16[1024,1024]{1,0:T(8,128)(2,1)} %get-tuple-element.130.right_ref.left_ref, ...), custom_call_target="tpu_custom_call" | custom-call | flops 4294967 | bytes 14680 | tf_op jit(solution)/shard_map/weight_grad/pallas_call | solution.py:1002
  303.2 11.6 %weight_grad.13 = bf16[512,4096]{1,0:T(8,128)(2,1)} custom-call(s32[1]{0:T(128)} %bitcast.core_ref.half_ref, bf16[1024,1024]{1,0:T(8,128)(2,1)} %get-tuple-element.117.h_ref.first_ref.second_ref, bf16[1024,1024]{1,0:T(8,128)(2,1)} %get-tuple-element.117.h_ref.first_ref.second_ref, ...), custom_call_target="tpu_custom_call" | custom-call | flops 4294967 | bytes 17825 | tf_op jit(solution)/shard_map/weight_grad/pallas_call | solution.py:1002
  317.9 22.1 %up_back_norm.1 = (f32[1024,1024]{1,0:T(8,128)}, bf16[1024,1024]{1,0:T(8,128)(2,1)}, bf16[1024,1024]{1,0:T(8,128)(2,1)}, f32[8,1024]{1,0:T(8,128)}) custom-call(s32[4]{0:T(128)} %pad_add_fusion.place_ref, bf16[1024,4096]{1,0:T(8,128)(2,1)} %get-tuple-element.132.right_ref.refs_0_.refs_1_.refs_2_.refs_3_, ...), custom_call_target="tpu_custom_call" | custom-call | flops 10737418 | bytes 33554 | tf_op jit(solution)/shard_map/up_back_norm/pallas_call | solution.py:927
  347.3 24.0 %attn_bwd.2 = (bf16[1024,1536]{1,0:T(8,128)(2,1)}, f32[4,1,384]{2,1,0:T(1,128)}) custom-call(s32[4]{0:T(128)} %get-tuple-element.202.start_ref, s32[4]{0:T(128)} %get-tuple-element.203.count_ref, bf16[1024,3072]{1,0:T(8,128)(2,1)} %qkv.1.qkv_ref, bf16[1024,1024]{1,0:T(8,128)(2,1)} %get-tuple-element.145.do_ref, f32[8,2,1024]{2,1,0:T(2,128)} %get-tuple-element.139.lse_ref, ...), custom_call_target="tpu_custom_call" | custom-call | flops 64424508 | bytes 18874 | tf_op jit(solution)/shard_map/attn_bwd/pallas_call | solution.py:437
  418.6 24.1 %attn_bwd.3 = (bf16[1024,1536]{1,0:T(8,128)(2,1)}, f32[4,1,384]{2,1,0:T(1,128)}) custom-call(s32[4]{0:T(128)} %get-tuple-element.202.start_ref, s32[4]{0:T(128)} %get-tuple-element.203.count_ref, bf16[1024,3072]{1,0:T(8,128)(2,1)} %qkv.1.qkv_ref, bf16[1024,1024]{1,0:T(8,128)(2,1)} %get-tuple-element.145.do_ref, f32[8,2,1024]{2,1,0:T(2,128)} %get-tuple-element.139.lse_ref, ...), custom_call_target="tpu_custom_call" | custom-call | flops 64424508 | bytes 18874 | tf_op jit(solution)/shard_map/attn_bwd/pallas_call | solution.py:437
  448.3 6.6 %collective-permute-start.16 = (bf16[512,1536]{1,0:T(8,128)(2,1)}, bf16[512,1536]{1,0:T(8,128)(2,1)}, u32[]{:S(2)}, u32[]{:S(2)}) collective-permute-start(bf16[512,1536]{1,0:T(8,128)(2,1)} %weight_grad.18), channel_id=1, source_target_pairs={{0,8},{1,9},{2,10},{3,11},{4,12},{5,13},{6,14},{7,15},{8,0},{9,1},... | collective-permute-start | bytes 4718600 | tf_op jit(solution)/shard_map/ppermute | solution.py:1094
  457.8 21.2 %collective-permute-done.14 = bf16[128,4096]{1,0:T(8,128)(2,1)} collective-permute-done((bf16[128,4096]{1,0:T(8,128)(2,1)}, bf16[128,4096]{1,0:T(8,128)(2,1)}, u32[]{:S(2)}, u32[]{:S(2)}) %collective-permute-start.14) | collective-permute-done | bytes 1048608 | tf_op jit(solution)/shard_map/ppermute | solution.py:1094
  523.1 6.0 inner_step.4
  537.8 12.4 %input_back.1 = bf16[1024,1024]{1,0:T(8,128)(2,1)} custom-call(bf16[1024,1536]{1,0:T(8,128)(2,1)} %get-tuple-element.159.right_ref.a_ref, bf16[1024,1536]{1,0:T(8,128)(2,1)} %get-tuple-element.151.right_ref.b_ref, bf16[1024,3072]{1,0:T(8,128)(2,1)} %get-tuple-element.110.w_ref, f32[1024,1024]{1,0:T(8,128)} %get-tuple-element.160.r_ref), custom_call_target="tpu_custom_call" | custom-call | flops 6442450 | bytes 18874 | tf_op jit(solution)/shard_map/input_back/pallas_call | solution.py:953
  568.6 6.4 %outer_step.3 = (f32[3,512,1024]{2,1,0:T(8,128)}, bf16[512,1024]{1,0:T(8,128)(2,1)}) custom-call(s32[1]{0:T(128)} %bitcast.core_ref.half_ref, f32[512,1024]{1,0:T(8,128)} %w_ref.6, f32[512,1024]{1,0:T(8,128)} %u_ref.2, bf16[256,1024]{1,0:T(8,128)(2,1)} %copy-done.13, bf16[256,1024]{1,0:T(8,128)(2,1)} %collective-permute-done.30.came_ref), custom_call_target="tpu_custom_call" | custom-call | flops 5242 | bytes 13631 | tf_op jit(solution)/shard_map/outer_step/pallas_call | solution.py:1057
  580.6 6.2 inner_step.5
  592.4 6.4 %outer_step.4 = (f32[3,128,4096]{2,1,0:T(8,128)}, bf16[128,4096]{1,0:T(8,128)(2,1)}) custom-call(s32[1]{0:T(128)} %bitcast.core_ref.half_ref, f32[128,4096]{1,0:T(8,128)} %w_ref.7, f32[128,4096]{1,0:T(8,128)} %u_ref.3, bf16[64,4096]{1,0:T(8,128)(2,1)} %add_convert_fusion.1.own_ref, bf16[64,4096]{1,0:T(8,128)(2,1)} %collective-permute-done.38.came_ref), custom_call_target="tpu_custom_call" | custom-call | flops 5242 | bytes 13631 | tf_op jit(solution)/shard_map/outer_step/pallas_call | solution.py:1057
  611.5 6.3 %outer_step.5 = (f32[3,512,1024]{2,1,0:T(8,128)}, bf16[512,1024]{1,0:T(8,128)(2,1)}) custom-call(s32[1]{0:T(128)} %bitcast.core_ref.half_ref, f32[512,1024]{1,0:T(8,128)} %bitcast.151, f32[512,1024]{1,0:T(8,128)} %bitcast.171, bf16[256,1024]{1,0:T(8,128)(2,1)} %copy-done.12, bf16[256,1024]{1,0:T(8,128)(2,1)} %copy-done.17), custom_call_target="tpu_custom_call" | custom-call | flops 5242 | bytes 13631 | tf_op jit(solution)/shard_map/outer_step/pallas_call | solution.py:1057
  (247 shorter events, 195.4 us)
Async XLA Ops:
  7.2 101.0 %all-gather.3.cloned.1.call-start = ((), (), s32[]{:S(2)}) async-start(), calls=%async_computation | async-start | bytes 2359296 | tf_op jit(solution)/shard_map/all_gather | solution.py:1169
  9.1 212.7 %all-gather.5.cloned.1.call-start = ((), (), s32[]{:S(2)}) async-start(), calls=%async_computation.1 | async-start | bytes 4718592 | tf_op jit(solution)/shard_map/all_gather | solution.py:1183
  108.2 65.9 %collective-permute-start.2 = (bf16[1024,1024]{1,0:T(8,128)(2,1)}, bf16[1024,1024]{1,0:T(8,128)(2,1)}, u32[]{:S(2)}, u32[]{:S(2)}) collective-permute-start(bf16[1024,1024]{1,0:T(8,128)(2,1)} %all-gather.3.cloned.1.call-done.refs_0_.refs_4_), channel_id=1, source_target_pairs={{0,16},{1,17},{2,18},{3,19},{4,20},{5,21},{6,22},{7,23},{8,24},{9,... | collective-permute-start | bytes 6291464 | tf_op jit(solution)/shard_map/ppermute | solution.py:1094
  108.5 75.8 %collective-permute-start = (bf16[1024,1024]{1,0:T(8,128)(2,1)}, bf16[1024,1024]{1,0:T(8,128)(2,1)}, u32[]{:S(2)}, u32[]{:S(2)}) collective-permute-start(bf16[1024,1024]{1,0:T(8,128)(2,1)} %param.20), channel_id=1, source_target_pairs={{2,8},{3,9},{6,12},{7,13},{8,2},{9,3},{12,6},{13,7},{18,24},{19,25... | collective-permute-start | bytes 6291464 | tf_op jit(solution)/shard_map/ppermute | solution.py:1094
  165.2 22.2 %collective-permute-start.1 = (bf16[1024,1024]{1,0:T(8,128)(2,1)S(1)}, bf16[1024,1024]{1,0:T(8,128)(2,1)}, u32[]{:S(2)}, u32[]{:S(2)}) collective-permute-start(bf16[1024,1024]{1,0:T(8,128)(2,1)S(1)} %copy-done.3), channel_id=1, source_target_pairs={{0,8},{1,9},{2,10},{3,11},{4,12},{5,13},{6,14},{7,15},{8,0},{9,1},... | collective-permute-start | bytes 6291464 | tf_op jit(solution)/shard_map/ppermute | solution.py:1094
  257.7 30.1 %collective-permute-start.6 = (bf16[2048,1024]{1,0:T(8,128)(2,1)}, bf16[2048,1024]{1,0:T(8,128)(2,1)}, u32[]{:S(2)}, u32[]{:S(2)}) collective-permute-start(bf16[2048,1024]{1,0:T(8,128)(2,1)} %weight_grad.10), channel_id=1, source_target_pairs={{0,8},{1,9},{2,10},{3,11},{4,12},{5,13},{6,14},{7,15},{8,0},{9,1},... | collective-permute-start | bytes 12582920 | tf_op jit(solution)/shard_map/ppermute | solution.py:1094
  285.5 58.7 %collective-permute-start.5 = (bf16[1024,1024]{1,0:T(8,128)(2,1)S(1)}, bf16[1024,1024]{1,0:T(8,128)(2,1)}, u32[]{:S(2)}, u32[]{:S(2)}) collective-permute-start(bf16[1024,1024]{1,0:T(8,128)(2,1)S(1)} %copy-done.7), channel_id=1, source_target_pairs={{2,8},{3,9},{6,12},{7,13},{8,2},{9,3},{12,6},{13,7},{18,24},{19,25... | collective-permute-start | bytes 6291464 | tf_op jit(solution)/shard_map/ppermute | solution.py:1094
  300.3 80.0 %collective-permute-start.9 = (bf16[2,512,1024]{2,1,0:T(8,128)(2,1)}, bf16[2,512,1024]{2,1,0:T(8,128)(2,1)}, u32[]{:S(2)}, u32[]{:S(2)}) collective-permute-start(bf16[2,512,1024]{2,1,0:T(8,128)(2,1)} %dynamic-slice_bitcast_fusion.1), channel_id=1, source_target_pairs={{0,1},{1,0},{2,3},{3,2},{4,5},{5,4},{6,7},{7,6},{8,9},{9,8},{10,11... | collective-permute-start | bytes 6291464 | tf_op jit(solution)/shard_map/ppermute | solution.py:1094
  317.9 87.6 %collective-permute-start.8 = (bf16[2,128,4096]{2,1,0:T(8,128)(2,1)}, bf16[2,128,4096]{2,1,0:T(8,128)(2,1)}, u32[]{:S(2)}, u32[]{:S(2)}) collective-permute-start(bf16[2,128,4096]{2,1,0:T(8,128)(2,1)} %dynamic-slice_bitcast_fusion), channel_id=1, source_target_pairs={{0,1},{1,0},{2,3},{3,2},{4,5},{5,4},{6,7},{7,6},{8,9},{9,8},{10,11... | collective-permute-start | bytes 6291464 | tf_op jit(solution)/shard_map/ppermute | solution.py:1094
  384.6 71.2 %collective-permute-start.15 = (bf16[512,1024]{1,0:T(8,128)(2,1)}, bf16[512,1024]{1,0:T(8,128)(2,1)}, u32[]{:S(2)}, u32[]{:S(2)}) collective-permute-start(bf16[512,1024]{1,0:T(8,128)(2,1)} %dynamic-slice_bitcast_fusion.3), channel_id=1, source_target_pairs={{0,4},{1,5},{2,6},{3,7},{4,0},{5,1},{6,2},{7,3},{8,12},{9,13},{10,... | collective-permute-start | bytes 3145736 | tf_op jit(solution)/shard_map/ppermute | solution.py:1094
  410.9 68.1 %collective-permute-start.14 = (bf16[128,4096]{1,0:T(8,128)(2,1)}, bf16[128,4096]{1,0:T(8,128)(2,1)}, u32[]{:S(2)}, u32[]{:S(2)}) collective-permute-start(bf16[128,4096]{1,0:T(8,128)(2,1)} %dynamic-slice_bitcast_fusion.2), channel_id=1, source_target_pairs={{0,4},{1,5},{2,6},{3,7},{4,0},{5,1},{6,2},{7,3},{8,12},{9,13},{10,... | collective-permute-start | bytes 3145736 | tf_op jit(solution)/shard_map/ppermute | solution.py:1094
  414.2 69.0 %collective-permute-start.13 = (bf16[2,128,1024]{1,2,0:T(8,128)(2,1)}, bf16[2,128,1024]{1,2,0:T(8,128)(2,1)}, u32[]{:S(2)}, u32[]{:S(2)}) collective-permute-start(bf16[2,128,1024]{1,2,0:T(8,128)(2,1)} %bitcast.183), channel_id=1, source_target_pairs={{0,1},{1,0},{2,3},{3,2},{4,5},{5,4},{6,7},{7,6},{8,9},{9,8},{10,11... | collective-permute-start | bytes 1572872 | tf_op jit(solution)/shard_map/ppermute | solution.py:1094
  416.4 71.7 %collective-permute-start.12 = (bf16[2,128,1536]{1,2,0:T(8,128)(2,1)}, bf16[2,128,1536]{1,2,0:T(8,128)(2,1)}, u32[]{:S(2)}, u32[]{:S(2)}) collective-permute-start(bf16[2,128,1536]{1,2,0:T(8,128)(2,1)} %bitcast.181), channel_id=1, source_target_pairs={{0,1},{1,0},{2,3},{3,2},{4,5},{5,4},{6,7},{7,6},{8,9},{9,8},{10,11... | collective-permute-start | bytes 2359304 | tf_op jit(solution)/shard_map/ppermute | solution.py:1094
  448.3 45.1 %collective-permute-start.16 = (bf16[512,1536]{1,0:T(8,128)(2,1)}, bf16[512,1536]{1,0:T(8,128)(2,1)}, u32[]{:S(2)}, u32[]{:S(2)}) collective-permute-start(bf16[512,1536]{1,0:T(8,128)(2,1)} %weight_grad.18), channel_id=1, source_target_pairs={{0,8},{1,9},{2,10},{3,11},{4,12},{5,13},{6,14},{7,15},{8,0},{9,1},... | collective-permute-start | bytes 4718600 | tf_op jit(solution)/shard_map/ppermute | solution.py:1094
  455.8 74.5 %collective-permute-start.24 = (f32[12,512]{1,0:T(8,128)}, f32[12,512]{1,0:T(8,128)}, u32[]{:S(2)}, u32[]{:S(2)}) collective-permute-start(f32[12,512]{1,0:T(8,128)} %constant_dynamic-slice_fusion.3), channel_id=1, source_target_pairs={{0,4},{1,5},{2,6},{3,7},{4,0},{5,1},{6,2},{7,3},{8,12},{9,13},{10,... | collective-permute-start | bytes 73736 | tf_op jit(solution)/shard_map/ppermute | solution.py:1094
  479.0 25.4 %collective-permute-start.19 = (bf16[512,1024]{1,0:T(8,128)(2,1)S(1)}, bf16[512,1024]{1,0:T(8,128)(2,1)}, u32[]{:S(2)}, u32[]{:S(2)}) collective-permute-start(bf16[512,1024]{1,0:T(8,128)(2,1)S(1)} %fusion.2), channel_id=1, source_target_pairs={{2,8},{3,9},{6,12},{7,13},{8,2},{9,3},{12,6},{13,7},{18,24},{19,25... | collective-permute-start | bytes 3145736 | tf_op jit(solution)/shard_map/ppermute | solution.py:1094
  483.2 37.5 %collective-permute-start.18 = (bf16[128,4096]{1,0:T(8,128)(2,1)S(1)}, bf16[128,4096]{1,0:T(8,128)(2,1)}, u32[]{:S(2)}, u32[]{:S(2)}) collective-permute-start(bf16[128,4096]{1,0:T(8,128)(2,1)S(1)} %fusion.3), channel_id=1, source_target_pairs={{2,8},{3,9},{6,12},{7,13},{8,2},{9,3},{12,6},{13,7},{18,24},{19,25... | collective-permute-start | bytes 3145736 | tf_op jit(solution)/shard_map/ppermute | solution.py:1094
  491.1 59.1 %collective-permute-start.28 = (bf16[128,1536]{0,1:T(8,128)(2,1)}, bf16[128,1536]{0,1:T(8,128)(2,1)S(1)}, u32[]{:S(2)}, u32[]{:S(2)}) collective-permute-start(bf16[128,1536]{0,1:T(8,128)(2,1)} %dynamic-slice_bitcast_fusion.8), channel_id=1, source_target_pairs={{0,4},{1,5},{2,6},{3,7},{4,0},{5,1},{6,2},{7,3},{8,12},{9,13},{10,... | collective-permute-start | bytes 1179656 | tf_op jit(solution)/shard_map/ppermute | solution.py:1094
  493.4 57.3 %collective-permute-start.27 = (bf16[128,1024]{0,1:T(8,128)(2,1)}, bf16[128,1024]{0,1:T(8,128)(2,1)}, u32[]{:S(2)}, u32[]{:S(2)}) collective-permute-start(bf16[128,1024]{0,1:T(8,128)(2,1)} %dynamic-slice_bitcast_fusion.9), channel_id=1, source_target_pairs={{0,4},{1,5},{2,6},{3,7},{4,0},{5,1},{6,2},{7,3},{8,12},{9,13},{10,... | collective-permute-start | bytes 786440 | tf_op jit(solution)/shard_map/ppermute | solution.py:1094
  504.4 27.4 %collective-permute-start.17 = (bf16[2,128,1536]{1,2,0:T(8,128)(2,1)}, bf16[2,128,1536]{1,2,0:T(8,128)(2,1)}, u32[]{:S(2)}, u32[]{:S(2)}) collective-permute-start(bf16[2,128,1536]{1,2,0:T(8,128)(2,1)} %bitcast.182), channel_id=1, source_target_pairs={{0,1},{1,0},{2,3},{3,2},{4,5},{5,4},{6,7},{7,6},{8,9},{9,8},{10,11... | collective-permute-start | bytes 2359304 | tf_op jit(solution)/shard_map/ppermute | solution.py:1094
  534.4 28.5 %collective-permute-start.22 = (bf16[128,1536]{0,1:T(8,128)(2,1)}, bf16[128,1536]{0,1:T(8,128)(2,1)}, u32[]{:S(2)}, u32[]{:S(2)}) collective-permute-start(bf16[128,1536]{0,1:T(8,128)(2,1)} %dynamic-slice_bitcast_fusion.7), channel_id=1, source_target_pairs={{0,4},{1,5},{2,6},{3,7},{4,0},{5,1},{6,2},{7,3},{8,12},{9,13},{10,... | collective-permute-start | bytes 1179656 | tf_op jit(solution)/shard_map/ppermute | solution.py:1094
  536.5 24.9 %collective-permute-start.23 = (bf16[256,1024]{1,0:T(8,128)(2,1)}, bf16[256,1024]{1,0:T(8,128)(2,1)}, u32[]{:S(2)}, u32[]{:S(2)}) collective-permute-start(bf16[256,1024]{1,0:T(8,128)(2,1)} %fusion.7), channel_id=1, source_target_pairs={{0,16},{1,17},{2,18},{3,19},{4,20},{5,21},{6,22},{7,23},{8,24},{9,... | collective-permute-start | bytes 1572872 | tf_op jit(solution)/shard_map/ppermute | solution.py:1094
  554.6 20.4 %collective-permute-start.33 = (bf16[128,2560]{0,1:T(8,128)(2,1)}, bf16[128,2560]{0,1:T(8,128)(2,1)}, u32[]{:S(2)}, u32[]{:S(2)}) collective-permute-start(bf16[128,2560]{0,1:T(8,128)(2,1)} %pad_maximum_fusion.2), channel_id=1, source_target_pairs={{2,8},{3,9},{6,12},{7,13},{8,2},{9,3},{12,6},{13,7},{18,24},{19,25... | collective-permute-start | bytes 1966088 | tf_op jit(solution)/shard_map/ppermute | solution.py:1094
  578.6 39.2 %collective-permute-start.32 = (bf16[1024,1024]{1,0:T(8,128)(2,1)S(1)}, bf16[1024,1024]{1,0:T(8,128)(2,1)}, u32[]{:S(2)}, u32[]{:S(2)}) collective-permute-start(bf16[1024,1024]{1,0:T(8,128)(2,1)S(1)} %copy-done), channel_id=1, source_target_pairs={{2,8},{3,9},{6,12},{7,13},{8,2},{9,3},{12,6},{13,7},{18,24},{19,25... | collective-permute-start | bytes 6291464 | tf_op jit(solution)/shard_map/ppermute | solution.py:1094
  (49 other events, 472.3 us)
Sparse Core Ops, SparseCore 0:
  10.7 63.0 all-gather.2
  108.3 77.8 all-gather.4

commit v6 on v5

--- a/solution.py
+++ b/solution.py
@@ -1226,9 +1226,7 @@
     came_b = exchange(send_b, "c")
     down_two = join(at, down_one, came_d, "z1", send_b)
     cross_d = cross(down_two)
-    up_two = join(at, up_one, came_u, "z1", down_two)
-    cross_u = cross(up_two)
-    proj_one = join(at, proj_total, came_p, "y", up_two)
+    proj_one = join(at, proj_total, came_p, "y", down_two)
     away_p, came_p = halve(at, proj_one, "z1")
     a_one = join(at, total_a, came_one, "y", away_p)
     away_a, came_a = halve(at, a_one, "z1")
@@ -1283,32 +1281,32 @@
     grad_contract = swapped(down_two, after(cross_d, away_b))
     contract_new = inner(contract_weight, grad_contract, contract_first, contract_second, 0.015, 0.1)
     sent_c, came_c = rep_send(contract_new[2])
-    vec_one = vector_join(vector_grad, vec_came, "z1", sent_c)
+    up_two = join(at, up_one, came_u, "z1", sent_c)
+    cross_u = cross(up_two)
+    vec_one = vector_join(vector_grad, vec_came, "z1", up_two)
     vec_came = vector_send(vec_one, "c")
-    grad_expand = swapped(up_two, after(cross_u, sent_c))
-    expand_new = inner(expand_weight, grad_expand, expand_first, expand_second, 0.03, 0.1)
-    sent_e, came_e = rep_send(expand_new[2])
-    b_one = join(at, total_b, came_b, "y", sent_e)
+    b_one = join(at, total_b, came_b, "y", up_two)
     away_b, came_b = halve(at, b_one, "z1")
     half_c = rep_join(contract_new[2], came_c, away_b)
     rest_c = exchange(half_c, "x")
-    half_e = rep_join(expand_new[2], came_e, half_c)
-    rest_e = exchange(half_e, "x")
-    vec_two = vector_join(vec_one, vec_came, "c", half_e)
+    vec_two = vector_join(vec_one, vec_came, "c", half_c)
     vec_came = vector_send(vec_two, "y")
-    input_grad = input_call(after(grad_a, away_b, half_e), grad_b, w_qkv, grad_resid)
-    proj_two = join(at, proj_one, came_p, "z1", input_grad)
-    a_two = join(at, a_one, came_a, "z1", input_grad)
+    input_grad = input_call(after(grad_a, away_b, half_c), grad_b, w_qkv, grad_resid)
+    grad_expand = swapped(up_two, after(cross_u, input_grad))
+    expand_new = inner(expand_weight, grad_expand, expand_first, expand_second, 0.03, 0.1)
+    sent_e, came_e = rep_send(expand_new[2])
+    proj_two = join(at, proj_one, came_p, "z1", sent_e)
+    a_two = join(at, a_one, came_a, "z1", sent_e)
     cross_pa = cross(jnp.concatenate([proj_two, a_two], axis=1))
     vec_three = vector_join(vec_two, vec_came, "y", proj_two, a_two)
     vec_cross = cross(vec_three)
     full_c = add_low(half_c, after(rest_c, vec_three))
     back_c = exchange(full_c, "c")
-    b_two = join(at, b_one, came_b, "z1", full_c)
+    half_e = rep_join(expand_new[2], came_e, full_c)
+    rest_e = exchange(half_e, "x")
+    b_two = join(at, b_one, came_b, "z1", half_e)
     cross_b = cross(b_two)
-    full_e = add_low(half_e, after(rest_e, b_two))
-    back_e = exchange(full_e, "c")
-    outer_c = outer(contract_weight, contract_momentum, full_c, after(back_c, full_e))
+    outer_c = outer(contract_weight, contract_momentum, full_c, after(back_c, b_two))
     grad_vectors = swapped(vec_three, after(vec_cross, outer_c[1]))
     inner_new, first_new, second_new = inner_step(
         vectors, grad_vectors, vectors_first[0], vectors_second[0], 0.2, 0.0
@@ -1324,7 +1322,9 @@
     sent_a, came_a = rep_send(attention_new[2])
     vec_half = add_low(vec_diff, after(vec_near, sent_a))
     vec_far = exchange(vec_half, "x")
-    half_a = rep_join(attention_new[2], came_a, vec_half)
+    full_e = add_low(half_e, after(rest_e, vec_half))
+    back_e = exchange(full_e, "c")
+    half_a = rep_join(attention_new[2], came_a, full_e)
     rest_a = exchange(half_a, "x")
     outer_e = outer(expand_weight, expand_momentum, full_e, after(back_e, half_a))
     full_a = add_low(half_a, after(rest_a, outer_e[1]))

time: 636 us -> 626 us (0.984)
  Pallas kernels: 411 us -> 426 us
  starting transfers between devices: 65 us -> 50.8 us
  waiting for transfers between devices: 39.6 us -> 29.9 us
    ppermute x41, starting transfers between devices: 64.9 us -> 50.7 us  [exchange(): return lax.ppermute(value, ('rep', 'fsdp'), xor_pairs(bits))]
    ppermute x41, waiting for transfers between devices: 39.5 us -> 29.8 us  [exchange(): return lax.ppermute(value, ('rep', 'fsdp'), xor_pairs(bits))]
    pallas_call x2, Pallas kernels: 48.1 us -> 56.7 us  [attn_bwd(): pl.pallas_call(bwd_kernel, out_shape=(jax.ShapeDtypeStruct((T, width // 2...]
    pallas_call x1, Pallas kernels: 37.9 us -> 44.6 us  [attn_fwd(): pl.pallas_call(fwd_kernel, out_shape=(jax.ShapeDtypeStruct((T, width // 3...]
  transfers between devices with their start and end apart: 43 -> 43, of which waited for: 7 -> 7; matrix products, arithmetic and copies ran while one was open for 14% -> 14% of each run, Pallas kernels for 61% -> 64%
where the time goes in v6:
time: 626 us; the launch traced here: 619 us
  Pallas kernels  426 us (68%)
  starting transfers between devices  50.8 us (8%)
  local copies, waits for them, and re-layouts  50.6 us (8%)
  other arithmetic  46.7 us (7%)
  waiting for transfers between devices  29.9 us (5%)
  between operations  15.1 us (2%)
    pallas_call x1, Pallas kernels, gather_all(): pl.pallas_call(gather_kernel, out_shape=(shape((8 * qkv.shape[0], qkv.sha...  91.8 us
    pallas_call x10, Pallas kernels, weight_call(): pl.pallas_call(weight_kernel, out_shape=SHAPE((rows // 2, width), BF), gr...  71.7 us
    pallas_call x2, Pallas kernels, attn_bwd(): pl.pallas_call(bwd_kernel, out_shape=(jax.ShapeDtypeStruct((T, width // 2...  56.7 us
    ppermute x41, starting transfers between devices, exchange(): return lax.ppermute(value, ('rep', 'fsdp'), xor_pairs(bits))  50.7 us
    pallas_call x1, Pallas kernels, attn_fwd(): pl.pallas_call(fwd_kernel, out_shape=(jax.ShapeDtypeStruct((T, width // 3...  44.6 us
    pallas_call x1, Pallas kernels, up_call(): pl.pallas_call(up_kernel, out_shape=(SHAPE((t, FF), BF), SHAPE((t, FF), B...  34.3 us
    ppermute x41, waiting for transfers between devices, exchange(): return lax.ppermute(value, ('rep', 'fsdp'), xor_pairs(bits))  29.8 us
    convert_element_type x17, other arithmetic, add_low(): (left.astype(jnp.float32) + right.astype(jnp.float32)).astype(jnp.bfloat16)  22.1 us
  transfers between devices with their start and end apart: 43, of which 7 were waited for; matrix products, arithmetic and copies ran while one was open for 14% of the time, Pallas kernels for 64%

profile of v6, /device:TPU:1, one launch (start us, length us, event | category | flops | bytes accessed | tf_op | source)
XLA Modules:
  0.0 618.9 jit_solution(3734145603223143139)
XLA Ops:
  14.2 91.8 %gather_weights.1 = (bf16[1024,3072]{1,0:T(8,128)(2,1)}, bf16[1024,1024]{1,0:T(8,128)(2,1)}, bf16[8,12,128]{2,1,0:T(8,128)(2,1)}, bf16[1024,1024]{1,0:T(8,128)(2,1)}, s32[1,1024]{1,0:T(1,128)}) custom-call(bf16[128,3072]{1,0:T(8,128)(2,1)} %copy.83.qkv_in, bf16[128,1024]{1,0:T(8,128)(2,1)} %slice_bitcast_fusion.1.wo_in, ...), custom_call_target="tpu_custom_call" | custom-call | tf_op jit(solution)/shard_map/gather_weights/pallas_call | solution.py:679
  115.7 10.8 %qkv.1.qkv_ref = bf16[1024,3072]{1,0:T(8,128)(2,1)} custom-call(bf16[1024,1024]{1,0:T(8,128)(2,1)} %get-tuple-element.109.x_ref.first_ref.second_ref, bf16[1024,3072]{1,0:T(8,128)(2,1)} %get-tuple-element.110.w_ref, f32[1,3072]{1,0:T(1,128)} %reshape.202.bias_ref, f32[1,3072]{1,0:T(1,128)} %constant.207.clone.1.scale_ref), custom_call_target="tpu_custom_call" | custom-call | flops 6442450 | bytes 14680 | tf_op jit(solution)/shard_map/qkv/pallas_call | solution.py:725
  127.2 44.6 %attn_fwd.1 = (bf16[1024,1024]{1,0:T(8,128)(2,1)}, f32[8,2,1024]{2,1,0:T(2,128)}) custom-call(s32[4]{0:T(128)} %get-tuple-element.202.start_ref, s32[4]{0:T(128)} %get-tuple-element.203.count_ref, bf16[1024,3072]{1,0:T(8,128)(2,1)} %qkv.1.qkv_ref, s32[1,1024]{1,0:T(1,128)} %get-tuple-element.108.segr_ref, s32[1024,1]{1,0:T(8,128)} %copy.84.segc_ref), custom_call_target="tpu_custom_call" | custom-call | flops 64424508 | bytes 9437 | tf_op jit(solution)/shard_map/attn_fwd/pallas_call | solution.py:413
  175.5 8.1 %mix_norm.1 = (f32[1024,1024]{1,0:T(8,128)}, f32[1024,1]{1,0:T(8,128)}, bf16[1024,1024]{1,0:T(8,128)(2,1)}) custom-call(bf16[1024,1024]{1,0:T(8,128)(2,1)} %get-tuple-element.112.c_ref.first_ref.second_ref, bf16[1024,1024]{1,0:T(8,128)(2,1)} %get-tuple-element.113.w_ref.refs_11_, bf16[1024,1024]{1,0:T(8,128)(2,1)} %get-tuple-element.109.x_ref.first_ref.second_ref, ...), custom_call_target="tpu_custom_call" | custom-call | flops 2147483 | bytes 14680 | tf_op jit(solution)/shard_map/mix_norm/pallas_call | solution.py:758
  187.4 34.3 %up_gelu.1 = (bf16[1024,4096]{1,0:T(8,128)(2,1)}, bf16[1024,4096]{1,0:T(8,128)(2,1)}) custom-call(s32[4]{0:T(128)} %pad_add_fusion.place_ref, bf16[1024,1024]{1,0:T(8,128)(2,1)} %get-tuple-element.117.h_ref.first_ref.second_ref, bf16[1024,1024]{1,0:T(8,128)(2,1)} %all-gather.3.cloned.1.call-done.refs_0_.refs_4_, ...), custom_call_target="tpu_custom_call" | custom-call | flops 8589934 | bytes 27262 | tf_op jit(solution)/shard_map/up_gelu/pallas_call | solution.py:795
  222.2 7.1 %collective-permute-done.4.came_ref = bf16[4096,512]{1,0:T(8,128)(2,1)} collective-permute-done((bf16[4096,512]{1,0:T(8,128)(2,1)}, bf16[4096,512]{1,0:T(8,128)(2,1)}, u32[]{:S(2)}, u32[]{:S(2)}) %collective-permute-start.4) | collective-permute-done | bytes 4194336 | tf_op jit(solution)/shard_map/ppermute | solution.py:1094
  229.4 19.9 %down_norm.1 = (bf16[1024,1024]{1,0:T(8,128)(2,1)}, f32[1024,1024]{1,0:T(8,128)}, bf16[1024,1024]{1,0:T(8,128)(2,1)}, f32[8,1024]{1,0:T(8,128)}) custom-call(s32[1]{0:T(128)} %bitcast.core_ref.half_ref, bf16[1024,4096]{1,0:T(8,128)(2,1)} %get-tuple-element.121.g_ref.first_ref.second_ref, bf16[4096,512]{1,0:T(8,128)(2,1)} %all-gather.5.cloned.1.call-done.own_ref, ...), custom_call_target="tpu_custom_call" | custom-call | flops 8589934 | bytes 31457 | tf_op jit(solution)/shard_map/down_norm/pallas_call | solution.py:848
  249.3 8.5 %weight_grad.10 = bf16[2048,1024]{1,0:T(8,128)(2,1)} custom-call(s32[1]{0:T(128)} %bitcast.16.half_ref, bf16[1024,4096]{1,0:T(8,128)(2,1)} %get-tuple-element.121.g_ref.first_ref.second_ref, bf16[1024,4096]{1,0:T(8,128)(2,1)} %get-tuple-element.121.g_ref.first_ref.second_ref, bf16[1024,1024]{1,0:T(8,128)(2,1)} %get-tuple-element.130.right_ref.left_ref), custom_call_target="tpu_custom_call" | custom-call | flops 4294967 | bytes 14680 | tf_op jit(solution)/shard_map/weight_grad/pallas_call | solution.py:1002
  258.1 16.3 %down_back.1 = (bf16[1024,4096]{1,0:T(8,128)(2,1)}, f32[1,4096]{1,0:T(1,128)}) custom-call(s32[1]{0:T(128)} %bitcast.core_ref.half_ref, bf16[1024,1024]{1,0:T(8,128)(2,1)} %get-tuple-element.130.right_ref.left_ref, bf16[1024,1024]{1,0:T(8,128)(2,1)} %get-tuple-element.130.right_ref.left_ref, bf16[4096,512]{1,0:T(8,128)(2,1)} %all-gather.5.cloned.1.call-done.own_ref, ...), custom_call_target="tpu_custom_call" | custom-call | flops 8589934 | bytes 27262 | tf_op jit(solution)/shard_map/down_back/pallas_call | solution.py:881
  274.4 10.8 %weight_grad.11 = bf16[512,4096]{1,0:T(8,128)(2,1)} custom-call(s32[1]{0:T(128)} %bitcast.16.half_ref, bf16[1024,1024]{1,0:T(8,128)(2,1)} %get-tuple-element.117.h_ref.first_ref.second_ref, bf16[1024,1024]{1,0:T(8,128)(2,1)} %get-tuple-element.117.h_ref.first_ref.second_ref, bf16[1024,4096]{1,0:T(8,128)(2,1)} %get-tuple-element.132.right_ref.refs_0_.refs_1_.refs_2_.refs_3_), custom_call_target="tpu_custom_call" | custom-call | flops 4294967 | bytes 17825 | tf_op jit(solution)/shard_map/weight_grad/pallas_call | solution.py:1002
  287.6 9.4 %weight_grad.12 = bf16[2048,1024]{1,0:T(8,128)(2,1)} custom-call(s32[1]{0:T(128)} %bitcast.core_ref.half_ref, bf16[1024,4096]{1,0:T(8,128)(2,1)} %get-tuple-element.121.g_ref.first_ref.second_ref, bf16[1024,4096]{1,0:T(8,128)(2,1)} %get-tuple-element.121.g_ref.first_ref.second_ref, bf16[1024,1024]{1,0:T(8,128)(2,1)} %get-tuple-element.130.right_ref.left_ref, ...), custom_call_target="tpu_custom_call" | custom-call | flops 4294967 | bytes 14680 | tf_op jit(solution)/shard_map/weight_grad/pallas_call | solution.py:1002
  303.0 11.5 %weight_grad.13 = bf16[512,4096]{1,0:T(8,128)(2,1)} custom-call(s32[1]{0:T(128)} %bitcast.core_ref.half_ref, bf16[1024,1024]{1,0:T(8,128)(2,1)} %get-tuple-element.117.h_ref.first_ref.second_ref, bf16[1024,1024]{1,0:T(8,128)(2,1)} %get-tuple-element.117.h_ref.first_ref.second_ref, ...), custom_call_target="tpu_custom_call" | custom-call | flops 4294967 | bytes 17825 | tf_op jit(solution)/shard_map/weight_grad/pallas_call | solution.py:1002
  317.6 22.1 %up_back_norm.1 = (f32[1024,1024]{1,0:T(8,128)}, bf16[1024,1024]{1,0:T(8,128)(2,1)}, bf16[1024,1024]{1,0:T(8,128)(2,1)}, f32[8,1024]{1,0:T(8,128)}) custom-call(s32[4]{0:T(128)} %pad_add_fusion.place_ref, bf16[1024,4096]{1,0:T(8,128)(2,1)} %get-tuple-element.132.right_ref.refs_0_.refs_1_.refs_2_.refs_3_, ...), custom_call_target="tpu_custom_call" | custom-call | flops 10737418 | bytes 33554 | tf_op jit(solution)/shard_map/up_back_norm/pallas_call | solution.py:927
  347.1 28.3 %attn_bwd.2 = (bf16[1024,1536]{1,0:T(8,128)(2,1)}, f32[4,1,384]{2,1,0:T(1,128)}) custom-call(s32[4]{0:T(128)} %get-tuple-element.202.start_ref, s32[4]{0:T(128)} %get-tuple-element.203.count_ref, bf16[1024,3072]{1,0:T(8,128)(2,1)} %qkv.1.qkv_ref, bf16[1024,1024]{1,0:T(8,128)(2,1)} %get-tuple-element.145.do_ref, f32[8,2,1024]{2,1,0:T(2,128)} %get-tuple-element.139.lse_ref, ...), custom_call_target="tpu_custom_call" | custom-call | flops 64424508 | bytes 18874 | tf_op jit(solution)/shard_map/attn_bwd/pallas_call | solution.py:437
  400.2 5.8 weight_grad.17
  413.8 28.4 %attn_bwd.3 = (bf16[1024,1536]{1,0:T(8,128)(2,1)}, f32[4,1,384]{2,1,0:T(1,128)}) custom-call(s32[4]{0:T(128)} %get-tuple-element.202.start_ref, s32[4]{0:T(128)} %get-tuple-element.203.count_ref, bf16[1024,3072]{1,0:T(8,128)(2,1)} %qkv.1.qkv_ref, bf16[1024,1024]{1,0:T(8,128)(2,1)} %get-tuple-element.145.do_ref, f32[8,2,1024]{2,1,0:T(2,128)} %get-tuple-element.139.lse_ref, ...), custom_call_target="tpu_custom_call" | custom-call | flops 64424508 | bytes 18874 | tf_op jit(solution)/shard_map/attn_bwd/pallas_call | solution.py:437
  453.7 6.5 %collective-permute-done.14 = bf16[512,1024]{1,0:T(8,128)(2,1)} collective-permute-done((bf16[512,1024]{1,0:T(8,128)(2,1)}, bf16[512,1024]{1,0:T(8,128)(2,1)}, u32[]{:S(2)}, u32[]{:S(2)}) %collective-permute-start.14) | collective-permute-done | bytes 1048608 | tf_op jit(solution)/shard_map/ppermute | solution.py:1094
  495.7 6.0 inner_step.3
  515.2 12.3 %input_back.1 = bf16[1024,1024]{1,0:T(8,128)(2,1)} custom-call(bf16[1024,1536]{1,0:T(8,128)(2,1)} %get-tuple-element.156.right_ref.a_ref, bf16[1024,1536]{1,0:T(8,128)(2,1)} %get-tuple-element.150.right_ref.b_ref, bf16[1024,3072]{1,0:T(8,128)(2,1)} %get-tuple-element.110.w_ref, f32[1024,1024]{1,0:T(8,128)} %get-tuple-element.157.r_ref), custom_call_target="tpu_custom_call" | custom-call | flops 6442450 | bytes 18874 | tf_op jit(solution)/shard_map/input_back/pallas_call | solution.py:953
  536.2 6.1 inner_step.4
  558.6 6.4 %outer_step.3 = (f32[3,512,1024]{2,1,0:T(8,128)}, bf16[512,1024]{1,0:T(8,128)(2,1)}) custom-call(s32[1]{0:T(128)} %bitcast.core_ref.half_ref, f32[512,1024]{1,0:T(8,128)} %w_ref.6, f32[512,1024]{1,0:T(8,128)} %u_ref.2, bf16[256,1024]{1,0:T(8,128)(2,1)} %copy-done.10, bf16[256,1024]{1,0:T(8,128)(2,1)} %collective-permute-done.30.came_ref), custom_call_target="tpu_custom_call" | custom-call | flops 5242 | bytes 13631 | tf_op jit(solution)/shard_map/outer_step/pallas_call | solution.py:1057
  572.6 6.0 inner_step.5
  583.5 6.3 %outer_step.4 = (f32[3,128,4096]{2,1,0:T(8,128)}, bf16[128,4096]{1,0:T(8,128)(2,1)}) custom-call(s32[1]{0:T(128)} %bitcast.core_ref.half_ref, f32[128,4096]{1,0:T(8,128)} %w_ref.7, f32[128,4096]{1,0:T(8,128)} %u_ref.3, bf16[64,4096]{1,0:T(8,128)(2,1)} %copy-done.11, bf16[64,4096]{1,0:T(8,128)(2,1)} %collective-permute-done.38.came_ref), custom_call_target="tpu_custom_call" | custom-call | flops 5242 | bytes 13631 | tf_op jit(solution)/shard_map/outer_step/pallas_call | solution.py:1057
  602.4 6.3 %outer_step.5 = (f32[3,512,1024]{2,1,0:T(8,128)}, bf16[512,1024]{1,0:T(8,128)(2,1)}) custom-call(s32[1]{0:T(128)} %bitcast.core_ref.half_ref, f32[512,1024]{1,0:T(8,128)} %bitcast.151, f32[512,1024]{1,0:T(8,128)} %bitcast.171, bf16[256,1024]{1,0:T(8,128)(2,1)} %copy-done.9, bf16[256,1024]{1,0:T(8,128)(2,1)} %copy-done.16), custom_call_target="tpu_custom_call" | custom-call | flops 5242 | bytes 13631 | tf_op jit(solution)/shard_map/outer_step/pallas_call | solution.py:1057
  (245 shorter events, 189.9 us)
Async XLA Ops:
  7.2 101.0 %all-gather.3.cloned.1.call-start = ((), (), s32[]{:S(2)}) async-start(), calls=%async_computation | async-start | bytes 2359296 | tf_op jit(solution)/shard_map/all_gather | solution.py:1169
  9.1 212.6 %all-gather.5.cloned.1.call-start = ((), (), s32[]{:S(2)}) async-start(), calls=%async_computation.1 | async-start | bytes 4718592 | tf_op jit(solution)/shard_map/all_gather | solution.py:1183
  108.2 65.9 %collective-permute-start.2 = (bf16[1024,1024]{1,0:T(8,128)(2,1)}, bf16[1024,1024]{1,0:T(8,128)(2,1)}, u32[]{:S(2)}, u32[]{:S(2)}) collective-permute-start(bf16[1024,1024]{1,0:T(8,128)(2,1)} %all-gather.3.cloned.1.call-done.refs_0_.refs_4_), channel_id=1, source_target_pairs={{0,16},{1,17},{2,18},{3,19},{4,20},{5,21},{6,22},{7,23},{8,24},{9,... | collective-permute-start | bytes 6291464 | tf_op jit(solution)/shard_map/ppermute | solution.py:1094
  108.5 75.7 %collective-permute-start = (bf16[1024,1024]{1,0:T(8,128)(2,1)}, bf16[1024,1024]{1,0:T(8,128)(2,1)}, u32[]{:S(2)}, u32[]{:S(2)}) collective-permute-start(bf16[1024,1024]{1,0:T(8,128)(2,1)} %param.20), channel_id=1, source_target_pairs={{2,8},{3,9},{6,12},{7,13},{8,2},{9,3},{12,6},{13,7},{18,24},{19,25... | collective-permute-start | bytes 6291464 | tf_op jit(solution)/shard_map/ppermute | solution.py:1094
  257.7 29.8 %collective-permute-start.6 = (bf16[2048,1024]{1,0:T(8,128)(2,1)}, bf16[2048,1024]{1,0:T(8,128)(2,1)}, u32[]{:S(2)}, u32[]{:S(2)}) collective-permute-start(bf16[2048,1024]{1,0:T(8,128)(2,1)} %weight_grad.10), channel_id=1, source_target_pairs={{0,8},{1,9},{2,10},{3,11},{4,12},{5,13},{6,14},{7,15},{8,0},{9,1},... | collective-permute-start | bytes 12582920 | tf_op jit(solution)/shard_map/ppermute | solution.py:1094
  285.3 58.6 %collective-permute-start.5 = (bf16[1024,1024]{1,0:T(8,128)(2,1)}, bf16[1024,1024]{1,0:T(8,128)(2,1)}, u32[]{:S(2)}, u32[]{:S(2)}) collective-permute-start(bf16[1024,1024]{1,0:T(8,128)(2,1)} %get-tuple-element.125), channel_id=1, source_target_pairs={{2,8},{3,9},{6,12},{7,13},{8,2},{9,3},{12,6},{13,7},{18,24},{19,25... | collective-permute-start | bytes 6291464 | tf_op jit(solution)/shard_map/ppermute | solution.py:1094
  300.1 84.6 %collective-permute-start.9 = (bf16[2,512,1024]{2,1,0:T(8,128)(2,1)}, bf16[2,512,1024]{2,1,0:T(8,128)(2,1)S(1)}, u32[]{:S(2)}, u32[]{:S(2)}) collective-permute-start(bf16[2,512,1024]{2,1,0:T(8,128)(2,1)} %dynamic-slice_bitcast_fusion.1), channel_id=1, source_target_pairs={{0,1},{1,0},{2,3},{3,2},{4,5},{5,4},{6,7},{7,6},{8,9},{9,8},{10,11... | collective-permute-start | bytes 6291464 | tf_op jit(solution)/shard_map/ppermute | solution.py:1094
  317.6 91.2 %collective-permute-start.8 = (bf16[2,128,4096]{2,1,0:T(8,128)(2,1)}, bf16[2,128,4096]{2,1,0:T(8,128)(2,1)}, u32[]{:S(2)}, u32[]{:S(2)}) collective-permute-start(bf16[2,128,4096]{2,1,0:T(8,128)(2,1)} %dynamic-slice_bitcast_fusion), channel_id=1, source_target_pairs={{0,1},{1,0},{2,3},{3,2},{4,5},{5,4},{6,7},{7,6},{8,9},{9,8},{10,11... | collective-permute-start | bytes 6291464 | tf_op jit(solution)/shard_map/ppermute | solution.py:1094
  381.0 19.2 %collective-permute-start.11 = (bf16[512,1536]{1,0:T(8,128)(2,1)}, bf16[512,1536]{1,0:T(8,128)(2,1)}, u32[]{:S(2)}, u32[]{:S(2)}) collective-permute-start(bf16[512,1536]{1,0:T(8,128)(2,1)} %weight_grad.15), channel_id=1, source_target_pairs={{0,8},{1,9},{2,10},{3,11},{4,12},{5,13},{6,14},{7,15},{8,0},{9,1},... | collective-permute-start | bytes 4718600 | tf_op jit(solution)/shard_map/ppermute | solution.py:1094
  389.7 70.5 %collective-permute-start.14 = (bf16[512,1024]{1,0:T(8,128)(2,1)}, bf16[512,1024]{1,0:T(8,128)(2,1)}, u32[]{:S(2)}, u32[]{:S(2)}) collective-permute-start(bf16[512,1024]{1,0:T(8,128)(2,1)} %dynamic-slice_bitcast_fusion.3), channel_id=1, source_target_pairs={{0,4},{1,5},{2,6},{3,7},{4,0},{5,1},{6,2},{7,3},{8,12},{9,13},{10,... | collective-permute-start | bytes 3145736 | tf_op jit(solution)/shard_map/ppermute | solution.py:1094
  398.9 63.2 %collective-permute-start.13 = (bf16[2,128,1024]{1,2,0:T(8,128)(2,1)}, bf16[2,128,1024]{1,2,0:T(8,128)(2,1)}, u32[]{:S(2)}, u32[]{:S(2)}) collective-permute-start(bf16[2,128,1024]{1,2,0:T(8,128)(2,1)} %bitcast.25), channel_id=1, source_target_pairs={{0,1},{1,0},{2,3},{3,2},{4,5},{5,4},{6,7},{7,6},{8,9},{9,8},{10,11... | collective-permute-start | bytes 1572872 | tf_op jit(solution)/shard_map/ppermute | solution.py:1094
  408.6 60.3 %collective-permute-start.12 = (bf16[2,128,1536]{1,2,0:T(8,128)(2,1)}, bf16[2,128,1536]{1,2,0:T(8,128)(2,1)}, u32[]{:S(2)}, u32[]{:S(2)}) collective-permute-start(bf16[2,128,1536]{1,2,0:T(8,128)(2,1)} %bitcast.27), channel_id=1, source_target_pairs={{0,1},{1,0},{2,3},{3,2},{4,5},{5,4},{6,7},{7,6},{8,9},{9,8},{10,11... | collective-permute-start | bytes 2359304 | tf_op jit(solution)/shard_map/ppermute | solution.py:1094
  412.9 89.9 %collective-permute-start.17 = (bf16[128,4096]{1,0:T(8,128)(2,1)}, bf16[128,4096]{1,0:T(8,128)(2,1)}, u32[]{:S(2)}, u32[]{:S(2)}) collective-permute-start(bf16[128,4096]{1,0:T(8,128)(2,1)} %dynamic-slice_bitcast_fusion.2), channel_id=1, source_target_pairs={{0,4},{1,5},{2,6},{3,7},{4,0},{5,1},{6,2},{7,3},{8,12},{9,13},{10,... | collective-permute-start | bytes 3145736 | tf_op jit(solution)/shard_map/ppermute | solution.py:1094
  447.7 24.2 %collective-permute-start.15 = (bf16[512,1536]{1,0:T(8,128)(2,1)}, bf16[512,1536]{1,0:T(8,128)(2,1)}, u32[]{:S(2)}, u32[]{:S(2)}) collective-permute-start(bf16[512,1536]{1,0:T(8,128)(2,1)} %weight_grad.18), channel_id=1, source_target_pairs={{0,8},{1,9},{2,10},{3,11},{4,12},{5,13},{6,14},{7,15},{8,0},{9,1},... | collective-permute-start | bytes 4718600 | tf_op jit(solution)/shard_map/ppermute | solution.py:1094
  460.2 44.3 %collective-permute-start.24 = (f32[12,512]{1,0:T(8,128)}, f32[12,512]{1,0:T(8,128)}, u32[]{:S(2)}, u32[]{:S(2)}) collective-permute-start(f32[12,512]{1,0:T(8,128)} %constant_dynamic-slice_fusion.3), channel_id=1, source_target_pairs={{0,4},{1,5},{2,6},{3,7},{4,0},{5,1},{6,2},{7,3},{8,12},{9,13},{10,... | collective-permute-start | bytes 73736 | tf_op jit(solution)/shard_map/ppermute | solution.py:1094
  462.1 29.9 %collective-permute-start.18 = (bf16[512,1024]{1,0:T(8,128)(2,1)S(1)}, bf16[512,1024]{1,0:T(8,128)(2,1)}, u32[]{:S(2)}, u32[]{:S(2)}) collective-permute-start(bf16[512,1024]{1,0:T(8,128)(2,1)S(1)} %fusion.3), channel_id=1, source_target_pairs={{2,8},{3,9},{6,12},{7,13},{8,2},{9,3},{12,6},{13,7},{18,24},{19,25... | collective-permute-start | bytes 3145736 | tf_op jit(solution)/shard_map/ppermute | solution.py:1094
  471.9 71.5 %collective-permute-start.28 = (bf16[128,1536]{0,1:T(8,128)(2,1)}, bf16[128,1536]{0,1:T(8,128)(2,1)S(1)}, u32[]{:S(2)}, u32[]{:S(2)}) collective-permute-start(bf16[128,1536]{0,1:T(8,128)(2,1)} %dynamic-slice_bitcast_fusion.8), channel_id=1, source_target_pairs={{0,4},{1,5},{2,6},{3,7},{4,0},{5,1},{6,2},{7,3},{8,12},{9,13},{10,... | collective-permute-start | bytes 1179656 | tf_op jit(solution)/shard_map/ppermute | solution.py:1094
  471.9 71.7 %collective-permute-start.27 = (bf16[128,1024]{0,1:T(8,128)(2,1)}, bf16[128,1024]{0,1:T(8,128)(2,1)}, u32[]{:S(2)}, u32[]{:S(2)}) collective-permute-start(bf16[128,1024]{0,1:T(8,128)(2,1)} %dynamic-slice_bitcast_fusion.9), channel_id=1, source_target_pairs={{0,4},{1,5},{2,6},{3,7},{4,0},{5,1},{6,2},{7,3},{8,12},{9,13},{10,... | collective-permute-start | bytes 786440 | tf_op jit(solution)/shard_map/ppermute | solution.py:1094
  504.4 28.1 %collective-permute-start.21 = (bf16[128,4096]{1,0:T(8,128)(2,1)S(1)}, bf16[128,4096]{1,0:T(8,128)(2,1)}, u32[]{:S(2)}, u32[]{:S(2)}) collective-permute-start(bf16[128,4096]{1,0:T(8,128)(2,1)S(1)} %fusion.2), channel_id=1, source_target_pairs={{2,8},{3,9},{6,12},{7,13},{8,2},{9,3},{12,6},{13,7},{18,24},{19,25... | collective-permute-start | bytes 3145736 | tf_op jit(solution)/shard_map/ppermute | solution.py:1094
  509.7 44.7 %collective-permute-start.20 = (bf16[128,1536]{0,1:T(8,128)(2,1)}, bf16[128,1536]{0,1:T(8,128)(2,1)}, u32[]{:S(2)}, u32[]{:S(2)}) collective-permute-start(bf16[128,1536]{0,1:T(8,128)(2,1)} %dynamic-slice_bitcast_fusion.7), channel_id=1, source_target_pairs={{0,4},{1,5},{2,6},{3,7},{4,0},{5,1},{6,2},{7,3},{8,12},{9,13},{10,... | collective-permute-start | bytes 1179656 | tf_op jit(solution)/shard_map/ppermute | solution.py:1094
  514.2 37.0 %collective-permute-start.23 = (bf16[256,1024]{1,0:T(8,128)(2,1)}, bf16[256,1024]{1,0:T(8,128)(2,1)}, u32[]{:S(2)}, u32[]{:S(2)}) collective-permute-start(bf16[256,1024]{1,0:T(8,128)(2,1)} %fusion.8), channel_id=1, source_target_pairs={{0,16},{1,17},{2,18},{3,19},{4,20},{5,21},{6,22},{7,23},{8,24},{9,... | collective-permute-start | bytes 1572872 | tf_op jit(solution)/shard_map/ppermute | solution.py:1094
  545.6 22.9 %collective-permute-start.32 = (bf16[128,2560]{0,1:T(8,128)(2,1)}, bf16[128,2560]{0,1:T(8,128)(2,1)}, u32[]{:S(2)}, u32[]{:S(2)}) collective-permute-start(bf16[128,2560]{0,1:T(8,128)(2,1)} %pad_maximum_fusion.2), channel_id=1, source_target_pairs={{2,8},{3,9},{6,12},{7,13},{8,2},{9,3},{12,6},{13,7},{18,24},{19,25... | collective-permute-start | bytes 1966088 | tf_op jit(solution)/shard_map/ppermute | solution.py:1094
  553.7 26.2 %collective-permute-start.35 = (bf16[64,4096]{1,0:T(8,128)(2,1)}, bf16[64,4096]{1,0:T(8,128)(2,1)}, u32[]{:S(2)}, u32[]{:S(2)}) collective-permute-start(bf16[64,4096]{1,0:T(8,128)(2,1)} %fusion.7), channel_id=1, source_target_pairs={{0,16},{1,17},{2,18},{3,19},{4,20},{5,21},{6,22},{7,23},{8,24},{9,... | collective-permute-start | bytes 1572872 | tf_op jit(solution)/shard_map/ppermute | solution.py:1094
  565.2 43.5 %collective-permute-start.31 = (bf16[1024,1024]{1,0:T(8,128)(2,1)S(1)}, bf16[1024,1024]{1,0:T(8,128)(2,1)}, u32[]{:S(2)}, u32[]{:S(2)}) collective-permute-start(bf16[1024,1024]{1,0:T(8,128)(2,1)S(1)} %copy-done), channel_id=1, source_target_pairs={{2,8},{3,9},{6,12},{7,13},{8,2},{9,3},{12,6},{13,7},{18,24},{19,25... | collective-permute-start | bytes 6291464 | tf_op jit(solution)/shard_map/ppermute | solution.py:1094
  (48 other events, 414.5 us)
Sparse Core Ops, SparseCore 0:
  10.7 63.0 all-gather.2
  108.3 78.3 all-gather.4

commit v7 on v6

--- a/solution.py
+++ b/solution.py
@@ -961,54 +961,80 @@
     )(part_a, part_b, w_qkv, resid)
 
 
-def weight_kernel(half_ref, first_ref, second_ref, right_ref, *refs):
-    o_ref, turned = refs[-2], refs[-1]
+def weight_kernel(at_ref, *refs):
+    left, right_ref, rest, turned = refs[:4], refs[4], refs[5:-1], refs[-1]
 
     @pl.when(pl.program_id(1) == 0)
     def _():
-        part = first_ref.shape[1]
-        turned[:part, :] = first_ref[...].T
-        turned[part:, :] = second_ref[...].T
+        part = left[0].shape[1]
+        for k in range(4):
+            turned[k * part:(k + 1) * part, :] = left[k][...].T
 
     value = dot(turned[...], right_ref[...], 1, 0)
-    if len(refs) == 3:
-        value = value + refs[0][...].astype(F32)
-    o_ref[...] = value.astype(BF)
-
-
-def weight_call(left, right, half, came=None):
+    if len(rest) == 1:
+        rest[0][...] = value.astype(BF)
+        return
+    came_ref, away_ref, keep_ref = rest
+    value = (value + came_ref[...].astype(F32)).astype(BF)
+    rows = away_ref.shape[0]
+    if rows < value.shape[0]:
+        away_ref[...] = value[:rows]
+        keep_ref[...] = value[rows:]
+    else:
+        first = pl.program_id(0) < pl.num_programs(0) // 2
+
+        @pl.when(first)
+        def _():
+            away_ref[...] = value
+
+        @pl.when(jnp.logical_not(first))
+        def _():
+            keep_ref[...] = value
+
+
+def weight_call(left, right, half, y, came=None):
     t, rows = left.shape
     width = right.shape[1]
     bm = 512
     bn = 1024 if width == 1024 else 512
     steps = rows // 2 // bm
-    if steps == 1:
-        first = lambda i, j, h: (0, h[0])
-        second = lambda i, j, h: (0, 2 + h[0])
+
+    def column(k):
+        def place(i, j, at):
+            if steps == 1:
+                side, z1 = (1 - at[1] if k < 2 else at[1]), k % 2
+                return (0, z1 * 4 + at[0] * 2 + side)
+            side = at[1] + (1 - 2 * at[1]) * (1 - i // 2)
+            return (0, (lax.rem(i, 2) * 4 + at[0] * 2 + side) * 4 + k)
+
+        return pl.BlockSpec((t, bm // 4), place)
+
+    specs = [column(k) for k in range(4)] + [pl.BlockSpec((t, bn), lambda i, j, at: (0, j))]
+    values = [left] * 4 + [right]
+    out = pl.BlockSpec((bm, bn), lambda i, j, at: (i, j))
+    if came is None:
+        shapes = SHAPE((rows // 2, width), BF)
     else:
-        block = lambda i, h: lax.div(i, steps // 2) * steps + h[0] * (steps // 2) + lax.rem(i, steps // 2)
-        first = lambda i, j, h: (0, 2 * block(i, h))
-        second = lambda i, j, h: (0, 2 * block(i, h) + 1)
-    specs = [
-        pl.BlockSpec((t, bm // 2), first),
-        pl.BlockSpec((t, bm // 2), second),
-        pl.BlockSpec((t, bn), lambda i, j, h: (0, j)),
-    ]
-    values = [left, left, right]
-    out = pl.BlockSpec((bm, bn), lambda i, j, h: (i, j))
-    if came is not None:
         specs.append(out)
         values.append(came)
+        shapes = (SHAPE((rows // 4, width), BF),) * 2
+        if steps == 1:
+            out = (pl.BlockSpec((bm // 2, bn), lambda i, j, at: (0, j)),) * 2
+        else:
+            out = (
+                pl.BlockSpec((bm, bn), lambda i, j, at: (jnp.minimum(i, steps // 2 - 1), j)),
+                pl.BlockSpec((bm, bn), lambda i, j, at: (jnp.maximum(i - steps // 2, 0), j)),
+            )
     return pl.pallas_call(
         weight_kernel,
-        out_shape=SHAPE((rows // 2, width), BF),
+        out_shape=shapes,
         grid_spec=pltpu.PrefetchScalarGridSpec(
             num_scalar_prefetch=1, grid=(steps, width // bn), in_specs=specs, out_specs=out,
             scratch_shapes=[pltpu.VMEM((bm, t), BF)],
         ),
         cost_estimate=cost(t * rows * width, t * rows + 2 * t * width + 2 * rows * width),
         name="weight_grad",
-    )(half.reshape(1), *values)
+    )(jnp.stack([half, y]), *values)
 
 
 def inner_kernel(rate, decay, w_ref, g_ref, m_ref, v_ref, m_out, v_out, d_out):
@@ -1102,21 +1128,17 @@
     return lax.dynamic_index_in_dim(value, index, axis, keepdims=False)
 
 
-def half_axis(total, which):
-    return 1 if which == "y" and total.ndim == 4 else 0
-
-
 def halve(at, total, which):
-    away = pick(total, 1 - at[which], half_axis(total, which))
+    away = pick(total.reshape(2, -1, total.shape[-1]), 1 - at[which], 0)
     return away, exchange(away, which)
 
 
 def join(at, total, came, which, *gates):
-    return add_low(pick(total, at[which], half_axis(total, which)), after(came, *gates))
-
-
-def slabs(total):
-    return total.reshape(2, 2, -1, total.shape[-1])
+    return add_low(pick(total.reshape(2, -1, total.shape[-1]), at[which], 0), after(came, *gates))
+
+
+def join_kept(kept, came, *gates):
+    return add_low(kept, after(came, *gates))
 
 
 def after(value, *earlier):
@@ -1157,6 +1179,7 @@
     bf, f32 = jnp.bfloat16, jnp.float32
     at = bits_of()
     core = at["c"].astype(jnp.int32)
+    side = at["y"].astype(jnp.int32)
     def swapped(value, came):
         return jnp.where(at["c"] != at["z0"], came, value)
 
@@ -1195,43 +1218,43 @@
         activated, down_own, down_other, normed, cot, rows, core
     )
     output_came = cross(layer_output)
-    down_send = weight_call(activated, grad_branch, 1 - core)
+    down_send = weight_call(activated, grad_branch, 1 - core, side)
     grad_pre, sums_up = slope_call(after(grad_branch, down_send), down_own, down_other, slope, core)
     down_came = exchange(down_send, "c")
-    up_send = weight_call(hidden_low, grad_pre, 1 - core)
-    down_total = slabs(weight_call(activated, after(grad_branch, up_send), core, down_came))
+    up_send = weight_call(hidden_low, grad_pre, 1 - core, side)
+    away_d, down_kept = weight_call(activated, after(grad_branch, up_send), core, side, down_came)
     up_came = exchange(up_send, "c")
-    away_d, came_d = halve(at, down_total, "y")
-    up_total = slabs(weight_call(hidden_low, after(grad_pre, away_d), core, up_came))
-    away_u, came_u = halve(at, up_total, "y")
+    came_d = exchange(away_d, "y")
+    away_u, up_kept = weight_call(hidden_low, after(grad_pre, away_d), core, side, up_came)
+    came_u = exchange(away_u, "y")
     grad_resid, grad_attn, grad_mixed, sums_one = hidden_call(
         after(grad_pre, away_u), in_parts, place, grad_sum, normed, inv, w_out, rows
     )
-    proj_send = weight_call(mixed, grad_attn, 1 - core)
+    proj_send = weight_call(mixed, grad_attn, 1 - core, side)
     proj_came = exchange(proj_send, "c")
     output = swapped(layer_output, after(output_came, proj_send))
     grad_a, sums_a = attn_bwd(qkv, after(grad_mixed, proj_send, output), log_sum, seg, 0)
-    send_a = weight_call(tok, grad_a, 1 - core)
+    send_a = weight_call(tok, grad_a, 1 - core, side)
     came_a = exchange(send_a, "c")
-    down_one = join(at, down_total, came_d, "y", send_a)
+    down_one = join_kept(down_kept, came_d, send_a)
     away_d, came_d = halve(at, down_one, "z1")
-    proj_total = slabs(weight_call(mixed, after(grad_attn, away_d), core, proj_came))
-    away_p, came_p = halve(at, proj_total, "y")
-    total_a = slabs(weight_call(tok, after(grad_a, away_p), core, came_a))
-    away_a, came_one = halve(at, total_a, "y")
-    up_one = join(at, up_total, came_u, "y", away_a)
+    away_p, proj_kept = weight_call(mixed, after(grad_attn, away_d), core, side, proj_came)
+    came_p = exchange(away_p, "y")
+    away_a, a_kept = weight_call(tok, after(grad_a, away_p), core, side, came_a)
+    came_one = exchange(away_a, "y")
+    up_one = join_kept(up_kept, came_u, away_a)
     away_u, came_u = halve(at, up_one, "z1")
     grad_b, sums_b = attn_bwd(qkv, after(grad_mixed, away_u), log_sum, seg, 1)
-    send_b = weight_call(tok, grad_b, 1 - core)
+    send_b = weight_call(tok, grad_b, 1 - core, side)
     came_b = exchange(send_b, "c")
     down_two = join(at, down_one, came_d, "z1", send_b)
     cross_d = cross(down_two)
-    proj_one = join(at, proj_total, came_p, "y", down_two)
+    proj_one = join_kept(proj_kept, came_p, down_two)
     away_p, came_p = halve(at, proj_one, "z1")
-    a_one = join(at, total_a, came_one, "y", away_p)
+    a_one = join_kept(a_kept, came_one, away_p)
     away_a, came_a = halve(at, a_one, "z1")
-    total_b = slabs(weight_call(tok, after(grad_b, away_a), core, came_b))
-    away_b, came_b = halve(at, total_b, "y")
+    away_b, b_kept = weight_call(tok, after(grad_b, away_a), core, side, came_b)
+    came_b = exchange(away_b, "y")
     sums_qkv = jnp.concatenate([sums_a, sums_b], axis=0).reshape(D // 128, 3, 128)
     vector_grad = jnp.concatenate(
         [
@@ -1285,7 +1308,7 @@
     cross_u = cross(up_two)
     vec_one = vector_join(vector_grad, vec_came, "z1", up_two)
     vec_came = vector_send(vec_one, "c")
-    b_one = join(at, total_b, came_b, "y", up_two)
+    b_one = join_kept(b_kept, came_b, up_two)
     away_b, came_b = halve(at, b_one, "z1")
     half_c = rep_join(contract_new[2], came_c, away_b)
     rest_c = exchange(half_c, "x")

time: 626 us -> 625 us (level)
  local copies, waits for them, and re-layouts: 50.6 us -> 34.9 us
  Pallas kernels: 426 us -> 438 us
  waiting for transfers between devices: 29.9 us -> 37.3 us
  starting transfers between devices: 50.8 us -> 44.2 us
    squeeze x10 -> x5, local copies, waits for them, and re-layouts: 14.1 us -> 6.32 us  [pick(): return lax.dynamic_index_in_dim(value, index, axis, keepdims=False)]
    ppermute x41, waiting for transfers between devices: 29.8 us -> 37.2 us  [exchange(): return lax.ppermute(value, ('rep', 'fsdp'), xor_pairs(bits))]
    pallas_call x10, Pallas kernels: 71.7 us -> 78.8 us  [weight_call(): pl.pallas_call(weight_kernel, out_shape=shapes, grid_spec=pltpu.PrefetchS...]
    ppermute x41, starting transfers between devices: 50.7 us -> 44.1 us  [exchange(): return lax.ppermute(value, ('rep', 'fsdp'), xor_pairs(bits))]
  transfers between devices with their start and end apart: 43 -> 43, of which waited for: 7 -> 7; matrix products, arithmetic and copies ran while one was open for 14% -> 12% of each run, Pallas kernels for 64% -> 66%
where the time goes in v7:
time: 625 us; the launch traced here: 619 us
  Pallas kernels  438 us (70%)
  other arithmetic  48.9 us (8%)
  starting transfers between devices  44.2 us (7%)
  waiting for transfers between devices  37.3 us (6%)
  local copies, waits for them, and re-layouts  34.9 us (6%)
  between operations  15.1 us (2%)
    pallas_call x1, Pallas kernels, gather_all(): pl.pallas_call(gather_kernel, out_shape=(shape((8 * qkv.shape[0], qkv.sha...  91.8 us
    pallas_call x10, Pallas kernels, weight_call(): pl.pallas_call(weight_kernel, out_shape=shapes, grid_spec=pltpu.PrefetchS...  78.8 us
    pallas_call x2, Pallas kernels, attn_bwd(): pl.pallas_call(bwd_kernel, out_shape=(jax.ShapeDtypeStruct((T, width // 2...  59.7 us
    pallas_call x1, Pallas kernels, attn_fwd(): pl.pallas_call(fwd_kernel, out_shape=(jax.ShapeDtypeStruct((T, width // 3...  47 us
    ppermute x41, starting transfers between devices, exchange(): return lax.ppermute(value, ('rep', 'fsdp'), xor_pairs(bits))  44.1 us
    ppermute x41, waiting for transfers between devices, exchange(): return lax.ppermute(value, ('rep', 'fsdp'), xor_pairs(bits))  37.2 us
    pallas_call x1, Pallas kernels, up_call(): pl.pallas_call(up_kernel, out_shape=(SHAPE((t, FF), BF), SHAPE((t, FF), B...  34.3 us
    convert_element_type x17, other arithmetic, add_low(): (left.astype(jnp.float32) + right.astype(jnp.float32)).astype(jnp.bfloat16)  24.2 us
  transfers between devices with their start and end apart: 43, of which 7 were waited for; matrix products, arithmetic and copies ran while one was open for 12% of the time, Pallas kernels for 66%

profile of v7, /device:TPU:1, one launch (start us, length us, event | category | flops | bytes accessed | tf_op | source)
XLA Modules:
  0.0 618.6 jit_solution(17101586407528950975)
XLA Ops:
  14.2 91.8 %gather_weights.1 = (bf16[1024,3072]{1,0:T(8,128)(2,1)}, bf16[1024,1024]{1,0:T(8,128)(2,1)}, bf16[8,12,128]{2,1,0:T(8,128)(2,1)}, bf16[1024,1024]{1,0:T(8,128)(2,1)}, s32[1,1024]{1,0:T(1,128)}) custom-call(bf16[128,3072]{1,0:T(8,128)(2,1)} %copy.76.qkv_in, bf16[128,1024]{1,0:T(8,128)(2,1)} %slice_bitcast_fusion.1.wo_in, ...), custom_call_target="tpu_custom_call" | custom-call | tf_op jit(solution)/shard_map/gather_weights/pallas_call | solution.py:679
  115.7 10.8 %qkv.1.qkv_ref = bf16[1024,3072]{1,0:T(8,128)(2,1)} custom-call(bf16[1024,1024]{1,0:T(8,128)(2,1)} %get-tuple-element.119.x_ref.refs_0_.refs_1_.refs_2_.refs_3_, bf16[1024,3072]{1,0:T(8,128)(2,1)} %get-tuple-element.120.w_ref, f32[1,3072]{1,0:T(1,128)} %reshape.185.bias_ref, f32[1,3072]{1,0:T(1,128)} %constant.178.clone.1.scale_ref), custom_call_target="tpu_custom_call" | custom-call | flops 6442450 | bytes 14680 | tf_op jit(solution)/shard_map/qkv/pallas_call | solution.py:725
  127.2 47.0 %attn_fwd.1 = (bf16[1024,1024]{1,0:T(8,128)(2,1)}, f32[8,2,1024]{2,1,0:T(2,128)}) custom-call(s32[4]{0:T(128)} %get-tuple-element.222.start_ref, s32[4]{0:T(128)} %get-tuple-element.223.count_ref, bf16[1024,3072]{1,0:T(8,128)(2,1)} %qkv.1.qkv_ref, s32[1,1024]{1,0:T(1,128)} %get-tuple-element.118.segr_ref, s32[1024,1]{1,0:T(8,128)} %copy.77.segc_ref), custom_call_target="tpu_custom_call" | custom-call | flops 64424508 | bytes 9437 | tf_op jit(solution)/shard_map/attn_fwd/pallas_call | solution.py:413
  176.1 8.1 %mix_norm.1 = (f32[1024,1024]{1,0:T(8,128)}, f32[1024,1]{1,0:T(8,128)}, bf16[1024,1024]{1,0:T(8,128)(2,1)}) custom-call(bf16[1024,1024]{1,0:T(8,128)(2,1)} %get-tuple-element.122.c_ref.refs_0_.refs_1_.refs_2_.refs_3_, bf16[1024,1024]{1,0:T(8,128)(2,1)} %get-tuple-element.123.w_ref.refs_11_, ...), custom_call_target="tpu_custom_call" | custom-call | flops 2147483 | bytes 14680 | tf_op jit(solution)/shard_map/mix_norm/pallas_call | solution.py:758
  187.9 34.3 %up_gelu.1 = (bf16[1024,4096]{1,0:T(8,128)(2,1)}, bf16[1024,4096]{1,0:T(8,128)(2,1)}) custom-call(s32[4]{0:T(128)} %pad_add_fusion.place_ref, bf16[1024,1024]{1,0:T(8,128)(2,1)} %get-tuple-element.127.h_ref.refs_0_.refs_1_.refs_2_.refs_3_, bf16[1024,1024]{1,0:T(8,128)(2,1)} %all-gather.3.cloned.1.call-done.refs_0_.refs_4_, ...), custom_call_target="tpu_custom_call" | custom-call | flops 8589934 | bytes 27262 | tf_op jit(solution)/shard_map/up_gelu/pallas_call | solution.py:795
  223.1 6.8 %collective-permute-done.4.came_ref = bf16[4096,512]{1,0:T(8,128)(2,1)} collective-permute-done((bf16[4096,512]{1,0:T(8,128)(2,1)}, bf16[4096,512]{1,0:T(8,128)(2,1)}, u32[]{:S(2)}, u32[]{:S(2)}) %collective-permute-start.4) | collective-permute-done | bytes 4194336 | tf_op jit(solution)/shard_map/ppermute | solution.py:1120
  229.9 19.9 %down_norm.1 = (bf16[1024,1024]{1,0:T(8,128)(2,1)}, f32[1024,1024]{1,0:T(8,128)}, bf16[1024,1024]{1,0:T(8,128)(2,1)}, f32[8,1024]{1,0:T(8,128)}) custom-call(s32[1]{0:T(128)} %bitcast.core_ref, bf16[1024,4096]{1,0:T(8,128)(2,1)} %get-tuple-element.131.g_ref.refs_0_.refs_1_.refs_2_.refs_3_, bf16[4096,512]{1,0:T(8,128)(2,1)} %all-gather.5.cloned.1.call-done.own_ref, ...), custom_call_target="tpu_custom_call" | custom-call | flops 8589934 | bytes 31457 | tf_op jit(solution)/shard_map/down_norm/pallas_call | solution.py:848
  249.8 9.3 %weight_grad.10 = bf16[2048,1024]{1,0:T(8,128)(2,1)} custom-call(s32[2]{0:T(128)} %pad_add_fusion.1.at_ref, bf16[1024,4096]{1,0:T(8,128)(2,1)} %get-tuple-element.131.g_ref.refs_0_.refs_1_.refs_2_.refs_3_, bf16[1024,4096]{1,0:T(8,128)(2,1)} %get-tuple-element.131.g_ref.refs_0_.refs_1_.refs_2_.refs_3_, ...), custom_call_target="tpu_custom_call" | custom-call | flops 4294967 | bytes 14680 | tf_op jit(solution)/shard_map/weight_grad/pallas_call | solution.py:1028
  259.2 16.3 %down_back.1 = (bf16[1024,4096]{1,0:T(8,128)(2,1)}, f32[1,4096]{1,0:T(1,128)}) custom-call(s32[1]{0:T(128)} %bitcast.core_ref, bf16[1024,1024]{1,0:T(8,128)(2,1)} %get-tuple-element.140.refs_4_.left_ref.right_ref, bf16[1024,1024]{1,0:T(8,128)(2,1)} %get-tuple-element.140.refs_4_.left_ref.right_ref, bf16[4096,512]{1,0:T(8,128)(2,1)} %all-gather.5.cloned.1.call-done.own_ref, ...), custom_call_target="tpu_custom_call" | custom-call | flops 8589934 | bytes 27262 | tf_op jit(solution)/shard_map/down_back/pallas_call | solution.py:881
  275.5 11.5 %weight_grad.11 = bf16[512,4096]{1,0:T(8,128)(2,1)} custom-call(s32[2]{0:T(128)} %pad_add_fusion.1.at_ref, bf16[1024,1024]{1,0:T(8,128)(2,1)} %get-tuple-element.127.h_ref.refs_0_.refs_1_.refs_2_.refs_3_, bf16[1024,1024]{1,0:T(8,128)(2,1)} %get-tuple-element.127.h_ref.refs_0_.refs_1_.refs_2_.refs_3_, ...), custom_call_target="tpu_custom_call" | custom-call | flops 4294967 | bytes 17825 | tf_op jit(solution)/shard_map/weight_grad/pallas_call | solution.py:1028
  290.0 10.7 %weight_grad.12 = (bf16[1024,1024]{1,0:T(8,128)(2,1)}, bf16[1024,1024]{1,0:T(8,128)(2,1)}) custom-call(s32[2]{0:T(128)} %pad_add_fusion.2.at_ref, bf16[1024,4096]{1,0:T(8,128)(2,1)} %get-tuple-element.131.g_ref.refs_0_.refs_1_.refs_2_.refs_3_, bf16[1024,4096]{1,0:T(8,128)(2,1)} %get-tuple-element.131.g_ref.refs_0_.refs_1_.refs_2_.refs_3_, ...), custom_call_target="tpu_custom_call" | custom-call | flops 4294967 | bytes 14680 | tf_op jit(solution)/shard_map/weight_grad/pallas_call | solution.py:1028
  301.5 11.9 %weight_grad.13 = (bf16[256,4096]{1,0:T(8,128)(2,1)}, bf16[256,4096]{1,0:T(8,128)(2,1)}) custom-call(s32[2]{0:T(128)} %pad_add_fusion.2.at_ref, bf16[1024,1024]{1,0:T(8,128)(2,1)} %get-tuple-element.127.h_ref.refs_0_.refs_1_.refs_2_.refs_3_, bf16[1024,1024]{1,0:T(8,128)(2,1)} %get-tuple-element.127.h_ref.refs_0_.refs_1_.refs_2_.refs_3_, ...), custom_call_target="tpu_custom_call" | custom-call | flops 4294967 | bytes 17825 | tf_op jit(solution)/shard_map/weight_grad/pallas_call | solution.py:1028
  314.1 22.1 %up_back_norm.1 = (f32[1024,1024]{1,0:T(8,128)}, bf16[1024,1024]{1,0:T(8,128)(2,1)}, bf16[1024,1024]{1,0:T(8,128)(2,1)}, f32[8,1024]{1,0:T(8,128)}) custom-call(s32[4]{0:T(128)} %pad_add_fusion.place_ref, bf16[1024,4096]{1,0:T(8,128)(2,1)} %get-tuple-element.144.refs_4_.refs_0_.refs_1_.refs_2_.refs_3_, ...), custom_call_target="tpu_custom_call" | custom-call | flops 10737418 | bytes 33554 | tf_op jit(solution)/shard_map/up_back_norm/pallas_call | solution.py:927
  344.2 29.8 %attn_bwd.2 = (bf16[1024,1536]{1,0:T(8,128)(2,1)}, f32[4,1,384]{2,1,0:T(1,128)}) custom-call(s32[4]{0:T(128)} %get-tuple-element.222.start_ref, s32[4]{0:T(128)} %get-tuple-element.223.count_ref, bf16[1024,3072]{1,0:T(8,128)(2,1)} %qkv.1.qkv_ref, bf16[1024,1024]{1,0:T(8,128)(2,1)} %get-tuple-element.161.do_ref, f32[8,2,1024]{2,1,0:T(2,128)} %get-tuple-element.151.lse_ref, ...), custom_call_target="tpu_custom_call" | custom-call | flops 64424508 | bytes 18874 | tf_op jit(solution)/shard_map/attn_bwd/pallas_call | solution.py:437
  374.1 6.3 %weight_grad.15 = bf16[512,1536]{1,0:T(8,128)(2,1)} custom-call(s32[2]{0:T(128)} %pad_add_fusion.1.at_ref, bf16[1024,1024]{1,0:T(8,128)(2,1)} %get-tuple-element.119.x_ref.refs_0_.refs_1_.refs_2_.refs_3_, bf16[1024,1024]{1,0:T(8,128)(2,1)} %get-tuple-element.119.x_ref.refs_0_.refs_1_.refs_2_.refs_3_, ...), custom_call_target="tpu_custom_call" | custom-call | flops 1610612 | bytes 7340 | tf_op jit(solution)/shard_map/weight_grad/pallas_call | solution.py:1028
  398.3 6.4 %weight_grad.17 = (bf16[256,1536]{1,0:T(8,128)(2,1)}, bf16[256,1536]{1,0:T(8,128)(2,1)}) custom-call(s32[2]{0:T(128)} %pad_add_fusion.2.at_ref, bf16[1024,1024]{1,0:T(8,128)(2,1)} %get-tuple-element.119.x_ref.refs_0_.refs_1_.refs_2_.refs_3_, bf16[1024,1024]{1,0:T(8,128)(2,1)} %get-tuple-element.119.x_ref.refs_0_.refs_1_.refs_2_.refs_3_, ...), custom_call_target="tpu_custom_call" | custom-call | flops 1610612 | bytes 7340 | tf_op jit(solution)/shard_map/weight_grad/pallas_call | solution.py:1028
  410.1 29.9 %attn_bwd.3 = (bf16[1024,1536]{1,0:T(8,128)(2,1)}, f32[4,1,384]{2,1,0:T(1,128)}) custom-call(s32[4]{0:T(128)} %get-tuple-element.222.start_ref, s32[4]{0:T(128)} %get-tuple-element.223.count_ref, bf16[1024,3072]{1,0:T(8,128)(2,1)} %qkv.1.qkv_ref, bf16[1024,1024]{1,0:T(8,128)(2,1)} %get-tuple-element.161.do_ref, f32[8,2,1024]{2,1,0:T(2,128)} %get-tuple-element.151.lse_ref, ...), custom_call_target="tpu_custom_call" | custom-call | flops 64424508 | bytes 18874 | tf_op jit(solution)/shard_map/attn_bwd/pallas_call | solution.py:437
  440.0 6.3 %weight_grad.18 = bf16[512,1536]{1,0:T(8,128)(2,1)} custom-call(s32[2]{0:T(128)} %pad_add_fusion.1.at_ref, bf16[1024,1024]{1,0:T(8,128)(2,1)} %get-tuple-element.119.x_ref.refs_0_.refs_1_.refs_2_.refs_3_, bf16[1024,1024]{1,0:T(8,128)(2,1)} %get-tuple-element.119.x_ref.refs_0_.refs_1_.refs_2_.refs_3_, ...), custom_call_target="tpu_custom_call" | custom-call | flops 1610612 | bytes 7340 | tf_op jit(solution)/shard_map/weight_grad/pallas_call | solution.py:1028
  447.1 13.3 %collective-permute-done.14 = bf16[512,1024]{1,0:T(8,128)(2,1)} collective-permute-done((bf16[512,1024]{1,0:T(8,128)(2,1)}, bf16[512,1024]{1,0:T(8,128)(2,1)}, u32[]{:S(2)}, u32[]{:S(2)}) %collective-permute-start.14) | collective-permute-done | bytes 1048608 | tf_op jit(solution)/shard_map/ppermute | solution.py:1120
  479.6 6.4 %weight_grad.19 = (bf16[256,1536]{1,0:T(8,128)(2,1)}, bf16[256,1536]{1,0:T(8,128)(2,1)}) custom-call(s32[2]{0:T(128)} %pad_add_fusion.2.at_ref, bf16[1024,1024]{1,0:T(8,128)(2,1)} %get-tuple-element.119.x_ref.refs_0_.refs_1_.refs_2_.refs_3_, bf16[1024,1024]{1,0:T(8,128)(2,1)} %get-tuple-element.119.x_ref.refs_0_.refs_1_.refs_2_.refs_3_, ...), custom_call_target="tpu_custom_call" | custom-call | flops 1610612 | bytes 7340 | tf_op jit(solution)/shard_map/weight_grad/pallas_call | solution.py:1028
  516.9 12.3 %input_back.1 = bf16[1024,1024]{1,0:T(8,128)(2,1)} custom-call(bf16[1024,1536]{1,0:T(8,128)(2,1)} %get-tuple-element.176.refs_4_.a_ref, bf16[1024,1536]{1,0:T(8,128)(2,1)} %get-tuple-element.168.refs_4_.b_ref, bf16[1024,3072]{1,0:T(8,128)(2,1)} %get-tuple-element.120.w_ref, f32[1024,1024]{1,0:T(8,128)} %get-tuple-element.177.r_ref), custom_call_target="tpu_custom_call" | custom-call | flops 6442450 | bytes 18874 | tf_op jit(solution)/shard_map/input_back/pallas_call | solution.py:953
  558.5 6.4 %outer_step.3 = (f32[3,512,1024]{2,1,0:T(8,128)}, bf16[512,1024]{1,0:T(8,128)(2,1)}) custom-call(s32[1]{0:T(128)} %bitcast.core_ref, f32[512,1024]{1,0:T(8,128)} %w_ref.6, f32[512,1024]{1,0:T(8,128)} %u_ref.2, bf16[256,1024]{1,0:T(8,128)(2,1)} %copy-done.5, bf16[256,1024]{1,0:T(8,128)(2,1)} %collective-permute-done.30.came_ref), custom_call_target="tpu_custom_call" | custom-call | flops 5242 | bytes 13631 | tf_op jit(solution)/shard_map/outer_step/pallas_call | solution.py:1083
  583.2 6.3 %outer_step.4 = (f32[3,128,4096]{2,1,0:T(8,128)}, bf16[128,4096]{1,0:T(8,128)(2,1)}) custom-call(s32[1]{0:T(128)} %bitcast.core_ref, f32[128,4096]{1,0:T(8,128)} %w_ref.7, f32[128,4096]{1,0:T(8,128)} %u_ref.3, bf16[64,4096]{1,0:T(8,128)(2,1)} %copy-done.6, bf16[64,4096]{1,0:T(8,128)(2,1)} %collective-permute-done.38.came_ref), custom_call_target="tpu_custom_call" | custom-call | flops 5242 | bytes 13631 | tf_op jit(solution)/shard_map/outer_step/pallas_call | solution.py:1083
  602.1 6.3 %outer_step.5 = (f32[3,512,1024]{2,1,0:T(8,128)}, bf16[512,1024]{1,0:T(8,128)(2,1)}) custom-call(s32[1]{0:T(128)} %bitcast.core_ref, f32[512,1024]{1,0:T(8,128)} %bitcast.123, f32[512,1024]{1,0:T(8,128)} %bitcast.143, bf16[256,1024]{1,0:T(8,128)(2,1)} %copy-done.4, bf16[256,1024]{1,0:T(8,128)(2,1)} %copy-done.12), custom_call_target="tpu_custom_call" | custom-call | flops 5242 | bytes 13631 | tf_op jit(solution)/shard_map/outer_step/pallas_call | solution.py:1083
  (230 shorter events, 173.0 us)
Async XLA Ops:
  7.2 101.0 %all-gather.3.cloned.1.call-start = ((), (), s32[]{:S(2)}) async-start(), calls=%async_computation | async-start | bytes 2359296 | tf_op jit(solution)/shard_map/all_gather | solution.py:1192
  9.1 213.2 %all-gather.5.cloned.1.call-start = ((), (), s32[]{:S(2)}) async-start(), calls=%async_computation.1 | async-start | bytes 4718592 | tf_op jit(solution)/shard_map/all_gather | solution.py:1206
  108.2 66.1 %collective-permute-start.2 = (bf16[1024,1024]{1,0:T(8,128)(2,1)}, bf16[1024,1024]{1,0:T(8,128)(2,1)}, u32[]{:S(2)}, u32[]{:S(2)}) collective-permute-start(bf16[1024,1024]{1,0:T(8,128)(2,1)} %all-gather.3.cloned.1.call-done.refs_0_.refs_4_), channel_id=1, source_target_pairs={{0,16},{1,17},{2,18},{3,19},{4,20},{5,21},{6,22},{7,23},{8,24},{9,... | collective-permute-start | bytes 6291464 | tf_op jit(solution)/shard_map/ppermute | solution.py:1120
  108.5 76.3 %collective-permute-start = (bf16[1024,1024]{1,0:T(8,128)(2,1)}, bf16[1024,1024]{1,0:T(8,128)(2,1)}, u32[]{:S(2)}, u32[]{:S(2)}) collective-permute-start(bf16[1024,1024]{1,0:T(8,128)(2,1)} %param.20), channel_id=1, source_target_pairs={{2,8},{3,9},{6,12},{7,13},{8,2},{9,3},{12,6},{13,7},{18,24},{19,25... | collective-permute-start | bytes 6291464 | tf_op jit(solution)/shard_map/ppermute | solution.py:1120
  259.1 30.9 %collective-permute-start.6 = (bf16[2048,1024]{1,0:T(8,128)(2,1)}, bf16[2048,1024]{1,0:T(8,128)(2,1)}, u32[]{:S(2)}, u32[]{:S(2)}) collective-permute-start(bf16[2048,1024]{1,0:T(8,128)(2,1)} %weight_grad.10), channel_id=1, source_target_pairs={{0,8},{1,9},{2,10},{3,11},{4,12},{5,13},{6,14},{7,15},{8,0},{9,1},... | collective-permute-start | bytes 12582920 | tf_op jit(solution)/shard_map/ppermute | solution.py:1120
  287.4 53.7 %collective-permute-start.5 = (bf16[1024,1024]{1,0:T(8,128)(2,1)}, bf16[1024,1024]{1,0:T(8,128)(2,1)}, u32[]{:S(2)}, u32[]{:S(2)}) collective-permute-start(bf16[1024,1024]{1,0:T(8,128)(2,1)} %get-tuple-element.135), channel_id=1, source_target_pairs={{2,8},{3,9},{6,12},{7,13},{8,2},{9,3},{12,6},{13,7},{18,24},{19,25... | collective-permute-start | bytes 6291464 | tf_op jit(solution)/shard_map/ppermute | solution.py:1120
  300.7 83.2 %collective-permute-start.9 = (bf16[1024,1024]{1,0:T(8,128)(2,1)}, bf16[1024,1024]{1,0:T(8,128)(2,1)}, u32[]{:S(2)}, u32[]{:S(2)}) collective-permute-start(bf16[1024,1024]{1,0:T(8,128)(2,1)} %get-tuple-element.141), channel_id=1, source_target_pairs={{0,1},{1,0},{2,3},{3,2},{4,5},{5,4},{6,7},{7,6},{8,9},{9,8},{10,11... | collective-permute-start | bytes 6291464 | tf_op jit(solution)/shard_map/ppermute | solution.py:1120
  313.4 91.3 %collective-permute-start.8 = (bf16[256,4096]{1,0:T(8,128)(2,1)}, bf16[256,4096]{1,0:T(8,128)(2,1)S(1)}, u32[]{:S(2)}, u32[]{:S(2)}) collective-permute-start(bf16[256,4096]{1,0:T(8,128)(2,1)} %get-tuple-element.143), channel_id=1, source_target_pairs={{0,1},{1,0},{2,3},{3,2},{4,5},{5,4},{6,7},{7,6},{8,9},{9,8},{10,11... | collective-permute-start | bytes 6291464 | tf_op jit(solution)/shard_map/ppermute | solution.py:1120
  380.4 17.9 %collective-permute-start.11 = (bf16[512,1536]{1,0:T(8,128)(2,1)}, bf16[512,1536]{1,0:T(8,128)(2,1)}, u32[]{:S(2)}, u32[]{:S(2)}) collective-permute-start(bf16[512,1536]{1,0:T(8,128)(2,1)} %weight_grad.15), channel_id=1, source_target_pairs={{0,8},{1,9},{2,10},{3,11},{4,12},{5,13},{6,14},{7,15},{8,0},{9,1},... | collective-permute-start | bytes 4718600 | tf_op jit(solution)/shard_map/ppermute | solution.py:1120
  389.5 71.0 %collective-permute-start.14 = (bf16[512,1024]{1,0:T(8,128)(2,1)}, bf16[512,1024]{1,0:T(8,128)(2,1)}, u32[]{:S(2)}, u32[]{:S(2)}) collective-permute-start(bf16[512,1024]{1,0:T(8,128)(2,1)} %dynamic-slice_bitcast_fusion.1), channel_id=1, source_target_pairs={{0,4},{1,5},{2,6},{3,7},{4,0},{5,1},{6,2},{7,3},{8,12},{9,13},{10,... | collective-permute-start | bytes 3145736 | tf_op jit(solution)/shard_map/ppermute | solution.py:1120
  396.0 66.4 %collective-permute-start.13 = (bf16[256,1024]{1,0:T(8,128)(2,1)}, bf16[256,1024]{1,0:T(8,128)(2,1)}, u32[]{:S(2)}, u32[]{:S(2)}) collective-permute-start(bf16[256,1024]{1,0:T(8,128)(2,1)} %get-tuple-element.157), channel_id=1, source_target_pairs={{0,1},{1,0},{2,3},{3,2},{4,5},{5,4},{6,7},{7,6},{8,9},{9,8},{10,11... | collective-permute-start | bytes 1572872 | tf_op jit(solution)/shard_map/ppermute | solution.py:1120
  404.7 66.3 %collective-permute-start.12 = (bf16[256,1536]{1,0:T(8,128)(2,1)}, bf16[256,1536]{1,0:T(8,128)(2,1)}, u32[]{:S(2)}, u32[]{:S(2)}) collective-permute-start(bf16[256,1536]{1,0:T(8,128)(2,1)} %get-tuple-element.159), channel_id=1, source_target_pairs={{0,1},{1,0},{2,3},{3,2},{4,5},{5,4},{6,7},{7,6},{8,9},{9,8},{10,11... | collective-permute-start | bytes 2359304 | tf_op jit(solution)/shard_map/ppermute | solution.py:1120
  410.1 94.1 %collective-permute-start.17 = (bf16[128,4096]{1,0:T(8,128)(2,1)}, bf16[128,4096]{1,0:T(8,128)(2,1)}, u32[]{:S(2)}, u32[]{:S(2)}) collective-permute-start(bf16[128,4096]{1,0:T(8,128)(2,1)} %dynamic-slice_bitcast_fusion), channel_id=1, source_target_pairs={{0,4},{1,5},{2,6},{3,7},{4,0},{5,1},{6,2},{7,3},{8,12},{9,13},{10,... | collective-permute-start | bytes 3145736 | tf_op jit(solution)/shard_map/ppermute | solution.py:1120
  446.3 30.9 %collective-permute-start.15 = (bf16[512,1536]{1,0:T(8,128)(2,1)}, bf16[512,1536]{1,0:T(8,128)(2,1)}, u32[]{:S(2)}, u32[]{:S(2)}) collective-permute-start(bf16[512,1536]{1,0:T(8,128)(2,1)} %weight_grad.18), channel_id=1, source_target_pairs={{0,8},{1,9},{2,10},{3,11},{4,12},{5,13},{6,14},{7,15},{8,0},{9,1},... | collective-permute-start | bytes 4718600 | tf_op jit(solution)/shard_map/ppermute | solution.py:1120
  460.5 45.2 %collective-permute-start.24 = (f32[12,512]{1,0:T(8,128)}, f32[12,512]{1,0:T(8,128)}, u32[]{:S(2)}, u32[]{:S(2)}) collective-permute-start(f32[12,512]{1,0:T(8,128)} %constant_dynamic-slice_fusion.4), channel_id=1, source_target_pairs={{0,4},{1,5},{2,6},{3,7},{4,0},{5,1},{6,2},{7,3},{8,12},{9,13},{10,... | collective-permute-start | bytes 73736 | tf_op jit(solution)/shard_map/ppermute | solution.py:1120
  462.4 29.9 %collective-permute-start.18 = (bf16[512,1024]{1,0:T(8,128)(2,1)S(1)}, bf16[512,1024]{1,0:T(8,128)(2,1)}, u32[]{:S(2)}, u32[]{:S(2)}) collective-permute-start(bf16[512,1024]{1,0:T(8,128)(2,1)S(1)} %fusion.1), channel_id=1, source_target_pairs={{2,8},{3,9},{6,12},{7,13},{8,2},{9,3},{12,6},{13,7},{18,24},{19,25... | collective-permute-start | bytes 3145736 | tf_op jit(solution)/shard_map/ppermute | solution.py:1120
  474.2 67.5 %collective-permute-start.28 = (bf16[128,1536]{0,1:T(8,128)(2,1)}, bf16[128,1536]{0,1:T(8,128)(2,1)}, u32[]{:S(2)}, u32[]{:S(2)}) collective-permute-start(bf16[128,1536]{0,1:T(8,128)(2,1)} %bitcast.153), channel_id=1, source_target_pairs={{0,4},{1,5},{2,6},{3,7},{4,0},{5,1},{6,2},{7,3},{8,12},{9,13},{10,... | collective-permute-start | bytes 1179656 | tf_op jit(solution)/shard_map/ppermute | solution.py:1120
  477.3 64.6 %collective-permute-start.27 = (bf16[128,1024]{0,1:T(8,128)(2,1)}, bf16[128,1024]{0,1:T(8,128)(2,1)}, u32[]{:S(2)}, u32[]{:S(2)}) collective-permute-start(bf16[128,1024]{0,1:T(8,128)(2,1)} %bitcast.156), channel_id=1, source_target_pairs={{0,4},{1,5},{2,6},{3,7},{4,0},{5,1},{6,2},{7,3},{8,12},{9,13},{10,... | collective-permute-start | bytes 786440 | tf_op jit(solution)/shard_map/ppermute | solution.py:1120
  505.6 26.1 %collective-permute-start.21 = (bf16[128,4096]{1,0:T(8,128)(2,1)S(1)}, bf16[128,4096]{1,0:T(8,128)(2,1)S(1)}, u32[]{:S(2)}, u32[]{:S(2)}) collective-permute-start(bf16[128,4096]{1,0:T(8,128)(2,1)S(1)} %fusion), channel_id=1, source_target_pairs={{2,8},{3,9},{6,12},{7,13},{8,2},{9,3},{12,6},{13,7},{18,24},{19,25... | collective-permute-start | bytes 3145736 | tf_op jit(solution)/shard_map/ppermute | solution.py:1120
  511.0 43.2 %collective-permute-start.20 = (bf16[128,1536]{0,1:T(8,128)(2,1)}, bf16[128,1536]{0,1:T(8,128)(2,1)}, u32[]{:S(2)}, u32[]{:S(2)}) collective-permute-start(bf16[128,1536]{0,1:T(8,128)(2,1)} %bitcast.154), channel_id=1, source_target_pairs={{0,4},{1,5},{2,6},{3,7},{4,0},{5,1},{6,2},{7,3},{8,12},{9,13},{10,... | collective-permute-start | bytes 1179656 | tf_op jit(solution)/shard_map/ppermute | solution.py:1120
  516.8 33.7 %collective-permute-start.23 = (bf16[256,1024]{1,0:T(8,128)(2,1)S(1)}, bf16[256,1024]{1,0:T(8,128)(2,1)}, u32[]{:S(2)}, u32[]{:S(2)}) collective-permute-start(bf16[256,1024]{1,0:T(8,128)(2,1)S(1)} %fusion.4), channel_id=1, source_target_pairs={{0,16},{1,17},{2,18},{3,19},{4,20},{5,21},{6,22},{7,23},{8,24},{9,... | collective-permute-start | bytes 1572872 | tf_op jit(solution)/shard_map/ppermute | solution.py:1120
  545.0 23.3 %collective-permute-start.32 = (bf16[128,2560]{0,1:T(8,128)(2,1)}, bf16[128,2560]{0,1:T(8,128)(2,1)}, u32[]{:S(2)}, u32[]{:S(2)}) collective-permute-start(bf16[128,2560]{0,1:T(8,128)(2,1)} %pad_maximum_fusion.2), channel_id=1, source_target_pairs={{2,8},{3,9},{6,12},{7,13},{8,2},{9,3},{12,6},{13,7},{18,24},{19,25... | collective-permute-start | bytes 1966088 | tf_op jit(solution)/shard_map/ppermute | solution.py:1120
  552.8 26.8 %collective-permute-start.35 = (bf16[64,4096]{1,0:T(8,128)(2,1)}, bf16[64,4096]{1,0:T(8,128)(2,1)}, u32[]{:S(2)}, u32[]{:S(2)}) collective-permute-start(bf16[64,4096]{1,0:T(8,128)(2,1)} %fusion.3), channel_id=1, source_target_pairs={{0,16},{1,17},{2,18},{3,19},{4,20},{5,21},{6,22},{7,23},{8,24},{9,... | collective-permute-start | bytes 1572872 | tf_op jit(solution)/shard_map/ppermute | solution.py:1120
  565.0 43.5 %collective-permute-start.31 = (bf16[1024,1024]{1,0:T(8,128)(2,1)S(1)}, bf16[1024,1024]{1,0:T(8,128)(2,1)}, u32[]{:S(2)}, u32[]{:S(2)}) collective-permute-start(bf16[1024,1024]{1,0:T(8,128)(2,1)S(1)} %copy-done), channel_id=1, source_target_pairs={{2,8},{3,9},{6,12},{7,13},{8,2},{9,3},{12,6},{13,7},{18,24},{19,25... | collective-permute-start | bytes 6291464 | tf_op jit(solution)/shard_map/ppermute | solution.py:1120
  (42 other events, 382.7 us)
Sparse Core Ops, SparseCore 0:
  10.7 63.0 all-gather.2
  108.3 77.4 all-gather.4

commit v8 on v7

--- a/solution.py
+++ b/solution.py
@@ -1233,12 +1233,12 @@
     proj_send = weight_call(mixed, grad_attn, 1 - core, side)
     proj_came = exchange(proj_send, "c")
     output = swapped(layer_output, after(output_came, proj_send))
-    grad_a, sums_a = attn_bwd(qkv, after(grad_mixed, proj_send, output), log_sum, seg, 0)
+    down_one = join_kept(down_kept, came_d, output)
+    away_d, came_d = halve(at, down_one, "z1")
+    grad_a, sums_a = attn_bwd(qkv, after(grad_mixed, proj_send, away_d), log_sum, seg, 0)
     send_a = weight_call(tok, grad_a, 1 - core, side)
     came_a = exchange(send_a, "c")
-    down_one = join_kept(down_kept, came_d, send_a)
-    away_d, came_d = halve(at, down_one, "z1")
-    away_p, proj_kept = weight_call(mixed, after(grad_attn, away_d), core, side, proj_came)
+    away_p, proj_kept = weight_call(mixed, after(grad_attn, send_a), core, side, proj_came)
     came_p = exchange(away_p, "y")
     away_a, a_kept = weight_call(tok, after(grad_a, away_p), core, side, came_a)
     came_one = exchange(away_a, "y")

time: 625 us -> 630 us (level)
  starting transfers between devices: 44.2 us -> 54.8 us
    ppermute x41, starting transfers between devices: 44.1 us -> 54.8 us  [exchange(): return lax.ppermute(value, ('rep', 'fsdp'), xor_pairs(bits))]
  transfers between devices with their start and end apart: 43 -> 43, of which waited for: 7 -> 7; matrix products, arithmetic and copies ran while one was open for 12% -> 12% of each run, Pallas kernels for 66% -> 65%
where the time goes in v8:
time: 630 us; the launch traced here: 623 us
  Pallas kernels  433 us (69%)
  starting transfers between devices  54.8 us (9%)
  other arithmetic  48.9 us (8%)
  waiting for transfers between devices  40.5 us (6%)
  local copies, waits for them, and re-layouts  31 us (5%)
  between operations  15.1 us (2%)
    pallas_call x1, Pallas kernels, gather_all(): pl.pallas_call(gather_kernel, out_shape=(shape((8 * qkv.shape[0], qkv.sha...  91.8 us
    pallas_call x10, Pallas kernels, weight_call(): pl.pallas_call(weight_kernel, out_shape=shapes, grid_spec=pltpu.PrefetchS...  78.8 us
    pallas_call x2, Pallas kernels, attn_bwd(): pl.pallas_call(bwd_kernel, out_shape=(jax.ShapeDtypeStruct((T, width // 2...  56.8 us
    ppermute x41, starting transfers between devices, exchange(): return lax.ppermute(value, ('rep', 'fsdp'), xor_pairs(bits))  54.8 us
    pallas_call x1, Pallas kernels, attn_fwd(): pl.pallas_call(fwd_kernel, out_shape=(jax.ShapeDtypeStruct((T, width // 3...  44.7 us
    ppermute x41, waiting for transfers between devices, exchange(): return lax.ppermute(value, ('rep', 'fsdp'), xor_pairs(bits))  40.4 us
    pallas_call x1, Pallas kernels, up_call(): pl.pallas_call(up_kernel, out_shape=(SHAPE((t, FF), BF), SHAPE((t, FF), B...  34.3 us
    convert_element_type x17, other arithmetic, add_low(): (left.astype(jnp.float32) + right.astype(jnp.float32)).astype(jnp.bfloat16)  23 us
  transfers between devices with their start and end apart: 43, of which 7 were waited for; matrix products, arithmetic and copies ran while one was open for 12% of the time, Pallas kernels for 65%

profile of v8, /device:TPU:1, one launch (start us, length us, event | category | flops | bytes accessed | tf_op | source)
XLA Modules:
  0.0 623.5 jit_solution(11803342572021643152)
XLA Ops:
  14.2 91.8 %gather_weights.1 = (bf16[1024,3072]{1,0:T(8,128)(2,1)}, bf16[1024,1024]{1,0:T(8,128)(2,1)}, bf16[8,12,128]{2,1,0:T(8,128)(2,1)}, bf16[1024,1024]{1,0:T(8,128)(2,1)}, s32[1,1024]{1,0:T(1,128)}) custom-call(bf16[128,3072]{1,0:T(8,128)(2,1)} %copy.76.qkv_in, bf16[128,1024]{1,0:T(8,128)(2,1)} %slice_bitcast_fusion.1.wo_in, ...), custom_call_target="tpu_custom_call" | custom-call | tf_op jit(solution)/shard_map/gather_weights/pallas_call | solution.py:679
  115.7 10.8 %qkv.1.qkv_ref = bf16[1024,3072]{1,0:T(8,128)(2,1)} custom-call(bf16[1024,1024]{1,0:T(8,128)(2,1)} %get-tuple-element.119.x_ref.refs_0_.refs_1_.refs_2_.refs_3_, bf16[1024,3072]{1,0:T(8,128)(2,1)} %get-tuple-element.120.w_ref, f32[1,3072]{1,0:T(1,128)} %reshape.185.bias_ref, f32[1,3072]{1,0:T(1,128)} %constant.178.clone.1.scale_ref), custom_call_target="tpu_custom_call" | custom-call | flops 6442450 | bytes 14680 | tf_op jit(solution)/shard_map/qkv/pallas_call | solution.py:725
  127.2 44.7 %attn_fwd.1 = (bf16[1024,1024]{1,0:T(8,128)(2,1)}, f32[8,2,1024]{2,1,0:T(2,128)}) custom-call(s32[4]{0:T(128)} %get-tuple-element.222.start_ref, s32[4]{0:T(128)} %get-tuple-element.223.count_ref, bf16[1024,3072]{1,0:T(8,128)(2,1)} %qkv.1.qkv_ref, s32[1,1024]{1,0:T(1,128)} %get-tuple-element.118.segr_ref, s32[1024,1]{1,0:T(8,128)} %copy.77.segc_ref), custom_call_target="tpu_custom_call" | custom-call | flops 64424508 | bytes 9437 | tf_op jit(solution)/shard_map/attn_fwd/pallas_call | solution.py:413
  175.6 8.1 %mix_norm.1 = (f32[1024,1024]{1,0:T(8,128)}, f32[1024,1]{1,0:T(8,128)}, bf16[1024,1024]{1,0:T(8,128)(2,1)}) custom-call(bf16[1024,1024]{1,0:T(8,128)(2,1)} %get-tuple-element.122.c_ref.refs_0_.refs_1_.refs_2_.refs_3_, bf16[1024,1024]{1,0:T(8,128)(2,1)} %get-tuple-element.123.w_ref.refs_11_, ...), custom_call_target="tpu_custom_call" | custom-call | flops 2147483 | bytes 14680 | tf_op jit(solution)/shard_map/mix_norm/pallas_call | solution.py:758
  187.5 34.3 %up_gelu.1 = (bf16[1024,4096]{1,0:T(8,128)(2,1)}, bf16[1024,4096]{1,0:T(8,128)(2,1)}) custom-call(s32[4]{0:T(128)} %pad_add_fusion.place_ref, bf16[1024,1024]{1,0:T(8,128)(2,1)} %get-tuple-element.127.h_ref.refs_0_.refs_1_.refs_2_.refs_3_, bf16[1024,1024]{1,0:T(8,128)(2,1)} %all-gather.3.cloned.1.call-done.refs_0_.refs_4_, ...), custom_call_target="tpu_custom_call" | custom-call | flops 8589934 | bytes 27262 | tf_op jit(solution)/shard_map/up_gelu/pallas_call | solution.py:795
  223.0 6.5 %collective-permute-done.4.came_ref = bf16[4096,512]{1,0:T(8,128)(2,1)} collective-permute-done((bf16[4096,512]{1,0:T(8,128)(2,1)}, bf16[4096,512]{1,0:T(8,128)(2,1)}, u32[]{:S(2)}, u32[]{:S(2)}) %collective-permute-start.4) | collective-permute-done | bytes 4194336 | tf_op jit(solution)/shard_map/ppermute | solution.py:1120
  229.5 19.9 %down_norm.1 = (bf16[1024,1024]{1,0:T(8,128)(2,1)}, f32[1024,1024]{1,0:T(8,128)}, bf16[1024,1024]{1,0:T(8,128)(2,1)}, f32[8,1024]{1,0:T(8,128)}) custom-call(s32[1]{0:T(128)} %bitcast.core_ref, bf16[1024,4096]{1,0:T(8,128)(2,1)} %get-tuple-element.131.g_ref.refs_0_.refs_1_.refs_2_.refs_3_, bf16[4096,512]{1,0:T(8,128)(2,1)} %all-gather.5.cloned.1.call-done.own_ref, ...), custom_call_target="tpu_custom_call" | custom-call | flops 8589934 | bytes 31457 | tf_op jit(solution)/shard_map/down_norm/pallas_call | solution.py:848
  249.4 9.3 %weight_grad.10 = bf16[2048,1024]{1,0:T(8,128)(2,1)} custom-call(s32[2]{0:T(128)} %pad_add_fusion.1.at_ref, bf16[1024,4096]{1,0:T(8,128)(2,1)} %get-tuple-element.131.g_ref.refs_0_.refs_1_.refs_2_.refs_3_, bf16[1024,4096]{1,0:T(8,128)(2,1)} %get-tuple-element.131.g_ref.refs_0_.refs_1_.refs_2_.refs_3_, ...), custom_call_target="tpu_custom_call" | custom-call | flops 4294967 | bytes 14680 | tf_op jit(solution)/shard_map/weight_grad/pallas_call | solution.py:1028
  259.1 16.2 %down_back.1 = (bf16[1024,4096]{1,0:T(8,128)(2,1)}, f32[1,4096]{1,0:T(1,128)}) custom-call(s32[1]{0:T(128)} %bitcast.core_ref, bf16[1024,1024]{1,0:T(8,128)(2,1)} %get-tuple-element.140.refs_4_.left_ref.right_ref, bf16[1024,1024]{1,0:T(8,128)(2,1)} %get-tuple-element.140.refs_4_.left_ref.right_ref, bf16[4096,512]{1,0:T(8,128)(2,1)} %all-gather.5.cloned.1.call-done.own_ref, ...), custom_call_target="tpu_custom_call" | custom-call | flops 8589934 | bytes 27262 | tf_op jit(solution)/shard_map/down_back/pallas_call | solution.py:881
  275.3 11.7 %weight_grad.11 = bf16[512,4096]{1,0:T(8,128)(2,1)} custom-call(s32[2]{0:T(128)} %pad_add_fusion.1.at_ref, bf16[1024,1024]{1,0:T(8,128)(2,1)} %get-tuple-element.127.h_ref.refs_0_.refs_1_.refs_2_.refs_3_, bf16[1024,1024]{1,0:T(8,128)(2,1)} %get-tuple-element.127.h_ref.refs_0_.refs_1_.refs_2_.refs_3_, ...), custom_call_target="tpu_custom_call" | custom-call | flops 4294967 | bytes 17825 | tf_op jit(solution)/shard_map/weight_grad/pallas_call | solution.py:1028
  289.6 10.7 %weight_grad.12 = (bf16[1024,1024]{1,0:T(8,128)(2,1)}, bf16[1024,1024]{1,0:T(8,128)(2,1)}) custom-call(s32[2]{0:T(128)} %pad_add_fusion.2.at_ref, bf16[1024,4096]{1,0:T(8,128)(2,1)} %get-tuple-element.131.g_ref.refs_0_.refs_1_.refs_2_.refs_3_, bf16[1024,4096]{1,0:T(8,128)(2,1)} %get-tuple-element.131.g_ref.refs_0_.refs_1_.refs_2_.refs_3_, ...), custom_call_target="tpu_custom_call" | custom-call | flops 4294967 | bytes 14680 | tf_op jit(solution)/shard_map/weight_grad/pallas_call | solution.py:1028
  302.0 11.9 %weight_grad.13 = (bf16[256,4096]{1,0:T(8,128)(2,1)}, bf16[256,4096]{1,0:T(8,128)(2,1)}) custom-call(s32[2]{0:T(128)} %pad_add_fusion.2.at_ref, bf16[1024,1024]{1,0:T(8,128)(2,1)} %get-tuple-element.127.h_ref.refs_0_.refs_1_.refs_2_.refs_3_, bf16[1024,1024]{1,0:T(8,128)(2,1)} %get-tuple-element.127.h_ref.refs_0_.refs_1_.refs_2_.refs_3_, ...), custom_call_target="tpu_custom_call" | custom-call | flops 4294967 | bytes 17825 | tf_op jit(solution)/shard_map/weight_grad/pallas_call | solution.py:1028
  314.0 22.1 %up_back_norm.1 = (f32[1024,1024]{1,0:T(8,128)}, bf16[1024,1024]{1,0:T(8,128)(2,1)}, bf16[1024,1024]{1,0:T(8,128)(2,1)}, f32[8,1024]{1,0:T(8,128)}) custom-call(s32[4]{0:T(128)} %pad_add_fusion.place_ref, bf16[1024,4096]{1,0:T(8,128)(2,1)} %get-tuple-element.144.refs_4_.refs_0_.refs_1_.refs_2_.refs_3_, ...), custom_call_target="tpu_custom_call" | custom-call | flops 10737418 | bytes 33554 | tf_op jit(solution)/shard_map/up_back_norm/pallas_call | solution.py:927
  351.5 28.4 %attn_bwd.2 = (bf16[1024,1536]{1,0:T(8,128)(2,1)}, f32[4,1,384]{2,1,0:T(1,128)}) custom-call(s32[4]{0:T(128)} %get-tuple-element.222.start_ref, s32[4]{0:T(128)} %get-tuple-element.223.count_ref, bf16[1024,3072]{1,0:T(8,128)(2,1)} %qkv.1.qkv_ref, bf16[1024,1024]{1,0:T(8,128)(2,1)} %get-tuple-element.161.do_ref, f32[8,2,1024]{2,1,0:T(2,128)} %get-tuple-element.153.lse_ref, ...), custom_call_target="tpu_custom_call" | custom-call | flops 64424508 | bytes 18874 | tf_op jit(solution)/shard_map/attn_bwd/pallas_call | solution.py:437
  379.9 6.3 %weight_grad.15 = bf16[512,1536]{1,0:T(8,128)(2,1)} custom-call(s32[2]{0:T(128)} %pad_add_fusion.1.at_ref, bf16[1024,1024]{1,0:T(8,128)(2,1)} %get-tuple-element.119.x_ref.refs_0_.refs_1_.refs_2_.refs_3_, bf16[1024,1024]{1,0:T(8,128)(2,1)} %get-tuple-element.119.x_ref.refs_0_.refs_1_.refs_2_.refs_3_, ...), custom_call_target="tpu_custom_call" | custom-call | flops 1610612 | bytes 7340 | tf_op jit(solution)/shard_map/weight_grad/pallas_call | solution.py:1028
  400.8 6.4 %weight_grad.17 = (bf16[256,1536]{1,0:T(8,128)(2,1)}, bf16[256,1536]{1,0:T(8,128)(2,1)}) custom-call(s32[2]{0:T(128)} %pad_add_fusion.2.at_ref, bf16[1024,1024]{1,0:T(8,128)(2,1)} %get-tuple-element.119.x_ref.refs_0_.refs_1_.refs_2_.refs_3_, bf16[1024,1024]{1,0:T(8,128)(2,1)} %get-tuple-element.119.x_ref.refs_0_.refs_1_.refs_2_.refs_3_, ...), custom_call_target="tpu_custom_call" | custom-call | flops 1610612 | bytes 7340 | tf_op jit(solution)/shard_map/weight_grad/pallas_call | solution.py:1028
  413.3 28.4 %attn_bwd.3 = (bf16[1024,1536]{1,0:T(8,128)(2,1)}, f32[4,1,384]{2,1,0:T(1,128)}) custom-call(s32[4]{0:T(128)} %get-tuple-element.222.start_ref, s32[4]{0:T(128)} %get-tuple-element.223.count_ref, bf16[1024,3072]{1,0:T(8,128)(2,1)} %qkv.1.qkv_ref, bf16[1024,1024]{1,0:T(8,128)(2,1)} %get-tuple-element.161.do_ref, f32[8,2,1024]{2,1,0:T(2,128)} %get-tuple-element.153.lse_ref, ...), custom_call_target="tpu_custom_call" | custom-call | flops 64424508 | bytes 18874 | tf_op jit(solution)/shard_map/attn_bwd/pallas_call | solution.py:437
  450.8 12.8 %collective-permute-done.14 = bf16[512,1024]{1,0:T(8,128)(2,1)} collective-permute-done((bf16[512,1024]{1,0:T(8,128)(2,1)}, bf16[512,1024]{1,0:T(8,128)(2,1)}, u32[]{:S(2)}, u32[]{:S(2)}) %collective-permute-start.14) | collective-permute-done | bytes 1048608 | tf_op jit(solution)/shard_map/ppermute | solution.py:1120
  478.7 6.4 %weight_grad.19 = (bf16[256,1536]{1,0:T(8,128)(2,1)}, bf16[256,1536]{1,0:T(8,128)(2,1)}) custom-call(s32[2]{0:T(128)} %pad_add_fusion.2.at_ref, bf16[1024,1024]{1,0:T(8,128)(2,1)} %get-tuple-element.119.x_ref.refs_0_.refs_1_.refs_2_.refs_3_, bf16[1024,1024]{1,0:T(8,128)(2,1)} %get-tuple-element.119.x_ref.refs_0_.refs_1_.refs_2_.refs_3_, ...), custom_call_target="tpu_custom_call" | custom-call | flops 1610612 | bytes 7340 | tf_op jit(solution)/shard_map/weight_grad/pallas_call | solution.py:1028
  485.0 8.6 %collective-permute-done.18 = bf16[512,1024]{1,0:T(8,128)(2,1)S(1)} collective-permute-done((bf16[512,1024]{1,0:T(8,128)(2,1)S(1)}, bf16[512,1024]{1,0:T(8,128)(2,1)S(1)}, u32[]{:S(2)}, u32[]{:S(2)}) %collective-permute-start.18) | collective-permute-done | bytes 1048608 | tf_op jit(solution)/shard_map/ppermute | solution.py:1120
  519.0 12.3 %input_back.1 = bf16[1024,1024]{1,0:T(8,128)(2,1)} custom-call(bf16[1024,1536]{1,0:T(8,128)(2,1)} %get-tuple-element.176.refs_4_.a_ref, bf16[1024,1536]{1,0:T(8,128)(2,1)} %get-tuple-element.168.refs_4_.b_ref, bf16[1024,3072]{1,0:T(8,128)(2,1)} %get-tuple-element.120.w_ref, f32[1024,1024]{1,0:T(8,128)} %get-tuple-element.177.r_ref), custom_call_target="tpu_custom_call" | custom-call | flops 6442450 | bytes 18874 | tf_op jit(solution)/shard_map/input_back/pallas_call | solution.py:953
  561.0 6.3 %outer_step.3 = (f32[3,512,1024]{2,1,0:T(8,128)}, bf16[512,1024]{1,0:T(8,128)(2,1)}) custom-call(s32[1]{0:T(128)} %bitcast.core_ref, f32[512,1024]{1,0:T(8,128)} %w_ref.6, f32[512,1024]{1,0:T(8,128)} %u_ref.2, bf16[256,1024]{1,0:T(8,128)(2,1)} %copy-done.7, bf16[256,1024]{1,0:T(8,128)(2,1)} %copy-done.17), custom_call_target="tpu_custom_call" | custom-call | flops 5242 | bytes 13631 | tf_op jit(solution)/shard_map/outer_step/pallas_call | solution.py:1083
  588.0 6.4 %outer_step.4 = (f32[3,128,4096]{2,1,0:T(8,128)}, bf16[128,4096]{1,0:T(8,128)(2,1)}) custom-call(s32[1]{0:T(128)} %bitcast.core_ref, f32[128,4096]{1,0:T(8,128)} %w_ref.7, f32[128,4096]{1,0:T(8,128)} %u_ref.3, bf16[64,4096]{1,0:T(8,128)(2,1)} %copy-done.8, bf16[64,4096]{1,0:T(8,128)(2,1)} %collective-permute-done.38.came_ref), custom_call_target="tpu_custom_call" | custom-call | flops 5242 | bytes 13631 | tf_op jit(solution)/shard_map/outer_step/pallas_call | solution.py:1083
  607.0 6.3 %outer_step.5 = (f32[3,512,1024]{2,1,0:T(8,128)}, bf16[512,1024]{1,0:T(8,128)(2,1)}) custom-call(s32[1]{0:T(128)} %bitcast.core_ref, f32[512,1024]{1,0:T(8,128)} %bitcast.123, f32[512,1024]{1,0:T(8,128)} %bitcast.143, bf16[256,1024]{1,0:T(8,128)(2,1)} %copy-done.6, bf16[256,1024]{1,0:T(8,128)(2,1)} %copy-done.16), custom_call_target="tpu_custom_call" | custom-call | flops 5242 | bytes 13631 | tf_op jit(solution)/shard_map/outer_step/pallas_call | solution.py:1083
  (248 shorter events, 181.8 us)
Async XLA Ops:
  7.2 101.0 %all-gather.3.cloned.1.call-start = ((), (), s32[]{:S(2)}) async-start(), calls=%async_computation | async-start | bytes 2359296 | tf_op jit(solution)/shard_map/all_gather | solution.py:1192
  9.1 212.8 %all-gather.5.cloned.1.call-start = ((), (), s32[]{:S(2)}) async-start(), calls=%async_computation.1 | async-start | bytes 4718592 | tf_op jit(solution)/shard_map/all_gather | solution.py:1206
  108.2 66.0 %collective-permute-start.2 = (bf16[1024,1024]{1,0:T(8,128)(2,1)}, bf16[1024,1024]{1,0:T(8,128)(2,1)}, u32[]{:S(2)}, u32[]{:S(2)}) collective-permute-start(bf16[1024,1024]{1,0:T(8,128)(2,1)} %all-gather.3.cloned.1.call-done.refs_0_.refs_4_), channel_id=1, source_target_pairs={{0,16},{1,17},{2,18},{3,19},{4,20},{5,21},{6,22},{7,23},{8,24},{9,... | collective-permute-start | bytes 6291464 | tf_op jit(solution)/shard_map/ppermute | solution.py:1120
  108.5 75.9 %collective-permute-start = (bf16[1024,1024]{1,0:T(8,128)(2,1)}, bf16[1024,1024]{1,0:T(8,128)(2,1)}, u32[]{:S(2)}, u32[]{:S(2)}) collective-permute-start(bf16[1024,1024]{1,0:T(8,128)(2,1)} %param.20), channel_id=1, source_target_pairs={{2,8},{3,9},{6,12},{7,13},{8,2},{9,3},{12,6},{13,7},{18,24},{19,25... | collective-permute-start | bytes 6291464 | tf_op jit(solution)/shard_map/ppermute | solution.py:1120
  258.7 30.9 %collective-permute-start.6 = (bf16[2048,1024]{1,0:T(8,128)(2,1)}, bf16[2048,1024]{1,0:T(8,128)(2,1)}, u32[]{:S(2)}, u32[]{:S(2)}) collective-permute-start(bf16[2048,1024]{1,0:T(8,128)(2,1)} %weight_grad.10), channel_id=1, source_target_pairs={{0,8},{1,9},{2,10},{3,11},{4,12},{5,13},{6,14},{7,15},{8,0},{9,1},... | collective-permute-start | bytes 12582920 | tf_op jit(solution)/shard_map/ppermute | solution.py:1120
  287.1 53.9 %collective-permute-start.5 = (bf16[1024,1024]{1,0:T(8,128)(2,1)S(1)}, bf16[1024,1024]{1,0:T(8,128)(2,1)}, u32[]{:S(2)}, u32[]{:S(2)}) collective-permute-start(bf16[1024,1024]{1,0:T(8,128)(2,1)S(1)} %copy-done.4), channel_id=1, source_target_pairs={{2,8},{3,9},{6,12},{7,13},{8,2},{9,3},{12,6},{13,7},{18,24},{19,25... | collective-permute-start | bytes 6291464 | tf_op jit(solution)/shard_map/ppermute | solution.py:1120
  300.3 47.6 %collective-permute-start.8 = (bf16[1024,1024]{1,0:T(8,128)(2,1)}, bf16[1024,1024]{1,0:T(8,128)(2,1)}, u32[]{:S(2)}, u32[]{:S(2)}) collective-permute-start(bf16[1024,1024]{1,0:T(8,128)(2,1)} %get-tuple-element.141), channel_id=1, source_target_pairs={{0,1},{1,0},{2,3},{3,2},{4,5},{5,4},{6,7},{7,6},{8,9},{9,8},{10,11... | collective-permute-start | bytes 6291464 | tf_op jit(solution)/shard_map/ppermute | solution.py:1120
  313.9 93.2 %collective-permute-start.9 = (bf16[256,4096]{1,0:T(8,128)(2,1)}, bf16[256,4096]{1,0:T(8,128)(2,1)}, u32[]{:S(2)}, u32[]{:S(2)}) collective-permute-start(bf16[256,4096]{1,0:T(8,128)(2,1)} %get-tuple-element.143), channel_id=1, source_target_pairs={{0,1},{1,0},{2,3},{3,2},{4,5},{5,4},{6,7},{7,6},{8,9},{9,8},{10,11... | collective-permute-start | bytes 6291464 | tf_op jit(solution)/shard_map/ppermute | solution.py:1120
  392.4 71.1 %collective-permute-start.14 = (bf16[512,1024]{1,0:T(8,128)(2,1)}, bf16[512,1024]{1,0:T(8,128)(2,1)}, u32[]{:S(2)}, u32[]{:S(2)}) collective-permute-start(bf16[512,1024]{1,0:T(8,128)(2,1)} %dynamic-slice_bitcast_fusion.1), channel_id=1, source_target_pairs={{0,4},{1,5},{2,6},{3,7},{4,0},{5,1},{6,2},{7,3},{8,12},{9,13},{10,... | collective-permute-start | bytes 3145736 | tf_op jit(solution)/shard_map/ppermute | solution.py:1120
  399.3 67.8 %collective-permute-start.13 = (bf16[256,1024]{1,0:T(8,128)(2,1)}, bf16[256,1024]{1,0:T(8,128)(2,1)}, u32[]{:S(2)}, u32[]{:S(2)}) collective-permute-start(bf16[256,1024]{1,0:T(8,128)(2,1)} %get-tuple-element.157), channel_id=1, source_target_pairs={{0,1},{1,0},{2,3},{3,2},{4,5},{5,4},{6,7},{7,6},{8,9},{9,8},{10,11... | collective-permute-start | bytes 1572872 | tf_op jit(solution)/shard_map/ppermute | solution.py:1120
  407.1 66.3 %collective-permute-start.12 = (bf16[256,1536]{1,0:T(8,128)(2,1)}, bf16[256,1536]{1,0:T(8,128)(2,1)}, u32[]{:S(2)}, u32[]{:S(2)}) collective-permute-start(bf16[256,1536]{1,0:T(8,128)(2,1)} %get-tuple-element.159), channel_id=1, source_target_pairs={{0,1},{1,0},{2,3},{3,2},{4,5},{5,4},{6,7},{7,6},{8,9},{9,8},{10,11... | collective-permute-start | bytes 2359304 | tf_op jit(solution)/shard_map/ppermute | solution.py:1120
  412.5 90.9 %collective-permute-start.17 = (bf16[128,4096]{1,0:T(8,128)(2,1)}, bf16[128,4096]{1,0:T(8,128)(2,1)}, u32[]{:S(2)}, u32[]{:S(2)}) collective-permute-start(bf16[128,4096]{1,0:T(8,128)(2,1)} %dynamic-slice_bitcast_fusion), channel_id=1, source_target_pairs={{0,4},{1,5},{2,6},{3,7},{4,0},{5,1},{6,2},{7,3},{8,12},{9,13},{10,... | collective-permute-start | bytes 3145736 | tf_op jit(solution)/shard_map/ppermute | solution.py:1120
  447.9 28.3 %collective-permute-start.15 = (bf16[512,1536]{1,0:T(8,128)(2,1)}, bf16[512,1536]{1,0:T(8,128)(2,1)}, u32[]{:S(2)}, u32[]{:S(2)}) collective-permute-start(bf16[512,1536]{1,0:T(8,128)(2,1)} %weight_grad.18), channel_id=1, source_target_pairs={{0,8},{1,9},{2,10},{3,11},{4,12},{5,13},{6,14},{7,15},{8,0},{9,1},... | collective-permute-start | bytes 4718600 | tf_op jit(solution)/shard_map/ppermute | solution.py:1120
  465.2 28.5 %collective-permute-start.18 = (bf16[512,1024]{1,0:T(8,128)(2,1)S(1)}, bf16[512,1024]{1,0:T(8,128)(2,1)S(1)}, u32[]{:S(2)}, u32[]{:S(2)}) collective-permute-start(bf16[512,1024]{1,0:T(8,128)(2,1)S(1)} %fusion.1), channel_id=1, source_target_pairs={{2,8},{3,9},{6,12},{7,13},{8,2},{9,3},{12,6},{13,7},{18,24},{19,25... | collective-permute-start | bytes 3145736 | tf_op jit(solution)/shard_map/ppermute | solution.py:1120
  469.3 76.9 %collective-permute-start.27 = (bf16[128,1024]{0,1:T(8,128)(2,1)}, bf16[128,1024]{0,1:T(8,128)(2,1)}, u32[]{:S(2)}, u32[]{:S(2)}) collective-permute-start(bf16[128,1024]{0,1:T(8,128)(2,1)} %bitcast.24), channel_id=1, source_target_pairs={{0,4},{1,5},{2,6},{3,7},{4,0},{5,1},{6,2},{7,3},{8,12},{9,13},{10,... | collective-permute-start | bytes 786440 | tf_op jit(solution)/shard_map/ppermute | solution.py:1120
  473.5 33.6 %collective-permute-start.24 = (f32[12,512]{1,0:T(8,128)}, f32[12,512]{1,0:T(8,128)}, u32[]{:S(2)}, u32[]{:S(2)}) collective-permute-start(f32[12,512]{1,0:T(8,128)} %constant_dynamic-slice_fusion.4), channel_id=1, source_target_pairs={{0,4},{1,5},{2,6},{3,7},{4,0},{5,1},{6,2},{7,3},{8,12},{9,13},{10,... | collective-permute-start | bytes 73736 | tf_op jit(solution)/shard_map/ppermute | solution.py:1120
  476.3 69.8 %collective-permute-start.28 = (bf16[128,1536]{0,1:T(8,128)(2,1)}, bf16[128,1536]{0,1:T(8,128)(2,1)}, u32[]{:S(2)}, u32[]{:S(2)}) collective-permute-start(bf16[128,1536]{0,1:T(8,128)(2,1)} %bitcast.153), channel_id=1, source_target_pairs={{0,4},{1,5},{2,6},{3,7},{4,0},{5,1},{6,2},{7,3},{8,12},{9,13},{10,... | collective-permute-start | bytes 1179656 | tf_op jit(solution)/shard_map/ppermute | solution.py:1120
  507.1 24.3 %collective-permute-start.21 = (bf16[128,4096]{1,0:T(8,128)(2,1)S(1)}, bf16[128,4096]{1,0:T(8,128)(2,1)}, u32[]{:S(2)}, u32[]{:S(2)}) collective-permute-start(bf16[128,4096]{1,0:T(8,128)(2,1)S(1)} %fusion), channel_id=1, source_target_pairs={{2,8},{3,9},{6,12},{7,13},{8,2},{9,3},{12,6},{13,7},{18,24},{19,25... | collective-permute-start | bytes 3145736 | tf_op jit(solution)/shard_map/ppermute | solution.py:1120
  514.2 40.7 %collective-permute-start.23 = (bf16[256,1024]{1,0:T(8,128)(2,1)S(1)}, bf16[256,1024]{1,0:T(8,128)(2,1)}, u32[]{:S(2)}, u32[]{:S(2)}) collective-permute-start(bf16[256,1024]{1,0:T(8,128)(2,1)S(1)} %fusion.4), channel_id=1, source_target_pairs={{0,16},{1,17},{2,18},{3,19},{4,20},{5,21},{6,22},{7,23},{8,24},{9,... | collective-permute-start | bytes 1572872 | tf_op jit(solution)/shard_map/ppermute | solution.py:1120
  515.7 41.5 %collective-permute-start.20 = (bf16[128,1536]{0,1:T(8,128)(2,1)}, bf16[128,1536]{0,1:T(8,128)(2,1)}, u32[]{:S(2)}, u32[]{:S(2)}) collective-permute-start(bf16[128,1536]{0,1:T(8,128)(2,1)} %bitcast.154), channel_id=1, source_target_pairs={{0,4},{1,5},{2,6},{3,7},{4,0},{5,1},{6,2},{7,3},{8,12},{9,13},{10,... | collective-permute-start | bytes 1179656 | tf_op jit(solution)/shard_map/ppermute | solution.py:1120
  531.4 19.8 %collective-permute-start.26 = (f32[12,128]{1,0:T(8,128)S(1)}, f32[12,128]{1,0:T(8,128)S(1)}, u32[]{:S(2)}, u32[]{:S(2)}) collective-permute-start(f32[12,128]{1,0:T(8,128)S(1)} %constant_dynamic-slice_fusion.2), channel_id=1, source_target_pairs={{0,1},{1,0},{2,3},{3,2},{4,5},{5,4},{6,7},{7,6},{8,9},{9,8},{10,11... | collective-permute-start | bytes 18440 | tf_op jit(solution)/shard_map/ppermute | solution.py:1120
  549.3 18.1 %collective-permute-start.32 = (bf16[128,2560]{0,1:T(8,128)(2,1)}, bf16[128,2560]{0,1:T(8,128)(2,1)}, u32[]{:S(2)}, u32[]{:S(2)}) collective-permute-start(bf16[128,2560]{0,1:T(8,128)(2,1)} %pad_maximum_fusion.2), channel_id=1, source_target_pairs={{2,8},{3,9},{6,12},{7,13},{8,2},{9,3},{12,6},{13,7},{18,24},{19,25... | collective-permute-start | bytes 1966088 | tf_op jit(solution)/shard_map/ppermute | solution.py:1120
  557.2 27.2 %collective-permute-start.35 = (bf16[64,4096]{1,0:T(8,128)(2,1)}, bf16[64,4096]{1,0:T(8,128)(2,1)}, u32[]{:S(2)}, u32[]{:S(2)}) collective-permute-start(bf16[64,4096]{1,0:T(8,128)(2,1)} %fusion.3), channel_id=1, source_target_pairs={{0,16},{1,17},{2,18},{3,19},{4,20},{5,21},{6,22},{7,23},{8,24},{9,... | collective-permute-start | bytes 1572872 | tf_op jit(solution)/shard_map/ppermute | solution.py:1120
  570.9 42.4 %collective-permute-start.31 = (bf16[1024,1024]{1,0:T(8,128)(2,1)S(1)}, bf16[1024,1024]{1,0:T(8,128)(2,1)}, u32[]{:S(2)}, u32[]{:S(2)}) collective-permute-start(bf16[1024,1024]{1,0:T(8,128)(2,1)S(1)} %copy-done), channel_id=1, source_target_pairs={{2,8},{3,9},{6,12},{7,13},{8,2},{9,3},{12,6},{13,7},{18,24},{19,25... | collective-permute-start | bytes 6291464 | tf_op jit(solution)/shard_map/ppermute | solution.py:1120
  (51 other events, 455.5 us)
Sparse Core Ops, SparseCore 0:
  10.7 63.0 all-gather.2
  108.3 77.9 all-gather.4
